TPU v7x, 128 devices: a whole 4x4x4 slice. The times are simulated.
128 devices in a mesh: leaf: 32 (over z, y, core), front: 4 (over x).
Axes of the slice: x: 4, y: 4, z: 4, core: 2. Of those that a mesh axis runs over, the one named last changes fastest.
Arguments:
- right_side: float32 [32, 4, 96, 512], P('leaf', 'front'), may hold values from -6 to 6
- factor_inverse: float32 [32, 4, 128, 7680], P('leaf', 'front'), may hold values from -1 to 1, as said below
- update_panel: float32 [32, 4, 128, 1792], P('leaf', 'front'), may hold values from -0.09375 to 0.09375
- update_targets: int32 [32, 14], P('leaf'), may hold values from 0 to 31, as said below
- pivot_pairs: int32 [32, 4, 256], P('leaf', 'front'), may hold values 0 or 1
- pivot_diagonal: float32 [32, 4, 512], P('leaf', 'front'), may hold values from 0.5 to 2
- pivot_coupling: float32 [32, 4, 256], P('leaf', 'front'), may hold values from 3 to 5
Outputs:
- solution: float32 [32, 4, 96, 512], P('leaf', 'front')
Inputs may be any that keep to these rules, and one draw needn't show every extreme that they name: `factor_inverse`: each front's inverse factor is lower triangular in the front's row order with ones on its diagonal. `update_targets`: each front's list names distinct blocks of its parent's pivot rows in rising order, and is repeated in the row of every leaf index of the front's group.
All inputs are finite; a program needn't handle non-finite values. No bound on the sum of `pivot_pairs` on one device may be relied on, other than what follows from the above.
Results may differ from a plain program's by a relative error of at most 0.0001.
Values sent between devices are 32-bit elements; how exact they have to be, the bound alone decides.
No kernel may reach another device: no remote copies, remote signals or barrier semaphores. Data moves between devices by JAX's collectives and lax.ppermute only.
A program may use at most 64 MiB of HBM per device.

v0:
```python
import jax
import jax.numpy as jnp
from jax import lax
from jax.sharding import PartitionSpec as P

LEVELS = 4
BLOCK = 128


exact_mode = lax.Precision.HIGHEST


def from_partner(block, axis, bit):
    count = lax.axis_size(axis)
    route = []
    for low in range(count):
        high = low | 1 << bit
        if high != low and high < count:
            route += [(low, high), (high, low)]
    return lax.ppermute(block, axis, route)


def joined_along(parts, dim):
    parts = jnp.moveaxis(parts, 0, dim)
    shape = parts.shape
    return parts.reshape(*shape[:dim], shape[dim] * shape[dim + 1], *shape[dim + 2 :])


def copy_for_each(value, axis):
    copies = jnp.broadcast_to(value, (lax.axis_size(axis), *value.shape))
    return lax.all_to_all(copies, axis, split_axis=0, concat_axis=0, tiled=True)


def gathered_copies(value, axis, dim):
    return joined_along(copy_for_each(value, axis), dim)


def in_blocks(value, dim, peers):
    shape = value.shape
    parts = value.reshape(*shape[:dim], peers, shape[dim] // peers, *shape[dim + 1 :])
    return jnp.moveaxis(parts, dim, 0)


def sum_at_owner(value, axis, dim):
    peers = lax.axis_size(axis)
    parts = lax.all_to_all(in_blocks(value, dim, peers), axis, 0, 0, tiled=True)
    return jnp.sum(parts, axis=0)


def taken_together(value, axis):
    everything = copy_for_each(value, axis)
    return jnp.sum(everything, axis=0)


def pair_gather(values, bit_count, leaf_index):
    for bit_index in range(bit_count):
        partner = from_partner(values, "leaf", bit_index)
        is_upper = leaf_index >> bit_index & 1 == 1
        values = jnp.where(
            is_upper, jnp.concatenate([partner, values], 1), jnp.concatenate([values, partner], 1)
        )
    return values


def group_gather(values, bit_count, leaf_index):
    joined = pair_gather(values, bit_count, leaf_index)
    return gathered_copies(joined, "front", 1)


def group_scatter(partial_terms, bit_count, leaf_index):
    share_sum = sum_at_owner(partial_terms, "front", 1)
    for bit_index in reversed(range(bit_count)):
        half_width = share_sum.shape[1] // 2
        lower_half = share_sum[:, :half_width]
        higher = share_sum[:, half_width:]
        is_upper = leaf_index >> bit_index & 1 == 1
        kept_half = jnp.where(is_upper, higher, lower_half)
        sent_half = jnp.where(is_upper, lower_half, higher)
        share_sum = kept_half + from_partner(sent_half, "leaf", bit_index)
    return share_sum


def update_total(partial_terms, bit_count):
    total_sum = taken_together(partial_terms, "front")
    for bit_index in range(bit_count):
        total_sum = total_sum + from_partner(total_sum, "leaf", bit_index)
    return total_sum


def chosen_total(partial_terms, bit_count):
    total_sum = taken_together(partial_terms, "front")
    for bit_index in range(bit_count):
        total_sum = total_sum + from_partner(total_sum, "leaf", bit_index)
    return total_sum


def row_offset(bit_count, which_leaf, pivots):
    group_width = 1 << bit_count
    return (lax.axis_index("front") * group_width + (which_leaf & group_width - 1)) * pivots


def own_rows(full_front, bit_count, leaf_index, pivots):
    return lax.dynamic_slice_in_dim(
        full_front, row_offset(bit_count, leaf_index, pivots), pivots, 1
    )


def put_rows(full_front, rows, bit_count, which_leaf, pivots):
    return lax.dynamic_update_slice_in_dim(
        full_front, rows, row_offset(bit_count, which_leaf, pivots), 1
    )


def block_table(target_list, parent_blocks):
    ids = jnp.arange(parent_blocks, dtype=jnp.int32)
    return (target_list[:, None] == ids[None, :]).astype(jnp.float32)


def pivot_solve(solved, pivot_diag, couple, pivot_kinds):
    side_count = solved.shape[0]
    paired = solved.reshape(side_count, -1, 2)
    pair_first = paired[:, :, 0]
    second = paired[:, :, 1]
    diag_first = pivot_diag[0::2][None, :]
    diag_second = pivot_diag[1::2][None, :]
    coupling = couple[None, :]
    pair_flag = (pivot_kinds == 1)[None, :]
    determinant = diag_first * diag_second - coupling * coupling
    two_first = (diag_second * pair_first - coupling * second) / determinant
    two_second = (diag_first * second - coupling * pair_first) / determinant
    result_first = jnp.where(pair_flag, two_first, pair_first / diag_first)
    result_second = jnp.where(pair_flag, two_second, second / diag_second)
    return jnp.stack([result_first, result_second], axis=2).reshape(solved.shape)


def per_device(
    right_side,
    factor_inverse,
    update_panel,
    update_targets,
    pivot_pairs,
    pivot_diagonal,
    pivot_coupling,
):
    right_sides = right_side[0, 0]
    inverse = factor_inverse[0, 0]
    update_rows = update_panel[0, 0]
    targets = update_targets[0]
    pivot_kinds = pivot_pairs[0, 0]
    pivot_diag = pivot_diagonal[0, 0]
    couple = pivot_coupling[0, 0]
    pivots = inverse.shape[0]
    half_pb = pivots // 2
    fronts = lax.axis_size("front")
    leaf_index = lax.axis_index("leaf")
    side_count = right_sides.shape[0]
    carried = jnp.zeros((side_count, pivots), jnp.float32)
    weighted = []
    for level_index in range(LEVELS):
        group_width = 1 << level_index
        front_span = fronts * pivots * group_width
        column_start = fronts * pivots * (group_width - 1)
        inverse_rows = inverse[:, column_start : column_start + front_span]
        own_side = right_sides[:, level_index * pivots : (level_index + 1) * pivots] - carried
        gathered = group_gather(own_side, level_index, leaf_index)
        solved = lax.dot_general(
            gathered,
            inverse_rows,
            (((1,), (1,)), ((), ())),
            precision=exact_mode,
            preferred_element_type=jnp.float32,
        )
        weighted.append(
            pivot_solve(
                solved,
                pivot_diag[level_index * pivots : (level_index + 1) * pivots],
                couple[level_index * half_pb : (level_index + 1) * half_pb],
                pivot_kinds[level_index * half_pb : (level_index + 1) * half_pb],
            )
        )
        if level_index + 1 < LEVELS:
            update_len = 2 * pivots * group_width
            update_start = 2 * pivots * (group_width - 1)
            block_count = update_len // BLOCK
            target_start = update_start // BLOCK
            onehot_table = block_table(
                targets[target_start : target_start + block_count], 2 * front_span // BLOCK
            )
            update_part = jnp.dot(
                solved,
                update_rows[:, update_start : update_start + update_len],
                precision=exact_mode,
                preferred_element_type=jnp.float32,
            )
            summed = update_total(update_part, level_index)
            spread = jnp.einsum(
                "rkc,kt->rtc",
                summed.reshape(side_count, block_count, BLOCK),
                onehot_table,
                precision=exact_mode,
            ).reshape(side_count, 2 * front_span)
            mine = own_rows(spread, level_index + 1, leaf_index, pivots)
            theirs = own_rows(spread, level_index + 1, leaf_index ^ group_width, pivots)
            carried = mine + from_partner(theirs, "leaf", level_index)
    answers = [None] * LEVELS
    for level_index in reversed(range(LEVELS)):
        group_width = 1 << level_index
        front_span = fronts * pivots * group_width
        column_start = fronts * pivots * (group_width - 1)
        inverse_rows = inverse[:, column_start : column_start + front_span]
        target = weighted[level_index]
        if level_index + 1 < LEVELS:
            update_len = 2 * pivots * group_width
            update_start = 2 * pivots * (group_width - 1)
            block_count = update_len // BLOCK
            target_start = update_start // BLOCK
            onehot_table = block_table(
                targets[target_start : target_start + block_count], 2 * front_span // BLOCK
            )
            parent_own = answers[level_index + 1]
            beside = from_partner(parent_own, "leaf", level_index)
            filled = jnp.zeros((side_count, 2 * front_span), jnp.float32)
            filled = put_rows(filled, parent_own, level_index + 1, leaf_index, pivots)
            filled = put_rows(filled, beside, level_index + 1, leaf_index ^ group_width, pivots)
            picked = jnp.einsum(
                "rtc,kt->rkc",
                filled.reshape(side_count, -1, BLOCK),
                onehot_table,
                precision=exact_mode,
            ).reshape(side_count, update_len)
            chosen = chosen_total(picked, level_index)
            target = target - lax.dot_general(
                chosen,
                update_rows[:, update_start : update_start + update_len],
                (((1,), (1,)), ((), ())),
                precision=exact_mode,
                preferred_element_type=jnp.float32,
            )
        partial_terms = jnp.dot(
            target, inverse_rows, precision=exact_mode, preferred_element_type=jnp.float32
        )
        answers[level_index] = group_scatter(partial_terms, level_index, leaf_index)
    result = jnp.concatenate(answers, 1)
    return result[None, None]


def solution(mesh):
    in_specs = (
        P("leaf", "front", None, None),
        P("leaf", "front", None, None),
        P("leaf", "front", None, None),
        P("leaf", None),
        P("leaf", "front", None),
        P("leaf", "front", None),
        P("leaf", "front", None),
    )
    out_specs = P("leaf", "front", None, None)
    return jax.shard_map(
        per_device, mesh=mesh, in_specs=in_specs, out_specs=out_specs, check_vma=False
    )
```

profile of v0, /device:TPU:1, one launch (start us, length us, event | category | flops | bytes accessed | tf_op | source)
XLA Modules:
  0.0 347.0 jit_solution(1417714473122486523)
XLA Ops:
  0.8 9.8 %all_to_all.70 = f32[4,96,128]{2,1,0:T(8,128)S(1)} all-to-all(f32[4,96,128]{2,1,0:T(8,128)S(1)} %broadcast_in_dim.106), channel_id=1, replica_groups=mesh['leaf'=32,'front'=4] {'front'}, dimensions={0} | all-to-all | bytes 393216 | tf_op jit(solution)/shard_map/all_to_all | solution.py:31
  13.9 3.5 all-to-all-start.1
  17.4 6.2 %all-to-all-done.1 = f32[4,96,256]{2,1,0:T(8,128)S(1)} async-done(((f32[4,96,256]{2,1,0:T(8,128)}), f32[4,96,256]{2,1,0:T(8,128)S(1)}, u32[]{:S(2)}, u32[]{:S(2)}) %all-to-all-start.1) | async-done | bytes 393248 | tf_op jit(solution)/shard_map/all_to_all | solution.py:31
  24.2 3.3 collective-permute-start
  29.8 10.2 %all_to_all.71 = f32[4,96,256]{2,1,0:T(8,128)S(1)} all-to-all(f32[4,96,256]{2,1,0:T(8,128)S(1)} %broadcast_in_dim.110), channel_id=1, replica_groups=mesh['leaf'=32,'front'=4] {'front'}, dimensions={0} | all-to-all | bytes 786432 | tf_op jit(solution)/shard_map/all_to_all | solution.py:31
  43.1 3.5 %all-to-all-start.3 = ((f32[4,96,512]{2,1,0:T(8,128)}), f32[4,96,512]{2,1,0:T(8,128)S(1)}, u32[]{:S(2)}, u32[]{:S(2)}) async-start(f32[4,96,512]{2,1,0:T(8,128)} %broadcast_in_dim.113), calls=%async_computation.3 | async-start | bytes 1572864 | tf_op jit(solution)/shard_map/all_to_all | solution.py:31
  46.6 11.1 %all-to-all-done.3 = f32[4,96,512]{2,1,0:T(8,128)S(1)} async-done(((f32[4,96,512]{2,1,0:T(8,128)}), f32[4,96,512]{2,1,0:T(8,128)S(1)}, u32[]{:S(2)}, u32[]{:S(2)}) %all-to-all-start.3) | async-done | bytes 786464 | tf_op jit(solution)/shard_map/all_to_all | solution.py:31
  57.8 2.1 collective-permute-start.2
  68.9 2.7 collective-permute-done.5
  71.7 13.6 %all_to_all.72 = f32[4,96,512]{2,1,0:T(8,128)S(1)} all-to-all(f32[4,96,512]{2,1,0:T(8,128)S(1)} %broadcast_in_dim.114), channel_id=1, replica_groups=mesh['leaf'=32,'front'=4] {'front'}, dimensions={0} | all-to-all | bytes 1572864 | tf_op jit(solution)/shard_map/all_to_all | solution.py:31
  85.4 2.3 fusion.4
  88.4 20.9 %all_to_all.73 = f32[4,96,1024]{2,1,0:T(8,128)S(1)} all-to-all(f32[4,96,1024]{2,1,0:T(8,128)S(1)} %broadcast_in_dim.117), channel_id=1, replica_groups=mesh['leaf'=32,'front'=4] {'front'}, dimensions={0} | all-to-all | bytes 3145728 | tf_op jit(solution)/shard_map/all_to_all | solution.py:31
  109.4 3.3 collective-permute-start.6
  115.6 8.9 %collective-permute-done.7 = f32[96,1024]{1,0:T(8,128)S(1)} collective-permute-done((f32[96,1024]{1,0:T(8,128)S(1)}, f32[96,1024]{1,0:T(8,128)S(1)}, u32[]{:S(2)}, u32[]{:S(2)}) %collective-permute-start.7) | collective-permute-done | bytes 393248 | tf_op jit(solution)/shard_map/ppermute | solution.py:20
  126.7 3.0 collective-permute-start.8
  131.2 2.5 collective-permute-start.9
  135.9 2.7 collective-permute-done.10
  138.7 3.0 collective-permute-start.11
  141.6 3.9 %collective-permute-done.11 = f32[96,512]{1,0:T(8,128)S(1)} collective-permute-done((f32[96,512]{1,0:T(8,128)S(1)}, f32[96,512]{1,0:T(8,128)S(1)}, u32[]{:S(2)}, u32[]{:S(2)}) %collective-permute-start.11) | collective-permute-done | bytes 196640 | tf_op jit(solution)/shard_map/ppermute | solution.py:20
  146.9 4.5 %all-to-all-start.6 = ((f32[4,96,1024]{2,1,0:T(8,128)}), f32[4,96,1024]{2,1,0:T(8,128)}, u32[]{:S(2)}, u32[]{:S(2)}) async-start(f32[4,96,1024]{2,1,0:T(8,128)} %broadcast_in_dim.118), calls=%async_computation.6 | async-start | bytes 3145728 | tf_op jit(solution)/shard_map/all_to_all | solution.py:31
  151.4 3.4 slice_bitcast_fusion.11
  156.1 3.5 dot_general.75
  159.5 1.8 copy.42
  161.6 8.5 %all-to-all-done.6 = f32[4,96,1024]{2,1,0:T(8,128)} async-done(((f32[4,96,1024]{2,1,0:T(8,128)}), f32[4,96,1024]{2,1,0:T(8,128)}, u32[]{:S(2)}, u32[]{:S(2)}) %all-to-all-start.6) | async-done | bytes 1572896 | tf_op jit(solution)/shard_map/all_to_all | solution.py:31
  170.1 3.6 %copy.39 = f32[96,4,1024]{2,1,0:T(4,128)} copy(f32[96,4,1024]{2,0,1:T(8,128)} %bitcast.32) | data formatting | bytes 3145728 | tf_op jit(solution)/shard_map/transpose | solution.py:24
  173.7 3.3 reshape.416
  177.0 4.3 %fusion = f32[96,64,2]{0,1,2:T(8,128)S(1)} fusion(f32[96,4096,1]{1,0,2:T(8,128)} %reshape.416, f32[64,2,4096]{2,1,0:T(2,128)S(1)} %copy-done.1), kind=kOutput, calls=%fused_computation | convolution fusion | flops 603979776 | bytes 3719168 | tf_op jit(solution)/shard_map/dot_general | solution.py:166
  181.5 2.1 convolution_bitcast_fusion
  183.6 20.1 %all_to_all.74 = f32[4,96,1024]{2,1,0:T(8,128)S(1)} all-to-all(f32[4,96,1024]{2,1,0:T(8,128)S(1)} %convolution_bitcast_fusion), channel_id=1, replica_groups=mesh['leaf'=32,'front'=4] {'front'}, dimensions={0} | all-to-all | bytes 3145728 | tf_op jit(solution)/shard_map/all_to_all | solution.py:46
  203.8 3.0 collective-permute-start.12
  206.8 3.1 collective-permute-done.12
  211.4 3.3 collective-permute-done.13
  214.7 5.7 %collective-permute-start.14 = (f32[96,128]{1,0:T(8,128)S(1)}, f32[96,128]{1,0:T(8,128)S(1)}, u32[]{:S(2)}, u32[]{:S(2)}) collective-permute-start(f32[96,128]{1,0:T(8,128)S(1)} %slice_select_fusion.5), channel_id=1, source_target_pairs={{0,4},{4,0},{8,12},{12,8},{16,20},{20,16},{24,28},{28,24},{32,36},... | collective-permute-start | bytes 147464 | tf_op jit(solution)/shard_map/ppermute | solution.py:20
  221.5 3.6 %collective-permute-start.15 = (f32[96,128]{1,0:T(8,128)S(1)}, f32[96,128]{1,0:T(8,128)S(1)}, u32[]{:S(2)}, u32[]{:S(2)}) collective-permute-start(f32[96,128]{1,0:T(8,128)S(1)} %get-tuple-element.10), channel_id=1, source_target_pairs={{0,16},{16,0},{4,20},{20,4},{8,24},{24,8},{12,28},{28,12},{32,48},... | collective-permute-start | bytes 147464 | tf_op jit(solution)/shard_map/ppermute | solution.py:20
  227.7 22.3 %all_to_all.75 = f32[4,96,1024]{2,1,0:T(8,128)S(1)} all-to-all(f32[4,96,1024]{2,1,0:T(8,128)S(1)} %broadcast_in_dim.119), channel_id=1, replica_groups=mesh['leaf'=32,'front'=4] {'front'}, dimensions={0} | all-to-all | bytes 3145728 | tf_op jit(solution)/shard_map/all_to_all | solution.py:31
  250.1 2.2 collective-permute-start.16
  256.0 8.0 %collective-permute-done.17 = f32[96,1024]{1,0:T(8,128)S(1)} collective-permute-done((f32[96,1024]{1,0:T(8,128)S(1)}, f32[96,1024]{1,0:T(8,128)S(1)}, u32[]{:S(2)}, u32[]{:S(2)}) %collective-permute-start.17) | collective-permute-done | bytes 393248 | tf_op jit(solution)/shard_map/ppermute | solution.py:20
  264.7 2.0 fusion.2
  266.8 13.6 %all_to_all.76 = f32[4,96,512]{2,1,0:T(8,128)S(1)} all-to-all(f32[4,96,512]{2,1,0:T(8,128)S(1)} %bitcast.187), channel_id=1, replica_groups=mesh['leaf'=32,'front'=4] {'front'}, dimensions={0} | all-to-all | bytes 1572864 | tf_op jit(solution)/shard_map/all_to_all | solution.py:46
  281.7 2.2 collective-permute-done.18
  284.0 3.3 collective-permute-start.19
  289.6 1.7 collective-permute-done.20
  292.0 13.0 %all_to_all.77 = f32[4,96,512]{2,1,0:T(8,128)S(1)} all-to-all(f32[4,96,512]{2,1,0:T(8,128)S(1)} %broadcast_in_dim.120), channel_id=1, replica_groups=mesh['leaf'=32,'front'=4] {'front'}, dimensions={0} | all-to-all | bytes 1572864 | tf_op jit(solution)/shard_map/all_to_all | solution.py:31
  305.1 2.7 collective-permute-start.21
  310.8 10.2 %all_to_all.78 = f32[4,96,256]{2,1,0:T(8,128)S(1)} all-to-all(f32[4,96,256]{2,1,0:T(8,128)S(1)} %bitcast.194), channel_id=1, replica_groups=mesh['leaf'=32,'front'=4] {'front'}, dimensions={0} | all-to-all | bytes 786432 | tf_op jit(solution)/shard_map/all_to_all | solution.py:46
  325.8 3.5 all-to-all-start.12
  329.9 7.2 %all-to-all-done.12 = f32[4,96,256]{2,1,0:T(8,128)S(1)} async-done(((f32[4,96,256]{2,1,0:T(8,128)}), f32[4,96,256]{2,1,0:T(8,128)S(1)}, u32[]{:S(2)}, u32[]{:S(2)}) %all-to-all-start.12) | async-done | bytes 393248 | tf_op jit(solution)/shard_map/all_to_all | solution.py:31
  338.7 7.5 %all_to_all.79 = f32[4,96,128]{2,1,0:T(8,128)S(1)} all-to-all(f32[4,96,128]{2,1,0:T(8,128)S(1)} %bitcast.203), channel_id=1, replica_groups=mesh['leaf'=32,'front'=4] {'front'}, dimensions={0} | all-to-all | bytes 393216 | tf_op jit(solution)/shard_map/all_to_all | solution.py:46
  (161 shorter events, 56.6 us)
Async XLA Ops:
  0.0 17.4 %copy-start.7 = (s32[1,14]{1,0:T(1,128)S(1)}, s32[1,14]{1,0:T(1,128)}, u32[]{:S(2)}) copy-start(s32[1,14]{1,0:T(1,128)} %param.10) | copy-start | bytes 172
  13.1 15.3 %copy-start.3 = (f32[1,1,96,512]{3,2,1,0:T(8,128)S(1)}, f32[1,1,96,512]{3,2,1,0:T(8,128)}, u32[]{:S(2)}) copy-start(f32[1,1,96,512]{3,2,1,0:T(8,128)} %param.7) | copy-start | bytes 589828
  13.9 9.7 %all-to-all-start.1 = ((f32[4,96,256]{2,1,0:T(8,128)}), f32[4,96,256]{2,1,0:T(8,128)S(1)}, u32[]{:S(2)}, u32[]{:S(2)}) async-start(f32[4,96,256]{2,1,0:T(8,128)} %broadcast_in_dim.109), calls=%async_computation.1 | async-start | bytes 786432 | tf_op jit(solution)/shard_map/all_to_all | solution.py:31
  24.2 4.2 %collective-permute-start = (f32[96,128]{1,0:T(8,128)S(1)}, f32[96,128]{1,0:T(8,128)S(1)}, u32[]{:S(2)}, u32[]{:S(2)}) collective-permute-start(f32[96,128]{1,0:T(8,128)S(1)} %constant_dynamic-slice_fusion.2), channel_id=1, source_target_pairs={{0,4},{4,0},{8,12},{12,8},{16,20},{20,16},{24,28},{28,24},{32,36},... | collective-permute-start | bytes 147464 | tf_op jit(solution)/shard_map/ppermute | solution.py:20
  28.5 1.3 collective-permute-start.1
  28.9 12.9 %copy-start.2 = (f32[1,1,128,1792]{3,2,1,0:T(8,128)S(1)}, f32[1,1,128,1792]{3,2,1,0:T(8,128)}, u32[]{:S(2)}) copy-start(f32[1,1,128,1792]{3,2,1,0:T(8,128)} %param.9) | copy-start | bytes 2752516
  43.1 14.6 %all-to-all-start.3 = ((f32[4,96,512]{2,1,0:T(8,128)}), f32[4,96,512]{2,1,0:T(8,128)S(1)}, u32[]{:S(2)}, u32[]{:S(2)}) async-start(f32[4,96,512]{2,1,0:T(8,128)} %broadcast_in_dim.113), calls=%async_computation.3 | async-start | bytes 1572864 | tf_op jit(solution)/shard_map/all_to_all | solution.py:31
  57.8 3.2 collective-permute-start.2
  62.0 3.0 collective-permute-start.3
  65.0 2.5 collective-permute-start.4
  67.5 4.1 %collective-permute-start.5 = (f32[96,256]{1,0:T(8,128)S(1)}, f32[96,256]{1,0:T(8,128)S(1)}, u32[]{:S(2)}, u32[]{:S(2)}) collective-permute-start(f32[96,256]{1,0:T(8,128)S(1)} %maximum_select_fusion.4), channel_id=1, source_target_pairs={{0,8},{8,0},{4,12},{12,4},{16,24},{24,16},{20,28},{28,20},{32,40},... | collective-permute-start | bytes 294920 | tf_op jit(solution)/shard_map/ppermute | solution.py:20
  109.4 4.6 %collective-permute-start.6 = (f32[96,1024]{1,0:T(8,128)S(1)}, f32[96,1024]{1,0:T(8,128)S(1)}, u32[]{:S(2)}, u32[]{:S(2)}) collective-permute-start(f32[96,1024]{1,0:T(8,128)S(1)} %reduce_sum.92), channel_id=1, source_target_pairs={{0,4},{4,0},{8,12},{12,8},{16,20},{20,16},{24,28},{28,24},{32,36},... | collective-permute-start | bytes 1179656 | tf_op jit(solution)/shard_map/ppermute | solution.py:20
  114.1 10.4 %collective-permute-start.7 = (f32[96,1024]{1,0:T(8,128)S(1)}, f32[96,1024]{1,0:T(8,128)S(1)}, u32[]{:S(2)}, u32[]{:S(2)}) collective-permute-start(f32[96,1024]{1,0:T(8,128)S(1)} %add.104), channel_id=1, source_target_pairs={{0,8},{8,0},{4,12},{12,4},{16,24},{24,16},{20,28},{28,20},{32,40},... | collective-permute-start | bytes 1179656 | tf_op jit(solution)/shard_map/ppermute | solution.py:20
  126.7 4.5 %collective-permute-start.8 = (f32[96,128]{1,0:T(8,128)S(1)}, f32[96,128]{1,0:T(8,128)S(1)}, u32[]{:S(2)}, u32[]{:S(2)}) collective-permute-start(f32[96,128]{1,0:T(8,128)S(1)} %constant_dynamic-slice_fusion), channel_id=1, source_target_pairs={{0,16},{16,0},{4,20},{20,4},{8,24},{24,8},{12,28},{28,12},{32,48},... | collective-permute-start | bytes 147464 | tf_op jit(solution)/shard_map/ppermute | solution.py:20
  131.2 3.3 collective-permute-start.9
  134.5 4.1 %collective-permute-start.10 = (f32[96,256]{1,0:T(8,128)S(1)}, f32[96,256]{1,0:T(8,128)S(1)}, u32[]{:S(2)}, u32[]{:S(2)}) collective-permute-start(f32[96,256]{1,0:T(8,128)S(1)} %maximum_select_fusion.5), channel_id=1, source_target_pairs={{0,8},{8,0},{4,12},{12,4},{16,24},{24,16},{20,28},{28,20},{32,40},... | collective-permute-start | bytes 294920 | tf_op jit(solution)/shard_map/ppermute | solution.py:20
  138.7 6.8 %collective-permute-start.11 = (f32[96,512]{1,0:T(8,128)S(1)}, f32[96,512]{1,0:T(8,128)S(1)}, u32[]{:S(2)}, u32[]{:S(2)}) collective-permute-start(f32[96,512]{1,0:T(8,128)S(1)} %maximum_select_fusion.2), channel_id=1, source_target_pairs={{0,16},{16,0},{4,20},{20,4},{8,24},{24,8},{12,28},{28,12},{32,48},... | collective-permute-start | bytes 589832 | tf_op jit(solution)/shard_map/ppermute | solution.py:20
  146.9 23.2 %all-to-all-start.6 = ((f32[4,96,1024]{2,1,0:T(8,128)}), f32[4,96,1024]{2,1,0:T(8,128)}, u32[]{:S(2)}, u32[]{:S(2)}) async-start(f32[4,96,1024]{2,1,0:T(8,128)} %broadcast_in_dim.118), calls=%async_computation.6 | async-start | bytes 3145728 | tf_op jit(solution)/shard_map/all_to_all | solution.py:31
  151.4 3.4 copy-start.6
  159.5 1.8 copy-start.4
  159.5 1.9 copy-start.5
  173.7 3.3 copy-start.1
  177.0 4.5 %copy-start = (f32[4096,128]{1,0:T(8,128)S(1)}, f32[4096,128]{1,0:T(8,128)}, u32[]{:S(2)}) copy-start(f32[4096,128]{1,0:T(8,128)} %copy.42) | copy-start | bytes 6291460
  203.8 6.1 %collective-permute-start.12 = (f32[96,512]{1,0:T(8,128)S(1)}, f32[96,512]{1,0:T(8,128)S(1)}, u32[]{:S(2)}, u32[]{:S(2)}) collective-permute-start(f32[96,512]{1,0:T(8,128)S(1)} %slice_select_fusion), channel_id=1, source_target_pairs={{0,16},{16,0},{4,20},{20,4},{8,24},{24,8},{12,28},{28,12},{32,48},... | collective-permute-start | bytes 589832 | tf_op jit(solution)/shard_map/ppermute | solution.py:20
  210.0 4.7 %collective-permute-start.13 = (f32[96,256]{1,0:T(8,128)S(1)}, f32[96,256]{1,0:T(8,128)S(1)}, u32[]{:S(2)}, u32[]{:S(2)}) collective-permute-start(f32[96,256]{1,0:T(8,128)S(1)} %slice_select_fusion.2), channel_id=1, source_target_pairs={{0,8},{8,0},{4,12},{12,4},{16,24},{24,16},{20,28},{28,20},{32,40},... | collective-permute-start | bytes 294920 | tf_op jit(solution)/shard_map/ppermute | solution.py:20
  214.7 6.6 %collective-permute-start.14 = (f32[96,128]{1,0:T(8,128)S(1)}, f32[96,128]{1,0:T(8,128)S(1)}, u32[]{:S(2)}, u32[]{:S(2)}) collective-permute-start(f32[96,128]{1,0:T(8,128)S(1)} %slice_select_fusion.5), channel_id=1, source_target_pairs={{0,4},{4,0},{8,12},{12,8},{16,20},{20,16},{24,28},{28,24},{32,36},... | collective-permute-start | bytes 147464 | tf_op jit(solution)/shard_map/ppermute | solution.py:20
  221.5 5.0 %collective-permute-start.15 = (f32[96,128]{1,0:T(8,128)S(1)}, f32[96,128]{1,0:T(8,128)S(1)}, u32[]{:S(2)}, u32[]{:S(2)}) collective-permute-start(f32[96,128]{1,0:T(8,128)S(1)} %get-tuple-element.10), channel_id=1, source_target_pairs={{0,16},{16,0},{4,20},{20,4},{8,24},{24,8},{12,28},{28,12},{32,48},... | collective-permute-start | bytes 147464 | tf_op jit(solution)/shard_map/ppermute | solution.py:20
  250.1 3.5 %collective-permute-start.16 = (f32[96,1024]{1,0:T(8,128)S(1)}, f32[96,1024]{1,0:T(8,128)S(1)}, u32[]{:S(2)}, u32[]{:S(2)}) collective-permute-start(f32[96,1024]{1,0:T(8,128)S(1)} %reduce_sum.94), channel_id=1, source_target_pairs={{0,4},{4,0},{8,12},{12,8},{16,20},{20,16},{24,28},{28,24},{32,36},... | collective-permute-start | bytes 1179656 | tf_op jit(solution)/shard_map/ppermute | solution.py:20
  253.7 10.4 %collective-permute-start.17 = (f32[96,1024]{1,0:T(8,128)S(1)}, f32[96,1024]{1,0:T(8,128)S(1)}, u32[]{:S(2)}, u32[]{:S(2)}) collective-permute-start(f32[96,1024]{1,0:T(8,128)S(1)} %add.114), channel_id=1, source_target_pairs={{0,8},{8,0},{4,12},{12,4},{16,24},{24,16},{20,28},{28,20},{32,40},... | collective-permute-start | bytes 1179656 | tf_op jit(solution)/shard_map/ppermute | solution.py:20
  280.4 3.5 %collective-permute-start.18 = (f32[96,256]{1,0:T(8,128)S(1)}, f32[96,256]{1,0:T(8,128)S(1)}, u32[]{:S(2)}, u32[]{:S(2)}) collective-permute-start(f32[96,256]{1,0:T(8,128)S(1)} %slice_select_fusion.1), channel_id=1, source_target_pairs={{0,8},{8,0},{4,12},{12,4},{16,24},{24,16},{20,28},{28,20},{32,40},... | collective-permute-start | bytes 294920 | tf_op jit(solution)/shard_map/ppermute | solution.py:20
  284.0 4.2 %collective-permute-start.19 = (f32[96,128]{1,0:T(8,128)S(1)}, f32[96,128]{1,0:T(8,128)S(1)}, u32[]{:S(2)}, u32[]{:S(2)}) collective-permute-start(f32[96,128]{1,0:T(8,128)S(1)} %slice_select_fusion.4), channel_id=1, source_target_pairs={{0,4},{4,0},{8,12},{12,8},{16,20},{20,16},{24,28},{28,24},{32,36},... | collective-permute-start | bytes 147464 | tf_op jit(solution)/shard_map/ppermute | solution.py:20
  288.3 3.0 collective-permute-start.20
  305.1 3.8 %collective-permute-start.21 = (f32[96,512]{1,0:T(8,128)S(1)}, f32[96,512]{1,0:T(8,128)S(1)}, u32[]{:S(2)}, u32[]{:S(2)}) collective-permute-start(f32[96,512]{1,0:T(8,128)S(1)} %reduce_sum.96), channel_id=1, source_target_pairs={{0,4},{4,0},{8,12},{12,8},{16,20},{20,16},{24,28},{28,24},{32,36},... | collective-permute-start | bytes 589832 | tf_op jit(solution)/shard_map/ppermute | solution.py:20
  321.0 2.2 collective-permute-start.22
  323.3 1.3 collective-permute-start.23
  325.8 11.3 %all-to-all-start.12 = ((f32[4,96,256]{2,1,0:T(8,128)}), f32[4,96,256]{2,1,0:T(8,128)S(1)}, u32[]{:S(2)}, u32[]{:S(2)}) async-start(f32[4,96,256]{2,1,0:T(8,128)} %broadcast_in_dim.121), calls=%async_computation.12 | async-start | bytes 786432 | tf_op jit(solution)/shard_map/all_to_all | solution.py:31
where the time goes:
time: 349 us; the launch traced here: 347 us
  blocking collectives  141 us (40%)
  waiting for transfers between devices  85.7 us (25%)
  starting transfers between devices  67.1 us (19%)
  local copies, waits for them, and re-layouts  25.6 us (7%)
  matrix products  23.1 us (7%)
  other arithmetic  3.61 us (1%)
    all_to_all x6, blocking collectives, copy_for_each(): return lax.all_to_all(copies, axis, split_axis=0, concat_axis=0, tiled=True)  89.8 us
    ppermute x24, waiting for transfers between devices, from_partner(): return lax.ppermute(block, axis, route)  52.7 us
    ppermute x24, starting transfers between devices, from_partner(): return lax.ppermute(block, axis, route)  52.2 us
    all_to_all x4, blocking collectives, sum_at_owner(): parts = lax.all_to_all(in_blocks(value, dim, peers), axis, 0, 0, tiled=True)  51.4 us
    all_to_all x4, waiting for transfers between devices, copy_for_each(): return lax.all_to_all(copies, axis, split_axis=0, concat_axis=0, tiled=True)  33 us
    all_to_all x4, starting transfers between devices, copy_for_each(): return lax.all_to_all(copies, axis, split_axis=0, concat_axis=0, tiled=True)  14.9 us
    dot_general x4, matrix products, per_device(): lax.dot_general(gathered, inverse_rows, (((1,), (1,)), ((), ())), precisi...  9.69 us
  transfers between devices with their start and end apart: 28, of which 28 were waited for; matrix products, arithmetic and copies ran while one was open for 4% of the time, Pallas kernels for 0%

commit v1 on v0

v1 whole, which is shorter than its diff:
```python
import jax
import jax.numpy as jnp
import numpy as np
from jax import lax
from jax.experimental import pallas as pl
from jax.experimental.pallas import tpu as pltpu
from jax.sharding import Mesh, PartitionSpec as P

LEVELS = 4
BLOCK = 128
PIVOTS = 128
SIDES = 96
HALF = SIDES // 2
AXES = ("z", "y1", "y0", "c", "x")

exact_mode = lax.Precision.HIGHEST


def dot_rows(left, right):
    return lax.dot_general(
        left, right, (((1,), (1,)), ((), ())), precision=exact_mode, preferred_element_type=jnp.float32
    )


def dot_cols(left, right):
    return lax.dot_general(
        left, right, (((1,), (0,)), ((), ())), precision=exact_mode, preferred_element_type=jnp.float32
    )


def exchange(value, axes):
    return lax.all_to_all(value, axes, 0, 0, tiled=True)


def with_partner(value):
    return lax.ppermute(value, "c", [(0, 1), (1, 0)])


def block_at(index):
    return pl.ds(pl.multiple_of(index * BLOCK, BLOCK), BLOCK)


def call(body, out_shapes, operands, specs, scratch=()):
    return pl.pallas_call(
        body,
        grid=(1,),
        in_specs=specs,
        out_specs=[pl.BlockSpec(s, lambda i, n=len(s): (0,) * n) for s in out_shapes],
        out_shape=[jax.ShapeDtypeStruct(s, jnp.float32) for s in out_shapes],
        scratch_shapes=list(scratch),
        compiler_params=pltpu.CompilerParams(vmem_limit_bytes=60 * 1024 * 1024),
    )(*operands)


class Inputs:
    def __init__(self):
        self.operands, self.specs = [], []

    def whole(self, value):
        shape = value.shape
        self.operands.append(value)
        self.specs.append(pl.BlockSpec(shape, lambda i, n=len(shape): (0,) * n))

    def scalars(self, value):
        self.operands.append(value)
        self.specs.append(pl.BlockSpec(memory_space=pltpu.SMEM))

    def columns(self, value, start, width, step):
        for k in range(width // step):
            self.operands.append(value)
            self.specs.append(
                pl.BlockSpec((value.shape[0], step), lambda i, at=start // step + k: (0, at))
            )


def pivot_apply(solved, own, swapped):
    lane = lax.broadcasted_iota(jnp.int32, solved.shape, 1)
    beside = jnp.where(lane % 2 == 0, pltpu.roll(solved, PIVOTS - 1, 1), pltpu.roll(solved, 1, 1))
    return own * solved + swapped * beside


def pivot_factors(kinds, diagonal, coupling):
    def body(kinds_ref, diagonal_ref, coupling_ref, out_ref):
        width = diagonal_ref.shape[1]
        row = lax.broadcasted_iota(jnp.int32, (width // 2, width), 0)
        col = lax.broadcasted_iota(jnp.int32, (width // 2, width), 1)
        widen = (col // 2 == row).astype(jnp.float32)
        pair = jnp.concatenate(
            [kinds_ref[...].astype(jnp.float32), coupling_ref[...], jnp.zeros((6, width // 2), jnp.float32)], 0
        )
        wide = dot_cols(pair, widen)
        is_pair = wide[0:1] > 0.5
        couple = wide[1:2]
        own = jnp.broadcast_to(diagonal_ref[...], (8, width))
        lane = lax.broadcasted_iota(jnp.int32, (8, width), 1)
        other = jnp.where(lane % 2 == 0, pltpu.roll(own, width - 1, 1), pltpu.roll(own, 1, 1))[0:1]
        own = own[0:1]
        determinant = own * other - couple * couple
        out_ref[0:1, :] = jnp.where(is_pair, other / determinant, 1.0 / own)
        out_ref[1:2, :] = jnp.where(is_pair, -couple / determinant, 0.0)

    args = Inputs()
    args.whole(kinds)
    args.whole(diagonal)
    args.whole(coupling)
    return call(body, [(2, diagonal.shape[1])], args.operands, args.specs)[0]


def level_zero_forward(first, inverse, update, factors):
    def body(first_ref, *refs):
        inverse_ref, update_ref, factors_ref, sent_ref, weighted_ref = refs
        inverse_rows = inverse_ref[...]
        solved = dot_rows(first_ref[0, :, :PIVOTS], inverse_rows[:, :PIVOTS])
        for q in range(1, 4):
            solved += dot_rows(first_ref[q, :, :PIVOTS], inverse_rows[:, q * PIVOTS : (q + 1) * PIVOTS])
        weighted_ref[...] = pivot_apply(solved, factors_ref[0:1, :], factors_ref[1:2, :])
        part = dot_cols(solved, update_ref[...])
        for c in range(2):
            for x in range(4):
                sent_ref[c * 4 + x] = part[c * HALF : (c + 1) * HALF]

    args = Inputs()
    args.whole(first)
    args.columns(inverse, 0, 512, 512)
    args.columns(update, 0, 256, 256)
    args.columns(factors, 0, PIVOTS, PIVOTS)
    return call(body, [(8, HALF, 256), (SIDES, PIVOTS)], args.operands, args.specs)


def forward(level, received, sides, targets, inverse, partner_inverse, update, partner_update, factors, partner_factors):
    width = 1 << level
    span = 4 * PIVOTS * width
    chunks = span // 512
    start = 4 * PIVOTS * (width - 1)
    update_len = 2 * PIVOTS * width
    update_start = 2 * PIVOTS * (width - 1)
    update_step = 256
    update_chunks = update_len // update_step if level < 3 else 0
    blocks = (2, 4, 8)[level - 1]
    table_at = (0, 4, 12)[level - 1]

    def body(*refs):
        refs = list(refs)
        targets_ref, received_ref, sides_ref = refs[:3]
        at = 3
        own_inverse = refs[at : at + chunks]
        at += chunks
        other_inverse = refs[at : at + chunks]
        at += chunks
        own_update = refs[at : at + update_chunks]
        at += update_chunks
        other_update = refs[at : at + update_chunks]
        at += update_chunks
        own_factors, other_factors = refs[at : at + 2]
        outs = refs[at + 2 : -1]
        b_ref = refs[-1]
        for i in range(span // 256):
            if level == 1:
                b_ref[:, i * 256 : i * 256 + 128] = sides_ref[i, 0:HALF, PIVOTS:]
                b_ref[:, i * 256 + 128 : i * 256 + 256] = sides_ref[i, HALF:, PIVOTS:]
            else:
                b_ref[:, i * 256 : (i + 1) * 256] = sides_ref[i]
        for child in range(2):
            if level < 3:
                if level == 1:
                    total = sum(received_ref[child * 4 + x] for x in range(4))
                else:
                    total = sum(received_ref[x * 2 + child] for x in range(4))
            for k in range(blocks):
                if level < 3:
                    piece = total[:, k * BLOCK : (k + 1) * BLOCK]
                else:
                    piece = received_ref[(k // 2) * 4 + child * 2 + k % 2]
                where = block_at(targets_ref[table_at + child * blocks + k])
                b_ref[:, where] = b_ref[:, where] - piece
        own = jnp.zeros((HALF, PIVOTS), jnp.float32)
        other = jnp.zeros((HALF, PIVOTS), jnp.float32)
        for k in range(chunks):
            rows = b_ref[:, k * 512 : (k + 1) * 512]
            own += dot_rows(rows, own_inverse[k][...])
            other += dot_rows(rows, other_inverse[k][...])
        own_weighted = pivot_apply(own, own_factors[0:1, :], own_factors[1:2, :])
        other_weighted = pivot_apply(other, other_factors[0:1, :], other_factors[1:2, :])
        if level < 3:
            sent_ref, weighted_ref = outs
            weighted_ref[0] = own_weighted
            weighted_ref[1] = other_weighted
            for k in range(update_chunks):
                part = dot_cols(own, own_update[k][...]) + dot_cols(other, other_update[k][...])
                if level == 1:
                    for i in range(8):
                        sent_ref[i, :, k * 256 : (k + 1) * 256] = part
                else:
                    sent_ref[2 * k] = part[:, :BLOCK]
                    sent_ref[2 * k + 1] = part[:, BLOCK:]
        else:
            sent_ref, full_ref = outs
            for k in range(chunks):
                part = dot_cols(own_weighted, own_inverse[k][...]) + dot_cols(other_weighted, other_inverse[k][...])
                b_ref[:, k * 512 : (k + 1) * 512] = part
                full_ref[2 * k] = part[:, :256]
                full_ref[2 * k + 1] = part[:, 256:]
            for child in range(2):
                for k in range(8):
                    where = block_at(targets_ref[table_at + child * 8 + k])
                    sent_ref[(k // 2) * 4 + child * 2 + k % 2] = b_ref[:, where]

    args = Inputs()
    args.scalars(targets)
    args.whole(received)
    args.whole(sides)
    args.columns(inverse, start, span, 512)
    args.columns(partner_inverse, start, span, 512)
    if level < 3:
        args.columns(update, update_start, update_len, update_step)
        args.columns(partner_update, update_start, update_len, update_step)
    args.columns(factors, level * PIVOTS, PIVOTS, PIVOTS)
    args.columns(partner_factors, level * PIVOTS, PIVOTS, PIVOTS)
    outs = {
        1: [(8, HALF, 512), (2, HALF, PIVOTS)],
        2: [(8, HALF, BLOCK), (2, HALF, PIVOTS)],
        3: [(16, HALF, BLOCK), (16, HALF, 256)],
    }[level]
    return call(body, outs, args.operands, args.specs, [pltpu.VMEM((HALF, span), jnp.float32)])


def backward(level, received, weighted, targets, inverse, partner_inverse, update, partner_update):
    width = 1 << level
    span = 4 * PIVOTS * width
    chunks = span // 512
    start = 4 * PIVOTS * (width - 1)
    update_len = 2 * PIVOTS * width
    update_start = 2 * PIVOTS * (width - 1)
    update_chunks = update_len // 256
    blocks = (2, 4)[level - 1]
    table_at = (0, 4)[level - 1]

    def body(*refs):
        refs = list(refs)
        targets_ref, received_ref, weighted_ref = refs[:3]
        at = 3
        own_inverse = refs[at : at + chunks]
        at += chunks
        other_inverse = refs[at : at + chunks]
        at += chunks
        own_update = refs[at : at + update_chunks]
        at += update_chunks
        other_update = refs[at : at + update_chunks]
        sent_ref, full_ref, x_ref = refs[-3:]
        own = weighted_ref[0]
        other = weighted_ref[1]
        if level == 1:
            total = sum(received_ref[i] for i in range(8))
        for k in range(update_chunks):
            if level == 1:
                chosen = total[:, k * 256 : (k + 1) * 256]
            else:
                chosen = jnp.concatenate([received_ref[2 * k], received_ref[2 * k + 1]], 1)
            own -= dot_rows(chosen, own_update[k][...])
            other -= dot_rows(chosen, other_update[k][...])
        for k in range(chunks):
            part = dot_cols(own, own_inverse[k][...]) + dot_cols(other, other_inverse[k][...])
            x_ref[:, k * 512 : (k + 1) * 512] = part
            full_ref[2 * k] = part[:, :256]
            full_ref[2 * k + 1] = part[:, 256:]
        for child in range(2):
            for k in range(blocks):
                where = block_at(targets_ref[table_at + child * blocks + k])
                piece = x_ref[:, where]
                for x in range(4):
                    sent_ref[x * 2 + child, :, k * BLOCK : (k + 1) * BLOCK] = piece

    args = Inputs()
    args.scalars(targets)
    args.whole(received)
    args.whole(weighted)
    args.columns(inverse, start, span, 512)
    args.columns(partner_inverse, start, span, 512)
    args.columns(update, update_start, update_len, 256)
    args.columns(partner_update, update_start, update_len, 256)
    outs = [(8, HALF, blocks * BLOCK), (span // 256, HALF, 256)]
    return call(body, outs, args.operands, args.specs, [pltpu.VMEM((HALF, span), jnp.float32)])


def level_zero_backward(received, weighted, inverse, update, upper):
    def body(received_ref, weighted_ref, inverse_ref, update_ref, upper_ref, sent_ref):
        update_rows = update_ref[...]
        inverse_rows = inverse_ref[...]
        for c in range(2):
            half = slice(c * HALF, (c + 1) * HALF)
            chosen = sum(received_ref[x * 2 + c] for x in range(4))
            target = weighted_ref[half] - dot_rows(chosen, update_rows)
            part = dot_cols(target, inverse_rows)
            for q in range(4):
                sent_ref[q, half, :PIVOTS] = part[:, q * PIVOTS : (q + 1) * PIVOTS]
                sent_ref[q, half, PIVOTS:] = upper_ref[q, :, c * PIVOTS : (c + 1) * PIVOTS]

    args = Inputs()
    args.whole(received)
    args.whole(weighted)
    args.columns(inverse, 0, 512, 512)
    args.columns(update, 0, 256, 256)
    args.whole(upper)
    return call(body, [(4, SIDES, 256)], args.operands, args.specs)[0]


def copies(value, count):
    return jnp.broadcast_to(value[None], (count, *value.shape))


def sibling_targets(targets):
    pairs = []
    for y1 in range(2):
        for y0 in range(2):
            here = y1 * 4 + y0 * 2
            pairs.append((here, y1 * 4 + (1 - y0) * 2))
            pairs.append((here + 1, (1 - y1) * 4 + y0 * 2 + 1))
    received = lax.ppermute(targets, ("y1", "y0", "c"), pairs)
    both = jnp.stack([targets, received])
    other = with_partner(both)
    c, y0, y1 = lax.axis_index("c"), lax.axis_index("y0"), lax.axis_index("y1")

    def ordered(own, sibling, bit):
        return jnp.where(bit == 0, jnp.concatenate([own, sibling]), jnp.concatenate([sibling, own]))

    side = jnp.where(c == 0, received, other[1])
    above = jnp.where(c == 0, other[1], received)
    return jnp.concatenate(
        [
            ordered(targets[0:2], other[0, 0:2], c),
            ordered(targets[2:6], side[2:6], y0),
            ordered(targets[6:14], above[6:14], y1),
        ]
    )


def per_device(right_side, factor_inverse, update_panel, update_targets, pivot_pairs, pivot_diagonal, pivot_coupling):
    sides = right_side[0, 0]
    inverse = factor_inverse[0, 0]
    update = update_panel[0, 0]
    c = lax.axis_index("c")
    targets = sibling_targets(update_targets[0])
    factors = pivot_factors(pivot_pairs[0], pivot_diagonal[0], pivot_coupling[0])
    partner_factors = with_partner(factors)
    partner_inverse = with_partner(inverse)
    partner_update = with_partner(update)

    upper = sides[:, PIVOTS:]
    kept = lax.dynamic_slice_in_dim(upper, c * HALF, HALF, 0)
    swapped = with_partner(lax.dynamic_slice_in_dim(upper, (1 - c) * HALF, HALF, 0))
    low = jnp.where(c == 0, kept, swapped)
    high = jnp.where(c == 0, swapped, kept)
    rows = [jnp.concatenate([low[:, i : i + PIVOTS], high[:, i : i + PIVOTS]], 1) for i in (0, 128, 256)]

    first = jnp.concatenate(
        [sides[:, :PIVOTS], jnp.concatenate([rows[0][:, :PIVOTS], rows[0][:, PIVOTS:]], 0)], 1
    )
    first = exchange(copies(first, 4), ("x",))
    sides2 = exchange(copies(rows[1], 8), ("x", "y0"))
    sides3 = exchange(copies(rows[2], 16), ("x", "y1", "y0"))

    sent, weighted0 = level_zero_forward(first, inverse, update, factors)
    received = exchange(sent, ("c", "x"))
    sent, weighted1 = forward(
        1, received, first, targets, inverse, partner_inverse, update, partner_update, factors, partner_factors
    )
    received = exchange(sent, ("x", "y0"))
    sent, weighted2 = forward(
        2, received, sides2, targets, inverse, partner_inverse, update, partner_update, factors, partner_factors
    )
    received = jnp.sum(exchange(sent, ("x", "y0")), 0)
    received = exchange(copies(received, 16), ("x", "y1", "y0"))
    sent, full3 = forward(
        3, received, sides3, targets, inverse, partner_inverse, update, partner_update, factors, partner_factors
    )
    received = jnp.sum(exchange(sent, ("x", "y1", "y0")), 0)
    received = exchange(copies(received, 8), ("x", "y0"))
    answer3 = exchange(full3, ("x", "y1", "y0"))
    sent, full2 = backward(2, received, weighted2, targets, inverse, partner_inverse, update, partner_update)
    received = exchange(sent, ("x", "y0"))
    answer2 = exchange(full2, ("x", "y0"))
    sent, full1 = backward(1, received, weighted1, targets, inverse, partner_inverse, update, partner_update)
    received = exchange(sent, ("x", "c"))
    sent = level_zero_backward(received, weighted0, inverse, update, full1)
    last = jnp.sum(exchange(sent, ("x",)), 0)

    answer1 = jnp.concatenate([last[:HALF, PIVOTS:], last[HALF:, PIVOTS:]], 1)
    answers = [answer1, jnp.sum(answer2, 0), jnp.sum(answer3, 0)]
    low = jnp.concatenate([a[:, :PIVOTS] for a in answers], 1)
    high = jnp.concatenate([a[:, PIVOTS:] for a in answers], 1)
    kept = jnp.where(c == 0, low, high)
    swapped = with_partner(jnp.where(c == 0, high, low))
    upper = jnp.where(c == 0, jnp.concatenate([kept, swapped], 0), jnp.concatenate([swapped, kept], 0))
    return jnp.concatenate([last[:, :PIVOTS], upper], 1)[None, None]


def solution(mesh):
    grid = np.array(mesh.devices).reshape(4, 2, 2, 2, 4)
    fine = Mesh(grid, AXES)
    leaf = ("z", "y1", "y0", "c")
    in_specs = (
        P(leaf, "x", None, None),
        P(leaf, "x", None, None),
        P(leaf, "x", None, None),
        P(leaf, None),
        P(leaf, "x", None),
        P(leaf, "x", None),
        P(leaf, "x", None),
    )
    out_specs = P(leaf, "x", None, None)
    return jax.shard_map(per_device, mesh=fine, in_specs=in_specs, out_specs=out_specs, check_vma=False)
```

time: 349 us -> 219 us (0.63)
  blocking collectives: 141 us -> 82.6 us
  waiting for transfers between devices: 85.7 us -> 49.4 us
  Pallas kernels: 0 us -> 35.7 us
  starting transfers between devices: 67.1 us -> 39 us
  matrix products: 23.1 us -> 0 us
  local copies, waits for them, and re-layouts: 25.6 us -> 8.36 us
    all_to_all x10 -> x6, blocking collectives: 141 us -> 82.6 us  [exchange(): return lax.all_to_all(value, axes, 0, 0, tiled=True)]
    ppermute x24 -> x7, waiting for transfers between devices: 52.7 us -> 0.92 us  [the longest x6 0.92 us: with_partner(): return lax.ppermute(value, 'c', [(0, 1), (1, 0)])]
    ppermute x24 -> x7, starting transfers between devices: 52.2 us -> 8.82 us  [the longest x6 5.79 us: with_partner(): return lax.ppermute(value, 'c', [(0, 1), (1, 0)])]
    pallas_call x0 -> x8, Pallas kernels: none -> 35.7 us  [call(): pl.pallas_call(body, grid=(1,), in_specs=specs, out_specs=[pl.BlockSpec(s...]
    dot_general x20 -> x0, matrix products: 23.1 us -> none  [the longest x4 9.69 us: per_device(): lax.dot_general(gathered, inverse_rows, (((1,), (1,)), ((), ())), precisi...]
    all_to_all x4 -> x8, waiting for transfers between devices: 33 us -> 48.4 us  [exchange(): return lax.all_to_all(value, axes, 0, 0, tiled=True)]
    all_to_all x4 -> x8, starting transfers between devices: 14.9 us -> 30.2 us  [exchange(): return lax.all_to_all(value, axes, 0, 0, tiled=True)]
    dot_general x6 -> x0, local copies, waits for them, and re-layouts: 8.9 us -> none  [the longest x2 5.18 us: per_device(): jnp.dot(target, inverse_rows, precision=exact_mode, preferred_element_typ...]
  transfers between devices with their start and end apart: 28 -> 15, of which waited for: 28 -> 9; matrix products, arithmetic and copies ran while one was open for 4% -> 3% of each run, Pallas kernels for 0% -> 7%
where the time goes in v1:
time: 219 us; the launch traced here: 218 us
  blocking collectives  82.6 us (38%)
  waiting for transfers between devices  49.4 us (23%)
  starting transfers between devices  39 us (18%)
  Pallas kernels  35.7 us (16%)
  local copies, waits for them, and re-layouts  8.36 us (4%)
  other arithmetic  2.37 us (1%)
    all_to_all x6, blocking collectives, exchange(): return lax.all_to_all(value, axes, 0, 0, tiled=True)  82.6 us
    all_to_all x8, waiting for transfers between devices, exchange(): return lax.all_to_all(value, axes, 0, 0, tiled=True)  48.4 us
    pallas_call x8, Pallas kernels, call(): pl.pallas_call(body, grid=(1,), in_specs=specs, out_specs=[pl.BlockSpec(s...  35.7 us
    all_to_all x8, starting transfers between devices, exchange(): return lax.all_to_all(value, axes, 0, 0, tiled=True)  30.2 us
    ppermute x6, starting transfers between devices, with_partner(): return lax.ppermute(value, 'c', [(0, 1), (1, 0)])  5.79 us
  transfers between devices with their start and end apart: 15, of which 9 were waited for; matrix products, arithmetic and copies ran while one was open for 3% of the time, Pallas kernels for 7%

profile of v1, /device:TPU:1, one launch (start us, length us, event | category | flops | bytes accessed | tf_op | source)
XLA Modules:
  0.0 217.7 jit_solution(15763195265151071164)
XLA Ops:
  0.0 1.4 collective-permute-start.3
  1.4 3.0 %collective-permute-start = (s32[14]{0:T(128)}, s32[14]{0:T(128)S(1)}, u32[]{:S(2)}, u32[]{:S(2)}) collective-permute-start(s32[14]{0:T(128)} %bitcast.65), channel_id=1, source_target_pairs={{0,8},{4,20},{8,0},{12,28},{16,24},{20,4},{24,16},{28,12},{1,9},{5... | collective-permute-start | bytes 176 | tf_op jit(solution)/shard_map/ppermute | solution.py:318
  4.4 0.9 slice.102
  5.9 1.6 shard_map.73.refs_2_.refs_11_.refs_19_
  7.7 0.7 slice_bitcast_fusion
  8.4 0.7 slice_bitcast_fusion.1
  9.1 0.8 slice.101
  10.0 0.8 broadcast_in_dim.12
  10.8 4.0 %all-to-all-start = ((f32[4,96,256]{2,1,0:T(8,128)}), f32[4,96,256]{2,1,0:T(8,128)S(1)}, u32[]{:S(2)}, u32[]{:S(2)}) async-start(f32[4,96,256]{2,1,0:T(8,128)} %broadcast_in_dim.12), calls=%async_computation | async-start | bytes 786432 | tf_op jit(solution)/shard_map/all_to_all | solution.py:32
  14.8 0.7 slice_bitcast_fusion.3
  15.5 0.7 pad_add_fusion
  16.1 0.7 collective-permute-start.1
  16.8 5.2 %all-to-all-done.first_ref.refs_2_ = f32[4,96,256]{2,1,0:T(8,128)S(1)} async-done(((f32[4,96,256]{2,1,0:T(8,128)}), f32[4,96,256]{2,1,0:T(8,128)S(1)}, u32[]{:S(2)}, u32[]{:S(2)}) %all-to-all-start) | async-done | bytes 393248 | tf_op jit(solution)/shard_map/all_to_all | solution.py:32
  22.0 0.7 copy-done.1
  22.7 2.8 %shard_map.74 = (f32[8,48,256]{2,1,0:T(8,128)}, f32[96,128]{1,0:T(8,128)}) custom-call(f32[4,96,256]{2,1,0:T(8,128)} %copy-done.1, f32[128,7680]{1,0:T(8,128)} %bitcast.22, f32[128,1792]{1,0:T(8,128)} %bitcast.45, f32[2,512]{1,0:T(2,128)} %shard_map.73.refs_2_.refs_11_.refs_19_), custom_call_target="tpu_custom_call" | custom-call | tf_op jit(solution)/shard_map/pallas_call | solution.py:44
  25.6 5.2 %all-to-all-start.1 = ((f32[8,48,256]{2,1,0:T(8,128)}), f32[8,48,256]{2,1,0:T(8,128)S(1)}, u32[]{:S(2)}, u32[]{:S(2)}) async-start(f32[8,48,256]{2,1,0:T(8,128)} %get-tuple-element.17), calls=%async_computation.1 | async-start | bytes 786432 | tf_op jit(solution)/shard_map/all_to_all | solution.py:32
  30.8 7.9 %all-to-all-done.1.refs_1_ = f32[8,48,256]{2,1,0:T(8,128)S(1)} async-done(((f32[8,48,256]{2,1,0:T(8,128)}), f32[8,48,256]{2,1,0:T(8,128)S(1)}, u32[]{:S(2)}, u32[]{:S(2)}) %all-to-all-start.1) | async-done | bytes 393248 | tf_op jit(solution)/shard_map/all_to_all | solution.py:32
  38.7 0.8 broadcast_in_dim.13
  39.6 3.5 %all-to-all-start.3 = ((f32[8,48,256]{2,1,0:T(8,128)}), f32[8,48,256]{2,1,0:T(8,128)S(1)}, u32[]{:S(2)}, u32[]{:S(2)}) async-start(f32[8,48,256]{2,1,0:T(8,128)} %broadcast_in_dim.13), calls=%async_computation.3 | async-start | bytes 786432 | tf_op jit(solution)/shard_map/all_to_all | solution.py:32
  43.4 0.6 pad_add_fusion.1.refs_0_
  44.0 0.6 copy-done.5
  44.9 4.1 %shard_map.75 = (f32[8,48,512]{2,1,0:T(8,128)}, f32[2,48,128]{2,1,0:T(8,128)}) custom-call(s32[28]{0:T(128)} %pad_add_fusion.1.refs_0_, f32[8,48,256]{2,1,0:T(8,128)} %copy-done.4, f32[4,96,256]{2,1,0:T(8,128)} %copy-done.1, f32[128,7680]{1,0:T(8,128)} %bitcast.23, f32[128,7680]{1,0:T(8,128)} %bitcast.24, ...), custom_call_target="tpu_custom_call" | custom-call | tf_op jit(solution)/shard_map/pallas_call | solution.py:44
  49.0 1.8 all-to-all-done.3.refs_2_
  50.9 15.5 %all_to_all.70.refs_1_ = f32[8,48,512]{2,1,0:T(8,128)} all-to-all(f32[8,48,512]{2,1,0:T(8,128)} %get-tuple-element.18), channel_id=1, replica_groups=mesh['z'=4,'y1'=2,'y0'=2,'c'=2,'x'=4] {'x','y0'}, dimensions={0} | all-to-all | bytes 1572864 | tf_op jit(solution)/shard_map/all_to_all | solution.py:32
  66.4 5.7 %shard_map.76 = (f32[8,48,128]{2,1,0:T(8,128)}, f32[2,48,128]{2,1,0:T(8,128)}) custom-call(s32[28]{0:T(128)} %pad_add_fusion.1.refs_0_, f32[8,48,512]{2,1,0:T(8,128)} %all_to_all.70.refs_1_, f32[8,48,256]{2,1,0:T(8,128)} %copy-done.3, f32[128,7680]{1,0:T(8,128)} %bitcast.25, f32[128,7680]{1,0:T(8,128)} %bitcast.26, f32[128,7680]{1,0:T(8,128)} %bitcast.27, ...), custom_call_target="tpu_custom_call" | custom-call | tf_op jit(solution)/shard_map/pallas_call | solution.py:44
  72.1 3.4 %all-to-all-start.4 = ((f32[8,48,128]{2,1,0:T(8,128)}), f32[8,48,128]{2,1,0:T(8,128)S(1)}, u32[]{:S(2)}, u32[]{:S(2)}) async-start(f32[8,48,128]{2,1,0:T(8,128)} %get-tuple-element.19), calls=%async_computation.4 | async-start | bytes 393216 | tf_op jit(solution)/shard_map/all_to_all | solution.py:32
  75.5 5.5 %all-to-all-done.4 = f32[8,48,128]{2,1,0:T(8,128)S(1)} async-done(((f32[8,48,128]{2,1,0:T(8,128)}), f32[8,48,128]{2,1,0:T(8,128)S(1)}, u32[]{:S(2)}, u32[]{:S(2)}) %all-to-all-start.4) | async-done | bytes 196640 | tf_op jit(solution)/shard_map/all_to_all | solution.py:32
  81.0 1.0 broadcast_in_dim.15
  82.0 3.6 %all-to-all-start.6 = ((f32[16,48,256]{2,1,0:T(8,128)}), f32[16,48,256]{2,1,0:T(8,128)S(1)}, u32[]{:S(2)}, u32[]{:S(2)}) async-start(f32[16,48,256]{2,1,0:T(8,128)} %broadcast_in_dim.15), calls=%async_computation.6 | async-start | bytes 1572864 | tf_op jit(solution)/shard_map/all_to_all | solution.py:32
  85.6 10.9 %all-to-all-done.6.refs_2_ = f32[16,48,256]{2,1,0:T(8,128)S(1)} async-done(((f32[16,48,256]{2,1,0:T(8,128)}), f32[16,48,256]{2,1,0:T(8,128)S(1)}, u32[]{:S(2)}, u32[]{:S(2)}) %all-to-all-start.6) | async-done | bytes 786464 | tf_op jit(solution)/shard_map/all_to_all | solution.py:32
  96.5 11.3 %all_to_all.71.refs_1_ = f32[16,48,128]{2,1,0:T(8,128)} all-to-all(f32[16,48,128]{2,1,0:T(8,128)S(1)} %broadcast_in_dim.14), channel_id=1, replica_groups=mesh['z'=4,'y1'=2,'y0'=2,'c'=2,'x'=4] {'x','y1','y0'}, dimensions={0} | all-to-all | bytes 786432 | tf_op jit(solution)/shard_map/all_to_all | solution.py:32
  107.9 9.9 %shard_map.77 = (f32[16,48,128]{2,1,0:T(8,128)}, f32[16,48,256]{2,1,0:T(8,128)}) custom-call(s32[28]{0:T(128)} %pad_add_fusion.1.refs_0_, f32[16,48,128]{2,1,0:T(8,128)} %all_to_all.71.refs_1_, f32[16,48,256]{2,1,0:T(8,128)} %copy-done.2, f32[128,7680]{1,0:T(8,128)} %bitcast.32, f32[128,7680]{1,0:T(8,128)} %bitcast.30, f32[128,7680]{1,0:T(8,128)} %bitcast.31, ...), custom_call_target="tpu_custom_call" | custom-call | tf_op jit(solution)/shard_map/pallas_call | solution.py:44
  117.8 11.5 %all_to_all.72 = f32[16,48,128]{2,1,0:T(8,128)S(1)} all-to-all(f32[16,48,128]{2,1,0:T(8,128)} %get-tuple-element.20), channel_id=1, replica_groups=mesh['z'=4,'y1'=2,'y0'=2,'c'=2,'x'=4] {'x','y1','y0'}, dimensions={0} | all-to-all | bytes 786432 | tf_op jit(solution)/shard_map/all_to_all | solution.py:32
  129.3 8.6 %all_to_all.73.refs_1_ = f32[8,48,128]{2,1,0:T(8,128)} all-to-all(f32[8,48,128]{2,1,0:T(8,128)S(1)} %broadcast_in_dim.16), channel_id=1, replica_groups=mesh['z'=4,'y1'=2,'y0'=2,'c'=2,'x'=4] {'x','y0'}, dimensions={0} | all-to-all | bytes 393216 | tf_op jit(solution)/shard_map/all_to_all | solution.py:32
  137.9 5.0 %shard_map.78 = (f32[8,48,512]{2,1,0:T(8,128)}, f32[8,48,256]{2,1,0:T(8,128)}) custom-call(s32[28]{0:T(128)} %pad_add_fusion.1.refs_0_, f32[8,48,128]{2,1,0:T(8,128)} %all_to_all.73.refs_1_, f32[2,48,128]{2,1,0:T(8,128)} %get-tuple-element.21.refs_2_, f32[128,7680]{1,0:T(8,128)} %bitcast.37, f32[128,7680]{1,0:T(8,128)} %bitcast.38, f32[128,7680]{1,0:T(8,128)} %bitcast.39, ...), custom_call_target="tpu_custom_call" | custom-call | tf_op jit(solution)/shard_map/pallas_call | solution.py:44
  142.9 12.8 %all_to_all.74.refs_1_ = f32[8,48,512]{2,1,0:T(8,128)} all-to-all(f32[8,48,512]{2,1,0:T(8,128)} %get-tuple-element.22), channel_id=1, replica_groups=mesh['z'=4,'y1'=2,'y0'=2,'c'=2,'x'=4] {'x','y0'}, dimensions={0} | all-to-all | bytes 1572864 | tf_op jit(solution)/shard_map/all_to_all | solution.py:32
  155.7 3.6 %all-to-all-start.13 = ((f32[16,48,256]{2,1,0:T(8,128)}), f32[16,48,256]{2,1,0:T(8,128)S(1)}, u32[]{:S(2)}, u32[]{:S(2)}) async-start(f32[16,48,256]{2,1,0:T(8,128)} %get-tuple-element.28), calls=%async_computation.13 | async-start | bytes 1572864 | tf_op jit(solution)/shard_map/all_to_all | solution.py:32
  159.4 3.6 %shard_map.79 = (f32[8,48,256]{2,1,0:T(8,128)}, f32[4,48,256]{2,1,0:T(8,128)}) custom-call(s32[28]{0:T(128)} %pad_add_fusion.1.refs_0_, f32[8,48,512]{2,1,0:T(8,128)} %all_to_all.74.refs_1_, f32[2,48,128]{2,1,0:T(8,128)} %get-tuple-element.23.refs_2_, f32[128,7680]{1,0:T(8,128)} %bitcast.41, f32[128,7680]{1,0:T(8,128)} %bitcast.42, ...), custom_call_target="tpu_custom_call" | custom-call | tf_op jit(solution)/shard_map/pallas_call | solution.py:44
  163.0 6.7 %all-to-all-done.13 = f32[16,48,256]{2,1,0:T(8,128)S(1)} async-done(((f32[16,48,256]{2,1,0:T(8,128)}), f32[16,48,256]{2,1,0:T(8,128)S(1)}, u32[]{:S(2)}, u32[]{:S(2)}) %all-to-all-start.13) | async-done | bytes 786464 | tf_op jit(solution)/shard_map/all_to_all | solution.py:32
  169.7 22.9 %all_to_all.75.received_ref = f32[8,48,256]{2,1,0:T(8,128)} all-to-all(f32[8,48,256]{2,1,0:T(8,128)} %get-tuple-element.24), channel_id=1, replica_groups=mesh['z'=4,'y1'=2,'y0'=2,'c'=2,'x'=4] {'x','c'}, dimensions={0} | all-to-all | bytes 786432 | tf_op jit(solution)/shard_map/all_to_all | solution.py:32
  192.6 3.5 %all-to-all-start.12 = ((f32[8,48,256]{2,1,0:T(8,128)}), f32[8,48,256]{2,1,0:T(8,128)S(1)}, u32[]{:S(2)}, u32[]{:S(2)}) async-start(f32[8,48,256]{2,1,0:T(8,128)} %get-tuple-element.27), calls=%async_computation.12 | async-start | bytes 786432 | tf_op jit(solution)/shard_map/all_to_all | solution.py:32
  196.1 2.8 %shard_map.80 = f32[4,96,256]{2,1,0:T(8,128)} custom-call(f32[8,48,256]{2,1,0:T(8,128)} %all_to_all.75.received_ref, f32[96,128]{1,0:T(8,128)} %get-tuple-element.25.weighted_ref, f32[128,7680]{1,0:T(8,128)} %bitcast.43, f32[128,1792]{1,0:T(8,128)} %bitcast.58, f32[4,48,256]{2,1,0:T(8,128)} %get-tuple-element.26.upper_ref), custom_call_target="tpu_custom_call" | custom-call | tf_op jit(solution)/shard_map/pallas_call | solution.py:44
  198.9 4.4 %all-to-all-done.12 = f32[8,48,256]{2,1,0:T(8,128)S(1)} async-done(((f32[8,48,256]{2,1,0:T(8,128)}), f32[8,48,256]{2,1,0:T(8,128)S(1)}, u32[]{:S(2)}, u32[]{:S(2)}) %all-to-all-start.12) | async-done | bytes 393248 | tf_op jit(solution)/shard_map/all_to_all | solution.py:32
  203.3 3.5 %all-to-all-start.11 = ((f32[4,96,256]{2,1,0:T(8,128)}), f32[4,96,256]{2,1,0:T(8,128)S(1)}, u32[]{:S(2)}, u32[]{:S(2)}) async-start(f32[4,96,256]{2,1,0:T(8,128)} %shard_map.80), calls=%async_computation.11 | async-start | bytes 786432 | tf_op jit(solution)/shard_map/all_to_all | solution.py:32
  206.8 6.1 %all-to-all-done.11 = f32[4,96,256]{2,1,0:T(8,128)S(1)} async-done(((f32[4,96,256]{2,1,0:T(8,128)}), f32[4,96,256]{2,1,0:T(8,128)S(1)}, u32[]{:S(2)}, u32[]{:S(2)}) %all-to-all-start.11) | async-done | bytes 393248 | tf_op jit(solution)/shard_map/all_to_all | solution.py:32
  213.0 3.0 %collective-permute-start.6 = (f32[48,384]{1,0:T(8,128)S(1)}, f32[48,384]{1,0:T(8,128)S(1)}, u32[]{:S(2)}, u32[]{:S(2)}) collective-permute-start(f32[48,384]{1,0:T(8,128)S(1)} %get-tuple-element.32), channel_id=1, source_target_pairs={{0,4},{4,0},{1,5},{5,1},{2,6},{6,2},{3,7},{7,3},{8,12},{12,8},{9,1... | collective-permute-start | bytes 221192 | tf_op jit(solution)/shard_map/ppermute | solution.py:36
  216.1 0.9 collective-permute-done.6
  217.0 0.7 maximum_bitcast_fusion
  (45 shorter events, 1.7 us)
Async XLA Ops:
  0.0 44.0 %collective-permute-start.3 = (f32[128,7680]{1,0:T(8,128)}, f32[128,7680]{1,0:T(8,128)}, u32[]{:S(2)}, u32[]{:S(2)}) collective-permute-start(f32[128,7680]{1,0:T(8,128)} %bitcast.21), channel_id=1, source_target_pairs={{0,4},{4,0},{1,5},{5,1},{2,6},{6,2},{3,7},{7,3},{8,12},{12,8},{9,1... | collective-permute-start | bytes 11796488 | tf_op jit(solution)/shard_map/ppermute | solution.py:36
  1.4 14.1 %collective-permute-start = (s32[14]{0:T(128)}, s32[14]{0:T(128)S(1)}, u32[]{:S(2)}, u32[]{:S(2)}) collective-permute-start(s32[14]{0:T(128)} %bitcast.65), channel_id=1, source_target_pairs={{0,8},{4,20},{8,0},{12,28},{16,24},{20,4},{24,16},{28,12},{1,9},{5... | collective-permute-start | bytes 176 | tf_op jit(solution)/shard_map/ppermute | solution.py:318
  5.4 4.6 %collective-permute-start.2 = (f32[48,384]{1,0:T(8,128)S(1)}, f32[48,384]{1,0:T(8,128)S(1)}, u32[]{:S(2)}, u32[]{:S(2)}) collective-permute-start(f32[48,384]{1,0:T(8,128)S(1)} %constant_dynamic-slice_fusion), channel_id=1, source_target_pairs={{0,4},{4,0},{1,5},{5,1},{2,6},{6,2},{3,7},{7,3},{8,12},{12,8},{9,1... | collective-permute-start | bytes 221192 | tf_op jit(solution)/shard_map/ppermute | solution.py:36
  5.4 38.5 %collective-permute-start.4 = (f32[128,1792]{1,0:T(8,128)}, f32[128,1792]{1,0:T(8,128)S(1)}, u32[]{:S(2)}, u32[]{:S(2)}) collective-permute-start(f32[128,1792]{1,0:T(8,128)} %bitcast.44), channel_id=1, source_target_pairs={{0,4},{4,0},{1,5},{5,1},{2,6},{6,2},{3,7},{7,3},{8,12},{12,8},{9,1... | collective-permute-start | bytes 2752520 | tf_op jit(solution)/shard_map/ppermute | solution.py:36
  7.6 36.4 %collective-permute-start.5 = (f32[2,512]{1,0:T(2,128)}, f32[2,512]{1,0:T(2,128)S(1)}, u32[]{:S(2)}, u32[]{:S(2)}) collective-permute-start(f32[2,512]{1,0:T(2,128)} %shard_map.73.refs_2_.refs_11_.refs_19_), channel_id=1, source_target_pairs={{0,4},{4,0},{1,5},{5,1},{2,6},{6,2},{3,7},{7,3},{8,12},{12,8},{9,1... | collective-permute-start | bytes 12296 | tf_op jit(solution)/shard_map/ppermute | solution.py:36
  10.8 11.2 %all-to-all-start = ((f32[4,96,256]{2,1,0:T(8,128)}), f32[4,96,256]{2,1,0:T(8,128)S(1)}, u32[]{:S(2)}, u32[]{:S(2)}) async-start(f32[4,96,256]{2,1,0:T(8,128)} %broadcast_in_dim.12), calls=%async_computation | async-start | bytes 786432 | tf_op jit(solution)/shard_map/all_to_all | solution.py:32
  16.1 14.7 %collective-permute-start.1 = (s32[2,14]{1,0:T(2,128)S(1)}, s32[2,14]{1,0:T(2,128)S(1)}, u32[]{:S(2)}, u32[]{:S(2)}) collective-permute-start(s32[2,14]{1,0:T(2,128)S(1)} %pad_add_fusion), channel_id=1, source_target_pairs={{0,4},{4,0},{1,5},{5,1},{2,6},{6,2},{3,7},{7,3},{8,12},{12,8},{9,1... | collective-permute-start | bytes 344 | tf_op jit(solution)/shard_map/ppermute | solution.py:36
  22.0 0.7 copy-start.1
  25.6 13.2 %all-to-all-start.1 = ((f32[8,48,256]{2,1,0:T(8,128)}), f32[8,48,256]{2,1,0:T(8,128)S(1)}, u32[]{:S(2)}, u32[]{:S(2)}) async-start(f32[8,48,256]{2,1,0:T(8,128)} %get-tuple-element.17), calls=%async_computation.1 | async-start | bytes 786432 | tf_op jit(solution)/shard_map/all_to_all | solution.py:32
  38.7 5.3 %copy-start.4 = (f32[8,48,256]{2,1,0:T(8,128)}, f32[8,48,256]{2,1,0:T(8,128)S(1)}, u32[]{:S(2)}) copy-start(f32[8,48,256]{2,1,0:T(8,128)S(1)} %all-to-all-done.1.refs_1_) | copy-start | bytes 1179652
  39.6 11.3 %all-to-all-start.3 = ((f32[8,48,256]{2,1,0:T(8,128)}), f32[8,48,256]{2,1,0:T(8,128)S(1)}, u32[]{:S(2)}, u32[]{:S(2)}) async-start(f32[8,48,256]{2,1,0:T(8,128)} %broadcast_in_dim.13), calls=%async_computation.3 | async-start | bytes 786432 | tf_op jit(solution)/shard_map/all_to_all | solution.py:32
  44.0 0.6 copy-start.5
  44.0 0.9 copy-start
  50.9 15.5 %copy-start.3 = (f32[8,48,256]{2,1,0:T(8,128)}, f32[8,48,256]{2,1,0:T(8,128)S(1)}, u32[]{:S(2)}) copy-start(f32[8,48,256]{2,1,0:T(8,128)S(1)} %all-to-all-done.3.refs_2_) | copy-start | bytes 1179652
  72.1 8.9 %all-to-all-start.4 = ((f32[8,48,128]{2,1,0:T(8,128)}), f32[8,48,128]{2,1,0:T(8,128)S(1)}, u32[]{:S(2)}, u32[]{:S(2)}) async-start(f32[8,48,128]{2,1,0:T(8,128)} %get-tuple-element.19), calls=%async_computation.4 | async-start | bytes 393216 | tf_op jit(solution)/shard_map/all_to_all | solution.py:32
  82.0 14.5 %all-to-all-start.6 = ((f32[16,48,256]{2,1,0:T(8,128)}), f32[16,48,256]{2,1,0:T(8,128)S(1)}, u32[]{:S(2)}, u32[]{:S(2)}) async-start(f32[16,48,256]{2,1,0:T(8,128)} %broadcast_in_dim.15), calls=%async_computation.6 | async-start | bytes 1572864 | tf_op jit(solution)/shard_map/all_to_all | solution.py:32
  96.5 11.4 %copy-start.2 = (f32[16,48,256]{2,1,0:T(8,128)}, f32[16,48,256]{2,1,0:T(8,128)S(1)}, u32[]{:S(2)}) copy-start(f32[16,48,256]{2,1,0:T(8,128)S(1)} %all-to-all-done.6.refs_2_) | copy-start | bytes 2359300
  155.7 13.9 %all-to-all-start.13 = ((f32[16,48,256]{2,1,0:T(8,128)}), f32[16,48,256]{2,1,0:T(8,128)S(1)}, u32[]{:S(2)}, u32[]{:S(2)}) async-start(f32[16,48,256]{2,1,0:T(8,128)} %get-tuple-element.28), calls=%async_computation.13 | async-start | bytes 1572864 | tf_op jit(solution)/shard_map/all_to_all | solution.py:32
  192.6 10.7 %all-to-all-start.12 = ((f32[8,48,256]{2,1,0:T(8,128)}), f32[8,48,256]{2,1,0:T(8,128)S(1)}, u32[]{:S(2)}, u32[]{:S(2)}) async-start(f32[8,48,256]{2,1,0:T(8,128)} %get-tuple-element.27), calls=%async_computation.12 | async-start | bytes 786432 | tf_op jit(solution)/shard_map/all_to_all | solution.py:32
  203.3 9.7 %all-to-all-start.11 = ((f32[4,96,256]{2,1,0:T(8,128)}), f32[4,96,256]{2,1,0:T(8,128)S(1)}, u32[]{:S(2)}, u32[]{:S(2)}) async-start(f32[4,96,256]{2,1,0:T(8,128)} %shard_map.80), calls=%async_computation.11 | async-start | bytes 786432 | tf_op jit(solution)/shard_map/all_to_all | solution.py:32
  213.0 4.0 %collective-permute-start.6 = (f32[48,384]{1,0:T(8,128)S(1)}, f32[48,384]{1,0:T(8,128)S(1)}, u32[]{:S(2)}, u32[]{:S(2)}) collective-permute-start(f32[48,384]{1,0:T(8,128)S(1)} %get-tuple-element.32), channel_id=1, source_target_pairs={{0,4},{4,0},{1,5},{5,1},{2,6},{6,2},{3,7},{7,3},{8,12},{12,8},{9,1... | collective-permute-start | bytes 221192 | tf_op jit(solution)/shard_map/ppermute | solution.py:36

commit v2 on v1

v2 whole, which is shorter than its diff:
```python
import jax
import jax.numpy as jnp
import numpy as np
from jax import lax
from jax.experimental import pallas as pl
from jax.experimental.pallas import tpu as pltpu
from jax.sharding import Mesh, PartitionSpec as P

LEVELS = 4
BLOCK = 128
PIVOTS = 128
SIDES = 96
HALF = SIDES // 2
AXES = ("z", "y1", "y0", "c", "x")

exact_mode = lax.Precision.HIGHEST


def dot_rows(left, right):
    return lax.dot_general(
        left, right, (((1,), (1,)), ((), ())), precision=exact_mode, preferred_element_type=jnp.float32
    )


def dot_cols(left, right):
    return lax.dot_general(
        left, right, (((1,), (0,)), ((), ())), precision=exact_mode, preferred_element_type=jnp.float32
    )


def dot_full(left, right):
    return lax.dot_general(
        left, right, (((1,), (0,)), ((), ())), precision=exact_mode, preferred_element_type=jnp.float32
    )


def exchange(value, axes):
    return lax.all_to_all(value, axes, 0, 0, tiled=True)


def with_partner(value):
    return lax.ppermute(value, "c", [(0, 1), (1, 0)])


def across(value, axis):
    return lax.ppermute(value, axis, [(0, 1), (1, 0)])


def block_at(index, size=BLOCK):
    return pl.ds(pl.multiple_of(index * size, size), size)


WHOLE = pl.BlockSpec(memory_space=pltpu.VMEM)
SCALARS = pl.BlockSpec(memory_space=pltpu.SMEM)
FAR = pl.BlockSpec(memory_space=pltpu.HBM)


def call(body, out_shapes, operands, specs, scratch=(), limit=16):
    return pl.pallas_call(
        body,
        in_specs=specs,
        out_specs=[WHOLE] * len(out_shapes),
        out_shape=[jax.ShapeDtypeStruct(s, jnp.float32) for s in out_shapes],
        scratch_shapes=list(scratch),
        compiler_params=pltpu.CompilerParams(vmem_limit_bytes=limit * 1024 * 1024),
    )(*operands)


class Stream:
    def __init__(self, pair, start, width, step, buffer, semaphores):
        self.step, self.buffer, self.moves = step, buffer, []
        for k in range(width // step):
            both = []
            for side, source in enumerate(pair):
                both.append(
                    pltpu.make_async_copy(
                        source.at[:, pl.ds(start + k * step, step)],
                        buffer.at[pl.ds(side * PIVOTS, PIVOTS), pl.ds(k * step, step)],
                        semaphores.at[k, side],
                    )
                )
            self.moves.append(both)

    def start(self):
        for both in self.moves:
            for move in both:
                move.start()

    def wait(self, k):
        for move in self.moves[k]:
            move.wait()

    def at(self, k):
        return self.buffer[:, k * self.step : (k + 1) * self.step]


def stream_scratch(pair, width, step):
    return [pltpu.VMEM((pair * PIVOTS, width), jnp.float32), pltpu.SemaphoreType.DMA((width // step, pair))]


def pivot_apply(solved, own, swapped):
    lane = lax.broadcasted_iota(jnp.int32, solved.shape, 1)
    width = solved.shape[1]
    beside = jnp.where(lane % 2 == 0, pltpu.roll(solved, width - 1, 1), pltpu.roll(solved, 1, 1))
    return own * solved + swapped * beside


def pivot_factors(kinds, diagonal, coupling):
    def body(kinds_ref, diagonal_ref, coupling_ref, out_ref):
        width = diagonal_ref.shape[1]
        row = lax.broadcasted_iota(jnp.int32, (width // 2, width), 0)
        col = lax.broadcasted_iota(jnp.int32, (width // 2, width), 1)
        widen = (col // 2 == row).astype(jnp.float32)
        pair = jnp.concatenate(
            [kinds_ref[...].astype(jnp.float32), coupling_ref[...], jnp.zeros((6, width // 2), jnp.float32)], 0
        )
        wide = dot_full(pair, widen)
        is_pair = wide[0:1] > 0.5
        couple = wide[1:2]
        own = jnp.broadcast_to(diagonal_ref[...], (8, width))
        lane = lax.broadcasted_iota(jnp.int32, (8, width), 1)
        other = jnp.where(lane % 2 == 0, pltpu.roll(own, width - 1, 1), pltpu.roll(own, 1, 1))[0:1]
        own = own[0:1]
        determinant = own * other - couple * couple
        out_ref[0:1, :] = jnp.where(is_pair, other / determinant, 1.0 / own)
        out_ref[1:2, :] = jnp.where(is_pair, -couple / determinant, 0.0)

    return call(body, [(2, diagonal.shape[1])], [kinds, diagonal, coupling], [WHOLE] * 3)[0]


def packed_sides(sides, beside):
    def body(sides_ref, beside_ref, out_ref):
        c = lax.axis_index("c")
        mine = pl.ds(pl.multiple_of(c * HALF, 8), HALF)
        theirs = pl.ds(pl.multiple_of((1 - c) * HALF, 8), HALF)
        own = sides_ref[mine, PIVOTS:]
        other = beside_ref[mine, PIVOTS:]
        for i in range(4):
            out_ref[i, :, :PIVOTS] = sides_ref[:, :PIVOTS]
            out_ref[i, mine, PIVOTS:] = own
            out_ref[i, theirs, PIVOTS:] = other

    return call(body, [(4, SIDES, 512)], [sides, beside], [WHOLE] * 2)[0]


def level_zero_forward(first, inverse, update, factors):
    def body(first_ref, inverse_ref, update_ref, factors_ref, sent_ref, weighted_ref, upper_ref, *scratch):
        weights = Stream([inverse_ref], 0, 512, 512, *scratch[:2])
        updates = Stream([update_ref], 0, 256, 256, *scratch[2:])
        weights.start()
        updates.start()
        for q in range(4):
            upper_ref[q] = first_ref[q, :, 2 * PIVOTS :]
        gathered = jnp.concatenate([first_ref[q, :, :PIVOTS] for q in range(4)], 1)
        weights.wait(0)
        solved = dot_rows(gathered, weights.at(0))
        weighted_ref[...] = pivot_apply(solved, factors_ref[0:1, :PIVOTS], factors_ref[1:2, :PIVOTS])
        updates.wait(0)
        part = dot_cols(solved, updates.at(0))
        for c in range(2):
            for x in range(4):
                sent_ref[c * 4 + x] = part[c * HALF : (c + 1) * HALF]

    return call(
        body,
        [(8, HALF, 256), (SIDES, PIVOTS), (4, SIDES, 256)],
        [first, inverse, update, factors],
        [WHOLE, FAR, FAR, WHOLE],
        stream_scratch(1, 512, 512) + stream_scratch(1, 256, 256),
    )


def child_block(level, tables, child, k):
    own_ref, side_ref, own_beside_ref, side_beside_ref = tables
    c = lax.axis_index("c")
    if level == 1:
        return jnp.where(c == child, own_ref[0, k], own_beside_ref[0, k])
    if level == 2:
        sibling = jnp.where(c == 0, side_ref[0, 2 + k], side_beside_ref[0, 2 + k])
        return jnp.where(lax.axis_index("y0") == child, own_ref[0, 2 + k], sibling)
    sibling = jnp.where(c == 0, side_beside_ref[0, 6 + k], side_ref[0, 6 + k])
    return jnp.where(lax.axis_index("y1") == child, own_ref[0, 6 + k], sibling)


def both_factors(level, factors, beside):
    c = lax.axis_index("c")
    at = slice(level * PIVOTS, (level + 1) * PIVOTS)
    return [jnp.concatenate([factors[i : i + 1, at], beside[i : i + 1, at]], 1) for i in range(2)]


def halves(rows):
    return jnp.concatenate([rows[:HALF], rows[HALF:]], 1)


def forward(level, received, sides, tables, weights_pair, update_pair, factors, partner_factors):
    width = 1 << level
    span = 4 * PIVOTS * width
    chunks = span // 512
    start = 4 * PIVOTS * (width - 1)
    update_len = 2 * PIVOTS * width if level < 3 else 0
    update_start = 2 * PIVOTS * (width - 1)
    blocks = (2, 4, 8)[level - 1]
    n_sides = len(sides)
    n_updates = 2 if level < 3 else 0

    def body(*refs):
        refs = list(refs)

        def take(count):
            taken, refs[:] = refs[:count], refs[count:]
            return taken

        tables_refs = take(4)
        (received_ref,) = take(1)
        sides_refs = take(n_sides)
        factors_ref, beside_ref = take(2)
        inverse_refs = take(2)
        update_refs = take(n_updates)
        outs = take(2 if level == 2 else 3)
        (b_ref,) = take(1)
        weights = Stream(inverse_refs, start, span, 512, *take(2))
        weights.start()
        if level < 3:
            updates = Stream(update_refs, update_start, update_len, 256, *take(2))
            updates.start()
        y0, y1 = lax.axis_index("y0"), lax.axis_index("y1")
        if level == 1:
            for x in range(4):
                b_ref[:, x * 256 : (x + 1) * 256] = halves(sides_refs[0][x, :, PIVOTS : 2 * PIVOTS])
            near, far = sides_refs[1], sides_refs[2]
            outs[2][0] = near[:, :, PIVOTS:]
            outs[2][1] = far[:, :, PIVOTS:]
        elif level == 2:
            for flip in range(2):
                for x in range(4):
                    b_ref[:, block_at(x * 2 + (y0 ^ flip), 256)] = halves(sides_refs[flip][x, :, :PIVOTS])
        else:
            for high in range(2):
                for flip in range(2):
                    for x in range(4):
                        where = block_at(x * 4 + (y1 ^ high) * 2 + (y0 ^ flip), 256)
                        b_ref[:, where] = halves(sides_refs[high][flip, x])
        for child in range(2):
            if level == 1:
                total = sum(received_ref[child * 4 + x] for x in range(4))
            elif level == 2:
                total = sum(received_ref[x * 2 + child] for x in range(4))
            for k in range(blocks):
                if level < 3:
                    piece = total[:, k * BLOCK : (k + 1) * BLOCK]
                else:
                    piece = received_ref[(k // 2) * 4 + child * 2 + k % 2]
                where = block_at(child_block(level, tables_refs, child, k))
                b_ref[:, where] = b_ref[:, where] - piece
        solved = jnp.zeros((HALF, 2 * PIVOTS), jnp.float32)
        for k in range(chunks):
            weights.wait(k)
            solved += dot_rows(b_ref[:, k * 512 : (k + 1) * 512], weights.at(k))
        weighted = pivot_apply(solved, *both_factors(level, factors_ref, beside_ref))
        if level < 3:
            outs[1][...] = weighted
            for k in range(update_len // 256):
                updates.wait(k)
                part = dot_cols(solved, updates.at(k))
                if level == 1:
                    for i in range(8):
                        outs[0][i, :, k * 256 : (k + 1) * 256] = part
                else:
                    outs[0][2 * k] = part[:, :BLOCK]
                    outs[0][2 * k + 1] = part[:, BLOCK:]
        else:
            sent_ref, keep_ref, far_ref = outs
            for k in range(chunks):
                b_ref[:, k * 512 : (k + 1) * 512] = dot_cols(weighted, weights.at(k))
            for child in range(2):
                for k in range(8):
                    where = block_at(child_block(3, tables_refs, child, k))
                    sent_ref[(k // 2) * 4 + child * 2 + k % 2] = b_ref[:, where]
            for x in range(4):
                for low in range(2):
                    keep_ref[x, low] = b_ref[:, block_at(x * 4 + y1 * 2 + low, 256)]
                    far_ref[x, low] = b_ref[:, block_at(x * 4 + (1 - y1) * 2 + low, 256)]

    outs = {
        1: [(8, HALF, 512), (HALF, 256), (2, 4, SIDES, PIVOTS)],
        2: [(8, HALF, BLOCK), (HALF, 256)],
        3: [(16, HALF, BLOCK), (4, 2, HALF, 256), (4, 2, HALF, 256)],
    }[level]
    scratch = [pltpu.VMEM((HALF, span), jnp.float32)] + stream_scratch(2, span, 512)
    operands = [*tables, received, *sides, factors, partner_factors, *weights_pair]
    specs = [SCALARS] * 4 + [WHOLE] * (3 + n_sides) + [FAR] * 2
    if level < 3:
        scratch += stream_scratch(2, update_len, 256)
        operands += update_pair
        specs += [FAR] * 2
    return call(body, outs, operands, specs, scratch, 20)


def backward(level, received, weighted, tables, weights_pair, update_pair, answers):
    width = 1 << level
    span = 4 * PIVOTS * width
    chunks = span // 512
    start = 4 * PIVOTS * (width - 1)
    update_len = 2 * PIVOTS * width
    update_start = 2 * PIVOTS * (width - 1)
    blocks = (2, 4)[level - 1]

    def body(*refs):
        refs = list(refs)

        def take(count):
            taken, refs[:] = refs[:count], refs[count:]
            return taken

        tables_refs = take(4)
        received_ref, weighted_ref = take(2)
        answer_refs = take(len(answers))
        inverse_refs = take(2)
        update_refs = take(2)
        outs = take(2 if level == 1 else 3)
        (x_ref,) = take(1)
        weights = Stream(inverse_refs, start, span, 512, *take(2))
        updates = Stream(update_refs, update_start, update_len, 256, *take(2))
        updates.start()
        weights.start()
        target = weighted_ref[...]
        if level == 1:
            total = sum(received_ref[i] for i in range(8))
        for k in range(update_len // 256):
            if level == 1:
                chosen = total[:, k * 256 : (k + 1) * 256]
            else:
                chosen = jnp.concatenate([received_ref[2 * k], received_ref[2 * k + 1]], 1)
            updates.wait(k)
            target -= dot_rows(chosen, updates.at(k))
        for k in range(chunks):
            weights.wait(k)
            x_ref[:, k * 512 : (k + 1) * 512] = dot_cols(target, weights.at(k))
        for child in range(2):
            for k in range(blocks):
                piece = x_ref[:, block_at(child_block(level, tables_refs, child, k))]
                for x in range(4):
                    outs[0][x * 2 + child, :, k * BLOCK : (k + 1) * BLOCK] = piece
        if level == 1:
            for x in range(4):
                outs[1][x] = x_ref[:, x * 256 : (x + 1) * 256]
        else:
            y0 = lax.axis_index("y0")
            keep_ref, far_ref = outs[1:]
            own_ref, other_ref = answer_refs
            for x in range(4):
                keep_ref[0, x] = x_ref[:, block_at(x * 2 + y0, 256)]
                far_ref[0, x] = x_ref[:, block_at(x * 2 + (1 - y0), 256)]
                keep_ref[1, x] = own_ref[x, y0] + other_ref[x, y0]
                far_ref[1, x] = own_ref[x, 1 - y0] + other_ref[x, 1 - y0]

    outs = [(8, HALF, blocks * BLOCK)]
    outs += [(4, HALF, 256)] if level == 1 else [(2, 4, HALF, 256), (2, 4, HALF, 256)]
    scratch = [pltpu.VMEM((HALF, span), jnp.float32)]
    scratch += stream_scratch(2, span, 512) + stream_scratch(2, update_len, 256)
    operands = [*tables, received, weighted, *answers, *weights_pair, *update_pair]
    specs = [SCALARS] * 4 + [WHOLE] * (2 + len(answers)) + [FAR] * 4
    return call(body, outs, operands, specs, scratch, 20)


def level_zero_backward(received, weighted, inverse, update, nearest, kept, other):
    def body(received_ref, weighted_ref, nearest_ref, kept_ref, other_ref, inverse_ref, update_ref, sent_ref, *scratch):
        weights = Stream([inverse_ref], 0, 512, 512, *scratch[:2])
        updates = Stream([update_ref], 0, 256, 256, *scratch[2:])
        updates.start()
        weights.start()
        for x in range(4):
            for c in range(2):
                half = slice(c * HALF, (c + 1) * HALF)
                at = slice(c * PIVOTS, (c + 1) * PIVOTS)
                sent_ref[x, half, PIVOTS : 2 * PIVOTS] = nearest_ref[x, :, at]
                for i in range(2):
                    piece = kept_ref[i, x, :, at] + other_ref[i, x, :, at]
                    sent_ref[x, half, (2 + i) * PIVOTS : (3 + i) * PIVOTS] = piece
        chosen = jnp.concatenate([sum(received_ref[x * 2 + c] for x in range(4)) for c in range(2)], 0)
        updates.wait(0)
        target = weighted_ref[...] - dot_rows(chosen, updates.at(0))
        weights.wait(0)
        part = dot_cols(target, weights.at(0))
        for q in range(4):
            sent_ref[q, :, :PIVOTS] = part[:, q * PIVOTS : (q + 1) * PIVOTS]

    return call(
        body,
        [(4, SIDES, 512)],
        [received, weighted, nearest, kept, other, inverse, update],
        [WHOLE] * 5 + [FAR] * 2,
        stream_scratch(1, 512, 512) + stream_scratch(1, 256, 256),
    )[0]


def summed(received):
    def body(received_ref, out_ref):
        out_ref[...] = (received_ref[0] + received_ref[1]) + (received_ref[2] + received_ref[3])

    return call(body, [(SIDES, 512)], [received], [WHOLE])[0]


def unpacked(total, beside):
    def body(total_ref, beside_ref, out_ref):
        c = lax.axis_index("c")
        mine = pl.ds(pl.multiple_of(c * HALF, 8), HALF)
        theirs = pl.ds(pl.multiple_of((1 - c) * HALF, 8), HALF)
        out_ref[:, :PIVOTS] = total_ref[:, :PIVOTS]
        out_ref[mine, PIVOTS:] = total_ref[mine, PIVOTS:]
        out_ref[theirs, PIVOTS:] = beside_ref[mine, PIVOTS:]

    return call(body, [(SIDES, 512)], [total, beside], [WHOLE] * 2)[0]


def summed_copies(received, count):
    total = jnp.sum(received, 0)
    return jnp.broadcast_to(total[None], (count, *total.shape))


def sibling_tables(targets):
    pairs = []
    for y1 in range(2):
        for y0 in range(2):
            here = y1 * 4 + y0 * 2
            pairs.append((here, y1 * 4 + (1 - y0) * 2))
            pairs.append((here + 1, (1 - y1) * 4 + y0 * 2 + 1))
    side = lax.ppermute(targets, ("y1", "y0", "c"), pairs)
    return [targets, side, with_partner(targets), with_partner(side)]


def per_device(right_side, factor_inverse, update_panel, update_targets, pivot_pairs, pivot_diagonal, pivot_coupling):
    sides = right_side[0, 0]
    inverse = factor_inverse[0, 0]
    update = update_panel[0, 0]
    plane = ("x", "y1", "y0")
    pair = ("x", "y0")

    first = exchange(packed_sides(sides, with_partner(sides)), ("x",))
    tables = sibling_tables(update_targets)
    factors = pivot_factors(pivot_pairs[0], pivot_diagonal[0], pivot_coupling[0])
    partner_factors = with_partner(factors)
    weights_pair = [inverse, with_partner(inverse)]
    update_pair = [update, with_partner(update)]

    sent, weighted0, near = level_zero_forward(first, inverse, update, factors)
    far = across(near, "y0")
    received = exchange(sent, ("c", "x"))
    sent, weighted1, near3 = forward(
        1, received, [first, near, far], tables, weights_pair, update_pair, factors, partner_factors
    )
    far3 = across(near3, "y1")
    received = exchange(sent, pair)
    sent, weighted2 = forward(2, received, [near, far], tables, weights_pair, update_pair, factors, partner_factors)
    received = exchange(summed_copies(exchange(sent, pair), 16), plane)
    sent, kept3, other3 = forward(
        3, received, [near3, far3], tables, weights_pair, None, factors, partner_factors
    )
    other3 = across(other3, "y1")
    received = exchange(summed_copies(exchange(sent, plane), 8), pair)
    sent, kept, other = backward(2, received, weighted2, tables, weights_pair, update_pair, [kept3, other3])
    other = across(other, "y0")
    received = exchange(sent, pair)
    sent, nearest = backward(1, received, weighted1, tables, weights_pair, update_pair, [])
    received = exchange(sent, ("x", "c"))
    sent = level_zero_backward(received, weighted0, inverse, update, nearest, kept, other)
    total = summed(exchange(sent, ("x",)))
    return unpacked(total, with_partner(total))[None, None]


def solution(mesh):
    grid = np.array(mesh.devices).reshape(4, 2, 2, 2, 4)
    fine = Mesh(grid, AXES)
    leaf = ("z", "y1", "y0", "c")
    in_specs = (
        P(leaf, "x", None, None),
        P(leaf, "x", None, None),
        P(leaf, "x", None, None),
        P(leaf, None),
        P(leaf, "x", None),
        P(leaf, "x", None),
        P(leaf, "x", None),
    )
    out_specs = P(leaf, "x", None, None)
    return jax.shard_map(per_device, mesh=fine, in_specs=in_specs, out_specs=out_specs, check_vma=False)
```

time: 219 us -> 205 us (0.936)
  blocking collectives: 82.6 us -> 27.7 us
  local copies, waits for them, and re-layouts: 8.36 us -> 25.8 us
  starting transfers between devices: 39 us -> 55.6 us
  waiting for transfers between devices: 49.4 us -> 57.7 us
  other arithmetic: 2.37 us -> 0.04 us
    all_to_all x6 -> x2, blocking collectives: 82.6 us -> 27.7 us  [exchange(): return lax.all_to_all(value, axes, 0, 0, tiled=True)]
    unnamed x12 -> x50, local copies, waits for them, and re-layouts: 1.66 us -> 24.3 us
    all_to_all x8, starting transfers between devices: 30.2 us -> 39.9 us  [exchange(): return lax.all_to_all(value, axes, 0, 0, tiled=True)]
    ppermute x6 -> x7, waiting for transfers between devices: 0.92 us -> 9.96 us  [with_partner(): return lax.ppermute(value, 'c', [(0, 1), (1, 0)])]
    ppermute x1 -> x5, starting transfers between devices: 3.03 us -> 11 us  [the longest x4 8.41 us: across(): return lax.ppermute(value, axis, [(0, 1), (1, 0)])]
    all_to_all x8, waiting for transfers between devices: 48.4 us -> 42.9 us  [exchange(): return lax.all_to_all(value, axes, 0, 0, tiled=True)]
    ppermute x1 -> x5, waiting for transfers between devices: 0.01 us -> 4.88 us  [the longest x4 3.28 us: across(): return lax.ppermute(value, axis, [(0, 1), (1, 0)])]
    slice x12 -> x0, local copies, waits for them, and re-layouts: 4.01 us -> none  [the longest x1 0.92 us: per_device(): upper = sides[:, PIVOTS:]]
  transfers between devices with their start and end apart: 15 -> 20, of which waited for: 9 -> 15; matrix products, arithmetic and copies ran while one was open for 3% -> 1% of each run, Pallas kernels for 7% -> 2%
where the time goes in v2:
time: 205 us; the launch traced here: 203 us
  waiting for transfers between devices  57.7 us (28%)
  starting transfers between devices  55.6 us (27%)
  Pallas kernels  36.3 us (18%)
  blocking collectives  27.7 us (14%)
  local copies, waits for them, and re-layouts  25.8 us (13%)
    all_to_all x8, waiting for transfers between devices, exchange(): return lax.all_to_all(value, axes, 0, 0, tiled=True)  42.9 us
    all_to_all x8, starting transfers between devices, exchange(): return lax.all_to_all(value, axes, 0, 0, tiled=True)  39.9 us
    pallas_call x11, Pallas kernels, call(): pl.pallas_call(body, in_specs=specs, out_specs=[WHOLE] * len(out_shapes),...  36.3 us
    all_to_all x2, blocking collectives, exchange(): return lax.all_to_all(value, axes, 0, 0, tiled=True)  27.7 us
    unnamed x50, local copies, waits for them, and re-layouts  24.3 us
    ppermute x7, waiting for transfers between devices, with_partner(): return lax.ppermute(value, 'c', [(0, 1), (1, 0)])  9.96 us
    ppermute x4, starting transfers between devices, across(): return lax.ppermute(value, axis, [(0, 1), (1, 0)])  8.41 us
    ppermute x7, starting transfers between devices, with_partner(): return lax.ppermute(value, 'c', [(0, 1), (1, 0)])  4.7 us
  transfers between devices with their start and end apart: 20, of which 15 were waited for; matrix products, arithmetic and copies ran while one was open for 1% of the time, Pallas kernels for 2%

profile of v2, /device:TPU:1, one launch (start us, length us, event | category | flops | bytes accessed | tf_op | source)
XLA Modules:
  0.0 203.5 jit_solution(14711396684102040579)
XLA Ops:
  0.0 1.4 collective-permute-start.6
  1.4 6.9 %collective-permute-done.3.beside_ref = f32[96,512]{1,0:T(8,128)S(1)} collective-permute-done((f32[96,512]{1,0:T(8,128)}, f32[96,512]{1,0:T(8,128)S(1)}, u32[]{:S(2)}, u32[]{:S(2)}) %collective-permute-start.3) | collective-permute-done | bytes 196640 | tf_op jit(solution)/shard_map/ppermute | solution.py:42
  8.3 0.9 copy-done.16
  9.2 1.0 shard_map.73
  10.2 4.3 %all-to-all-start = ((f32[4,96,512]{2,1,0:T(8,128)}), f32[4,96,512]{2,1,0:T(8,128)S(1)}, u32[]{:S(2)}, u32[]{:S(2)}) async-start(f32[4,96,512]{2,1,0:T(8,128)} %shard_map.73), calls=%async_computation | async-start | bytes 1572864 | tf_op jit(solution)/shard_map/all_to_all | solution.py:38
  17.5 8.7 %all-to-all-done.first_ref.refs_5_ = f32[4,96,512]{2,1,0:T(8,128)S(1)} async-done(((f32[4,96,512]{2,1,0:T(8,128)}), f32[4,96,512]{2,1,0:T(8,128)S(1)}, u32[]{:S(2)}, u32[]{:S(2)}) %all-to-all-start) | async-done | bytes 786464 | tf_op jit(solution)/shard_map/all_to_all | solution.py:38
  26.2 2.1 %copy-done = f32[1,1,128,7680]{3,2,1,0:T(8,128)S(1)} copy-done((f32[1,1,128,7680]{3,2,1,0:T(8,128)S(1)}, f32[1,1,128,7680]{3,2,1,0:T(8,128)}, u32[]{:S(2)}) %copy-start) | copy-done | bytes 3932184
  28.3 1.2 copy-done.7
  29.5 0.9 shard_map.75
  31.1 1.3 collective-permute-start.4
  32.4 5.2 %all-to-all-start.1 = ((f32[8,48,256]{2,1,0:T(8,128)}), f32[8,48,256]{2,1,0:T(8,128)S(1)}, u32[]{:S(2)}, u32[]{:S(2)}) async-start(f32[8,48,256]{2,1,0:T(8,128)} %copy-done.11), calls=%async_computation.1 | async-start | bytes 786432 | tf_op jit(solution)/shard_map/all_to_all | solution.py:38
  38.9 2.6 %collective-permute-start = (s32[1,14]{1,0:T(1,128)S(1)}, s32[1,14]{1,0:T(1,128)S(1)}, u32[]{:S(2)}, u32[]{:S(2)}) collective-permute-start(s32[1,14]{1,0:T(1,128)S(1)} %copy-done.19), channel_id=1, source_target_pairs={{0,8},{4,20},{8,0},{12,28},{16,24},{20,4},{24,16},{28,12},{1,9},{5... | collective-permute-start | bytes 176 | tf_op jit(solution)/shard_map/ppermute | solution.py:428
  41.5 1.6 collective-permute-done.refs_1_
  43.1 1.2 collective-permute-done.2.refs_3_
  44.3 1.2 all-to-all-done.1.refs_4_
  45.6 2.1 %copy-done.1 = f32[1,1,128,7680]{3,2,1,0:T(8,128)S(1)} copy-done((f32[1,1,128,7680]{3,2,1,0:T(8,128)S(1)}, f32[1,1,128,7680]{3,2,1,0:T(8,128)}, u32[]{:S(2)}) %copy-start.1) | copy-done | bytes 3932184
  47.7 4.4 %shard_map.76 = (f32[8,48,512]{2,1,0:T(8,128)S(1)}, f32[48,256]{1,0:T(8,128)S(1)}, f32[2,4,96,128]{3,2,1,0:T(8,128)S(1)}) custom-call(s32[1,14]{1,0:T(1,128)S(1)} %copy-done.19, s32[1,14]{1,0:T(1,128)S(1)} %collective-permute-done.refs_1_, s32[1,14]{1,0:T(1,128)S(1)} %collective-permute-done.1.refs_2_, s32[1,14]{1,0:T(1,128)S(1)} %collective-permute-done.2.refs_3_, ...), custom_call_target="tpu_custom_call" | custom-call | tf_op jit(solution)/shard_map/pallas_call | solution.py:59
  52.8 14.1 %all_to_all.50.refs_4_ = f32[8,48,512]{2,1,0:T(8,128)S(1)} all-to-all(f32[8,48,512]{2,1,0:T(8,128)S(1)} %get-tuple-element.23), channel_id=1, replica_groups=mesh['z'=4,'y1'=2,'y0'=2,'c'=2,'x'=4] {'x','y0'}, dimensions={0} | all-to-all | bytes 1572864 | tf_op jit(solution)/shard_map/all_to_all | solution.py:38
  67.0 7.5 %shard_map.77 = (f32[8,48,128]{2,1,0:T(8,128)}, f32[48,256]{1,0:T(8,128)S(1)}) custom-call(s32[1,14]{1,0:T(1,128)S(1)} %copy-done.19, s32[1,14]{1,0:T(1,128)S(1)} %collective-permute-done.refs_1_, s32[1,14]{1,0:T(1,128)S(1)} %collective-permute-done.1.refs_2_, s32[1,14]{1,0:T(1,128)S(1)} %collective-permute-done.2.refs_3_, ...), custom_call_target="tpu_custom_call" | custom-call | tf_op jit(solution)/shard_map/pallas_call | solution.py:59
  75.1 3.6 %all-to-all-start.3 = ((f32[8,48,128]{2,1,0:T(8,128)}), f32[8,48,128]{2,1,0:T(8,128)S(1)}, u32[]{:S(2)}, u32[]{:S(2)}) async-start(f32[8,48,128]{2,1,0:T(8,128)} %get-tuple-element.24), calls=%async_computation.3 | async-start | bytes 393216 | tf_op jit(solution)/shard_map/all_to_all | solution.py:38
  78.7 2.9 %collective-permute-start.8 = (f32[2,4,96,128]{3,2,1,0:T(8,128)S(1)}, f32[2,4,96,128]{3,2,1,0:T(8,128)S(1)}, u32[]{:S(2)}, u32[]{:S(2)}) collective-permute-start(f32[2,4,96,128]{3,2,1,0:T(8,128)S(1)} %copy-done.10), channel_id=1, source_target_pairs={{0,16},{16,0},{1,17},{17,1},{2,18},{18,2},{3,19},{19,3},{4,20},{20... | collective-permute-start | bytes 1179656 | tf_op jit(solution)/shard_map/ppermute | solution.py:46
  81.6 2.7 %all-to-all-done.3 = f32[8,48,128]{2,1,0:T(8,128)S(1)} async-done(((f32[8,48,128]{2,1,0:T(8,128)}), f32[8,48,128]{2,1,0:T(8,128)S(1)}, u32[]{:S(2)}, u32[]{:S(2)}) %all-to-all-start.3) | async-done | bytes 196640 | tf_op jit(solution)/shard_map/all_to_all | solution.py:38
  85.1 5.0 %all-to-all-start.4 = ((f32[16,48,128]{2,1,0:T(8,128)}), f32[16,48,128]{2,1,0:T(8,128)S(1)}, u32[]{:S(2)}, u32[]{:S(2)}) async-start(f32[16,48,128]{2,1,0:T(8,128)} %broadcast_in_dim.6), calls=%async_computation.4 | async-start | bytes 786432 | tf_op jit(solution)/shard_map/all_to_all | solution.py:38
  90.1 1.7 collective-permute-done.8.refs_6_
  91.8 6.4 %all-to-all-done.4.refs_4_ = f32[16,48,128]{2,1,0:T(8,128)S(1)} async-done(((f32[16,48,128]{2,1,0:T(8,128)}), f32[16,48,128]{2,1,0:T(8,128)S(1)}, u32[]{:S(2)}, u32[]{:S(2)}) %all-to-all-start.4) | async-done | bytes 393248 | tf_op jit(solution)/shard_map/all_to_all | solution.py:38
  98.2 2.1 %copy-done.3 = f32[1,1,128,7680]{3,2,1,0:T(8,128)S(1)} copy-done((f32[1,1,128,7680]{3,2,1,0:T(8,128)S(1)}, f32[1,1,128,7680]{3,2,1,0:T(8,128)}, u32[]{:S(2)}) %copy-start.3) | copy-done | bytes 3932184
  100.3 12.1 %shard_map.78 = (f32[16,48,128]{2,1,0:T(8,128)S(1)}, f32[4,2,48,256]{3,2,1,0:T(8,128)S(1)}, f32[4,2,48,256]{3,2,1,0:T(8,128)S(1)}) custom-call(s32[1,14]{1,0:T(1,128)S(1)} %copy-done.19, s32[1,14]{1,0:T(1,128)S(1)} %collective-permute-done.refs_1_, s32[1,14]{1,0:T(1,128)S(1)} %collective-permute-done.1.refs_2_, s32[1,14]{1,0:T(1,128)S(1)} %collective-permute-done.2.refs_3_, ...), custom_call_target="tpu_custom_call" | custom-call | tf_op jit(solution)/shard_map/pallas_call | solution.py:59
  114.0 3.6 %all-to-all-start.5 = ((f32[16,48,128]{2,1,0:T(8,128)}), f32[16,48,128]{2,1,0:T(8,128)S(1)}, u32[]{:S(2)}, u32[]{:S(2)}) async-start(f32[16,48,128]{2,1,0:T(8,128)} %copy-done.13), calls=%async_computation.5 | async-start | bytes 786432 | tf_op jit(solution)/shard_map/all_to_all | solution.py:38
  117.6 2.9 %collective-permute-start.9 = (f32[4,2,48,256]{3,2,1,0:T(8,128)}, f32[4,2,48,256]{3,2,1,0:T(8,128)S(1)}, u32[]{:S(2)}, u32[]{:S(2)}) collective-permute-start(f32[4,2,48,256]{3,2,1,0:T(8,128)} %copy-done.24), channel_id=1, source_target_pairs={{0,16},{16,0},{1,17},{17,1},{2,18},{18,2},{3,19},{19,3},{4,20},{20... | collective-permute-start | bytes 1179656 | tf_op jit(solution)/shard_map/ppermute | solution.py:46
  120.5 5.2 %all-to-all-done.5 = f32[16,48,128]{2,1,0:T(8,128)S(1)} async-done(((f32[16,48,128]{2,1,0:T(8,128)}), f32[16,48,128]{2,1,0:T(8,128)S(1)}, u32[]{:S(2)}, u32[]{:S(2)}) %all-to-all-start.5) | async-done | bytes 393248 | tf_op jit(solution)/shard_map/all_to_all | solution.py:38
  126.4 3.4 %all-to-all-start.6 = ((f32[8,48,128]{2,1,0:T(8,128)}), f32[8,48,128]{2,1,0:T(8,128)S(1)}, u32[]{:S(2)}, u32[]{:S(2)}) async-start(f32[8,48,128]{2,1,0:T(8,128)} %broadcast_in_dim.7), calls=%async_computation.6 | async-start | bytes 393216 | tf_op jit(solution)/shard_map/all_to_all | solution.py:38
  129.8 1.6 collective-permute-done.9.refs_7_
  131.4 3.9 %all-to-all-done.6.refs_4_ = f32[8,48,128]{2,1,0:T(8,128)S(1)} async-done(((f32[8,48,128]{2,1,0:T(8,128)}), f32[8,48,128]{2,1,0:T(8,128)S(1)}, u32[]{:S(2)}, u32[]{:S(2)}) %all-to-all-start.6) | async-done | bytes 196640 | tf_op jit(solution)/shard_map/all_to_all | solution.py:38
  135.4 2.1 %copy-done.4 = f32[1,1,128,7680]{3,2,1,0:T(8,128)S(1)} copy-done((f32[1,1,128,7680]{3,2,1,0:T(8,128)S(1)}, f32[1,1,128,7680]{3,2,1,0:T(8,128)}, u32[]{:S(2)}) %copy-start.4) | copy-done | bytes 3932184
  138.3 5.8 %shard_map.79 = (f32[8,48,512]{2,1,0:T(8,128)}, f32[2,4,48,256]{3,2,1,0:T(8,128)S(1)}, f32[2,4,48,256]{3,2,1,0:T(8,128)S(1)}) custom-call(s32[1,14]{1,0:T(1,128)S(1)} %copy-done.19, s32[1,14]{1,0:T(1,128)S(1)} %collective-permute-done.refs_1_, s32[1,14]{1,0:T(1,128)S(1)} %collective-permute-done.1.refs_2_, s32[1,14]{1,0:T(1,128)S(1)} %collective-permute-done.2.refs_3_, ...), custom_call_target="tpu_custom_call" | custom-call | tf_op jit(solution)/shard_map/pallas_call | solution.py:59
  144.8 3.5 %all-to-all-start.7 = ((f32[8,48,512]{2,1,0:T(8,128)}), f32[8,48,512]{2,1,0:T(8,128)S(1)}, u32[]{:S(2)}, u32[]{:S(2)}) async-start(f32[8,48,512]{2,1,0:T(8,128)} %get-tuple-element.30), calls=%async_computation.7 | async-start | bytes 1572864 | tf_op jit(solution)/shard_map/all_to_all | solution.py:38
  148.4 1.4 collective-permute-start.10
  149.7 7.0 %all-to-all-done.7.refs_4_ = f32[8,48,512]{2,1,0:T(8,128)S(1)} async-done(((f32[8,48,512]{2,1,0:T(8,128)}), f32[8,48,512]{2,1,0:T(8,128)S(1)}, u32[]{:S(2)}, u32[]{:S(2)}) %all-to-all-start.7) | async-done | bytes 786464 | tf_op jit(solution)/shard_map/all_to_all | solution.py:38
  156.7 2.1 %copy-done.5 = f32[1,1,128,7680]{3,2,1,0:T(8,128)S(1)} copy-done((f32[1,1,128,7680]{3,2,1,0:T(8,128)S(1)}, f32[1,1,128,7680]{3,2,1,0:T(8,128)}, u32[]{:S(2)}) %copy-start.5) | copy-done | bytes 3932184
  158.8 2.7 %shard_map.80 = (f32[8,48,256]{2,1,0:T(8,128)S(1)}, f32[4,48,256]{2,1,0:T(8,128)S(1)}) custom-call(s32[1,14]{1,0:T(1,128)S(1)} %copy-done.19, s32[1,14]{1,0:T(1,128)S(1)} %collective-permute-done.refs_1_, s32[1,14]{1,0:T(1,128)S(1)} %collective-permute-done.1.refs_2_, s32[1,14]{1,0:T(1,128)S(1)} %collective-permute-done.2.refs_3_, ...), custom_call_target="tpu_custom_call" | custom-call | tf_op jit(solution)/shard_map/pallas_call | solution.py:59
  163.0 11.3 %all-to-all-start.8 = ((f32[8,48,256]{2,1,0:T(8,128)}), f32[8,48,256]{2,1,0:T(8,128)S(1)}, u32[]{:S(2)}, u32[]{:S(2)}) async-start(f32[8,48,256]{2,1,0:T(8,128)} %copy-done.12), calls=%async_computation.8 | async-start | bytes 786432 | tf_op jit(solution)/shard_map/all_to_all | solution.py:38
  174.3 7.7 %all-to-all-done.8.received_ref = f32[8,48,256]{2,1,0:T(8,128)S(1)} async-done(((f32[8,48,256]{2,1,0:T(8,128)}), f32[8,48,256]{2,1,0:T(8,128)S(1)}, u32[]{:S(2)}, u32[]{:S(2)}) %all-to-all-start.8) | async-done | bytes 393248 | tf_op jit(solution)/shard_map/all_to_all | solution.py:38
  182.0 2.1 %copy-done.6 = f32[1,1,128,7680]{3,2,1,0:T(8,128)S(1)} copy-done((f32[1,1,128,7680]{3,2,1,0:T(8,128)S(1)}, f32[1,1,128,7680]{3,2,1,0:T(8,128)}, u32[]{:S(2)}) %copy-start.6) | copy-done | bytes 3932184
  184.1 0.9 copy-done.15
  185.0 0.9 shard_map.81
  185.9 13.6 %all_to_all.51.received_ref = f32[4,96,512]{2,1,0:T(8,128)S(1)} all-to-all(f32[4,96,512]{2,1,0:T(8,128)S(1)} %shard_map.81), channel_id=1, replica_groups=mesh['z'=4,'y1'=2,'y0'=2,'c'=2,'x'=4] {'x'}, dimensions={0} | all-to-all | bytes 1572864 | tf_op jit(solution)/shard_map/all_to_all | solution.py:38
  199.5 2.2 %collective-permute-start.11 = (f32[96,512]{1,0:T(8,128)S(1)}, f32[96,512]{1,0:T(8,128)S(1)}, u32[]{:S(2)}, u32[]{:S(2)}) collective-permute-start(f32[96,512]{1,0:T(8,128)S(1)} %shard_map.82.total_ref), channel_id=1, source_target_pairs={{0,4},{4,0},{1,5},{5,1},{2,6},{6,2},{3,7},{7,3},{8,12},{12,8},{9,1... | collective-permute-start | bytes 589832 | tf_op jit(solution)/shard_map/ppermute | solution.py:42
  201.7 1.1 collective-permute-done.11.beside_ref
  (59 shorter events, 13.2 us)
Async XLA Ops:
  0.0 45.5 %collective-permute-start.6 = (f32[128,7680]{1,0:T(8,128)}, f32[128,7680]{1,0:T(8,128)}, u32[]{:S(2)}, u32[]{:S(2)}) collective-permute-start(f32[128,7680]{1,0:T(8,128)} %bitcast.7), channel_id=1, source_target_pairs={{0,4},{4,0},{1,5},{5,1},{2,6},{6,2},{3,7},{7,3},{8,12},{12,8},{9,1... | collective-permute-start | bytes 11796488 | tf_op jit(solution)/shard_map/ppermute | solution.py:42
  1.4 6.9 %collective-permute-start.3 = (f32[96,512]{1,0:T(8,128)}, f32[96,512]{1,0:T(8,128)S(1)}, u32[]{:S(2)}, u32[]{:S(2)}) collective-permute-start(f32[96,512]{1,0:T(8,128)} %bitcast.22), channel_id=1, source_target_pairs={{0,4},{4,0},{1,5},{5,1},{2,6},{6,2},{3,7},{7,3},{8,12},{12,8},{9,1... | collective-permute-start | bytes 589832 | tf_op jit(solution)/shard_map/ppermute | solution.py:42
  8.3 0.9 copy-start.16
  10.2 27.6 %copy-start.19 = (s32[1,14]{1,0:T(1,128)S(1)}, s32[1,14]{1,0:T(1,128)}, u32[]{:S(2)}) copy-start(s32[1,14]{1,0:T(1,128)} %refs_0_.9) | copy-start | bytes 172
  10.2 35.3 %copy-start.8 = (f32[1,1,128,1792]{3,2,1,0:T(8,128)S(1)}, f32[1,1,128,1792]{3,2,1,0:T(8,128)}, u32[]{:S(2)}) copy-start(f32[1,1,128,1792]{3,2,1,0:T(8,128)} %param.9) | copy-start | bytes 2752516
  10.2 16.0 %all-to-all-start = ((f32[4,96,512]{2,1,0:T(8,128)}), f32[4,96,512]{2,1,0:T(8,128)S(1)}, u32[]{:S(2)}, u32[]{:S(2)}) async-start(f32[4,96,512]{2,1,0:T(8,128)} %shard_map.73), calls=%async_computation | async-start | bytes 1572864 | tf_op jit(solution)/shard_map/all_to_all | solution.py:38
  14.5 29.8 %collective-permute-start.7 = (f32[128,1792]{1,0:T(8,128)}, f32[128,1792]{1,0:T(8,128)S(1)}, u32[]{:S(2)}, u32[]{:S(2)}) collective-permute-start(f32[128,1792]{1,0:T(8,128)} %bitcast.15), channel_id=1, source_target_pairs={{0,4},{4,0},{1,5},{5,1},{2,6},{6,2},{3,7},{7,3},{8,12},{12,8},{9,1... | collective-permute-start | bytes 2752520 | tf_op jit(solution)/shard_map/ppermute | solution.py:42
  15.1 0.7 copy-start.20
  15.8 0.7 copy-start.21
  16.5 0.7 copy-start.22
  26.2 2.1 %copy-start = (f32[1,1,128,7680]{3,2,1,0:T(8,128)S(1)}, f32[1,1,128,7680]{3,2,1,0:T(8,128)}, u32[]{:S(2)}) copy-start(f32[1,1,128,7680]{3,2,1,0:T(8,128)} %param.8) | copy-start | bytes 11796484
  28.3 1.2 copy-start.7
  30.4 0.7 copy-start.11
  31.1 14.4 %collective-permute-start.4 = (f32[4,96,256]{2,1,0:T(8,128)S(1)}, f32[4,96,256]{2,1,0:T(8,128)}, u32[]{:S(2)}, u32[]{:S(2)}) collective-permute-start(f32[4,96,256]{2,1,0:T(8,128)S(1)} %get-tuple-element.22.refs_6_.refs_5_), channel_id=1, source_target_pairs={{0,8},{8,0},{1,9},{9,1},{2,10},{10,2},{3,11},{11,3},{4,12},{12,4},... | collective-permute-start | bytes 1179656 | tf_op jit(solution)/shard_map/ppermute | solution.py:46
  32.4 13.1 %all-to-all-start.1 = ((f32[8,48,256]{2,1,0:T(8,128)}), f32[8,48,256]{2,1,0:T(8,128)S(1)}, u32[]{:S(2)}, u32[]{:S(2)}) async-start(f32[8,48,256]{2,1,0:T(8,128)} %copy-done.11), calls=%async_computation.1 | async-start | bytes 786432 | tf_op jit(solution)/shard_map/all_to_all | solution.py:38
  37.6 6.7 %collective-permute-start.5 = (f32[2,512]{1,0:T(2,128)S(1)}, f32[2,512]{1,0:T(2,128)S(1)}, u32[]{:S(2)}, u32[]{:S(2)}) collective-permute-start(f32[2,512]{1,0:T(2,128)S(1)} %shard_map.74.factors_ref.refs_8_.refs_7_), channel_id=1, source_target_pairs={{0,4},{4,0},{1,5},{5,1},{2,6},{6,2},{3,7},{7,3},{8,12},{12,8},{9,1... | collective-permute-start | bytes 12296 | tf_op jit(solution)/shard_map/ppermute | solution.py:42
  37.7 1.2 collective-permute-start.1
  38.9 4.2 %collective-permute-start = (s32[1,14]{1,0:T(1,128)S(1)}, s32[1,14]{1,0:T(1,128)S(1)}, u32[]{:S(2)}, u32[]{:S(2)}) collective-permute-start(s32[1,14]{1,0:T(1,128)S(1)} %copy-done.19), channel_id=1, source_target_pairs={{0,8},{4,20},{8,0},{12,28},{16,24},{20,4},{24,16},{28,12},{1,9},{5... | collective-permute-start | bytes 176 | tf_op jit(solution)/shard_map/ppermute | solution.py:428
  43.1 1.2 collective-permute-start.2
  45.5 2.1 %copy-start.1 = (f32[1,1,128,7680]{3,2,1,0:T(8,128)S(1)}, f32[1,1,128,7680]{3,2,1,0:T(8,128)}, u32[]{:S(2)}) copy-start(f32[1,1,128,7680]{3,2,1,0:T(8,128)} %param.8) | copy-start | bytes 11796484
  47.7 19.3 %copy-start.2 = (f32[1,1,128,7680]{3,2,1,0:T(8,128)S(1)}, f32[1,1,128,7680]{3,2,1,0:T(8,128)}, u32[]{:S(2)}) copy-start(f32[1,1,128,7680]{3,2,1,0:T(8,128)} %param.8) | copy-start | bytes 11796484
  52.1 0.7 copy-start.9
  67.0 11.7 %copy-start.10 = (f32[2,4,96,128]{3,2,1,0:T(8,128)S(1)}, f32[2,4,96,128]{3,2,1,0:T(8,128)}, u32[]{:S(2)}) copy-start(f32[2,4,96,128]{3,2,1,0:T(8,128)} %copy-done.9) | copy-start | bytes 1179652
  74.5 0.6 copy-start.17
  75.1 9.2 %all-to-all-start.3 = ((f32[8,48,128]{2,1,0:T(8,128)}), f32[8,48,128]{2,1,0:T(8,128)S(1)}, u32[]{:S(2)}, u32[]{:S(2)}) async-start(f32[8,48,128]{2,1,0:T(8,128)} %get-tuple-element.24), calls=%async_computation.3 | async-start | bytes 393216 | tf_op jit(solution)/shard_map/all_to_all | solution.py:38
  78.7 13.1 %collective-permute-start.8 = (f32[2,4,96,128]{3,2,1,0:T(8,128)S(1)}, f32[2,4,96,128]{3,2,1,0:T(8,128)S(1)}, u32[]{:S(2)}, u32[]{:S(2)}) collective-permute-start(f32[2,4,96,128]{3,2,1,0:T(8,128)S(1)} %copy-done.10), channel_id=1, source_target_pairs={{0,16},{16,0},{1,17},{17,1},{2,18},{18,2},{3,19},{19,3},{4,20},{20... | collective-permute-start | bytes 1179656 | tf_op jit(solution)/shard_map/ppermute | solution.py:46
  85.1 13.1 %all-to-all-start.4 = ((f32[16,48,128]{2,1,0:T(8,128)}), f32[16,48,128]{2,1,0:T(8,128)S(1)}, u32[]{:S(2)}, u32[]{:S(2)}) async-start(f32[16,48,128]{2,1,0:T(8,128)} %broadcast_in_dim.6), calls=%async_computation.4 | async-start | bytes 786432 | tf_op jit(solution)/shard_map/all_to_all | solution.py:38
  98.2 2.1 %copy-start.3 = (f32[1,1,128,7680]{3,2,1,0:T(8,128)S(1)}, f32[1,1,128,7680]{3,2,1,0:T(8,128)}, u32[]{:S(2)}) copy-start(f32[1,1,128,7680]{3,2,1,0:T(8,128)} %param.8) | copy-start | bytes 11796484
  112.4 0.8 copy-start.13
  113.2 0.7 copy-start.24
  114.0 11.7 %all-to-all-start.5 = ((f32[16,48,128]{2,1,0:T(8,128)}), f32[16,48,128]{2,1,0:T(8,128)S(1)}, u32[]{:S(2)}, u32[]{:S(2)}) async-start(f32[16,48,128]{2,1,0:T(8,128)} %copy-done.13), calls=%async_computation.5 | async-start | bytes 786432 | tf_op jit(solution)/shard_map/all_to_all | solution.py:38
  117.6 13.8 %collective-permute-start.9 = (f32[4,2,48,256]{3,2,1,0:T(8,128)}, f32[4,2,48,256]{3,2,1,0:T(8,128)S(1)}, u32[]{:S(2)}, u32[]{:S(2)}) collective-permute-start(f32[4,2,48,256]{3,2,1,0:T(8,128)} %copy-done.24), channel_id=1, source_target_pairs={{0,16},{16,0},{1,17},{17,1},{2,18},{18,2},{3,19},{19,3},{4,20},{20... | collective-permute-start | bytes 1179656 | tf_op jit(solution)/shard_map/ppermute | solution.py:46
  126.4 8.9 %all-to-all-start.6 = ((f32[8,48,128]{2,1,0:T(8,128)}), f32[8,48,128]{2,1,0:T(8,128)S(1)}, u32[]{:S(2)}, u32[]{:S(2)}) async-start(f32[8,48,128]{2,1,0:T(8,128)} %broadcast_in_dim.7), calls=%async_computation.6 | async-start | bytes 393216 | tf_op jit(solution)/shard_map/all_to_all | solution.py:38
  135.4 2.1 %copy-start.4 = (f32[1,1,128,7680]{3,2,1,0:T(8,128)S(1)}, f32[1,1,128,7680]{3,2,1,0:T(8,128)}, u32[]{:S(2)}) copy-start(f32[1,1,128,7680]{3,2,1,0:T(8,128)} %param.8) | copy-start | bytes 11796484
  137.5 0.8 copy-start.18
  144.0 0.8 copy-start.23
  144.8 11.9 %all-to-all-start.7 = ((f32[8,48,512]{2,1,0:T(8,128)}), f32[8,48,512]{2,1,0:T(8,128)S(1)}, u32[]{:S(2)}, u32[]{:S(2)}) async-start(f32[8,48,512]{2,1,0:T(8,128)} %get-tuple-element.30), calls=%async_computation.7 | async-start | bytes 1572864 | tf_op jit(solution)/shard_map/all_to_all | solution.py:38
  148.4 25.9 %collective-permute-start.10 = (f32[2,4,48,256]{3,2,1,0:T(8,128)}, f32[2,4,48,256]{3,2,1,0:T(8,128)S(1)}, u32[]{:S(2)}, u32[]{:S(2)}) collective-permute-start(f32[2,4,48,256]{3,2,1,0:T(8,128)} %copy-done.23), channel_id=1, source_target_pairs={{0,8},{8,0},{1,9},{9,1},{2,10},{10,2},{3,11},{11,3},{4,12},{12,4},... | collective-permute-start | bytes 1179656 | tf_op jit(solution)/shard_map/ppermute | solution.py:46
  156.7 2.1 %copy-start.5 = (f32[1,1,128,7680]{3,2,1,0:T(8,128)S(1)}, f32[1,1,128,7680]{3,2,1,0:T(8,128)}, u32[]{:S(2)}) copy-start(f32[1,1,128,7680]{3,2,1,0:T(8,128)} %param.8) | copy-start | bytes 11796484
  161.6 0.8 copy-start.12
  162.3 0.7 copy-start.14
  163.0 19.0 %all-to-all-start.8 = ((f32[8,48,256]{2,1,0:T(8,128)}), f32[8,48,256]{2,1,0:T(8,128)S(1)}, u32[]{:S(2)}, u32[]{:S(2)}) async-start(f32[8,48,256]{2,1,0:T(8,128)} %copy-done.12), calls=%async_computation.8 | async-start | bytes 786432 | tf_op jit(solution)/shard_map/all_to_all | solution.py:38
  182.0 2.1 %copy-start.6 = (f32[1,1,128,7680]{3,2,1,0:T(8,128)S(1)}, f32[1,1,128,7680]{3,2,1,0:T(8,128)}, u32[]{:S(2)}) copy-start(f32[1,1,128,7680]{3,2,1,0:T(8,128)} %param.8) | copy-start | bytes 11796484
  184.1 0.9 copy-start.15
  199.5 3.2 %collective-permute-start.11 = (f32[96,512]{1,0:T(8,128)S(1)}, f32[96,512]{1,0:T(8,128)S(1)}, u32[]{:S(2)}, u32[]{:S(2)}) collective-permute-start(f32[96,512]{1,0:T(8,128)S(1)} %shard_map.82.total_ref), channel_id=1, source_target_pairs={{0,4},{4,0},{1,5},{5,1},{2,6},{6,2},{3,7},{7,3},{8,12},{12,8},{9,1... | collective-permute-start | bytes 589832 | tf_op jit(solution)/shard_map/ppermute | solution.py:42

commit v3 on v2

v3 whole, which is shorter than its diff:
```python
import jax
import jax.numpy as jnp
import numpy as np
from jax import lax
from jax.experimental import pallas as pl
from jax.experimental.pallas import tpu as pltpu
from jax.sharding import Mesh, PartitionSpec as P

LEVELS = 4
BLOCK = 128
PIVOTS = 128
SIDES = 96
HALF = SIDES // 2
AXES = ("z", "y1", "y0", "c", "x")

exact_mode = lax.Precision.HIGHEST


def parts(value):
    high = value.astype(jnp.bfloat16)
    return high, (value - high.astype(jnp.float32)).astype(jnp.bfloat16)


def product(left, high, low, side):
    left_high, left_low = parts(left)
    dims = (((1,), (side,)), ((), ()))

    def dot(a, b):
        return lax.dot_general(a, b, dims, preferred_element_type=jnp.float32)

    return dot(left_high, high) + (dot(left_high, low) + dot(left_low, high))


def dot_full(left, right):
    return lax.dot_general(
        left, right, (((1,), (0,)), ((), ())), precision=exact_mode, preferred_element_type=jnp.float32
    )


def exchange(value, axes):
    return lax.all_to_all(value, axes, 0, 0, tiled=True)


def with_partner(value):
    return lax.ppermute(value, "c", [(0, 1), (1, 0)])


def across(value, axis):
    return lax.ppermute(value, axis, [(0, 1), (1, 0)])


def block_at(index, size=BLOCK):
    return pl.ds(pl.multiple_of(index * size, size), size)


WHOLE = pl.BlockSpec(memory_space=pltpu.VMEM)
SCALARS = pl.BlockSpec(memory_space=pltpu.SMEM)
FAR = pl.BlockSpec(memory_space=pltpu.HBM)


def call(body, out_shapes, operands, specs, scratch=(), limit=16):
    return pl.pallas_call(
        body,
        in_specs=specs,
        out_specs=[WHOLE] * len(out_shapes),
        out_shape=[jax.ShapeDtypeStruct(s, jnp.float32) for s in out_shapes],
        scratch_shapes=list(scratch),
        compiler_params=pltpu.CompilerParams(vmem_limit_bytes=limit * 1024 * 1024),
    )(*operands)


def prepared(pair, spans, after):
    def body(*refs):
        sources = refs[: len(pair)]
        outs = refs[len(pair) + 1 :][: len(spans)]
        buffers = refs[len(pair) + 1 + len(spans) : -1]
        semaphores = refs[-1]
        moves = []
        for i, (start, width) in enumerate(spans):
            for side, source in enumerate(sources):
                move = pltpu.make_async_copy(
                    source.at[:, pl.ds(start, width)],
                    buffers[i].at[pl.ds(side * PIVOTS, PIVOTS), :],
                    semaphores.at[i, side],
                )
                move.start()
                moves.append((i, side, move))
        for i, side, move in moves:
            move.wait()
            rows = slice(side * PIVOTS, (side + 1) * PIVOTS)
            width = spans[i][1]
            step = min(width, 512)
            for at in range(0, width, step):
                high, low = parts(buffers[i][rows, at : at + step])
                outs[i][0, rows, at : at + step] = high
                outs[i][1, rows, at : at + step] = low

    count = len(pair) * PIVOTS
    return pl.pallas_call(
        body,
        in_specs=[FAR] * len(pair) + [FAR],
        out_specs=[WHOLE] * len(spans),
        out_shape=[jax.ShapeDtypeStruct((2, count, width), jnp.bfloat16) for _, width in spans],
        scratch_shapes=[pltpu.VMEM((count, width), jnp.float32) for _, width in spans]
        + [pltpu.SemaphoreType.DMA((len(spans), len(pair)))],
        compiler_params=pltpu.CompilerParams(vmem_limit_bytes=24 * 1024 * 1024),
    )(*pair, after)


def pivot_apply(solved, own, swapped):
    lane = lax.broadcasted_iota(jnp.int32, solved.shape, 1)
    width = solved.shape[1]
    beside = jnp.where(lane % 2 == 0, pltpu.roll(solved, width - 1, 1), pltpu.roll(solved, 1, 1))
    return own * solved + swapped * beside


def pivot_factors(kinds, diagonal, coupling):
    def body(kinds_ref, diagonal_ref, coupling_ref, out_ref):
        width = diagonal_ref.shape[1]
        row = lax.broadcasted_iota(jnp.int32, (width // 2, width), 0)
        col = lax.broadcasted_iota(jnp.int32, (width // 2, width), 1)
        widen = (col // 2 == row).astype(jnp.float32)
        pair = jnp.concatenate(
            [kinds_ref[...].astype(jnp.float32), coupling_ref[...], jnp.zeros((6, width // 2), jnp.float32)], 0
        )
        wide = dot_full(pair, widen)
        is_pair = wide[0:1] > 0.5
        couple = wide[1:2]
        own = jnp.broadcast_to(diagonal_ref[...], (8, width))
        lane = lax.broadcasted_iota(jnp.int32, (8, width), 1)
        other = jnp.where(lane % 2 == 0, pltpu.roll(own, width - 1, 1), pltpu.roll(own, 1, 1))[0:1]
        own = own[0:1]
        determinant = own * other - couple * couple
        out_ref[0:1, :] = jnp.where(is_pair, other / determinant, 1.0 / own)
        out_ref[1:2, :] = jnp.where(is_pair, -couple / determinant, 0.0)

    return call(body, [(2, diagonal.shape[1])], [kinds, diagonal, coupling], [WHOLE] * 3)[0]


def packed_sides(sides, beside):
    def body(sides_ref, beside_ref, out_ref):
        c = lax.axis_index("c")
        mine = pl.ds(pl.multiple_of(c * HALF, 8), HALF)
        theirs = pl.ds(pl.multiple_of((1 - c) * HALF, 8), HALF)
        out_ref[mine] = sides_ref[mine, 2 * PIVOTS :]
        out_ref[theirs] = beside_ref[mine, 2 * PIVOTS :]

    return call(body, [(SIDES, 256)], [sides, beside], [WHOLE] * 2)[0]


def level_zero_forward(first, sides, weights, updates, factors):
    def body(first_ref, sides_ref, weights_ref, updates_ref, factors_ref, sent_ref, weighted_ref):
        gathered = jnp.concatenate([first_ref[q] for q in range(4)], 1)
        solved = product(gathered, weights_ref[0], weights_ref[1], 1)
        weighted_ref[...] = pivot_apply(solved, factors_ref[0:1, :PIVOTS], factors_ref[1:2, :PIVOTS])
        part = product(solved, updates_ref[0], updates_ref[1], 0)
        for c in range(2):
            half = slice(c * HALF, (c + 1) * HALF)
            for x in range(4):
                sent_ref[c * 4 + x, :, :256] = part[half]
                sent_ref[c * 4 + x, :, 256:] = sides_ref[half, PIVOTS : 2 * PIVOTS]

    return call(
        body,
        [(8, HALF, 384), (SIDES, PIVOTS)],
        [first, sides, weights, updates, factors],
        [WHOLE] * 5,
    )


def child_block(level, tables, child, k):
    own_ref, side_ref, own_beside_ref, side_beside_ref = tables
    c = lax.axis_index("c")
    if level == 1:
        return jnp.where(c == child, own_ref[0, k], own_beside_ref[0, k])
    if level == 2:
        sibling = jnp.where(c == 0, side_ref[0, 2 + k], side_beside_ref[0, 2 + k])
        return jnp.where(lax.axis_index("y0") == child, own_ref[0, 2 + k], sibling)
    sibling = jnp.where(c == 0, side_beside_ref[0, 6 + k], side_ref[0, 6 + k])
    return jnp.where(lax.axis_index("y1") == child, own_ref[0, 6 + k], sibling)


def both_factors(level, factors, beside):
    c = lax.axis_index("c")
    at = slice(level * PIVOTS, (level + 1) * PIVOTS)
    return [jnp.concatenate([factors[i : i + 1, at], beside[i : i + 1, at]], 1) for i in range(2)]


def halves(rows):
    return jnp.concatenate([rows[:HALF], rows[HALF:]], 1)


def forward(level, received, sides, tables, weights, updates, factors, partner_factors):
    width = 1 << level
    span = 4 * PIVOTS * width
    chunks = span // 512
    update_len = 2 * PIVOTS * width if level < 3 else 0
    blocks = (2, 4, 8)[level - 1]
    n_sides = len(sides)
    n_updates = 1 if level < 3 else 0

    def body(*refs):
        refs = list(refs)

        def take(count):
            taken, refs[:] = refs[:count], refs[count:]
            return taken

        tables_refs = take(4)
        (received_ref,) = take(1)
        sides_refs = take(n_sides)
        factors_ref, beside_ref, weights_ref = take(3)
        updates_ref = take(n_updates)
        outs = take(2 if level < 3 else 3)
        (b_ref,) = take(1)
        x0, y0, y1 = lax.axis_index("x"), lax.axis_index("y0"), lax.axis_index("y1")
        if level == 1:
            for x in range(4):
                for c in range(2):
                    b_ref[:, (x * 2 + c) * PIVOTS : (x * 2 + c + 1) * PIVOTS] = received_ref[c * 4 + x, :, 256:]
        elif level == 2:
            for flip in range(2):
                for x in range(4):
                    b_ref[:, block_at((x0 ^ x) * 2 + (y0 ^ flip), 256)] = halves(sides_refs[flip][x, :, :PIVOTS])
        else:
            for high in range(2):
                for flip in range(2):
                    for x in range(4):
                        where = block_at((x0 ^ x) * 4 + (y1 ^ high) * 2 + (y0 ^ flip), 256)
                        b_ref[:, where] = halves(sides_refs[high][flip, x])
        for child in range(2):
            if level == 1:
                total = sum(received_ref[child * 4 + x, :, :256] for x in range(4))
            elif level == 2:
                total = sum(received_ref[x * 2 + child] for x in range(4))
            for k in range(blocks):
                if level < 3:
                    piece = total[:, k * BLOCK : (k + 1) * BLOCK]
                else:
                    piece = received_ref[(k // 2) * 4 + child * 2 + k % 2]
                where = block_at(child_block(level, tables_refs, child, k))
                b_ref[:, where] = b_ref[:, where] - piece
        solved = jnp.zeros((HALF, 2 * PIVOTS), jnp.float32)
        for k in range(chunks):
            at = slice(k * 512, (k + 1) * 512)
            solved += product(b_ref[:, at], weights_ref[0, :, at], weights_ref[1, :, at], 1)
        weighted = pivot_apply(solved, *both_factors(level, factors_ref, beside_ref))
        if level < 3:
            outs[1][...] = weighted
            for k in range(update_len // 256):
                at = slice(k * 256, (k + 1) * 256)
                part = product(solved, updates_ref[0][0, :, at], updates_ref[0][1, :, at], 0)
                if level == 1:
                    for i in range(8):
                        outs[0][i, :, at] = part
                else:
                    outs[0][2 * k] = part[:, :BLOCK]
                    outs[0][2 * k + 1] = part[:, BLOCK:]
        else:
            sent_ref, keep_ref, far_ref = outs
            for k in range(chunks):
                at = slice(k * 512, (k + 1) * 512)
                b_ref[:, at] = product(weighted, weights_ref[0, :, at], weights_ref[1, :, at], 0)
            for child in range(2):
                for k in range(8):
                    where = block_at(child_block(3, tables_refs, child, k))
                    sent_ref[(k // 2) * 4 + child * 2 + k % 2] = b_ref[:, where]
            for x in range(4):
                for low in range(2):
                    keep_ref[x, low] = b_ref[:, block_at(x * 4 + y1 * 2 + low, 256)]
                    far_ref[x, low] = b_ref[:, block_at(x * 4 + (1 - y1) * 2 + low, 256)]

    outs = {
        1: [(8, HALF, 512), (HALF, 256)],
        2: [(8, HALF, BLOCK), (HALF, 256)],
        3: [(16, HALF, BLOCK), (4, 2, HALF, 256), (4, 2, HALF, 256)],
    }[level]
    operands = [*tables, received, *sides, factors, partner_factors, weights]
    if level < 3:
        operands.append(updates)
    specs = [SCALARS] * 4 + [WHOLE] * (len(operands) - 4)
    return call(body, outs, operands, specs, [pltpu.VMEM((HALF, span), jnp.float32)])


def backward(level, received, weighted, tables, weights, updates, answers):
    width = 1 << level
    span = 4 * PIVOTS * width
    chunks = span // 512
    update_len = 2 * PIVOTS * width
    blocks = (2, 4)[level - 1]

    def body(*refs):
        refs = list(refs)

        def take(count):
            taken, refs[:] = refs[:count], refs[count:]
            return taken

        tables_refs = take(4)
        received_ref, weighted_ref = take(2)
        answer_refs = take(len(answers))
        weights_ref, updates_ref = take(2)
        outs = take(2 if level == 1 else 3)
        (x_ref,) = take(1)
        target = weighted_ref[...]
        if level == 1:
            total = sum(received_ref[i] for i in range(8))
        for k in range(update_len // 256):
            at = slice(k * 256, (k + 1) * 256)
            if level == 1:
                chosen = total[:, at]
            else:
                chosen = jnp.concatenate([received_ref[2 * k], received_ref[2 * k + 1]], 1)
            target -= product(chosen, updates_ref[0, :, at], updates_ref[1, :, at], 1)
        for k in range(chunks):
            at = slice(k * 512, (k + 1) * 512)
            x_ref[:, at] = product(target, weights_ref[0, :, at], weights_ref[1, :, at], 0)
        for child in range(2):
            for k in range(blocks):
                piece = x_ref[:, block_at(child_block(level, tables_refs, child, k))]
                for x in range(4):
                    outs[0][x * 2 + child, :, k * BLOCK : (k + 1) * BLOCK] = piece
        if level == 1:
            for x in range(4):
                outs[1][x] = x_ref[:, x * 256 : (x + 1) * 256]
        else:
            y0 = lax.axis_index("y0")
            keep_ref, far_ref = outs[1:]
            own_ref, other_ref = answer_refs
            for x in range(4):
                keep_ref[0, x] = x_ref[:, block_at(x * 2 + y0, 256)]
                far_ref[0, x] = x_ref[:, block_at(x * 2 + (1 - y0), 256)]
                keep_ref[1, x] = own_ref[x, y0] + other_ref[x, y0]
                far_ref[1, x] = own_ref[x, 1 - y0] + other_ref[x, 1 - y0]

    outs = [(8, HALF, blocks * BLOCK)]
    outs += [(4, HALF, 256)] if level == 1 else [(2, 4, HALF, 256), (2, 4, HALF, 256)]
    operands = [*tables, received, weighted, *answers, weights, updates]
    specs = [SCALARS] * 4 + [WHOLE] * (len(operands) - 4)
    return call(body, outs, operands, specs, [pltpu.VMEM((HALF, span), jnp.float32)])


def level_zero_backward(received, weighted, weights, updates, nearest, kept, other):
    def body(received_ref, weighted_ref, nearest_ref, kept_ref, other_ref, weights_ref, updates_ref, sent_ref):
        for x in range(4):
            for c in range(2):
                half = slice(c * HALF, (c + 1) * HALF)
                at = slice(c * PIVOTS, (c + 1) * PIVOTS)
                sent_ref[x, half, PIVOTS : 2 * PIVOTS] = nearest_ref[x, :, at]
                for i in range(2):
                    piece = kept_ref[i, x, :, at] + other_ref[i, x, :, at]
                    sent_ref[x, half, (2 + i) * PIVOTS : (3 + i) * PIVOTS] = piece
        chosen = jnp.concatenate([sum(received_ref[x * 2 + c] for x in range(4)) for c in range(2)], 0)
        target = weighted_ref[...] - product(chosen, updates_ref[0], updates_ref[1], 1)
        part = product(target, weights_ref[0], weights_ref[1], 0)
        for q in range(4):
            sent_ref[q, :, :PIVOTS] = part[:, q * PIVOTS : (q + 1) * PIVOTS]

    return call(
        body,
        [(4, SIDES, 512)],
        [received, weighted, nearest, kept, other, weights, updates],
        [WHOLE] * 7,
    )[0]


def summed(received):
    def body(received_ref, out_ref):
        out_ref[...] = (received_ref[0] + received_ref[1]) + (received_ref[2] + received_ref[3])

    return call(body, [(SIDES, 512)], [received], [WHOLE])[0]


def unpacked(total, beside):
    def body(total_ref, beside_ref, out_ref):
        c = lax.axis_index("c")
        mine = pl.ds(pl.multiple_of(c * HALF, 8), HALF)
        theirs = pl.ds(pl.multiple_of((1 - c) * HALF, 8), HALF)
        out_ref[:, :PIVOTS] = total_ref[:, :PIVOTS]
        out_ref[mine, PIVOTS:] = total_ref[mine, PIVOTS:]
        out_ref[theirs, PIVOTS:] = beside_ref[mine, PIVOTS:]

    return call(body, [(SIDES, 512)], [total, beside], [WHOLE] * 2)[0]


def summed_copies(received, count):
    total = jnp.sum(received, 0)
    return jnp.broadcast_to(total[None], (count, *total.shape))


def sibling_tables(targets):
    pairs = []
    for y1 in range(2):
        for y0 in range(2):
            here = y1 * 4 + y0 * 2
            pairs.append((here, y1 * 4 + (1 - y0) * 2))
            pairs.append((here + 1, (1 - y1) * 4 + y0 * 2 + 1))
    side = lax.ppermute(targets, ("y1", "y0", "c"), pairs)
    return [targets, side, with_partner(targets), with_partner(side)]


def per_device(right_side, factor_inverse, update_panel, update_targets, pivot_pairs, pivot_diagonal, pivot_coupling):
    sides = right_side[0, 0]
    inverse = factor_inverse[0, 0]
    update = update_panel[0, 0]
    plane = ("x", "y1", "y0")
    pair = ("x", "y0")

    copies = jnp.broadcast_to(sides[None, :, :PIVOTS], (4, SIDES, PIVOTS))
    first = exchange(copies, ("x",))
    factors = pivot_factors(pivot_pairs[0], pivot_diagonal[0], pivot_coupling[0])
    (weights0,) = prepared([inverse], [(0, 512)], copies)
    (updates0,) = prepared([update], [(0, 256)], copies)
    packed = packed_sides(sides, with_partner(sides))
    inverse_after, update_after, _ = lax.optimization_barrier((inverse, update, packed))
    partner_inverse = with_partner(inverse_after)
    partner_update = with_partner(update_after)
    two = jnp.stack([packed, lax.ppermute(packed, "x", [(0, 1), (1, 0), (2, 3), (3, 2)])])

    sent, weighted0 = level_zero_forward(first, sides, weights0, updates0, factors)
    received = exchange(sent, ("c", "x"))
    partner_factors = with_partner(factors)
    tables = sibling_tables(update_targets)
    near = jnp.concatenate([two, lax.ppermute(two, "x", [(0, 2), (2, 0), (1, 3), (3, 1)])])
    weights1, weights2, weights3 = prepared(
        [inverse, partner_inverse], [(512, 1024), (1536, 2048), (3584, 4096)], sent
    )
    updates1, updates2 = prepared([update, partner_update], [(256, 512), (768, 1024)], sent)
    sent, weighted1 = forward(1, received, [], tables, weights1, updates1, factors, partner_factors)
    far = across(near, "y0")
    near3 = jnp.stack([near[:, :, PIVOTS:], far[:, :, PIVOTS:]])
    received = exchange(sent, pair)
    sent, weighted2 = forward(2, received, [near, far], tables, weights2, updates2, factors, partner_factors)
    far3 = across(near3, "y1")
    received = exchange(summed_copies(exchange(sent, pair), 16), plane)
    sent, kept3, other3 = forward(3, received, [near3, far3], tables, weights3, None, factors, partner_factors)
    other3 = across(other3, "y1")
    received = exchange(summed_copies(exchange(sent, plane), 8), pair)
    sent, kept, other = backward(2, received, weighted2, tables, weights2, updates2, [kept3, other3])
    other = across(other, "y0")
    received = exchange(sent, pair)
    sent, nearest = backward(1, received, weighted1, tables, weights1, updates1, [])
    received = exchange(sent, ("x", "c"))
    sent = level_zero_backward(received, weighted0, weights0, updates0, nearest, kept, other)
    total = summed(exchange(sent, ("x",)))
    return unpacked(total, with_partner(total))[None, None]


def solution(mesh):
    grid = np.array(mesh.devices).reshape(4, 2, 2, 2, 4)
    fine = Mesh(grid, AXES)
    leaf = ("z", "y1", "y0", "c")
    in_specs = (
        P(leaf, "x", None, None),
        P(leaf, "x", None, None),
        P(leaf, "x", None, None),
        P(leaf, None),
        P(leaf, "x", None),
        P(leaf, "x", None),
        P(leaf, "x", None),
    )
    out_specs = P(leaf, "x", None, None)
    return jax.shard_map(per_device, mesh=fine, in_specs=in_specs, out_specs=out_specs, check_vma=False)
```

time: 205 us -> 214 us (1.044)
  blocking collectives: 27.7 us -> 13.6 us
  Pallas kernels: 36.3 us -> 22.2 us
  local copies, waits for them, and re-layouts: 25.8 us -> 39.2 us
  starting transfers between devices: 55.6 us -> 66.1 us
  waiting for transfers between devices: 57.7 us -> 65.9 us
  other arithmetic: 0.04 us -> 4.22 us
    pallas_call x11, Pallas kernels: 36.3 us -> 19.1 us  [call(): pl.pallas_call(body, in_specs=specs, out_specs=[WHOLE] * len(out_shapes),...]
    ppermute x4, waiting for transfers between devices: 3.28 us -> 17.9 us  [across(): return lax.ppermute(value, axis, [(0, 1), (1, 0)])]
    all_to_all x2 -> x1, blocking collectives: 27.7 us -> 13.6 us  [exchange(): return lax.all_to_all(value, axes, 0, 0, tiled=True)]
    unnamed x50 -> x102, local copies, waits for them, and re-layouts: 24.3 us -> 34 us
    ppermute x0 -> x2, waiting for transfers between devices: none -> 9.33 us  [the longest x1 9.33 us: per_device(): lax.ppermute(packed, 'x', [(0, 1), (1, 0), (2, 3), (3, 2)])]
    all_to_all x8 -> x9, waiting for transfers between devices: 42.9 us -> 34.9 us  [exchange(): return lax.all_to_all(value, axes, 0, 0, tiled=True)]
    ppermute x7, waiting for transfers between devices: 9.96 us -> 2.36 us  [with_partner(): return lax.ppermute(value, 'c', [(0, 1), (1, 0)])]
    all_to_all x8 -> x9, starting transfers between devices: 39.9 us -> 44.9 us  [exchange(): return lax.all_to_all(value, axes, 0, 0, tiled=True)]
  transfers between devices with their start and end apart: 20 -> 23, of which waited for: 15 -> 14; matrix products, arithmetic and copies ran while one was open for 1% -> 4% of each run, Pallas kernels for 2% -> 4%
where the time goes in v3:
time: 214 us; the launch traced here: 212 us
  starting transfers between devices  66.1 us (31%)
  waiting for transfers between devices  65.9 us (31%)
  local copies, waits for them, and re-layouts  39.2 us (18%)
  Pallas kernels  22.2 us (10%)
  blocking collectives  13.6 us (6%)
  other arithmetic  4.22 us (2%)
    all_to_all x9, starting transfers between devices, exchange(): return lax.all_to_all(value, axes, 0, 0, tiled=True)  44.9 us
    all_to_all x9, waiting for transfers between devices, exchange(): return lax.all_to_all(value, axes, 0, 0, tiled=True)  34.9 us
    unnamed x102, local copies, waits for them, and re-layouts  34 us
    pallas_call x11, Pallas kernels, call(): pl.pallas_call(body, in_specs=specs, out_specs=[WHOLE] * len(out_shapes),...  19.1 us
    ppermute x4, waiting for transfers between devices, across(): return lax.ppermute(value, axis, [(0, 1), (1, 0)])  17.9 us
    all_to_all x1, blocking collectives, exchange(): return lax.all_to_all(value, axes, 0, 0, tiled=True)  13.6 us
    ppermute x1, waiting for transfers between devices, per_device(): lax.ppermute(packed, 'x', [(0, 1), (1, 0), (2, 3), (3, 2)])  9.33 us
    ppermute x4, starting transfers between devices, across(): return lax.ppermute(value, axis, [(0, 1), (1, 0)])  8.63 us
  transfers between devices with their start and end apart: 23, of which 14 were waited for; matrix products, arithmetic and copies ran while one was open for 4% of the time, Pallas kernels for 4%

profile of v3, /device:TPU:1, one launch (start us, length us, event | category | flops | bytes accessed | tf_op | source)
XLA Modules:
  0.0 211.7 jit_solution(5139523159458076162)
XLA Ops:
  0.0 1.4 collective-permute-start.4
  1.4 1.3 collective-permute-done.4.beside_ref
  4.9 4.1 %all-to-all-start = ((f32[4,96,128]{2,1,0:T(8,128)}), f32[4,96,128]{2,1,0:T(8,128)S(1)}, u32[]{:S(2)}, u32[]{:S(2)}) async-start(f32[4,96,128]{2,1,0:T(8,128)} %broadcast_in_dim.8.refs_1_), calls=%async_computation | async-start | bytes 393216 | tf_op jit(solution)/shard_map/all_to_all | solution.py:41
  9.1 2.1 copy-done
  11.7 2.5 %all-to-all-done.first_ref = f32[4,96,128]{2,1,0:T(8,128)S(1)} async-done(((f32[4,96,128]{2,1,0:T(8,128)}), f32[4,96,128]{2,1,0:T(8,128)S(1)}, u32[]{:S(2)}, u32[]{:S(2)}) %all-to-all-start) | async-done | bytes 196640 | tf_op jit(solution)/shard_map/all_to_all | solution.py:41
  14.3 1.3 shard_map.76
  15.6 5.9 %all-to-all-start.1 = ((f32[8,48,384]{2,1,0:T(8,128)}), f32[8,48,384]{2,1,0:T(8,128)}, u32[]{:S(2)}, u32[]{:S(2)}) async-start(f32[8,48,384]{2,1,0:T(8,128)} %get-tuple-element.26.refs_2_), calls=%async_computation.1 | async-start | bytes 1179648 | tf_op jit(solution)/shard_map/all_to_all | solution.py:41
  21.4 1.4 collective-permute-start.7
  22.8 9.3 %collective-permute-done.7 = f32[96,256]{1,0:T(8,128)S(1)} collective-permute-done((f32[96,256]{1,0:T(8,128)S(1)}, f32[96,256]{1,0:T(8,128)S(1)}, u32[]{:S(2)}, u32[]{:S(2)}) %collective-permute-start.7) | collective-permute-done | bytes 98336 | tf_op jit(solution)/shard_map/ppermute | solution.py:418
  32.1 2.5 %collective-permute-start.8 = (f32[2,96,256]{2,1,0:T(8,128)S(1)}, f32[2,96,256]{2,1,0:T(8,128)}, u32[]{:S(2)}, u32[]{:S(2)}) collective-permute-start(f32[2,96,256]{2,1,0:T(8,128)S(1)} %pad_maximum_fusion.2), channel_id=1, source_target_pairs={{0,2},{2,0},{1,3},{3,1},{4,6},{6,4},{5,7},{7,5},{8,10},{10,8},{9,1... | collective-permute-start | bytes 589832 | tf_op jit(solution)/shard_map/ppermute | solution.py:424
  34.6 1.2 collective-permute-start.3
  35.9 2.9 %collective-permute-start = (s32[1,14]{1,0:T(1,128)S(1)}, s32[1,14]{1,0:T(1,128)S(1)}, u32[]{:S(2)}, u32[]{:S(2)}) collective-permute-start(s32[1,14]{1,0:T(1,128)S(1)} %copy-done.36), channel_id=1, source_target_pairs={{0,8},{4,20},{8,0},{12,28},{16,24},{20,4},{24,16},{28,12},{1,9},{5... | collective-permute-start | bytes 176 | tf_op jit(solution)/shard_map/ppermute | solution.py:398
  38.8 1.4 collective-permute-done.refs_1_
  43.0 2.1 copy-done.1
  45.1 2.5 %shard_map.78 = (bf16[2,256,1024]{2,1,0:T(8,128)(2,1)S(1)}, bf16[2,256,2048]{2,1,0:T(8,128)(2,1)S(1)}, bf16[2,256,4096]{2,1,0:T(8,128)(2,1)S(1)}) custom-call(f32[128,7680]{1,0:T(8,128)S(1)} %bitcast.15, f32[128,7680]{1,0:T(8,128)} %collective-permute-done.5.refs_1_, f32[8,48,384]{2,1,0:T(8,128)} %get-tuple-element.26.refs_2_), custom_call_target="tpu_custom_call" | custom-call | tf_op jit(solution)/shard_map/pallas_call | solution.py:99
  47.6 2.0 copy-done.2
  50.7 2.1 shard_map.80
  54.3 4.2 %all-to-all-start.2 = ((f32[8,48,512]{2,1,0:T(8,128)}), f32[8,48,512]{2,1,0:T(8,128)}, u32[]{:S(2)}, u32[]{:S(2)}) async-start(f32[8,48,512]{2,1,0:T(8,128)} %copy-done.20), calls=%async_computation.2 | async-start | bytes 1572864 | tf_op jit(solution)/shard_map/all_to_all | solution.py:41
  59.6 1.4 collective-permute-start.9
  61.7 16.0 %collective-permute-done.9.refs_6_ = f32[4,96,256]{2,1,0:T(8,128)S(1)} collective-permute-done((f32[4,96,256]{2,1,0:T(8,128)S(1)}, f32[4,96,256]{2,1,0:T(8,128)S(1)}, u32[]{:S(2)}, u32[]{:S(2)}) %collective-permute-start.9) | collective-permute-done | bytes 393248 | tf_op jit(solution)/shard_map/ppermute | solution.py:49
  78.5 1.2 copy-done.5
  82.0 2.9 %shard_map.81 = (f32[8,48,128]{2,1,0:T(8,128)S(1)}, f32[48,256]{1,0:T(8,128)S(1)}) custom-call(s32[1,14]{1,0:T(1,128)S(1)} %copy-done.36, s32[1,14]{1,0:T(1,128)S(1)} %collective-permute-done.refs_1_, s32[1,14]{1,0:T(1,128)S(1)} %copy-done.38, s32[1,14]{1,0:T(1,128)S(1)} %copy-done.42, f32[8,48,512]{2,1,0:T(8,128)} %all-to-all-done.2.refs_4_, ...), custom_call_target="tpu_custom_call" | custom-call | tf_op jit(solution)/shard_map/pallas_call | solution.py:62
  86.2 4.4 %all-to-all-start.3 = ((f32[8,48,128]{2,1,0:T(8,128)}), f32[8,48,128]{2,1,0:T(8,128)}, u32[]{:S(2)}, u32[]{:S(2)}) async-start(f32[8,48,128]{2,1,0:T(8,128)} %copy-done.29), calls=%async_computation.3 | async-start | bytes 393216 | tf_op jit(solution)/shard_map/all_to_all | solution.py:41
  92.5 3.0 %collective-permute-start.10 = (f32[2,4,96,128]{3,2,1,0:T(8,128)S(1)}, f32[2,4,96,128]{3,2,1,0:T(8,128)}, u32[]{:S(2)}, u32[]{:S(2)}) collective-permute-start(f32[2,4,96,128]{3,2,1,0:T(8,128)S(1)} %pad_maximum_fusion.1.refs_5_), channel_id=1, source_target_pairs={{0,16},{16,0},{1,17},{17,1},{2,18},{18,2},{3,19},{19,3},{4,20},{20... | collective-permute-start | bytes 1179656 | tf_op jit(solution)/shard_map/ppermute | solution.py:49
  96.5 1.6 reduce_sum.18
  98.1 1.5 broadcast_in_dim.9
  99.6 5.3 %all-to-all-start.4 = ((f32[16,48,128]{2,1,0:T(8,128)}), f32[16,48,128]{2,1,0:T(8,128)}, u32[]{:S(2)}, u32[]{:S(2)}) async-start(f32[16,48,128]{2,1,0:T(8,128)} %broadcast_in_dim.9), calls=%async_computation.4 | async-start | bytes 786432 | tf_op jit(solution)/shard_map/all_to_all | solution.py:41
  104.8 1.2 collective-permute-done.10.refs_6_
  106.0 6.9 %all-to-all-done.4.refs_4_ = f32[16,48,128]{2,1,0:T(8,128)} async-done(((f32[16,48,128]{2,1,0:T(8,128)}), f32[16,48,128]{2,1,0:T(8,128)}, u32[]{:S(2)}, u32[]{:S(2)}) %all-to-all-start.4) | async-done | bytes 393248 | tf_op jit(solution)/shard_map/all_to_all | solution.py:41
  112.9 2.2 %copy-done.3 = bf16[2,256,4096]{2,1,0:T(8,128)(2,1)S(1)} copy-done((bf16[2,256,4096]{2,1,0:T(8,128)(2,1)S(1)}, bf16[2,256,4096]{2,1,0:T(8,128)(2,1)}, u32[]{:S(2)}) %copy-start.3) | copy-done | bytes 4194328
  116.3 5.8 %shard_map.82 = (f32[16,48,128]{2,1,0:T(8,128)S(1)}, f32[4,2,48,256]{3,2,1,0:T(8,128)S(1)}, f32[4,2,48,256]{3,2,1,0:T(8,128)S(1)}) custom-call(s32[1,14]{1,0:T(1,128)S(1)} %copy-done.36, s32[1,14]{1,0:T(1,128)S(1)} %collective-permute-done.refs_1_, s32[1,14]{1,0:T(1,128)S(1)} %copy-done.39, s32[1,14]{1,0:T(1,128)S(1)} %copy-done.43, ...), custom_call_target="tpu_custom_call" | custom-call | tf_op jit(solution)/shard_map/pallas_call | solution.py:62
  124.4 3.7 %all-to-all-start.5 = ((f32[16,48,128]{2,1,0:T(8,128)}), f32[16,48,128]{2,1,0:T(8,128)S(1)}, u32[]{:S(2)}, u32[]{:S(2)}) async-start(f32[16,48,128]{2,1,0:T(8,128)} %copy-done.26), calls=%async_computation.5 | async-start | bytes 786432 | tf_op jit(solution)/shard_map/all_to_all | solution.py:41
  128.1 2.9 %collective-permute-start.11 = (f32[4,2,48,256]{3,2,1,0:T(8,128)}, f32[4,2,48,256]{3,2,1,0:T(8,128)}, u32[]{:S(2)}, u32[]{:S(2)}) collective-permute-start(f32[4,2,48,256]{3,2,1,0:T(8,128)} %copy-done.49), channel_id=1, source_target_pairs={{0,16},{16,0},{1,17},{17,1},{2,18},{18,2},{3,19},{19,3},{4,20},{20... | collective-permute-start | bytes 1179656 | tf_op jit(solution)/shard_map/ppermute | solution.py:49
  131.0 5.3 %all-to-all-done.5 = f32[16,48,128]{2,1,0:T(8,128)S(1)} async-done(((f32[16,48,128]{2,1,0:T(8,128)}), f32[16,48,128]{2,1,0:T(8,128)S(1)}, u32[]{:S(2)}, u32[]{:S(2)}) %all-to-all-start.5) | async-done | bytes 393248 | tf_op jit(solution)/shard_map/all_to_all | solution.py:41
  137.0 1.4 broadcast_in_dim.10
  138.4 3.6 %all-to-all-start.6 = ((f32[8,48,128]{2,1,0:T(8,128)}), f32[8,48,128]{2,1,0:T(8,128)S(1)}, u32[]{:S(2)}, u32[]{:S(2)}) async-start(f32[8,48,128]{2,1,0:T(8,128)} %broadcast_in_dim.10), calls=%async_computation.6 | async-start | bytes 393216 | tf_op jit(solution)/shard_map/all_to_all | solution.py:41
  142.7 4.5 %all-to-all-done.6.refs_4_ = f32[8,48,128]{2,1,0:T(8,128)S(1)} async-done(((f32[8,48,128]{2,1,0:T(8,128)}), f32[8,48,128]{2,1,0:T(8,128)S(1)}, u32[]{:S(2)}, u32[]{:S(2)}) %all-to-all-start.6) | async-done | bytes 196640 | tf_op jit(solution)/shard_map/all_to_all | solution.py:41
  147.9 1.2 copy-done.6
  153.1 2.4 %shard_map.83 = (f32[8,48,512]{2,1,0:T(8,128)S(1)}, f32[2,4,48,256]{3,2,1,0:T(8,128)S(1)}, f32[2,4,48,256]{3,2,1,0:T(8,128)S(1)}) custom-call(s32[1,14]{1,0:T(1,128)S(1)} %copy-done.36, s32[1,14]{1,0:T(1,128)S(1)} %collective-permute-done.refs_1_, s32[1,14]{1,0:T(1,128)S(1)} %copy-done.40, s32[1,14]{1,0:T(1,128)S(1)} %copy-done.44, ...), custom_call_target="tpu_custom_call" | custom-call | tf_op jit(solution)/shard_map/pallas_call | solution.py:62
  157.9 3.7 %all-to-all-start.7 = ((f32[8,48,512]{2,1,0:T(8,128)}), f32[8,48,512]{2,1,0:T(8,128)S(1)}, u32[]{:S(2)}, u32[]{:S(2)}) async-start(f32[8,48,512]{2,1,0:T(8,128)} %copy-done.21), calls=%async_computation.7 | async-start | bytes 1572864 | tf_op jit(solution)/shard_map/all_to_all | solution.py:41
  161.6 1.4 collective-permute-start.12
  163.0 7.0 %all-to-all-done.7.refs_4_ = f32[8,48,512]{2,1,0:T(8,128)S(1)} async-done(((f32[8,48,512]{2,1,0:T(8,128)}), f32[8,48,512]{2,1,0:T(8,128)S(1)}, u32[]{:S(2)}, u32[]{:S(2)}) %all-to-all-start.7) | async-done | bytes 786464 | tf_op jit(solution)/shard_map/all_to_all | solution.py:41
  171.8 2.0 shard_map.84
  173.9 10.0 %all-to-all-start.8 = ((f32[8,48,256]{2,1,0:T(8,128)}), f32[8,48,256]{2,1,0:T(8,128)S(1)}, u32[]{:S(2)}, u32[]{:S(2)}) async-start(f32[8,48,256]{2,1,0:T(8,128)} %get-tuple-element.42), calls=%async_computation.8 | async-start | bytes 786432 | tf_op jit(solution)/shard_map/all_to_all | solution.py:41
  183.9 7.7 %all-to-all-done.8.received_ref = f32[8,48,256]{2,1,0:T(8,128)S(1)} async-done(((f32[8,48,256]{2,1,0:T(8,128)}), f32[8,48,256]{2,1,0:T(8,128)S(1)}, u32[]{:S(2)}, u32[]{:S(2)}) %all-to-all-start.8) | async-done | bytes 393248 | tf_op jit(solution)/shard_map/all_to_all | solution.py:41
  192.6 1.5 shard_map.85
  194.1 13.6 %all_to_all.50.received_ref = f32[4,96,512]{2,1,0:T(8,128)S(1)} all-to-all(f32[4,96,512]{2,1,0:T(8,128)S(1)} %shard_map.85), channel_id=1, replica_groups=mesh['z'=4,'y1'=2,'y0'=2,'c'=2,'x'=4] {'x'}, dimensions={0} | all-to-all | bytes 1572864 | tf_op jit(solution)/shard_map/all_to_all | solution.py:41
  207.7 2.2 %collective-permute-start.13 = (f32[96,512]{1,0:T(8,128)S(1)}, f32[96,512]{1,0:T(8,128)S(1)}, u32[]{:S(2)}, u32[]{:S(2)}) collective-permute-start(f32[96,512]{1,0:T(8,128)S(1)} %shard_map.86.total_ref), channel_id=1, source_target_pairs={{0,4},{4,0},{1,5},{5,1},{2,6},{6,2},{3,7},{7,3},{8,12},{12,8},{9,1... | collective-permute-start | bytes 589832 | tf_op jit(solution)/shard_map/ppermute | solution.py:45
  (127 shorter events, 33.7 us)
Async XLA Ops:
  0.0 11.3 %copy-start.7 = (f32[1,1,128,1792]{3,2,1,0:T(8,128)S(1)}, f32[1,1,128,1792]{3,2,1,0:T(8,128)}, u32[]{:S(2)}) copy-start(f32[1,1,128,1792]{3,2,1,0:T(8,128)} %param.9) | copy-start | bytes 2752516
  0.0 2.7 %collective-permute-start.4 = (f32[96,512]{1,0:T(8,128)}, f32[96,512]{1,0:T(8,128)S(1)}, u32[]{:S(2)}, u32[]{:S(2)}) collective-permute-start(f32[96,512]{1,0:T(8,128)} %bitcast.19), channel_id=1, source_target_pairs={{0,4},{4,0},{1,5},{5,1},{2,6},{6,2},{3,7},{7,3},{8,12},{12,8},{9,1... | collective-permute-start | bytes 589832 | tf_op jit(solution)/shard_map/ppermute | solution.py:45
  3.6 7.7 %copy-start.45 = (f32[1,1,512]{2,1,0:T(1,128)S(1)}, f32[1,1,512]{2,1,0:T(1,128)}, u32[]{:S(2)}) copy-start(f32[1,1,512]{2,1,0:T(1,128)} %param.12) | copy-start | bytes 6148
  3.6 7.7 %copy-start.46 = (s32[1,1,256]{2,1,0:T(1,128)S(1)}, s32[1,1,256]{2,1,0:T(1,128)}, u32[]{:S(2)}) copy-start(s32[1,1,256]{2,1,0:T(1,128)} %param.11) | copy-start | bytes 3076
  3.6 7.8 %copy-start.47 = (f32[1,1,256]{2,1,0:T(1,128)S(1)}, f32[1,1,256]{2,1,0:T(1,128)}, u32[]{:S(2)}) copy-start(f32[1,1,256]{2,1,0:T(1,128)} %param.13) | copy-start | bytes 3076
  3.6 10.7 %copy-start.16 = (f32[1,1,96,512]{3,2,1,0:T(8,128)S(1)}, f32[1,1,96,512]{3,2,1,0:T(8,128)}, u32[]{:S(2)}) copy-start(f32[1,1,96,512]{3,2,1,0:T(8,128)} %param.7) | copy-start | bytes 589828
  3.6 28.5 %copy-start.19 = (f32[96,256]{1,0:T(8,128)}, f32[96,256]{1,0:T(8,128)S(1)}, u32[]{:S(2)}) copy-start(f32[96,256]{1,0:T(8,128)S(1)} %shard_map.77) | copy-start | bytes 294916
  3.6 39.3 %collective-permute-start.5 = (f32[128,7680]{1,0:T(8,128)}, f32[128,7680]{1,0:T(8,128)}, u32[]{:S(2)}, u32[]{:S(2)}) collective-permute-start(f32[128,7680]{1,0:T(8,128)} %bitcast.13), channel_id=1, source_target_pairs={{0,4},{4,0},{1,5},{5,1},{2,6},{6,2},{3,7},{7,3},{8,12},{12,8},{9,1... | collective-permute-start | bytes 11796488 | tf_op jit(solution)/shard_map/ppermute | solution.py:45
  4.1 36.1 %collective-permute-start.6 = (f32[128,1792]{1,0:T(8,128)}, f32[128,1792]{1,0:T(8,128)S(1)}, u32[]{:S(2)}, u32[]{:S(2)}) collective-permute-start(f32[128,1792]{1,0:T(8,128)} %bitcast.16), channel_id=1, source_target_pairs={{0,4},{4,0},{1,5},{5,1},{2,6},{6,2},{3,7},{7,3},{8,12},{12,8},{9,1... | collective-permute-start | bytes 2752520 | tf_op jit(solution)/shard_map/ppermute | solution.py:45
  4.9 9.3 %all-to-all-start = ((f32[4,96,128]{2,1,0:T(8,128)}), f32[4,96,128]{2,1,0:T(8,128)S(1)}, u32[]{:S(2)}, u32[]{:S(2)}) async-start(f32[4,96,128]{2,1,0:T(8,128)} %broadcast_in_dim.8.refs_1_), calls=%async_computation | async-start | bytes 393216 | tf_op jit(solution)/shard_map/all_to_all | solution.py:41
  9.1 2.1 copy-start
  11.2 24.7 %copy-start.36 = (s32[1,14]{1,0:T(1,128)S(1)}, s32[1,14]{1,0:T(1,128)}, u32[]{:S(2)}) copy-start(s32[1,14]{1,0:T(1,128)} %refs_0_.9) | copy-start | bytes 172
  11.3 29.8 %copy-start.8 = (bf16[2,128,512]{2,1,0:T(8,128)(2,1)}, bf16[2,128,512]{2,1,0:T(8,128)(2,1)S(1)}, u32[]{:S(2)}) copy-start(bf16[2,128,512]{2,1,0:T(8,128)(2,1)S(1)} %shard_map.73.weights_ref) | copy-start | bytes 786436
  11.3 29.8 %copy-start.13 = (bf16[2,128,256]{2,1,0:T(8,128)(2,1)}, bf16[2,128,256]{2,1,0:T(8,128)(2,1)S(1)}, u32[]{:S(2)}) copy-start(bf16[2,128,256]{2,1,0:T(8,128)(2,1)S(1)} %shard_map.74.updates_ref) | copy-start | bytes 393220
  15.6 25.6 %copy-start.30 = (f32[96,128]{1,0:T(8,128)}, f32[96,128]{1,0:T(8,128)S(1)}, u32[]{:S(2)}) copy-start(f32[96,128]{1,0:T(8,128)S(1)} %get-tuple-element.43.weighted_ref) | copy-start | bytes 147460
  15.6 34.1 %all-to-all-start.1 = ((f32[8,48,384]{2,1,0:T(8,128)}), f32[8,48,384]{2,1,0:T(8,128)}, u32[]{:S(2)}, u32[]{:S(2)}) async-start(f32[8,48,384]{2,1,0:T(8,128)} %get-tuple-element.26.refs_2_), calls=%async_computation.1 | async-start | bytes 1179648 | tf_op jit(solution)/shard_map/all_to_all | solution.py:41
  21.4 10.7 %collective-permute-start.7 = (f32[96,256]{1,0:T(8,128)S(1)}, f32[96,256]{1,0:T(8,128)S(1)}, u32[]{:S(2)}, u32[]{:S(2)}) collective-permute-start(f32[96,256]{1,0:T(8,128)S(1)} %shard_map.77), channel_id=1, source_target_pairs={{0,1},{1,0},{2,3},{3,2},{4,5},{5,4},{6,7},{7,6},{8,9},{9,8},{10,11... | collective-permute-start | bytes 294920 | tf_op jit(solution)/shard_map/ppermute | solution.py:418
  32.1 9.0 %copy-start.50 = (f32[96,256]{1,0:T(8,128)}, f32[96,256]{1,0:T(8,128)S(1)}, u32[]{:S(2)}) copy-start(f32[96,256]{1,0:T(8,128)S(1)} %collective-permute-done.7) | copy-start | bytes 294916
  32.1 26.4 %collective-permute-start.8 = (f32[2,96,256]{2,1,0:T(8,128)S(1)}, f32[2,96,256]{2,1,0:T(8,128)}, u32[]{:S(2)}, u32[]{:S(2)}) collective-permute-start(f32[2,96,256]{2,1,0:T(8,128)S(1)} %pad_maximum_fusion.2), channel_id=1, source_target_pairs={{0,2},{2,0},{1,3},{3,1},{4,6},{6,4},{5,7},{7,5},{8,10},{10,8},{9,1... | collective-permute-start | bytes 589832 | tf_op jit(solution)/shard_map/ppermute | solution.py:424
  34.6 15.0 %collective-permute-start.3 = (f32[2,512]{1,0:T(2,128)S(1)}, f32[2,512]{1,0:T(2,128)S(1)}, u32[]{:S(2)}, u32[]{:S(2)}) collective-permute-start(f32[2,512]{1,0:T(2,128)S(1)} %shard_map.75.factors_ref.refs_5_.refs_7_), channel_id=1, source_target_pairs={{0,4},{4,0},{1,5},{5,1},{2,6},{6,2},{3,7},{7,3},{8,12},{12,8},{9,1... | collective-permute-start | bytes 12296 | tf_op jit(solution)/shard_map/ppermute | solution.py:45
  35.9 4.3 %collective-permute-start = (s32[1,14]{1,0:T(1,128)S(1)}, s32[1,14]{1,0:T(1,128)S(1)}, u32[]{:S(2)}, u32[]{:S(2)}) collective-permute-start(s32[1,14]{1,0:T(1,128)S(1)} %copy-done.36), channel_id=1, source_target_pairs={{0,8},{4,20},{8,0},{12,28},{16,24},{20,4},{24,16},{28,12},{1,9},{5... | collective-permute-start | bytes 176 | tf_op jit(solution)/shard_map/ppermute | solution.py:398
  40.2 9.5 %collective-permute-start.1 = (s32[1,14]{1,0:T(1,128)S(1)}, s32[1,14]{1,0:T(1,128)S(1)}, u32[]{:S(2)}, u32[]{:S(2)}) collective-permute-start(s32[1,14]{1,0:T(1,128)S(1)} %copy-done.36), channel_id=1, source_target_pairs={{0,4},{4,0},{1,5},{5,1},{2,6},{6,2},{3,7},{7,3},{8,12},{12,8},{9,1... | collective-permute-start | bytes 176 | tf_op jit(solution)/shard_map/ppermute | solution.py:45
  40.2 9.5 %collective-permute-start.2 = (s32[1,14]{1,0:T(1,128)S(1)}, s32[1,14]{1,0:T(1,128)S(1)}, u32[]{:S(2)}, u32[]{:S(2)}) collective-permute-start(s32[1,14]{1,0:T(1,128)S(1)} %collective-permute-done.refs_1_), channel_id=1, source_target_pairs={{0,4},{4,0},{1,5},{5,1},{2,6},{6,2},{3,7},{7,3},{8,12},{12,8},{9,1... | collective-permute-start | bytes 176 | tf_op jit(solution)/shard_map/ppermute | solution.py:45
  43.0 2.1 copy-start.1
  47.6 2.0 copy-start.2
  49.6 8.9 %copy-start.37 = (s32[1,14]{1,0:T(1,128)}, s32[1,14]{1,0:T(1,128)S(1)}, u32[]{:S(2)}) copy-start(s32[1,14]{1,0:T(1,128)S(1)} %collective-permute-done.1.refs_2_) | copy-start | bytes 172
  49.6 8.9 %copy-start.41 = (s32[1,14]{1,0:T(1,128)}, s32[1,14]{1,0:T(1,128)S(1)}, u32[]{:S(2)}) copy-start(s32[1,14]{1,0:T(1,128)S(1)} %collective-permute-done.2.refs_3_) | copy-start | bytes 172
  49.7 1.0 copy-start.11
  54.3 24.2 %all-to-all-start.2 = ((f32[8,48,512]{2,1,0:T(8,128)}), f32[8,48,512]{2,1,0:T(8,128)}, u32[]{:S(2)}, u32[]{:S(2)}) async-start(f32[8,48,512]{2,1,0:T(8,128)} %copy-done.20), calls=%async_computation.2 | async-start | bytes 1572864 | tf_op jit(solution)/shard_map/all_to_all | solution.py:41
  59.6 18.1 %collective-permute-start.9 = (f32[4,96,256]{2,1,0:T(8,128)S(1)}, f32[4,96,256]{2,1,0:T(8,128)S(1)}, u32[]{:S(2)}, u32[]{:S(2)}) collective-permute-start(f32[4,96,256]{2,1,0:T(8,128)S(1)} %pad_maximum_fusion.refs_5_), channel_id=1, source_target_pairs={{0,8},{8,0},{1,9},{9,1},{2,10},{10,2},{3,11},{11,3},{4,12},{12,4},... | collective-permute-start | bytes 1179656 | tf_op jit(solution)/shard_map/ppermute | solution.py:49
  78.5 1.2 copy-start.5
  86.2 10.3 %all-to-all-start.3 = ((f32[8,48,128]{2,1,0:T(8,128)}), f32[8,48,128]{2,1,0:T(8,128)}, u32[]{:S(2)}, u32[]{:S(2)}) async-start(f32[8,48,128]{2,1,0:T(8,128)} %copy-done.29), calls=%async_computation.3 | async-start | bytes 393216 | tf_op jit(solution)/shard_map/all_to_all | solution.py:41
  92.5 13.5 %collective-permute-start.10 = (f32[2,4,96,128]{3,2,1,0:T(8,128)S(1)}, f32[2,4,96,128]{3,2,1,0:T(8,128)}, u32[]{:S(2)}, u32[]{:S(2)}) collective-permute-start(f32[2,4,96,128]{3,2,1,0:T(8,128)S(1)} %pad_maximum_fusion.1.refs_5_), channel_id=1, source_target_pairs={{0,16},{16,0},{1,17},{17,1},{2,18},{18,2},{3,19},{19,3},{4,20},{20... | collective-permute-start | bytes 1179656 | tf_op jit(solution)/shard_map/ppermute | solution.py:49
  99.6 13.3 %all-to-all-start.4 = ((f32[16,48,128]{2,1,0:T(8,128)}), f32[16,48,128]{2,1,0:T(8,128)}, u32[]{:S(2)}, u32[]{:S(2)}) async-start(f32[16,48,128]{2,1,0:T(8,128)} %broadcast_in_dim.9), calls=%async_computation.4 | async-start | bytes 786432 | tf_op jit(solution)/shard_map/all_to_all | solution.py:41
  112.9 2.2 %copy-start.3 = (bf16[2,256,4096]{2,1,0:T(8,128)(2,1)S(1)}, bf16[2,256,4096]{2,1,0:T(8,128)(2,1)}, u32[]{:S(2)}) copy-start(bf16[2,256,4096]{2,1,0:T(8,128)(2,1)} %copy-done.2) | copy-start | bytes 12582916
  124.4 11.9 %all-to-all-start.5 = ((f32[16,48,128]{2,1,0:T(8,128)}), f32[16,48,128]{2,1,0:T(8,128)S(1)}, u32[]{:S(2)}, u32[]{:S(2)}) async-start(f32[16,48,128]{2,1,0:T(8,128)} %copy-done.26), calls=%async_computation.5 | async-start | bytes 786432 | tf_op jit(solution)/shard_map/all_to_all | solution.py:41
  128.1 14.6 %collective-permute-start.11 = (f32[4,2,48,256]{3,2,1,0:T(8,128)}, f32[4,2,48,256]{3,2,1,0:T(8,128)}, u32[]{:S(2)}, u32[]{:S(2)}) collective-permute-start(f32[4,2,48,256]{3,2,1,0:T(8,128)} %copy-done.49), channel_id=1, source_target_pairs={{0,16},{16,0},{1,17},{17,1},{2,18},{18,2},{3,19},{19,3},{4,20},{20... | collective-permute-start | bytes 1179656 | tf_op jit(solution)/shard_map/ppermute | solution.py:49
  138.4 8.9 %all-to-all-start.6 = ((f32[8,48,128]{2,1,0:T(8,128)}), f32[8,48,128]{2,1,0:T(8,128)S(1)}, u32[]{:S(2)}, u32[]{:S(2)}) async-start(f32[8,48,128]{2,1,0:T(8,128)} %broadcast_in_dim.10), calls=%async_computation.6 | async-start | bytes 393216 | tf_op jit(solution)/shard_map/all_to_all | solution.py:41
  147.9 1.2 copy-start.6
  153.1 38.4 %copy-start.9 = (bf16[2,128,512]{2,1,0:T(8,128)(2,1)S(1)}, bf16[2,128,512]{2,1,0:T(8,128)(2,1)}, u32[]{:S(2)}) copy-start(bf16[2,128,512]{2,1,0:T(8,128)(2,1)} %copy-done.8) | copy-start | bytes 786436
  153.1 38.4 %copy-start.14 = (bf16[2,128,256]{2,1,0:T(8,128)(2,1)S(1)}, bf16[2,128,256]{2,1,0:T(8,128)(2,1)}, u32[]{:S(2)}) copy-start(bf16[2,128,256]{2,1,0:T(8,128)(2,1)} %copy-done.13) | copy-start | bytes 393220
  157.9 33.7 %copy-start.31 = (f32[96,128]{1,0:T(8,128)S(1)}, f32[96,128]{1,0:T(8,128)}, u32[]{:S(2)}) copy-start(f32[96,128]{1,0:T(8,128)} %copy-done.30) | copy-start | bytes 147460
  157.9 12.0 %all-to-all-start.7 = ((f32[8,48,512]{2,1,0:T(8,128)}), f32[8,48,512]{2,1,0:T(8,128)S(1)}, u32[]{:S(2)}, u32[]{:S(2)}) async-start(f32[8,48,512]{2,1,0:T(8,128)} %copy-done.21), calls=%async_computation.7 | async-start | bytes 1572864 | tf_op jit(solution)/shard_map/all_to_all | solution.py:41
  161.6 22.3 %collective-permute-start.12 = (f32[2,4,48,256]{3,2,1,0:T(8,128)}, f32[2,4,48,256]{3,2,1,0:T(8,128)}, u32[]{:S(2)}, u32[]{:S(2)}) collective-permute-start(f32[2,4,48,256]{3,2,1,0:T(8,128)} %copy-done.48), channel_id=1, source_target_pairs={{0,8},{8,0},{1,9},{9,1},{2,10},{10,2},{3,11},{11,3},{4,12},{12,4},... | collective-permute-start | bytes 1179656 | tf_op jit(solution)/shard_map/ppermute | solution.py:49
  170.0 1.0 copy-start.12
  173.9 17.7 %all-to-all-start.8 = ((f32[8,48,256]{2,1,0:T(8,128)}), f32[8,48,256]{2,1,0:T(8,128)S(1)}, u32[]{:S(2)}, u32[]{:S(2)}) async-start(f32[8,48,256]{2,1,0:T(8,128)} %get-tuple-element.42), calls=%async_computation.8 | async-start | bytes 786432 | tf_op jit(solution)/shard_map/all_to_all | solution.py:41
  191.6 1.0 copy-start.25
  207.7 3.2 %collective-permute-start.13 = (f32[96,512]{1,0:T(8,128)S(1)}, f32[96,512]{1,0:T(8,128)S(1)}, u32[]{:S(2)}, u32[]{:S(2)}) collective-permute-start(f32[96,512]{1,0:T(8,128)S(1)} %shard_map.86.total_ref), channel_id=1, source_target_pairs={{0,4},{4,0},{1,5},{5,1},{2,6},{6,2},{3,7},{7,3},{8,12},{12,8},{9,1... | collective-permute-start | bytes 589832 | tf_op jit(solution)/shard_map/ppermute | solution.py:45
  (26 other events, 20.0 us)

commit v4 on v2

--- a/solution.py
+++ b/solution.py
@@ -16,16 +16,28 @@
 exact_mode = lax.Precision.HIGHEST
 
 
+def parts(value):
+    high = value.astype(jnp.bfloat16)
+    return high, (value - high.astype(jnp.float32)).astype(jnp.bfloat16)
+
+
+def product(left, right, side):
+    left_high, left_low = parts(left)
+    high, low = parts(right)
+    dims = (((1,), (side,)), ((), ()))
+
+    def dot(a, b):
+        return lax.dot_general(a, b, dims, preferred_element_type=jnp.float32)
+
+    return dot(left_high, high) + (dot(left_high, low) + dot(left_low, high))
+
+
 def dot_rows(left, right):
-    return lax.dot_general(
-        left, right, (((1,), (1,)), ((), ())), precision=exact_mode, preferred_element_type=jnp.float32
-    )
+    return product(left, right, 1)
 
 
 def dot_cols(left, right):
-    return lax.dot_general(
-        left, right, (((1,), (0,)), ((), ())), precision=exact_mode, preferred_element_type=jnp.float32
-    )
+    return product(left, right, 0)
 
 
 def dot_full(left, right):
@@ -55,12 +67,18 @@
 FAR = pl.BlockSpec(memory_space=pltpu.HBM)
 
 
-def call(body, out_shapes, operands, specs, scratch=(), limit=16):
+def far(value):
+    return pltpu.with_memory_space_constraint(value, pltpu.HBM)
+
+
+def call(body, out_shapes, operands, specs, scratch=(), limit=20, out_space=pltpu.HBM):
     return pl.pallas_call(
         body,
         in_specs=specs,
         out_specs=[WHOLE] * len(out_shapes),
-        out_shape=[jax.ShapeDtypeStruct(s, jnp.float32) for s in out_shapes],
+        out_shape=[
+            out_space(s, jnp.float32) if out_space else jax.ShapeDtypeStruct(s, jnp.float32) for s in out_shapes
+        ],
         scratch_shapes=list(scratch),
         compiler_params=pltpu.CompilerParams(vmem_limit_bytes=limit * 1024 * 1024),
     )(*operands)
@@ -125,7 +143,8 @@
         out_ref[0:1, :] = jnp.where(is_pair, other / determinant, 1.0 / own)
         out_ref[1:2, :] = jnp.where(is_pair, -couple / determinant, 0.0)
 
-    return call(body, [(2, diagonal.shape[1])], [kinds, diagonal, coupling], [WHOLE] * 3)[0]
+    operands = [far(kinds), far(diagonal), far(coupling)]
+    return call(body, [(2, diagonal.shape[1])], operands, [WHOLE] * 3)[0]
 
 
 def packed_sides(sides, beside):
@@ -140,16 +159,17 @@
             out_ref[i, mine, PIVOTS:] = own
             out_ref[i, theirs, PIVOTS:] = other
 
-    return call(body, [(4, SIDES, 512)], [sides, beside], [WHOLE] * 2)[0]
+    return call(body, [(4, SIDES, 512)], [far(sides), beside], [WHOLE] * 2)[0]
 
 
 def level_zero_forward(first, inverse, update, factors):
-    def body(first_ref, inverse_ref, update_ref, factors_ref, sent_ref, weighted_ref, upper_ref, *scratch):
+    def body(first_ref, inverse_ref, update_ref, factors_ref, sent_ref, weighted_ref, one_ref, upper_ref, *scratch):
         weights = Stream([inverse_ref], 0, 512, 512, *scratch[:2])
         updates = Stream([update_ref], 0, 256, 256, *scratch[2:])
         weights.start()
         updates.start()
         for q in range(4):
+            one_ref[q] = first_ref[q, :, PIVOTS : 2 * PIVOTS]
             upper_ref[q] = first_ref[q, :, 2 * PIVOTS :]
         gathered = jnp.concatenate([first_ref[q, :, :PIVOTS] for q in range(4)], 1)
         weights.wait(0)
@@ -163,8 +183,8 @@
 
     return call(
         body,
-        [(8, HALF, 256), (SIDES, PIVOTS), (4, SIDES, 256)],
-        [first, inverse, update, factors],
+        [(8, HALF, 256), (SIDES, PIVOTS), (4, SIDES, PIVOTS), (4, SIDES, 256)],
+        [first, far(inverse), far(update), far(factors)],
         [WHOLE, FAR, FAR, WHOLE],
         stream_scratch(1, 512, 512) + stream_scratch(1, 256, 256),
     )
@@ -226,7 +246,7 @@
         y0, y1 = lax.axis_index("y0"), lax.axis_index("y1")
         if level == 1:
             for x in range(4):
-                b_ref[:, x * 256 : (x + 1) * 256] = halves(sides_refs[0][x, :, PIVOTS : 2 * PIVOTS])
+                b_ref[:, x * 256 : (x + 1) * 256] = halves(sides_refs[0][x])
             near, far = sides_refs[1], sides_refs[2]
             outs[2][0] = near[:, :, PIVOTS:]
             outs[2][1] = far[:, :, PIVOTS:]
@@ -287,11 +307,12 @@
         3: [(16, HALF, BLOCK), (4, 2, HALF, 256), (4, 2, HALF, 256)],
     }[level]
     scratch = [pltpu.VMEM((HALF, span), jnp.float32)] + stream_scratch(2, span, 512)
-    operands = [*tables, received, *sides, factors, partner_factors, *weights_pair]
+    operands = [*map(far, tables), received, *map(far, sides[: 3 if level < 3 else 1]), *sides[3 if level < 3 else 1 :], far(factors), far(partner_factors)]
+    operands += map(far, weights_pair)
     specs = [SCALARS] * 4 + [WHOLE] * (3 + n_sides) + [FAR] * 2
     if level < 3:
         scratch += stream_scratch(2, update_len, 256)
-        operands += update_pair
+        operands += map(far, update_pair)
         specs += [FAR] * 2
     return call(body, outs, operands, specs, scratch, 20)
 
@@ -358,7 +379,8 @@
     outs += [(4, HALF, 256)] if level == 1 else [(2, 4, HALF, 256), (2, 4, HALF, 256)]
     scratch = [pltpu.VMEM((HALF, span), jnp.float32)]
     scratch += stream_scratch(2, span, 512) + stream_scratch(2, update_len, 256)
-    operands = [*tables, received, weighted, *answers, *weights_pair, *update_pair]
+    operands = [*map(far, tables), received, far(weighted), *map(far, answers[:1]), *answers[1:]]
+    operands += map(far, [*weights_pair, *update_pair])
     specs = [SCALARS] * 4 + [WHOLE] * (2 + len(answers)) + [FAR] * 4
     return call(body, outs, operands, specs, scratch, 20)
 
@@ -388,7 +410,7 @@
     return call(
         body,
         [(4, SIDES, 512)],
-        [received, weighted, nearest, kept, other, inverse, update],
+        [received, *map(far, [weighted, nearest, kept]), other, far(inverse), far(update)],
         [WHOLE] * 5 + [FAR] * 2,
         stream_scratch(1, 512, 512) + stream_scratch(1, 256, 256),
     )[0]
@@ -398,7 +420,7 @@
     def body(received_ref, out_ref):
         out_ref[...] = (received_ref[0] + received_ref[1]) + (received_ref[2] + received_ref[3])
 
-    return call(body, [(SIDES, 512)], [received], [WHOLE])[0]
+    return call(body, [(SIDES, 512)], [received], [WHOLE], out_space=None)[0]
 
 
 def unpacked(total, beside):
@@ -410,7 +432,7 @@
         out_ref[mine, PIVOTS:] = total_ref[mine, PIVOTS:]
         out_ref[theirs, PIVOTS:] = beside_ref[mine, PIVOTS:]
 
-    return call(body, [(SIDES, 512)], [total, beside], [WHOLE] * 2)[0]
+    return call(body, [(SIDES, 512)], [total, beside], [WHOLE] * 2, out_space=None)[0]
 
 
 def summed_copies(received, count):
@@ -436,22 +458,24 @@
     plane = ("x", "y1", "y0")
     pair = ("x", "y0")
 
-    first = exchange(packed_sides(sides, with_partner(sides)), ("x",))
+    packed = packed_sides(sides, with_partner(sides))
+    first = exchange(packed, ("x",))
     tables = sibling_tables(update_targets)
     factors = pivot_factors(pivot_pairs[0], pivot_diagonal[0], pivot_coupling[0])
     partner_factors = with_partner(factors)
-    weights_pair = [inverse, with_partner(inverse)]
-    update_pair = [update, with_partner(update)]
-
-    sent, weighted0, near = level_zero_forward(first, inverse, update, factors)
-    far = across(near, "y0")
+    inverse_after, update_after, _ = lax.optimization_barrier((inverse, update, packed))
+    weights_pair = [inverse, with_partner(inverse_after)]
+    update_pair = [update, with_partner(update_after)]
+
+    sent, weighted0, sides1, near = level_zero_forward(first, inverse, update, factors)
+    far_side = across(near, "y0")
     received = exchange(sent, ("c", "x"))
     sent, weighted1, near3 = forward(
-        1, received, [first, near, far], tables, weights_pair, update_pair, factors, partner_factors
+        1, received, [sides1, near, far_side], tables, weights_pair, update_pair, factors, partner_factors
     )
     far3 = across(near3, "y1")
     received = exchange(sent, pair)
-    sent, weighted2 = forward(2, received, [near, far], tables, weights_pair, update_pair, factors, partner_factors)
+    sent, weighted2 = forward(2, received, [near, far_side], tables, weights_pair, update_pair, factors, partner_factors)
     received = exchange(summed_copies(exchange(sent, pair), 16), plane)
     sent, kept3, other3 = forward(
         3, received, [near3, far3], tables, weights_pair, None, factors, partner_factors

time: 205 us -> 182 us (0.89)
  local copies, waits for them, and re-layouts: 25.8 us -> 2.22 us
  waiting for transfers between devices: 57.7 us -> 53.2 us
  Pallas kernels: 36.3 us -> 39.9 us
  blocking collectives: 27.7 us -> 30.4 us
    unnamed x50 -> x18, local copies, waits for them, and re-layouts: 24.3 us -> 0.74 us
    ppermute x7, waiting for transfers between devices: 9.96 us -> 4.34 us  [with_partner(): return lax.ppermute(value, 'c', [(0, 1), (1, 0)])]
    pallas_call x11, Pallas kernels: 36.3 us -> 39.9 us  [call(): pl.pallas_call(body, in_specs=specs, out_specs=[WHOLE] * len(out_shapes),...]
    all_to_all x2, blocking collectives: 27.7 us -> 30.4 us  [exchange(): return lax.all_to_all(value, axes, 0, 0, tiled=True)]
  transfers between devices with their start and end apart: 20 -> 20, of which waited for: 15 -> 15; matrix products, arithmetic and copies ran while one was open for 1% -> 1% of each run, Pallas kernels for 2% -> 5%
where the time goes in v4:
time: 182 us; the launch traced here: 181 us
  starting transfers between devices  54.7 us (30%)
  waiting for transfers between devices  53.2 us (29%)
  Pallas kernels  39.9 us (22%)
  blocking collectives  30.4 us (17%)
  local copies, waits for them, and re-layouts  2.22 us (1%)
    all_to_all x8, waiting for transfers between devices, exchange(): return lax.all_to_all(value, axes, 0, 0, tiled=True)  43 us
    pallas_call x11, Pallas kernels, call(): pl.pallas_call(body, in_specs=specs, out_specs=[WHOLE] * len(out_shapes),...  39.9 us
    all_to_all x8, starting transfers between devices, exchange(): return lax.all_to_all(value, axes, 0, 0, tiled=True)  39 us
    all_to_all x2, blocking collectives, exchange(): return lax.all_to_all(value, axes, 0, 0, tiled=True)  30.4 us
    ppermute x4, starting transfers between devices, across(): return lax.ppermute(value, axis, [(0, 1), (1, 0)])  8.3 us
    ppermute x7, starting transfers between devices, with_partner(): return lax.ppermute(value, 'c', [(0, 1), (1, 0)])  4.84 us
    ppermute x7, waiting for transfers between devices, with_partner(): return lax.ppermute(value, 'c', [(0, 1), (1, 0)])  4.34 us
    ppermute x4, waiting for transfers between devices, across(): return lax.ppermute(value, axis, [(0, 1), (1, 0)])  3.9 us
  transfers between devices with their start and end apart: 20, of which 15 were waited for; matrix products, arithmetic and copies ran while one was open for 1% of the time, Pallas kernels for 5%

profile of v4, /device:TPU:1, one launch (start us, length us, event | category | flops | bytes accessed | tf_op | source)
XLA Modules:
  0.0 180.6 jit_solution(6542320497938852255)
XLA Ops:
  0.0 1.4 collective-permute-start.3
  1.4 1.3 collective-permute-done.3.beside_ref
  2.7 1.9 %shard_map.73 = f32[4,96,512]{2,1,0:T(8,128)} custom-call(f32[96,512]{1,0:T(8,128)} %bitcast.23, f32[96,512]{1,0:T(8,128)S(1)} %collective-permute-done.3.beside_ref), custom_call_target="tpu_custom_call" | custom-call | tf_op jit(solution)/shard_map/pallas_call | solution.py:75
  4.6 0.4 collective-permute-start.6
  4.9 4.1 %all-to-all-start = ((f32[4,96,512]{2,1,0:T(8,128)}), f32[4,96,512]{2,1,0:T(8,128)S(1)}, u32[]{:S(2)}, u32[]{:S(2)}) async-start(f32[4,96,512]{2,1,0:T(8,128)} %shard_map.73), calls=%async_computation | async-start | bytes 1572864 | tf_op jit(solution)/shard_map/all_to_all | solution.py:50
  9.1 0.4 collective-permute-start.7
  9.5 1.6 shard_map.74.factors_ref.refs_8_.refs_7_
  11.1 9.9 %all-to-all-done.first_ref = f32[4,96,512]{2,1,0:T(8,128)S(1)} async-done(((f32[4,96,512]{2,1,0:T(8,128)}), f32[4,96,512]{2,1,0:T(8,128)S(1)}, u32[]{:S(2)}, u32[]{:S(2)}) %all-to-all-start) | async-done | bytes 786464 | tf_op jit(solution)/shard_map/all_to_all | solution.py:50
  21.0 3.0 %shard_map.75 = (f32[8,48,256]{2,1,0:T(8,128)}, f32[96,128]{1,0:T(8,128)}, f32[4,96,128]{2,1,0:T(8,128)}, f32[4,96,256]{2,1,0:T(8,128)}) custom-call(f32[4,96,512]{2,1,0:T(8,128)S(1)} %all-to-all-done.first_ref, f32[128,7680]{1,0:T(8,128)} %bitcast.8, f32[128,1792]{1,0:T(8,128)} %bitcast.16, f32[2,512]{1,0:T(2,128)} %shard_map.74.factors_ref.refs_8_.refs_7_), custom_call_target="tpu_custom_call" | custom-call | tf_op jit(solution)/shard_map/pallas_call | solution.py:75
  24.0 1.4 collective-permute-start.4
  25.4 4.9 %all-to-all-start.1 = ((f32[8,48,256]{2,1,0:T(8,128)}), f32[8,48,256]{2,1,0:T(8,128)S(1)}, u32[]{:S(2)}, u32[]{:S(2)}) async-start(f32[8,48,256]{2,1,0:T(8,128)} %get-tuple-element.24), calls=%async_computation.1 | async-start | bytes 786432 | tf_op jit(solution)/shard_map/all_to_all | solution.py:50
  30.5 0.3 collective-permute-start.1
  30.9 0.8 collective-permute-done.1.refs_2_
  31.7 2.6 %collective-permute-start = (s32[1,14]{1,0:T(1,128)S(1)}, s32[1,14]{1,0:T(1,128)S(1)}, u32[]{:S(2)}, u32[]{:S(2)}) collective-permute-start(s32[1,14]{1,0:T(1,128)S(1)} %copy-done.5), channel_id=1, source_target_pairs={{0,8},{4,20},{8,0},{12,28},{16,24},{20,4},{24,16},{28,12},{1,9},{5... | collective-permute-start | bytes 176 | tf_op jit(solution)/shard_map/ppermute | solution.py:450
  34.3 1.9 %collective-permute-done.refs_1_ = s32[1,14]{1,0:T(1,128)S(1)} collective-permute-done((s32[1,14]{1,0:T(1,128)S(1)}, s32[1,14]{1,0:T(1,128)S(1)}, u32[]{:S(2)}, u32[]{:S(2)}) %collective-permute-start) | collective-permute-done | bytes 88 | tf_op jit(solution)/shard_map/ppermute | solution.py:450
  36.2 1.2 collective-permute-done.2.refs_3_
  37.4 0.9 all-to-all-done.1.refs_4_
  38.3 0.7 copy-done.1
  39.1 4.9 %shard_map.76 = (f32[8,48,512]{2,1,0:T(8,128)}, f32[48,256]{1,0:T(8,128)}, f32[2,4,96,128]{3,2,1,0:T(8,128)}) custom-call(s32[1,14]{1,0:T(1,128)} %refs_0_.9, s32[1,14]{1,0:T(1,128)} %copy-done.7, s32[1,14]{1,0:T(1,128)} %copy-done.6, s32[1,14]{1,0:T(1,128)} %copy-done.8, f32[8,48,256]{2,1,0:T(8,128)S(1)} %all-to-all-done.1.refs_4_, ...), custom_call_target="tpu_custom_call" | custom-call | tf_op jit(solution)/shard_map/pallas_call | solution.py:75
  43.9 15.7 %all_to_all.50.refs_4_ = f32[8,48,512]{2,1,0:T(8,128)S(1)} all-to-all(f32[8,48,512]{2,1,0:T(8,128)} %get-tuple-element.29), channel_id=1, replica_groups=mesh['z'=4,'y1'=2,'y0'=2,'c'=2,'x'=4] {'x','y0'}, dimensions={0} | all-to-all | bytes 1572864 | tf_op jit(solution)/shard_map/all_to_all | solution.py:50
  59.7 5.8 %shard_map.77 = (f32[8,48,128]{2,1,0:T(8,128)}, f32[48,256]{1,0:T(8,128)}) custom-call(s32[1,14]{1,0:T(1,128)} %refs_0_.9, s32[1,14]{1,0:T(1,128)} %copy-done.7, s32[1,14]{1,0:T(1,128)} %copy-done.6, s32[1,14]{1,0:T(1,128)} %copy-done.8, f32[8,48,512]{2,1,0:T(8,128)S(1)} %all_to_all.50.refs_4_, f32[4,96,256]{2,1,0:T(8,128)} %get-tuple-element.26.refs_6_.refs_5_, ...), custom_call_target="tpu_custom_call" | custom-call | tf_op jit(solution)/shard_map/pallas_call | solution.py:75
  65.5 3.4 %all-to-all-start.3 = ((f32[8,48,128]{2,1,0:T(8,128)}), f32[8,48,128]{2,1,0:T(8,128)S(1)}, u32[]{:S(2)}, u32[]{:S(2)}) async-start(f32[8,48,128]{2,1,0:T(8,128)} %get-tuple-element.30), calls=%async_computation.3 | async-start | bytes 393216 | tf_op jit(solution)/shard_map/all_to_all | solution.py:50
  68.9 2.7 %collective-permute-start.8 = (f32[2,4,96,128]{3,2,1,0:T(8,128)S(1)}, f32[2,4,96,128]{3,2,1,0:T(8,128)S(1)}, u32[]{:S(2)}, u32[]{:S(2)}) collective-permute-start(f32[2,4,96,128]{3,2,1,0:T(8,128)S(1)} %copy-done.2), channel_id=1, source_target_pairs={{0,16},{16,0},{1,17},{17,1},{2,18},{18,2},{3,19},{19,3},{4,20},{20... | collective-permute-start | bytes 1179656 | tf_op jit(solution)/shard_map/ppermute | solution.py:58
  71.6 2.9 %all-to-all-done.3 = f32[8,48,128]{2,1,0:T(8,128)S(1)} async-done(((f32[8,48,128]{2,1,0:T(8,128)}), f32[8,48,128]{2,1,0:T(8,128)S(1)}, u32[]{:S(2)}, u32[]{:S(2)}) %all-to-all-start.3) | async-done | bytes 196640 | tf_op jit(solution)/shard_map/all_to_all | solution.py:50
  74.5 0.8 broadcast_in_dim.6
  75.3 5.0 %all-to-all-start.4 = ((f32[16,48,128]{2,1,0:T(8,128)}), f32[16,48,128]{2,1,0:T(8,128)S(1)}, u32[]{:S(2)}, u32[]{:S(2)}) async-start(f32[16,48,128]{2,1,0:T(8,128)} %broadcast_in_dim.6), calls=%async_computation.4 | async-start | bytes 786432 | tf_op jit(solution)/shard_map/all_to_all | solution.py:50
  80.2 2.0 %collective-permute-done.8.refs_6_ = f32[2,4,96,128]{3,2,1,0:T(8,128)S(1)} collective-permute-done((f32[2,4,96,128]{3,2,1,0:T(8,128)S(1)}, f32[2,4,96,128]{3,2,1,0:T(8,128)S(1)}, u32[]{:S(2)}, u32[]{:S(2)}) %collective-permute-start.8) | collective-permute-done | bytes 393248 | tf_op jit(solution)/shard_map/ppermute | solution.py:58
  82.3 6.0 %all-to-all-done.4.refs_4_ = f32[16,48,128]{2,1,0:T(8,128)S(1)} async-done(((f32[16,48,128]{2,1,0:T(8,128)}), f32[16,48,128]{2,1,0:T(8,128)S(1)}, u32[]{:S(2)}, u32[]{:S(2)}) %all-to-all-start.4) | async-done | bytes 393248 | tf_op jit(solution)/shard_map/all_to_all | solution.py:50
  88.3 8.8 %shard_map.78 = (f32[16,48,128]{2,1,0:T(8,128)}, f32[4,2,48,256]{3,2,1,0:T(8,128)}, f32[4,2,48,256]{3,2,1,0:T(8,128)}) custom-call(s32[1,14]{1,0:T(1,128)} %refs_0_.9, s32[1,14]{1,0:T(1,128)} %copy-done.7, s32[1,14]{1,0:T(1,128)} %copy-done.6, s32[1,14]{1,0:T(1,128)} %copy-done.8, f32[16,48,128]{2,1,0:T(8,128)S(1)} %all-to-all-done.4.refs_4_, ...), custom_call_target="tpu_custom_call" | custom-call | tf_op jit(solution)/shard_map/pallas_call | solution.py:75
  97.0 3.7 %all-to-all-start.5 = ((f32[16,48,128]{2,1,0:T(8,128)}), f32[16,48,128]{2,1,0:T(8,128)S(1)}, u32[]{:S(2)}, u32[]{:S(2)}) async-start(f32[16,48,128]{2,1,0:T(8,128)} %get-tuple-element.32), calls=%async_computation.5 | async-start | bytes 786432 | tf_op jit(solution)/shard_map/all_to_all | solution.py:50
  100.8 2.9 %collective-permute-start.9 = (f32[4,2,48,256]{3,2,1,0:T(8,128)}, f32[4,2,48,256]{3,2,1,0:T(8,128)S(1)}, u32[]{:S(2)}, u32[]{:S(2)}) collective-permute-start(f32[4,2,48,256]{3,2,1,0:T(8,128)} %get-tuple-element.35), channel_id=1, source_target_pairs={{0,16},{16,0},{1,17},{17,1},{2,18},{18,2},{3,19},{19,3},{4,20},{20... | collective-permute-start | bytes 1179656 | tf_op jit(solution)/shard_map/ppermute | solution.py:58
  103.6 5.2 %all-to-all-done.5 = f32[16,48,128]{2,1,0:T(8,128)S(1)} async-done(((f32[16,48,128]{2,1,0:T(8,128)}), f32[16,48,128]{2,1,0:T(8,128)S(1)}, u32[]{:S(2)}, u32[]{:S(2)}) %all-to-all-start.5) | async-done | bytes 393248 | tf_op jit(solution)/shard_map/all_to_all | solution.py:50
  108.9 0.7 broadcast_in_dim.7
  109.6 3.6 %all-to-all-start.6 = ((f32[8,48,128]{2,1,0:T(8,128)}), f32[8,48,128]{2,1,0:T(8,128)S(1)}, u32[]{:S(2)}, u32[]{:S(2)}) async-start(f32[8,48,128]{2,1,0:T(8,128)} %broadcast_in_dim.7), calls=%async_computation.6 | async-start | bytes 393216 | tf_op jit(solution)/shard_map/all_to_all | solution.py:50
  113.2 1.9 %collective-permute-done.9.refs_7_ = f32[4,2,48,256]{3,2,1,0:T(8,128)S(1)} collective-permute-done((f32[4,2,48,256]{3,2,1,0:T(8,128)}, f32[4,2,48,256]{3,2,1,0:T(8,128)S(1)}, u32[]{:S(2)}, u32[]{:S(2)}) %collective-permute-start.9) | collective-permute-done | bytes 393248 | tf_op jit(solution)/shard_map/ppermute | solution.py:58
  115.1 3.5 %all-to-all-done.6.refs_4_ = f32[8,48,128]{2,1,0:T(8,128)S(1)} async-done(((f32[8,48,128]{2,1,0:T(8,128)}), f32[8,48,128]{2,1,0:T(8,128)S(1)}, u32[]{:S(2)}, u32[]{:S(2)}) %all-to-all-start.6) | async-done | bytes 196640 | tf_op jit(solution)/shard_map/all_to_all | solution.py:50
  118.5 5.8 %shard_map.79 = (f32[8,48,512]{2,1,0:T(8,128)}, f32[2,4,48,256]{3,2,1,0:T(8,128)}, f32[2,4,48,256]{3,2,1,0:T(8,128)}) custom-call(s32[1,14]{1,0:T(1,128)} %refs_0_.9, s32[1,14]{1,0:T(1,128)} %copy-done.7, s32[1,14]{1,0:T(1,128)} %copy-done.6, s32[1,14]{1,0:T(1,128)} %copy-done.8, f32[8,48,128]{2,1,0:T(8,128)S(1)} %all-to-all-done.6.refs_4_, ...), custom_call_target="tpu_custom_call" | custom-call | tf_op jit(solution)/shard_map/pallas_call | solution.py:75
  124.4 3.6 %all-to-all-start.7 = ((f32[8,48,512]{2,1,0:T(8,128)}), f32[8,48,512]{2,1,0:T(8,128)S(1)}, u32[]{:S(2)}, u32[]{:S(2)}) async-start(f32[8,48,512]{2,1,0:T(8,128)} %get-tuple-element.36), calls=%async_computation.7 | async-start | bytes 1572864 | tf_op jit(solution)/shard_map/all_to_all | solution.py:50
  127.9 1.4 collective-permute-start.10
  129.3 7.0 %all-to-all-done.7.refs_4_ = f32[8,48,512]{2,1,0:T(8,128)S(1)} async-done(((f32[8,48,512]{2,1,0:T(8,128)}), f32[8,48,512]{2,1,0:T(8,128)S(1)}, u32[]{:S(2)}, u32[]{:S(2)}) %all-to-all-start.7) | async-done | bytes 786464 | tf_op jit(solution)/shard_map/all_to_all | solution.py:50
  136.3 3.9 %shard_map.80 = (f32[8,48,256]{2,1,0:T(8,128)}, f32[4,48,256]{2,1,0:T(8,128)}) custom-call(s32[1,14]{1,0:T(1,128)} %refs_0_.9, s32[1,14]{1,0:T(1,128)} %copy-done.7, s32[1,14]{1,0:T(1,128)} %copy-done.6, s32[1,14]{1,0:T(1,128)} %copy-done.8, f32[8,48,512]{2,1,0:T(8,128)S(1)} %all-to-all-done.7.refs_4_, f32[48,256]{1,0:T(8,128)} %get-tuple-element.37.refs_5_, ...), custom_call_target="tpu_custom_call" | custom-call | tf_op jit(solution)/shard_map/pallas_call | solution.py:75
  140.2 10.7 %all-to-all-start.8 = ((f32[8,48,256]{2,1,0:T(8,128)}), f32[8,48,256]{2,1,0:T(8,128)S(1)}, u32[]{:S(2)}, u32[]{:S(2)}) async-start(f32[8,48,256]{2,1,0:T(8,128)} %get-tuple-element.38), calls=%async_computation.8 | async-start | bytes 786432 | tf_op jit(solution)/shard_map/all_to_all | solution.py:50
  150.9 7.7 %all-to-all-done.8.received_ref = f32[8,48,256]{2,1,0:T(8,128)S(1)} async-done(((f32[8,48,256]{2,1,0:T(8,128)}), f32[8,48,256]{2,1,0:T(8,128)S(1)}, u32[]{:S(2)}, u32[]{:S(2)}) %all-to-all-start.8) | async-done | bytes 393248 | tf_op jit(solution)/shard_map/all_to_all | solution.py:50
  158.6 3.4 %shard_map.81 = f32[4,96,512]{2,1,0:T(8,128)} custom-call(f32[8,48,256]{2,1,0:T(8,128)S(1)} %all-to-all-done.8.received_ref, f32[96,128]{1,0:T(8,128)} %get-tuple-element.39.weighted_ref, f32[4,48,256]{2,1,0:T(8,128)} %get-tuple-element.40.nearest_ref, f32[2,4,48,256]{3,2,1,0:T(8,128)} %get-tuple-element.41.kept_ref, ...), custom_call_target="tpu_custom_call" | custom-call | tf_op jit(solution)/shard_map/pallas_call | solution.py:75
  162.0 14.6 %all_to_all.51.received_ref = f32[4,96,512]{2,1,0:T(8,128)S(1)} all-to-all(f32[4,96,512]{2,1,0:T(8,128)} %shard_map.81), channel_id=1, replica_groups=mesh['z'=4,'y1'=2,'y0'=2,'c'=2,'x'=4] {'x'}, dimensions={0} | all-to-all | bytes 1572864 | tf_op jit(solution)/shard_map/all_to_all | solution.py:50
  176.7 2.2 %collective-permute-start.11 = (f32[96,512]{1,0:T(8,128)S(1)}, f32[96,512]{1,0:T(8,128)S(1)}, u32[]{:S(2)}, u32[]{:S(2)}) collective-permute-start(f32[96,512]{1,0:T(8,128)S(1)} %shard_map.82.total_ref), channel_id=1, source_target_pairs={{0,4},{4,0},{1,5},{5,1},{2,6},{6,2},{3,7},{7,3},{8,12},{12,8},{9,1... | collective-permute-start | bytes 589832 | tf_op jit(solution)/shard_map/ppermute | solution.py:54
  178.9 1.1 collective-permute-done.11.beside_ref
  179.9 0.7 shard_map.83
  (27 shorter events, 0.3 us)
Async XLA Ops:
  0.0 2.7 %collective-permute-start.3 = (f32[96,512]{1,0:T(8,128)}, f32[96,512]{1,0:T(8,128)S(1)}, u32[]{:S(2)}, u32[]{:S(2)}) collective-permute-start(f32[96,512]{1,0:T(8,128)} %bitcast.22), channel_id=1, source_target_pairs={{0,4},{4,0},{1,5},{5,1},{2,6},{6,2},{3,7},{7,3},{8,12},{12,8},{9,1... | collective-permute-start | bytes 589832 | tf_op jit(solution)/shard_map/ppermute | solution.py:54
  4.6 26.0 %copy-start.5 = (s32[1,14]{1,0:T(1,128)S(1)}, s32[1,14]{1,0:T(1,128)}, u32[]{:S(2)}) copy-start(s32[1,14]{1,0:T(1,128)} %refs_0_.9) | copy-start | bytes 172
  4.6 33.7 %collective-permute-start.6 = (f32[128,7680]{1,0:T(8,128)}, f32[128,7680]{1,0:T(8,128)}, u32[]{:S(2)}, u32[]{:S(2)}) collective-permute-start(f32[128,7680]{1,0:T(8,128)} %bitcast.7), channel_id=1, source_target_pairs={{0,4},{4,0},{1,5},{5,1},{2,6},{6,2},{3,7},{7,3},{8,12},{12,8},{9,1... | collective-permute-start | bytes 11796488 | tf_op jit(solution)/shard_map/ppermute | solution.py:54
  4.9 16.1 %all-to-all-start = ((f32[4,96,512]{2,1,0:T(8,128)}), f32[4,96,512]{2,1,0:T(8,128)S(1)}, u32[]{:S(2)}, u32[]{:S(2)}) async-start(f32[4,96,512]{2,1,0:T(8,128)} %shard_map.73), calls=%async_computation | async-start | bytes 1572864 | tf_op jit(solution)/shard_map/all_to_all | solution.py:50
  9.1 28.3 %collective-permute-start.7 = (f32[128,1792]{1,0:T(8,128)}, f32[128,1792]{1,0:T(8,128)S(1)}, u32[]{:S(2)}, u32[]{:S(2)}) collective-permute-start(f32[128,1792]{1,0:T(8,128)} %bitcast.15), channel_id=1, source_target_pairs={{0,4},{4,0},{1,5},{5,1},{2,6},{6,2},{3,7},{7,3},{8,12},{12,8},{9,1... | collective-permute-start | bytes 2752520 | tf_op jit(solution)/shard_map/ppermute | solution.py:54
  11.1 19.2 %copy-start.3 = (f32[2,512]{1,0:T(2,128)S(1)}, f32[2,512]{1,0:T(2,128)}, u32[]{:S(2)}) copy-start(f32[2,512]{1,0:T(2,128)} %shard_map.74.factors_ref.refs_8_.refs_7_) | copy-start | bytes 12292
  24.0 14.3 %collective-permute-start.4 = (f32[4,96,256]{2,1,0:T(8,128)}, f32[4,96,256]{2,1,0:T(8,128)S(1)}, u32[]{:S(2)}, u32[]{:S(2)}) collective-permute-start(f32[4,96,256]{2,1,0:T(8,128)} %get-tuple-element.26.refs_6_.refs_5_), channel_id=1, source_target_pairs={{0,8},{8,0},{1,9},{9,1},{2,10},{10,2},{3,11},{11,3},{4,12},{12,4},... | collective-permute-start | bytes 1179656 | tf_op jit(solution)/shard_map/ppermute | solution.py:58
  25.4 12.9 %all-to-all-start.1 = ((f32[8,48,256]{2,1,0:T(8,128)}), f32[8,48,256]{2,1,0:T(8,128)S(1)}, u32[]{:S(2)}, u32[]{:S(2)}) async-start(f32[8,48,256]{2,1,0:T(8,128)} %get-tuple-element.24), calls=%async_computation.1 | async-start | bytes 786432 | tf_op jit(solution)/shard_map/all_to_all | solution.py:50
  30.3 7.0 %collective-permute-start.5 = (f32[2,512]{1,0:T(2,128)S(1)}, f32[2,512]{1,0:T(2,128)S(1)}, u32[]{:S(2)}, u32[]{:S(2)}) collective-permute-start(f32[2,512]{1,0:T(2,128)S(1)} %copy-done.3), channel_id=1, source_target_pairs={{0,4},{4,0},{1,5},{5,1},{2,6},{6,2},{3,7},{7,3},{8,12},{12,8},{9,1... | collective-permute-start | bytes 12296 | tf_op jit(solution)/shard_map/ppermute | solution.py:54
  30.5 1.2 collective-permute-start.1
  31.7 6.6 %copy-start.6 = (s32[1,14]{1,0:T(1,128)}, s32[1,14]{1,0:T(1,128)S(1)}, u32[]{:S(2)}) copy-start(s32[1,14]{1,0:T(1,128)S(1)} %collective-permute-done.1.refs_2_) | copy-start | bytes 172
  31.7 4.5 %collective-permute-start = (s32[1,14]{1,0:T(1,128)S(1)}, s32[1,14]{1,0:T(1,128)S(1)}, u32[]{:S(2)}, u32[]{:S(2)}) collective-permute-start(s32[1,14]{1,0:T(1,128)S(1)} %copy-done.5), channel_id=1, source_target_pairs={{0,8},{4,20},{8,0},{12,28},{16,24},{20,4},{24,16},{28,12},{1,9},{5... | collective-permute-start | bytes 176 | tf_op jit(solution)/shard_map/ppermute | solution.py:450
  36.2 2.1 %copy-start.7 = (s32[1,14]{1,0:T(1,128)}, s32[1,14]{1,0:T(1,128)S(1)}, u32[]{:S(2)}) copy-start(s32[1,14]{1,0:T(1,128)S(1)} %collective-permute-done.refs_1_) | copy-start | bytes 172
  36.2 1.2 collective-permute-start.2
  37.3 1.0 copy-start.8
  37.3 1.0 copy-start.4
  37.4 1.0 copy-start
  38.3 0.8 copy-start.1
  59.7 9.2 %copy-start.2 = (f32[2,4,96,128]{3,2,1,0:T(8,128)S(1)}, f32[2,4,96,128]{3,2,1,0:T(8,128)}, u32[]{:S(2)}) copy-start(f32[2,4,96,128]{3,2,1,0:T(8,128)} %get-tuple-element.31.refs_5_) | copy-start | bytes 1179652
  65.5 9.0 %all-to-all-start.3 = ((f32[8,48,128]{2,1,0:T(8,128)}), f32[8,48,128]{2,1,0:T(8,128)S(1)}, u32[]{:S(2)}, u32[]{:S(2)}) async-start(f32[8,48,128]{2,1,0:T(8,128)} %get-tuple-element.30), calls=%async_computation.3 | async-start | bytes 393216 | tf_op jit(solution)/shard_map/all_to_all | solution.py:50
  68.9 13.4 %collective-permute-start.8 = (f32[2,4,96,128]{3,2,1,0:T(8,128)S(1)}, f32[2,4,96,128]{3,2,1,0:T(8,128)S(1)}, u32[]{:S(2)}, u32[]{:S(2)}) collective-permute-start(f32[2,4,96,128]{3,2,1,0:T(8,128)S(1)} %copy-done.2), channel_id=1, source_target_pairs={{0,16},{16,0},{1,17},{17,1},{2,18},{18,2},{3,19},{19,3},{4,20},{20... | collective-permute-start | bytes 1179656 | tf_op jit(solution)/shard_map/ppermute | solution.py:58
  75.3 13.0 %all-to-all-start.4 = ((f32[16,48,128]{2,1,0:T(8,128)}), f32[16,48,128]{2,1,0:T(8,128)S(1)}, u32[]{:S(2)}, u32[]{:S(2)}) async-start(f32[16,48,128]{2,1,0:T(8,128)} %broadcast_in_dim.6), calls=%async_computation.4 | async-start | bytes 786432 | tf_op jit(solution)/shard_map/all_to_all | solution.py:50
  97.0 11.8 %all-to-all-start.5 = ((f32[16,48,128]{2,1,0:T(8,128)}), f32[16,48,128]{2,1,0:T(8,128)S(1)}, u32[]{:S(2)}, u32[]{:S(2)}) async-start(f32[16,48,128]{2,1,0:T(8,128)} %get-tuple-element.32), calls=%async_computation.5 | async-start | bytes 786432 | tf_op jit(solution)/shard_map/all_to_all | solution.py:50
  100.8 14.3 %collective-permute-start.9 = (f32[4,2,48,256]{3,2,1,0:T(8,128)}, f32[4,2,48,256]{3,2,1,0:T(8,128)S(1)}, u32[]{:S(2)}, u32[]{:S(2)}) collective-permute-start(f32[4,2,48,256]{3,2,1,0:T(8,128)} %get-tuple-element.35), channel_id=1, source_target_pairs={{0,16},{16,0},{1,17},{17,1},{2,18},{18,2},{3,19},{19,3},{4,20},{20... | collective-permute-start | bytes 1179656 | tf_op jit(solution)/shard_map/ppermute | solution.py:58
  109.6 8.9 %all-to-all-start.6 = ((f32[8,48,128]{2,1,0:T(8,128)}), f32[8,48,128]{2,1,0:T(8,128)S(1)}, u32[]{:S(2)}, u32[]{:S(2)}) async-start(f32[8,48,128]{2,1,0:T(8,128)} %broadcast_in_dim.7), calls=%async_computation.6 | async-start | bytes 393216 | tf_op jit(solution)/shard_map/all_to_all | solution.py:50
  124.4 11.9 %all-to-all-start.7 = ((f32[8,48,512]{2,1,0:T(8,128)}), f32[8,48,512]{2,1,0:T(8,128)S(1)}, u32[]{:S(2)}, u32[]{:S(2)}) async-start(f32[8,48,512]{2,1,0:T(8,128)} %get-tuple-element.36), calls=%async_computation.7 | async-start | bytes 1572864 | tf_op jit(solution)/shard_map/all_to_all | solution.py:50
  127.9 22.9 %collective-permute-start.10 = (f32[2,4,48,256]{3,2,1,0:T(8,128)}, f32[2,4,48,256]{3,2,1,0:T(8,128)S(1)}, u32[]{:S(2)}, u32[]{:S(2)}) collective-permute-start(f32[2,4,48,256]{3,2,1,0:T(8,128)} %get-tuple-element.42), channel_id=1, source_target_pairs={{0,8},{8,0},{1,9},{9,1},{2,10},{10,2},{3,11},{11,3},{4,12},{12,4},... | collective-permute-start | bytes 1179656 | tf_op jit(solution)/shard_map/ppermute | solution.py:58
  140.2 18.4 %all-to-all-start.8 = ((f32[8,48,256]{2,1,0:T(8,128)}), f32[8,48,256]{2,1,0:T(8,128)S(1)}, u32[]{:S(2)}, u32[]{:S(2)}) async-start(f32[8,48,256]{2,1,0:T(8,128)} %get-tuple-element.38), calls=%async_computation.8 | async-start | bytes 786432 | tf_op jit(solution)/shard_map/all_to_all | solution.py:50
  176.7 3.2 %collective-permute-start.11 = (f32[96,512]{1,0:T(8,128)S(1)}, f32[96,512]{1,0:T(8,128)S(1)}, u32[]{:S(2)}, u32[]{:S(2)}) collective-permute-start(f32[96,512]{1,0:T(8,128)S(1)} %shard_map.82.total_ref), channel_id=1, source_target_pairs={{0,4},{4,0},{1,5},{5,1},{2,6},{6,2},{3,7},{7,3},{8,12},{12,8},{9,1... | collective-permute-start | bytes 589832 | tf_op jit(solution)/shard_map/ppermute | solution.py:54

commit v5 on v3

--- a/solution.py
+++ b/solution.py
@@ -58,18 +58,29 @@
 FAR = pl.BlockSpec(memory_space=pltpu.HBM)
 
 
-def call(body, out_shapes, operands, specs, scratch=(), limit=16):
+def far(value):
+    return pltpu.with_memory_space_constraint(value, pltpu.HBM)
+
+
+def close(value):
+    return pltpu.with_memory_space_constraint(value, pltpu.VMEM)
+
+
+def call(body, out_shapes, operands, specs, scratch=(), limit=20, spaces=None):
     return pl.pallas_call(
         body,
         in_specs=specs,
-        out_specs=[WHOLE] * len(out_shapes),
-        out_shape=[jax.ShapeDtypeStruct(s, jnp.float32) for s in out_shapes],
+        out_specs=[FAR if k == "H" else WHOLE for k in spaces or "-" * len(out_shapes)],
+        out_shape=[
+            {"H": pltpu.HBM, "h": pltpu.HBM, "v": pltpu.VMEM, "-": jax.ShapeDtypeStruct}[k](s, jnp.float32)
+            for s, k in zip(out_shapes, spaces or "-" * len(out_shapes))
+        ],
         scratch_shapes=list(scratch),
         compiler_params=pltpu.CompilerParams(vmem_limit_bytes=limit * 1024 * 1024),
     )(*operands)
 
 
-def prepared(pair, spans, after):
+def prepared(pair, spans, after, space=pltpu.HBM):
     def body(*refs):
         sources = refs[: len(pair)]
         outs = refs[len(pair) + 1 :][: len(spans)]
@@ -100,11 +111,11 @@
         body,
         in_specs=[FAR] * len(pair) + [FAR],
         out_specs=[WHOLE] * len(spans),
-        out_shape=[jax.ShapeDtypeStruct((2, count, width), jnp.bfloat16) for _, width in spans],
+        out_shape=[space((2, count, width), jnp.bfloat16) for _, width in spans],
         scratch_shapes=[pltpu.VMEM((count, width), jnp.float32) for _, width in spans]
         + [pltpu.SemaphoreType.DMA((len(spans), len(pair)))],
         compiler_params=pltpu.CompilerParams(vmem_limit_bytes=24 * 1024 * 1024),
-    )(*pair, after)
+    )(*map(far, pair), after)
 
 
 def pivot_apply(solved, own, swapped):
@@ -134,7 +145,8 @@
         out_ref[0:1, :] = jnp.where(is_pair, other / determinant, 1.0 / own)
         out_ref[1:2, :] = jnp.where(is_pair, -couple / determinant, 0.0)
 
-    return call(body, [(2, diagonal.shape[1])], [kinds, diagonal, coupling], [WHOLE] * 3)[0]
+    operands = [far(kinds), far(diagonal), far(coupling)]
+    return call(body, [(2, diagonal.shape[1])], operands, [WHOLE] * 3, spaces="v")[0]
 
 
 def packed_sides(sides, beside):
@@ -142,29 +154,66 @@
         c = lax.axis_index("c")
         mine = pl.ds(pl.multiple_of(c * HALF, 8), HALF)
         theirs = pl.ds(pl.multiple_of((1 - c) * HALF, 8), HALF)
-        out_ref[mine] = sides_ref[mine, 2 * PIVOTS :]
-        out_ref[theirs] = beside_ref[mine, 2 * PIVOTS :]
-
-    return call(body, [(SIDES, 256)], [sides, beside], [WHOLE] * 2)[0]
-
-
-def level_zero_forward(first, sides, weights, updates, factors):
-    def body(first_ref, sides_ref, weights_ref, updates_ref, factors_ref, sent_ref, weighted_ref):
-        gathered = jnp.concatenate([first_ref[q] for q in range(4)], 1)
+        own = sides_ref[mine, PIVOTS:]
+        other = beside_ref[mine, PIVOTS:]
+        for i in range(4):
+            out_ref[i, :, :PIVOTS] = sides_ref[:, :PIVOTS]
+            out_ref[i, mine, PIVOTS:] = own
+            out_ref[i, theirs, PIVOTS:] = other
+
+    return call(body, [(4, SIDES, 512)], [far(sides), beside], [WHOLE] * 2, spaces="h")[0]
+
+
+class Moves:
+    def __init__(self, semaphores):
+        self.semaphores, self.started = semaphores, []
+
+    def start(self, source, target):
+        move = pltpu.make_async_copy(source, target, self.semaphores.at[len(self.started)])
+        move.start()
+        self.started.append(move)
+        return move
+
+    def columns(self, source, target, step):
+        width = source.shape[2]
+        spans = [pl.ds(at, step) for at in range(0, width, step)]
+        return [self.start(source.at[:, :, span], target.at[:, :, span]) for span in spans]
+
+
+def finish(moves):
+    for move in moves:
+        move.wait()
+
+
+def level_zero_forward(first, weights, updates, factors):
+    def body(first_ref, weights_ref, updates_ref, factors_ref, *refs):
+        sent_ref, weighted_ref, one_ref, upper_ref, part_ref, own_ref, semaphores = refs
+        moves = Moves(semaphores)
+        leaving = [
+            moves.start(first_ref.at[:, :, pl.ds(PIVOTS, PIVOTS)], one_ref),
+            moves.start(first_ref.at[:, :, pl.ds(2 * PIVOTS, 2 * PIVOTS)], upper_ref),
+        ]
+        gathered = jnp.concatenate([first_ref[q, :, :PIVOTS] for q in range(4)], 1)
         solved = product(gathered, weights_ref[0], weights_ref[1], 1)
-        weighted_ref[...] = pivot_apply(solved, factors_ref[0:1, :PIVOTS], factors_ref[1:2, :PIVOTS])
-        part = product(solved, updates_ref[0], updates_ref[1], 0)
+        part_ref[...] = product(solved, updates_ref[0], updates_ref[1], 0)
         for c in range(2):
-            half = slice(c * HALF, (c + 1) * HALF)
             for x in range(4):
-                sent_ref[c * 4 + x, :, :256] = part[half]
-                sent_ref[c * 4 + x, :, 256:] = sides_ref[half, PIVOTS : 2 * PIVOTS]
+                leaving.append(moves.start(part_ref.at[pl.ds(c * HALF, HALF)], sent_ref.at[c * 4 + x]))
+        own_ref[...] = pivot_apply(solved, factors_ref[0:1, :PIVOTS], factors_ref[1:2, :PIVOTS])
+        leaving.append(moves.start(own_ref, weighted_ref))
+        finish(leaving)
 
     return call(
         body,
-        [(8, HALF, 384), (SIDES, PIVOTS)],
-        [first, sides, weights, updates, factors],
-        [WHOLE] * 5,
+        [(8, HALF, 256), (SIDES, PIVOTS), (4, SIDES, PIVOTS), (4, SIDES, 256)],
+        [close(first), close(weights), close(updates), close(factors)],
+        [WHOLE] * 4,
+        [
+            pltpu.VMEM((SIDES, 256), jnp.float32),
+            pltpu.VMEM((SIDES, PIVOTS), jnp.float32),
+            pltpu.SemaphoreType.DMA((16,)),
+        ],
+        spaces="HHHH",
     )
 
 
@@ -198,6 +247,7 @@
     blocks = (2, 4, 8)[level - 1]
     n_sides = len(sides)
     n_updates = 1 if level < 3 else 0
+    n_outs = (3, 2, 3)[level - 1]
 
     def body(*refs):
         refs = list(refs)
@@ -207,79 +257,106 @@
             return taken
 
         tables_refs = take(4)
-        (received_ref,) = take(1)
+        received_ref, factors_ref, beside_ref = take(3)
         sides_refs = take(n_sides)
-        factors_ref, beside_ref, weights_ref = take(3)
-        updates_ref = take(n_updates)
-        outs = take(2 if level < 3 else 3)
-        (b_ref,) = take(1)
+        (weights_far,) = take(1)
+        updates_far = take(n_updates)
+        outs = take(n_outs)
+        semaphores, b_ref, own_ref, weights_ref = take(4)
+        moves = Moves(semaphores)
         x0, y0, y1 = lax.axis_index("x"), lax.axis_index("y0"), lax.axis_index("y1")
+
+        arriving, leaving = [], []
+
+        def bring(source, block):
+            for c in range(2):
+                arriving.append(moves.start(source.at[pl.ds(c * HALF, HALF)], b_ref.at[:, block_at(block * 2 + c)]))
+
         if level == 1:
             for x in range(4):
-                for c in range(2):
-                    b_ref[:, (x * 2 + c) * PIVOTS : (x * 2 + c + 1) * PIVOTS] = received_ref[c * 4 + x, :, 256:]
+                bring(sides_refs[0].at[x], x)
         elif level == 2:
             for flip in range(2):
                 for x in range(4):
-                    b_ref[:, block_at((x0 ^ x) * 2 + (y0 ^ flip), 256)] = halves(sides_refs[flip][x, :, :PIVOTS])
+                    bring(sides_refs[flip].at[x, :, pl.ds(0, PIVOTS)], x * 2 + (y0 ^ flip))
         else:
             for high in range(2):
                 for flip in range(2):
                     for x in range(4):
-                        where = block_at((x0 ^ x) * 4 + (y1 ^ high) * 2 + (y0 ^ flip), 256)
-                        b_ref[:, where] = halves(sides_refs[high][flip, x])
+                        bring(sides_refs[high].at[flip, x], x * 4 + (y1 ^ high) * 2 + (y0 ^ flip))
+        columns = moves.columns(weights_far, weights_ref, 512)
+        if level < 3:
+            updates_ref, part_ref = refs
+            update_columns = moves.columns(updates_far[0], updates_ref, 256)
+        if level == 1:
+            for flip in range(2):
+                leaving.append(moves.start(sides_refs[1 + flip].at[:, :, pl.ds(PIVOTS, PIVOTS)], outs[2].at[flip]))
+        totals = [None, None]
         for child in range(2):
             if level == 1:
-                total = sum(received_ref[child * 4 + x, :, :256] for x in range(4))
+                totals[child] = sum(received_ref[child * 4 + x] for x in range(4))
             elif level == 2:
-                total = sum(received_ref[x * 2 + child] for x in range(4))
+                totals[child] = sum(received_ref[x * 2 + child] for x in range(4))
+        finish(arriving)
+        for child in range(2):
             for k in range(blocks):
                 if level < 3:
-                    piece = total[:, k * BLOCK : (k + 1) * BLOCK]
+                    piece = totals[child][:, k * BLOCK : (k + 1) * BLOCK]
                 else:
                     piece = received_ref[(k // 2) * 4 + child * 2 + k % 2]
                 where = block_at(child_block(level, tables_refs, child, k))
                 b_ref[:, where] = b_ref[:, where] - piece
         solved = jnp.zeros((HALF, 2 * PIVOTS), jnp.float32)
         for k in range(chunks):
+            columns[k].wait()
             at = slice(k * 512, (k + 1) * 512)
             solved += product(b_ref[:, at], weights_ref[0, :, at], weights_ref[1, :, at], 1)
         weighted = pivot_apply(solved, *both_factors(level, factors_ref, beside_ref))
         if level < 3:
-            outs[1][...] = weighted
+            own_ref[...] = weighted
+            leaving.append(moves.start(own_ref, outs[1]))
             for k in range(update_len // 256):
+                update_columns[k].wait()
                 at = slice(k * 256, (k + 1) * 256)
-                part = product(solved, updates_ref[0][0, :, at], updates_ref[0][1, :, at], 0)
-                if level == 1:
-                    for i in range(8):
-                        outs[0][i, :, at] = part
-                else:
-                    outs[0][2 * k] = part[:, :BLOCK]
-                    outs[0][2 * k + 1] = part[:, BLOCK:]
+                part_ref[:, at] = product(solved, updates_ref[0, :, at], updates_ref[1, :, at], 0)
+            for i in range(8):
+                source = part_ref if level == 1 else part_ref.at[:, pl.ds(i * BLOCK, BLOCK)]
+                leaving.append(moves.start(source, outs[0].at[i]))
         else:
-            sent_ref, keep_ref, far_ref = outs
+            sent_ref, keep_ref, beyond_ref = outs
             for k in range(chunks):
                 at = slice(k * 512, (k + 1) * 512)
                 b_ref[:, at] = product(weighted, weights_ref[0, :, at], weights_ref[1, :, at], 0)
             for child in range(2):
                 for k in range(8):
                     where = block_at(child_block(3, tables_refs, child, k))
-                    sent_ref[(k // 2) * 4 + child * 2 + k % 2] = b_ref[:, where]
-            for x in range(4):
-                for low in range(2):
-                    keep_ref[x, low] = b_ref[:, block_at(x * 4 + y1 * 2 + low, 256)]
-                    far_ref[x, low] = b_ref[:, block_at(x * 4 + (1 - y1) * 2 + low, 256)]
+                    leaving.append(
+                        moves.start(b_ref.at[:, where], sent_ref.at[(k // 2) * 4 + child * 2 + k % 2])
+                    )
+            for out, bit in ((beyond_ref, 1 - y1), (keep_ref, y1)):
+                for x in range(4):
+                    for low in range(2):
+                        where = block_at(x * 4 + bit * 2 + low, 256)
+                        leaving.append(moves.start(b_ref.at[:, where], out.at[x, low]))
+        finish(leaving)
 
     outs = {
-        1: [(8, HALF, 512), (HALF, 256)],
+        1: [(8, HALF, 512), (HALF, 256), (2, 4, SIDES, PIVOTS)],
         2: [(8, HALF, BLOCK), (HALF, 256)],
         3: [(16, HALF, BLOCK), (4, 2, HALF, 256), (4, 2, HALF, 256)],
     }[level]
-    operands = [*tables, received, *sides, factors, partner_factors, weights]
+    operands = [*map(far, tables), received, close(factors), close(partner_factors)]
+    operands += map(far, [*sides, weights] + ([updates] if level < 3 else []))
+    specs = [SCALARS] * 4 + [WHOLE] * 3 + [FAR] * (len(operands) - 7)
+    scratch = [
+        pltpu.SemaphoreType.DMA((80,)),
+        pltpu.VMEM((HALF, span), jnp.float32),
+        pltpu.VMEM((HALF, 256), jnp.float32),
+        pltpu.VMEM((2, 256, span), jnp.bfloat16),
+    ]
     if level < 3:
-        operands.append(updates)
-    specs = [SCALARS] * 4 + [WHOLE] * (len(operands) - 4)
-    return call(body, outs, operands, specs, [pltpu.VMEM((HALF, span), jnp.float32)])
+        scratch += [pltpu.VMEM((2, 256, update_len), jnp.bfloat16), pltpu.VMEM((HALF, update_len), jnp.float32)]
+    return call(body, outs, operands, specs, scratch, spaces="H" * n_outs)
 
 
 def backward(level, received, weighted, tables, weights, updates, answers):
@@ -288,6 +365,8 @@
     chunks = span // 512
     update_len = 2 * PIVOTS * width
     blocks = (2, 4)[level - 1]
+    n_answers = len(answers)
+    n_outs = (2, 3)[level - 1]
 
     def body(*refs):
         refs = list(refs)
@@ -297,47 +376,73 @@
             return taken
 
         tables_refs = take(4)
-        received_ref, weighted_ref = take(2)
-        answer_refs = take(len(answers))
-        weights_ref, updates_ref = take(2)
-        outs = take(2 if level == 1 else 3)
-        (x_ref,) = take(1)
-        target = weighted_ref[...]
+        (received_ref,) = take(1)
+        weighted_far, weights_far, updates_far = take(3)
+        answers_far = take(n_answers)
+        outs = take(n_outs)
+        semaphores, x_ref, weighted_ref, weights_ref, updates_ref, pieces_ref = take(6)
+        moves = Moves(semaphores)
+        arriving = moves.start(weighted_far, weighted_ref)
+        update_columns = moves.columns(updates_far, updates_ref, 256)
+        columns = moves.columns(weights_far, weights_ref, 512)
+        leaving = []
+        if level == 2:
+            own_ref, other_ref, sums_ref = refs
+            both = [moves.start(answers_far[0], own_ref), moves.start(answers_far[1], other_ref)]
         if level == 1:
             total = sum(received_ref[i] for i in range(8))
+        arriving.wait()
+        target = weighted_ref[...]
         for k in range(update_len // 256):
             at = slice(k * 256, (k + 1) * 256)
             if level == 1:
                 chosen = total[:, at]
             else:
                 chosen = jnp.concatenate([received_ref[2 * k], received_ref[2 * k + 1]], 1)
+            update_columns[k].wait()
             target -= product(chosen, updates_ref[0, :, at], updates_ref[1, :, at], 1)
         for k in range(chunks):
+            columns[k].wait()
             at = slice(k * 512, (k + 1) * 512)
             x_ref[:, at] = product(target, weights_ref[0, :, at], weights_ref[1, :, at], 0)
         for child in range(2):
             for k in range(blocks):
-                piece = x_ref[:, block_at(child_block(level, tables_refs, child, k))]
-                for x in range(4):
-                    outs[0][x * 2 + child, :, k * BLOCK : (k + 1) * BLOCK] = piece
+                where = block_at(child_block(level, tables_refs, child, k))
+                pieces_ref[child, :, k * BLOCK : (k + 1) * BLOCK] = x_ref[:, where]
+            for x in range(4):
+                leaving.append(moves.start(pieces_ref.at[child], outs[0].at[x * 2 + child]))
         if level == 1:
             for x in range(4):
-                outs[1][x] = x_ref[:, x * 256 : (x + 1) * 256]
+                leaving.append(moves.start(x_ref.at[:, pl.ds(x * 256, 256)], outs[1].at[x]))
         else:
             y0 = lax.axis_index("y0")
-            keep_ref, far_ref = outs[1:]
-            own_ref, other_ref = answer_refs
-            for x in range(4):
-                keep_ref[0, x] = x_ref[:, block_at(x * 2 + y0, 256)]
-                far_ref[0, x] = x_ref[:, block_at(x * 2 + (1 - y0), 256)]
-                keep_ref[1, x] = own_ref[x, y0] + other_ref[x, y0]
-                far_ref[1, x] = own_ref[x, 1 - y0] + other_ref[x, 1 - y0]
+            keep_out, beyond_out = outs[1:]
+            for out, bit in ((beyond_out, 1 - y0), (keep_out, y0)):
+                for x in range(4):
+                    where = block_at(x * 2 + bit, 256)
+                    leaving.append(moves.start(x_ref.at[:, where], out.at[0, x]))
+            finish(both)
+            for i, (out, bit) in enumerate(((beyond_out, 1 - y0), (keep_out, y0))):
+                for x in range(4):
+                    sums_ref[i, x] = own_ref[x, bit] + other_ref[x, bit]
+                leaving.append(moves.start(sums_ref.at[i], out.at[1]))
+        finish(leaving)
 
     outs = [(8, HALF, blocks * BLOCK)]
     outs += [(4, HALF, 256)] if level == 1 else [(2, 4, HALF, 256), (2, 4, HALF, 256)]
-    operands = [*tables, received, weighted, *answers, weights, updates]
-    specs = [SCALARS] * 4 + [WHOLE] * (len(operands) - 4)
-    return call(body, outs, operands, specs, [pltpu.VMEM((HALF, span), jnp.float32)])
+    operands = [*map(far, tables), received, *map(far, [weighted, weights, updates, *answers])]
+    specs = [SCALARS] * 4 + [WHOLE] + [FAR] * (len(operands) - 5)
+    scratch = [
+        pltpu.SemaphoreType.DMA((64,)),
+        pltpu.VMEM((HALF, span), jnp.float32),
+        pltpu.VMEM((HALF, 256), jnp.float32),
+        pltpu.VMEM((2, 256, span), jnp.bfloat16),
+        pltpu.VMEM((2, 256, update_len), jnp.bfloat16),
+        pltpu.VMEM((2, HALF, blocks * BLOCK), jnp.float32),
+    ]
+    if level == 2:
+        scratch += [pltpu.VMEM((4, 2, HALF, 256), jnp.float32)] * 2 + [pltpu.VMEM((2, 4, HALF, 256), jnp.float32)]
+    return call(body, outs, operands, specs, scratch, spaces="H" * n_outs)
 
 
 def level_zero_backward(received, weighted, weights, updates, nearest, kept, other):
@@ -359,8 +464,9 @@
     return call(
         body,
         [(4, SIDES, 512)],
-        [received, weighted, nearest, kept, other, weights, updates],
+        [received, *map(far, [weighted, nearest, kept]), other, close(weights), close(updates)],
         [WHOLE] * 7,
+        spaces="h",
     )[0]
 
 
@@ -406,34 +512,32 @@
     plane = ("x", "y1", "y0")
     pair = ("x", "y0")
 
-    copies = jnp.broadcast_to(sides[None, :, :PIVOTS], (4, SIDES, PIVOTS))
-    first = exchange(copies, ("x",))
+    packed = packed_sides(sides, with_partner(sides))
+    first = exchange(packed, ("x",))
     factors = pivot_factors(pivot_pairs[0], pivot_diagonal[0], pivot_coupling[0])
-    (weights0,) = prepared([inverse], [(0, 512)], copies)
-    (updates0,) = prepared([update], [(0, 256)], copies)
-    packed = packed_sides(sides, with_partner(sides))
+    partner_factors = with_partner(factors)
     inverse_after, update_after, _ = lax.optimization_barrier((inverse, update, packed))
     partner_inverse = with_partner(inverse_after)
     partner_update = with_partner(update_after)
-    two = jnp.stack([packed, lax.ppermute(packed, "x", [(0, 1), (1, 0), (2, 3), (3, 2)])])
-
-    sent, weighted0 = level_zero_forward(first, sides, weights0, updates0, factors)
+    (weights0,) = prepared([inverse], [(0, 512)], far(packed), pltpu.VMEM)
+    (updates0,) = prepared([update], [(0, 256)], far(packed), pltpu.VMEM)
+    tables = sibling_tables(update_targets)
+
+    sent, weighted0, sides1, near = level_zero_forward(first, weights0, updates0, factors)
+    beyond = across(near, "y0")
     received = exchange(sent, ("c", "x"))
-    partner_factors = with_partner(factors)
-    tables = sibling_tables(update_targets)
-    near = jnp.concatenate([two, lax.ppermute(two, "x", [(0, 2), (2, 0), (1, 3), (3, 1)])])
     weights1, weights2, weights3 = prepared(
-        [inverse, partner_inverse], [(512, 1024), (1536, 2048), (3584, 4096)], sent
+        [inverse, partner_inverse], [(512, 1024), (1536, 2048), (3584, 4096)], far(sent)
     )
-    updates1, updates2 = prepared([update, partner_update], [(256, 512), (768, 1024)], sent)
-    sent, weighted1 = forward(1, received, [], tables, weights1, updates1, factors, partner_factors)
-    far = across(near, "y0")
-    near3 = jnp.stack([near[:, :, PIVOTS:], far[:, :, PIVOTS:]])
+    updates1, updates2 = prepared([update, partner_update], [(256, 512), (768, 1024)], far(sent))
+    sent, weighted1, near3 = forward(
+        1, received, [sides1, near, beyond], tables, weights1, updates1, factors, partner_factors
+    )
+    beyond3 = across(near3, "y1")
     received = exchange(sent, pair)
-    sent, weighted2 = forward(2, received, [near, far], tables, weights2, updates2, factors, partner_factors)
-    far3 = across(near3, "y1")
+    sent, weighted2 = forward(2, received, [near, beyond], tables, weights2, updates2, factors, partner_factors)
     received = exchange(summed_copies(exchange(sent, pair), 16), plane)
-    sent, kept3, other3 = forward(3, received, [near3, far3], tables, weights3, None, factors, partner_factors)
+    sent, kept3, other3 = forward(3, received, [near3, beyond3], tables, weights3, None, factors, partner_factors)
     other3 = across(other3, "y1")
     received = exchange(summed_copies(exchange(sent, plane), 8), pair)
     sent, kept, other = backward(2, received, weighted2, tables, weights2, updates2, [kept3, other3])

time: 214 us -> 198 us (0.925)
  local copies, waits for them, and re-layouts: 39.2 us -> 2.76 us
  Pallas kernels: 22.2 us -> 58 us
  waiting for transfers between devices: 65.9 us -> 49.6 us
  blocking collectives: 13.6 us -> 29.8 us
  starting transfers between devices: 66.1 us -> 56 us
  other arithmetic: 4.22 us -> 0.04 us
    unnamed x102 -> x18, local copies, waits for them, and re-layouts: 34 us -> 1.26 us
    pallas_call x11, Pallas kernels: 19.1 us -> 47.2 us  [call(): pl.pallas_call(body, in_specs=specs, out_specs=[FAR if k == 'H' else WHOL...]
    all_to_all x1 -> x2, blocking collectives: 13.6 us -> 29.8 us  [exchange(): return lax.all_to_all(value, axes, 0, 0, tiled=True)]
    ppermute x4, waiting for transfers between devices: 17.9 us -> 3.88 us  [across(): return lax.ppermute(value, axis, [(0, 1), (1, 0)])]
    ppermute x2 -> x0, waiting for transfers between devices: 9.33 us -> none  [the longest x1 9.33 us: per_device(): lax.ppermute(packed, 'x', [(0, 1), (1, 0), (2, 3), (3, 2)])]
    pallas_call x4, Pallas kernels: 3.04 us -> 10.8 us  [prepared(): pl.pallas_call(body, in_specs=[FAR] * len(pair) + [FAR], out_specs=[WHOLE...]
    all_to_all x9 -> x8, waiting for transfers between devices: 34.9 us -> 40.3 us  [exchange(): return lax.all_to_all(value, axes, 0, 0, tiled=True)]
    all_to_all x9 -> x8, starting transfers between devices: 44.9 us -> 39.5 us  [exchange(): return lax.all_to_all(value, axes, 0, 0, tiled=True)]
  transfers between devices with their start and end apart: 23 -> 20, of which waited for: 14 -> 12; matrix products, arithmetic and copies ran while one was open for 4% -> 1% of each run, Pallas kernels for 4% -> 9%
where the time goes in v5:
time: 198 us; the launch traced here: 196 us
  Pallas kernels  58 us (29%)
  starting transfers between devices  56 us (28%)
  waiting for transfers between devices  49.6 us (25%)
  blocking collectives  29.8 us (15%)
  local copies, waits for them, and re-layouts  2.76 us (1%)
    pallas_call x11, Pallas kernels, call(): pl.pallas_call(body, in_specs=specs, out_specs=[FAR if k == 'H' else WHOL...  47.2 us
    all_to_all x8, waiting for transfers between devices, exchange(): return lax.all_to_all(value, axes, 0, 0, tiled=True)  40.3 us
    all_to_all x8, starting transfers between devices, exchange(): return lax.all_to_all(value, axes, 0, 0, tiled=True)  39.5 us
    all_to_all x2, blocking collectives, exchange(): return lax.all_to_all(value, axes, 0, 0, tiled=True)  29.8 us
    pallas_call x4, Pallas kernels, prepared(): pl.pallas_call(body, in_specs=[FAR] * len(pair) + [FAR], out_specs=[WHOLE...  10.8 us
    ppermute x4, starting transfers between devices, across(): return lax.ppermute(value, axis, [(0, 1), (1, 0)])  8.83 us
    ppermute x7, starting transfers between devices, with_partner(): return lax.ppermute(value, 'c', [(0, 1), (1, 0)])  4.99 us
  transfers between devices with their start and end apart: 20, of which 12 were waited for; matrix products, arithmetic and copies ran while one was open for 1% of the time, Pallas kernels for 9%

profile of v5, /device:TPU:1, one launch (start us, length us, event | category | flops | bytes accessed | tf_op | source)
XLA Modules:
  0.0 196.4 jit_solution(10290625617893744684)
XLA Ops:
  0.0 1.4 collective-permute-start.3
  1.4 1.3 collective-permute-done.3.beside_ref
  2.7 1.9 shard_map.73.refs_1_
  4.9 4.1 %all-to-all-start = ((f32[4,96,512]{2,1,0:T(8,128)}), f32[4,96,512]{2,1,0:T(8,128)S(1)}, u32[]{:S(2)}, u32[]{:S(2)}) async-start(f32[4,96,512]{2,1,0:T(8,128)} %shard_map.73.refs_1_), calls=%async_computation | async-start | bytes 1572864 | tf_op jit(solution)/shard_map/all_to_all | solution.py:41
  9.5 1.1 shard_map.76.factors_ref.refs_5_
  10.5 1.0 shard_map.74.weights_ref
  11.6 0.9 shard_map.75.updates_ref
  12.5 8.5 %all-to-all-done.first_ref = f32[4,96,512]{2,1,0:T(8,128)S(1)} async-done(((f32[4,96,512]{2,1,0:T(8,128)}), f32[4,96,512]{2,1,0:T(8,128)S(1)}, u32[]{:S(2)}, u32[]{:S(2)}) %all-to-all-start) | async-done | bytes 786464 | tf_op jit(solution)/shard_map/all_to_all | solution.py:41
  21.0 1.3 shard_map.77
  22.4 1.4 collective-permute-start.5
  23.7 4.9 %all-to-all-start.1 = ((f32[8,48,256]{2,1,0:T(8,128)}), f32[8,48,256]{2,1,0:T(8,128)S(1)}, u32[]{:S(2)}, u32[]{:S(2)}) async-start(f32[8,48,256]{2,1,0:T(8,128)} %get-tuple-element.29.refs_2_), calls=%async_computation.1 | async-start | bytes 786432 | tf_op jit(solution)/shard_map/all_to_all | solution.py:41
  28.8 2.6 %collective-permute-start = (s32[1,14]{1,0:T(1,128)S(1)}, s32[1,14]{1,0:T(1,128)S(1)}, u32[]{:S(2)}, u32[]{:S(2)}) collective-permute-start(s32[1,14]{1,0:T(1,128)S(1)} %copy-done.5), channel_id=1, source_target_pairs={{0,8},{4,20},{8,0},{12,28},{16,24},{20,4},{24,16},{28,12},{1,9},{5... | collective-permute-start | bytes 176 | tf_op jit(solution)/shard_map/ppermute | solution.py:504
  31.5 3.1 %collective-permute-done.refs_1_ = s32[1,14]{1,0:T(1,128)S(1)} collective-permute-done((s32[1,14]{1,0:T(1,128)S(1)}, s32[1,14]{1,0:T(1,128)S(1)}, u32[]{:S(2)}, u32[]{:S(2)}) %collective-permute-start) | collective-permute-done | bytes 88 | tf_op jit(solution)/shard_map/ppermute | solution.py:504
  34.5 0.5 collective-permute-start.2
  35.0 0.5 copy-done.1
  35.5 2.6 %shard_map.79 = (bf16[2,256,512]{2,1,0:T(8,128)(2,1)}, bf16[2,256,1024]{2,1,0:T(8,128)(2,1)}) custom-call(f32[128,1792]{1,0:T(8,128)} %bitcast.12, f32[128,1792]{1,0:T(8,128)} %copy-done.1, f32[8,48,256]{2,1,0:T(8,128)} %get-tuple-element.29.refs_2_), custom_call_target="tpu_custom_call" | custom-call | tf_op jit(solution)/shard_map/pallas_call | solution.py:110
  38.2 6.2 %shard_map.78 = (bf16[2,256,1024]{2,1,0:T(8,128)(2,1)}, bf16[2,256,2048]{2,1,0:T(8,128)(2,1)}, bf16[2,256,4096]{2,1,0:T(8,128)(2,1)}) custom-call(f32[128,7680]{1,0:T(8,128)} %bitcast.9, f32[128,7680]{1,0:T(8,128)} %collective-permute-done.6.refs_1_, f32[8,48,256]{2,1,0:T(8,128)} %get-tuple-element.29.refs_2_), custom_call_target="tpu_custom_call" | custom-call | tf_op jit(solution)/shard_map/pallas_call | solution.py:110
  44.5 0.5 copy-done.7
  45.3 14.4 %shard_map.80 = (f32[8,48,512]{2,1,0:T(8,128)}, f32[48,256]{1,0:T(8,128)}, f32[2,4,96,128]{3,2,1,0:T(8,128)}) custom-call(s32[1,14]{1,0:T(1,128)} %refs_0_.9, s32[1,14]{1,0:T(1,128)} %copy-done.6, s32[1,14]{1,0:T(1,128)} %copy-done.7, s32[1,14]{1,0:T(1,128)} %copy-done.8, f32[8,48,256]{2,1,0:T(8,128)S(1)} %all-to-all-done.1.refs_4_, ...), custom_call_target="tpu_custom_call" | custom-call | tf_op jit(solution)/shard_map/pallas_call | solution.py:70
  59.7 15.2 %all_to_all.50.refs_4_ = f32[8,48,512]{2,1,0:T(8,128)S(1)} all-to-all(f32[8,48,512]{2,1,0:T(8,128)} %get-tuple-element.36), channel_id=1, replica_groups=mesh['z'=4,'y1'=2,'y0'=2,'c'=2,'x'=4] {'x','y0'}, dimensions={0} | all-to-all | bytes 1572864 | tf_op jit(solution)/shard_map/all_to_all | solution.py:41
  74.9 6.0 %shard_map.81 = (f32[8,48,128]{2,1,0:T(8,128)}, f32[48,256]{1,0:T(8,128)}) custom-call(s32[1,14]{1,0:T(1,128)} %refs_0_.9, s32[1,14]{1,0:T(1,128)} %copy-done.6, s32[1,14]{1,0:T(1,128)} %copy-done.7, s32[1,14]{1,0:T(1,128)} %copy-done.8, f32[8,48,512]{2,1,0:T(8,128)S(1)} %all_to_all.50.refs_4_, f32[2,512]{1,0:T(2,128)S(1)} %shard_map.76.factors_ref.refs_5_, ...), custom_call_target="tpu_custom_call" | custom-call | tf_op jit(solution)/shard_map/pallas_call | solution.py:70
  80.9 3.5 %all-to-all-start.3 = ((f32[8,48,128]{2,1,0:T(8,128)}), f32[8,48,128]{2,1,0:T(8,128)S(1)}, u32[]{:S(2)}, u32[]{:S(2)}) async-start(f32[8,48,128]{2,1,0:T(8,128)} %get-tuple-element.39), calls=%async_computation.3 | async-start | bytes 393216 | tf_op jit(solution)/shard_map/all_to_all | solution.py:41
  84.5 3.2 %collective-permute-start.8 = (f32[2,4,96,128]{3,2,1,0:T(8,128)S(1)}, f32[2,4,96,128]{3,2,1,0:T(8,128)S(1)}, u32[]{:S(2)}, u32[]{:S(2)}) collective-permute-start(f32[2,4,96,128]{3,2,1,0:T(8,128)S(1)} %copy-done.2), channel_id=1, source_target_pairs={{0,16},{16,0},{1,17},{17,1},{2,18},{18,2},{3,19},{19,3},{4,20},{20... | collective-permute-start | bytes 1179656 | tf_op jit(solution)/shard_map/ppermute | solution.py:49
  87.7 2.4 %all-to-all-done.3 = f32[8,48,128]{2,1,0:T(8,128)S(1)} async-done(((f32[8,48,128]{2,1,0:T(8,128)}), f32[8,48,128]{2,1,0:T(8,128)S(1)}, u32[]{:S(2)}, u32[]{:S(2)}) %all-to-all-start.3) | async-done | bytes 196640 | tf_op jit(solution)/shard_map/all_to_all | solution.py:41
  90.1 0.8 broadcast_in_dim.6
  90.9 5.4 %all-to-all-start.4 = ((f32[16,48,128]{2,1,0:T(8,128)}), f32[16,48,128]{2,1,0:T(8,128)S(1)}, u32[]{:S(2)}, u32[]{:S(2)}) async-start(f32[16,48,128]{2,1,0:T(8,128)} %broadcast_in_dim.6), calls=%async_computation.4 | async-start | bytes 786432 | tf_op jit(solution)/shard_map/all_to_all | solution.py:41
  96.4 2.0 %collective-permute-done.8.refs_8_ = f32[2,4,96,128]{3,2,1,0:T(8,128)S(1)} collective-permute-done((f32[2,4,96,128]{3,2,1,0:T(8,128)S(1)}, f32[2,4,96,128]{3,2,1,0:T(8,128)S(1)}, u32[]{:S(2)}, u32[]{:S(2)}) %collective-permute-start.8) | collective-permute-done | bytes 393248 | tf_op jit(solution)/shard_map/ppermute | solution.py:49
  98.4 6.0 %all-to-all-done.4.refs_4_ = f32[16,48,128]{2,1,0:T(8,128)S(1)} async-done(((f32[16,48,128]{2,1,0:T(8,128)}), f32[16,48,128]{2,1,0:T(8,128)S(1)}, u32[]{:S(2)}, u32[]{:S(2)}) %all-to-all-start.4) | async-done | bytes 393248 | tf_op jit(solution)/shard_map/all_to_all | solution.py:41
  104.4 9.2 %shard_map.82 = (f32[16,48,128]{2,1,0:T(8,128)}, f32[4,2,48,256]{3,2,1,0:T(8,128)}, f32[4,2,48,256]{3,2,1,0:T(8,128)}) custom-call(s32[1,14]{1,0:T(1,128)} %refs_0_.9, s32[1,14]{1,0:T(1,128)} %copy-done.6, s32[1,14]{1,0:T(1,128)} %copy-done.7, s32[1,14]{1,0:T(1,128)} %copy-done.8, f32[16,48,128]{2,1,0:T(8,128)S(1)} %all-to-all-done.4.refs_4_, ...), custom_call_target="tpu_custom_call" | custom-call | tf_op jit(solution)/shard_map/pallas_call | solution.py:70
  113.6 3.7 %all-to-all-start.5 = ((f32[16,48,128]{2,1,0:T(8,128)}), f32[16,48,128]{2,1,0:T(8,128)S(1)}, u32[]{:S(2)}, u32[]{:S(2)}) async-start(f32[16,48,128]{2,1,0:T(8,128)} %get-tuple-element.42), calls=%async_computation.5 | async-start | bytes 786432 | tf_op jit(solution)/shard_map/all_to_all | solution.py:41
  117.3 2.9 %collective-permute-start.9 = (f32[4,2,48,256]{3,2,1,0:T(8,128)}, f32[4,2,48,256]{3,2,1,0:T(8,128)S(1)}, u32[]{:S(2)}, u32[]{:S(2)}) collective-permute-start(f32[4,2,48,256]{3,2,1,0:T(8,128)} %get-tuple-element.45), channel_id=1, source_target_pairs={{0,16},{16,0},{1,17},{17,1},{2,18},{18,2},{3,19},{19,3},{4,20},{20... | collective-permute-start | bytes 1179656 | tf_op jit(solution)/shard_map/ppermute | solution.py:49
  120.2 5.2 %all-to-all-done.5 = f32[16,48,128]{2,1,0:T(8,128)S(1)} async-done(((f32[16,48,128]{2,1,0:T(8,128)}), f32[16,48,128]{2,1,0:T(8,128)S(1)}, u32[]{:S(2)}, u32[]{:S(2)}) %all-to-all-start.5) | async-done | bytes 393248 | tf_op jit(solution)/shard_map/all_to_all | solution.py:41
  125.4 0.7 broadcast_in_dim.7
  126.1 3.6 %all-to-all-start.6 = ((f32[8,48,128]{2,1,0:T(8,128)}), f32[8,48,128]{2,1,0:T(8,128)S(1)}, u32[]{:S(2)}, u32[]{:S(2)}) async-start(f32[8,48,128]{2,1,0:T(8,128)} %broadcast_in_dim.7), calls=%async_computation.6 | async-start | bytes 393216 | tf_op jit(solution)/shard_map/all_to_all | solution.py:41
  129.7 1.9 collective-permute-done.9.refs_9_
  131.6 3.5 %all-to-all-done.6.refs_4_ = f32[8,48,128]{2,1,0:T(8,128)S(1)} async-done(((f32[8,48,128]{2,1,0:T(8,128)}), f32[8,48,128]{2,1,0:T(8,128)S(1)}, u32[]{:S(2)}, u32[]{:S(2)}) %all-to-all-start.6) | async-done | bytes 196640 | tf_op jit(solution)/shard_map/all_to_all | solution.py:41
  135.1 5.8 %shard_map.83 = (f32[8,48,512]{2,1,0:T(8,128)}, f32[2,4,48,256]{3,2,1,0:T(8,128)}, f32[2,4,48,256]{3,2,1,0:T(8,128)}) custom-call(s32[1,14]{1,0:T(1,128)} %refs_0_.9, s32[1,14]{1,0:T(1,128)} %copy-done.6, s32[1,14]{1,0:T(1,128)} %copy-done.7, s32[1,14]{1,0:T(1,128)} %copy-done.8, f32[8,48,128]{2,1,0:T(8,128)S(1)} %all-to-all-done.6.refs_4_, ...), custom_call_target="tpu_custom_call" | custom-call | tf_op jit(solution)/shard_map/pallas_call | solution.py:70
  140.9 3.6 %all-to-all-start.7 = ((f32[8,48,512]{2,1,0:T(8,128)}), f32[8,48,512]{2,1,0:T(8,128)S(1)}, u32[]{:S(2)}, u32[]{:S(2)}) async-start(f32[8,48,512]{2,1,0:T(8,128)} %get-tuple-element.46), calls=%async_computation.7 | async-start | bytes 1572864 | tf_op jit(solution)/shard_map/all_to_all | solution.py:41
  144.4 1.4 collective-permute-start.10
  145.8 7.0 %all-to-all-done.7.refs_4_ = f32[8,48,512]{2,1,0:T(8,128)S(1)} async-done(((f32[8,48,512]{2,1,0:T(8,128)}), f32[8,48,512]{2,1,0:T(8,128)S(1)}, u32[]{:S(2)}, u32[]{:S(2)}) %all-to-all-start.7) | async-done | bytes 786464 | tf_op jit(solution)/shard_map/all_to_all | solution.py:41
  152.8 4.2 %shard_map.84 = (f32[8,48,256]{2,1,0:T(8,128)}, f32[4,48,256]{2,1,0:T(8,128)}) custom-call(s32[1,14]{1,0:T(1,128)} %refs_0_.9, s32[1,14]{1,0:T(1,128)} %copy-done.6, s32[1,14]{1,0:T(1,128)} %copy-done.7, s32[1,14]{1,0:T(1,128)} %copy-done.8, f32[8,48,512]{2,1,0:T(8,128)S(1)} %all-to-all-done.7.refs_4_, f32[48,256]{1,0:T(8,128)} %get-tuple-element.47.refs_5_, ...), custom_call_target="tpu_custom_call" | custom-call | tf_op jit(solution)/shard_map/pallas_call | solution.py:70
  157.0 10.7 %all-to-all-start.8 = ((f32[8,48,256]{2,1,0:T(8,128)}), f32[8,48,256]{2,1,0:T(8,128)S(1)}, u32[]{:S(2)}, u32[]{:S(2)}) async-start(f32[8,48,256]{2,1,0:T(8,128)} %get-tuple-element.48), calls=%async_computation.8 | async-start | bytes 786432 | tf_op jit(solution)/shard_map/all_to_all | solution.py:41
  167.6 7.7 %all-to-all-done.8.received_ref = f32[8,48,256]{2,1,0:T(8,128)S(1)} async-done(((f32[8,48,256]{2,1,0:T(8,128)}), f32[8,48,256]{2,1,0:T(8,128)S(1)}, u32[]{:S(2)}, u32[]{:S(2)}) %all-to-all-start.8) | async-done | bytes 393248 | tf_op jit(solution)/shard_map/all_to_all | solution.py:41
  175.3 2.5 %shard_map.85 = f32[4,96,512]{2,1,0:T(8,128)} custom-call(f32[8,48,256]{2,1,0:T(8,128)S(1)} %all-to-all-done.8.received_ref, f32[96,128]{1,0:T(8,128)} %get-tuple-element.49.weighted_ref, f32[4,48,256]{2,1,0:T(8,128)} %get-tuple-element.50.nearest_ref, f32[2,4,48,256]{3,2,1,0:T(8,128)} %get-tuple-element.51.kept_ref, ...), custom_call_target="tpu_custom_call" | custom-call | tf_op jit(solution)/shard_map/pallas_call | solution.py:70
  177.8 14.6 %all_to_all.51.received_ref = f32[4,96,512]{2,1,0:T(8,128)S(1)} all-to-all(f32[4,96,512]{2,1,0:T(8,128)} %shard_map.85), channel_id=1, replica_groups=mesh['z'=4,'y1'=2,'y0'=2,'c'=2,'x'=4] {'x'}, dimensions={0} | all-to-all | bytes 1572864 | tf_op jit(solution)/shard_map/all_to_all | solution.py:41
  192.5 2.2 %collective-permute-start.11 = (f32[96,512]{1,0:T(8,128)S(1)}, f32[96,512]{1,0:T(8,128)S(1)}, u32[]{:S(2)}, u32[]{:S(2)}) collective-permute-start(f32[96,512]{1,0:T(8,128)S(1)} %shard_map.86.total_ref), channel_id=1, source_target_pairs={{0,4},{4,0},{1,5},{5,1},{2,6},{6,2},{3,7},{7,3},{8,12},{12,8},{9,1... | collective-permute-start | bytes 589832 | tf_op jit(solution)/shard_map/ppermute | solution.py:45
  194.6 1.1 collective-permute-done.11.beside_ref
  195.7 0.7 shard_map.87
  (31 shorter events, 1.3 us)
Async XLA Ops:
  0.0 2.7 %collective-permute-start.3 = (f32[96,512]{1,0:T(8,128)}, f32[96,512]{1,0:T(8,128)S(1)}, u32[]{:S(2)}, u32[]{:S(2)}) collective-permute-start(f32[96,512]{1,0:T(8,128)} %bitcast.13), channel_id=1, source_target_pairs={{0,4},{4,0},{1,5},{5,1},{2,6},{6,2},{3,7},{7,3},{8,12},{12,8},{9,1... | collective-permute-start | bytes 589832 | tf_op jit(solution)/shard_map/ppermute | solution.py:45
  4.6 33.6 %collective-permute-start.6 = (f32[128,7680]{1,0:T(8,128)}, f32[128,7680]{1,0:T(8,128)}, u32[]{:S(2)}, u32[]{:S(2)}) collective-permute-start(f32[128,7680]{1,0:T(8,128)} %bitcast.7), channel_id=1, source_target_pairs={{0,4},{4,0},{1,5},{5,1},{2,6},{6,2},{3,7},{7,3},{8,12},{12,8},{9,1... | collective-permute-start | bytes 11796488 | tf_op jit(solution)/shard_map/ppermute | solution.py:45
  4.9 16.1 %all-to-all-start = ((f32[4,96,512]{2,1,0:T(8,128)}), f32[4,96,512]{2,1,0:T(8,128)S(1)}, u32[]{:S(2)}, u32[]{:S(2)}) async-start(f32[4,96,512]{2,1,0:T(8,128)} %shard_map.73.refs_1_), calls=%async_computation | async-start | bytes 1572864 | tf_op jit(solution)/shard_map/all_to_all | solution.py:41
  9.1 25.5 %collective-permute-start.7 = (f32[128,1792]{1,0:T(8,128)}, f32[128,1792]{1,0:T(8,128)S(1)}, u32[]{:S(2)}, u32[]{:S(2)}) collective-permute-start(f32[128,1792]{1,0:T(8,128)} %bitcast.10), channel_id=1, source_target_pairs={{0,4},{4,0},{1,5},{5,1},{2,6},{6,2},{3,7},{7,3},{8,12},{12,8},{9,1... | collective-permute-start | bytes 2752520 | tf_op jit(solution)/shard_map/ppermute | solution.py:45
  10.5 18.3 %copy-start.5 = (s32[1,14]{1,0:T(1,128)S(1)}, s32[1,14]{1,0:T(1,128)}, u32[]{:S(2)}) copy-start(s32[1,14]{1,0:T(1,128)} %refs_0_.9) | copy-start | bytes 172
  22.4 22.2 %collective-permute-start.5 = (f32[4,96,256]{2,1,0:T(8,128)}, f32[4,96,256]{2,1,0:T(8,128)S(1)}, u32[]{:S(2)}, u32[]{:S(2)}) collective-permute-start(f32[4,96,256]{2,1,0:T(8,128)} %get-tuple-element.31.refs_8_.refs_7_), channel_id=1, source_target_pairs={{0,8},{8,0},{1,9},{9,1},{2,10},{10,2},{3,11},{11,3},{4,12},{12,4},... | collective-permute-start | bytes 1179656 | tf_op jit(solution)/shard_map/ppermute | solution.py:49
  23.7 20.8 %all-to-all-start.1 = ((f32[8,48,256]{2,1,0:T(8,128)}), f32[8,48,256]{2,1,0:T(8,128)S(1)}, u32[]{:S(2)}, u32[]{:S(2)}) async-start(f32[8,48,256]{2,1,0:T(8,128)} %get-tuple-element.29.refs_2_), calls=%async_computation.1 | async-start | bytes 786432 | tf_op jit(solution)/shard_map/all_to_all | solution.py:41
  28.7 15.8 %collective-permute-start.4 = (f32[2,512]{1,0:T(2,128)S(1)}, f32[2,512]{1,0:T(2,128)S(1)}, u32[]{:S(2)}, u32[]{:S(2)}) collective-permute-start(f32[2,512]{1,0:T(2,128)S(1)} %shard_map.76.factors_ref.refs_5_), channel_id=1, source_target_pairs={{0,4},{4,0},{1,5},{5,1},{2,6},{6,2},{3,7},{7,3},{8,12},{12,8},{9,1... | collective-permute-start | bytes 12296 | tf_op jit(solution)/shard_map/ppermute | solution.py:45
  28.8 5.7 %collective-permute-start = (s32[1,14]{1,0:T(1,128)S(1)}, s32[1,14]{1,0:T(1,128)S(1)}, u32[]{:S(2)}, u32[]{:S(2)}) collective-permute-start(s32[1,14]{1,0:T(1,128)S(1)} %copy-done.5), channel_id=1, source_target_pairs={{0,8},{4,20},{8,0},{12,28},{16,24},{20,4},{24,16},{28,12},{1,9},{5... | collective-permute-start | bytes 176 | tf_op jit(solution)/shard_map/ppermute | solution.py:504
  34.5 10.0 %copy-start.6 = (s32[1,14]{1,0:T(1,128)}, s32[1,14]{1,0:T(1,128)S(1)}, u32[]{:S(2)}) copy-start(s32[1,14]{1,0:T(1,128)S(1)} %collective-permute-done.refs_1_) | copy-start | bytes 172
  34.5 9.9 %collective-permute-start.1 = (s32[1,14]{1,0:T(1,128)S(1)}, s32[1,14]{1,0:T(1,128)S(1)}, u32[]{:S(2)}, u32[]{:S(2)}) collective-permute-start(s32[1,14]{1,0:T(1,128)S(1)} %copy-done.5), channel_id=1, source_target_pairs={{0,4},{4,0},{1,5},{5,1},{2,6},{6,2},{3,7},{7,3},{8,12},{12,8},{9,1... | collective-permute-start | bytes 176 | tf_op jit(solution)/shard_map/ppermute | solution.py:45
  34.5 1.0 copy-start.1
  34.5 9.9 %collective-permute-start.2 = (s32[1,14]{1,0:T(1,128)S(1)}, s32[1,14]{1,0:T(1,128)S(1)}, u32[]{:S(2)}, u32[]{:S(2)}) collective-permute-start(s32[1,14]{1,0:T(1,128)S(1)} %collective-permute-done.refs_1_), channel_id=1, source_target_pairs={{0,4},{4,0},{1,5},{5,1},{2,6},{6,2},{3,7},{7,3},{8,12},{12,8},{9,1... | collective-permute-start | bytes 176 | tf_op jit(solution)/shard_map/ppermute | solution.py:45
  44.5 0.6 copy-start.7
  44.5 0.6 copy-start.8
  44.5 0.7 copy-start
  59.7 24.7 %copy-start.2 = (f32[2,4,96,128]{3,2,1,0:T(8,128)S(1)}, f32[2,4,96,128]{3,2,1,0:T(8,128)}, u32[]{:S(2)}) copy-start(f32[2,4,96,128]{3,2,1,0:T(8,128)} %get-tuple-element.40.refs_7_) | copy-start | bytes 1179652
  80.9 9.1 %all-to-all-start.3 = ((f32[8,48,128]{2,1,0:T(8,128)}), f32[8,48,128]{2,1,0:T(8,128)S(1)}, u32[]{:S(2)}, u32[]{:S(2)}) async-start(f32[8,48,128]{2,1,0:T(8,128)} %get-tuple-element.39), calls=%async_computation.3 | async-start | bytes 393216 | tf_op jit(solution)/shard_map/all_to_all | solution.py:41
  84.5 13.9 %collective-permute-start.8 = (f32[2,4,96,128]{3,2,1,0:T(8,128)S(1)}, f32[2,4,96,128]{3,2,1,0:T(8,128)S(1)}, u32[]{:S(2)}, u32[]{:S(2)}) collective-permute-start(f32[2,4,96,128]{3,2,1,0:T(8,128)S(1)} %copy-done.2), channel_id=1, source_target_pairs={{0,16},{16,0},{1,17},{17,1},{2,18},{18,2},{3,19},{19,3},{4,20},{20... | collective-permute-start | bytes 1179656 | tf_op jit(solution)/shard_map/ppermute | solution.py:49
  90.9 13.5 %all-to-all-start.4 = ((f32[16,48,128]{2,1,0:T(8,128)}), f32[16,48,128]{2,1,0:T(8,128)S(1)}, u32[]{:S(2)}, u32[]{:S(2)}) async-start(f32[16,48,128]{2,1,0:T(8,128)} %broadcast_in_dim.6), calls=%async_computation.4 | async-start | bytes 786432 | tf_op jit(solution)/shard_map/all_to_all | solution.py:41
  98.4 6.0 %copy-start.3 = (f32[2,4,96,128]{3,2,1,0:T(8,128)}, f32[2,4,96,128]{3,2,1,0:T(8,128)S(1)}, u32[]{:S(2)}) copy-start(f32[2,4,96,128]{3,2,1,0:T(8,128)S(1)} %collective-permute-done.8.refs_8_) | copy-start | bytes 1179652
  113.6 11.8 %all-to-all-start.5 = ((f32[16,48,128]{2,1,0:T(8,128)}), f32[16,48,128]{2,1,0:T(8,128)S(1)}, u32[]{:S(2)}, u32[]{:S(2)}) async-start(f32[16,48,128]{2,1,0:T(8,128)} %get-tuple-element.42), calls=%async_computation.5 | async-start | bytes 786432 | tf_op jit(solution)/shard_map/all_to_all | solution.py:41
  117.3 14.3 %collective-permute-start.9 = (f32[4,2,48,256]{3,2,1,0:T(8,128)}, f32[4,2,48,256]{3,2,1,0:T(8,128)S(1)}, u32[]{:S(2)}, u32[]{:S(2)}) collective-permute-start(f32[4,2,48,256]{3,2,1,0:T(8,128)} %get-tuple-element.45), channel_id=1, source_target_pairs={{0,16},{16,0},{1,17},{17,1},{2,18},{18,2},{3,19},{19,3},{4,20},{20... | collective-permute-start | bytes 1179656 | tf_op jit(solution)/shard_map/ppermute | solution.py:49
  126.1 8.9 %all-to-all-start.6 = ((f32[8,48,128]{2,1,0:T(8,128)}), f32[8,48,128]{2,1,0:T(8,128)S(1)}, u32[]{:S(2)}, u32[]{:S(2)}) async-start(f32[8,48,128]{2,1,0:T(8,128)} %broadcast_in_dim.7), calls=%async_computation.6 | async-start | bytes 393216 | tf_op jit(solution)/shard_map/all_to_all | solution.py:41
  131.6 3.5 %copy-start.4 = (f32[4,2,48,256]{3,2,1,0:T(8,128)}, f32[4,2,48,256]{3,2,1,0:T(8,128)S(1)}, u32[]{:S(2)}) copy-start(f32[4,2,48,256]{3,2,1,0:T(8,128)S(1)} %collective-permute-done.9.refs_9_) | copy-start | bytes 1179652
  140.9 11.9 %all-to-all-start.7 = ((f32[8,48,512]{2,1,0:T(8,128)}), f32[8,48,512]{2,1,0:T(8,128)S(1)}, u32[]{:S(2)}, u32[]{:S(2)}) async-start(f32[8,48,512]{2,1,0:T(8,128)} %get-tuple-element.46), calls=%async_computation.7 | async-start | bytes 1572864 | tf_op jit(solution)/shard_map/all_to_all | solution.py:41
  144.4 23.2 %collective-permute-start.10 = (f32[2,4,48,256]{3,2,1,0:T(8,128)}, f32[2,4,48,256]{3,2,1,0:T(8,128)S(1)}, u32[]{:S(2)}, u32[]{:S(2)}) collective-permute-start(f32[2,4,48,256]{3,2,1,0:T(8,128)} %get-tuple-element.52), channel_id=1, source_target_pairs={{0,8},{8,0},{1,9},{9,1},{2,10},{10,2},{3,11},{11,3},{4,12},{12,4},... | collective-permute-start | bytes 1179656 | tf_op jit(solution)/shard_map/ppermute | solution.py:49
  157.0 18.4 %all-to-all-start.8 = ((f32[8,48,256]{2,1,0:T(8,128)}), f32[8,48,256]{2,1,0:T(8,128)S(1)}, u32[]{:S(2)}, u32[]{:S(2)}) async-start(f32[8,48,256]{2,1,0:T(8,128)} %get-tuple-element.48), calls=%async_computation.8 | async-start | bytes 786432 | tf_op jit(solution)/shard_map/all_to_all | solution.py:41
  192.5 3.2 %collective-permute-start.11 = (f32[96,512]{1,0:T(8,128)S(1)}, f32[96,512]{1,0:T(8,128)S(1)}, u32[]{:S(2)}, u32[]{:S(2)}) collective-permute-start(f32[96,512]{1,0:T(8,128)S(1)} %shard_map.86.total_ref), channel_id=1, source_target_pairs={{0,4},{4,0},{1,5},{5,1},{2,6},{6,2},{3,7},{7,3},{8,12},{12,8},{9,1... | collective-permute-start | bytes 589832 | tf_op jit(solution)/shard_map/ppermute | solution.py:45

commit v6 on v5

--- a/solution.py
+++ b/solution.py
@@ -80,14 +80,14 @@
     )(*operands)
 
 
-def prepared(pair, spans, after, space=pltpu.HBM):
+def prepared(pair, spans, after):
     def body(*refs):
         sources = refs[: len(pair)]
         outs = refs[len(pair) + 1 :][: len(spans)]
         buffers = refs[len(pair) + 1 + len(spans) : -1]
         semaphores = refs[-1]
         moves = []
-        for i, (start, width) in enumerate(spans):
+        for i, (start, width, _) in enumerate(spans):
             for side, source in enumerate(sources):
                 move = pltpu.make_async_copy(
                     source.at[:, pl.ds(start, width)],
@@ -99,23 +99,27 @@
         for i, side, move in moves:
             move.wait()
             rows = slice(side * PIVOTS, (side + 1) * PIVOTS)
-            width = spans[i][1]
-            step = min(width, 512)
-            for at in range(0, width, step):
-                high, low = parts(buffers[i][rows, at : at + step])
-                outs[i][0, rows, at : at + step] = high
-                outs[i][1, rows, at : at + step] = low
+            _, width, step = spans[i]
+            for k, at in enumerate(range(0, width, step or width)):
+                high, low = parts(buffers[i][rows, at : at + (step or width)])
+                place = outs[i].at[k] if step else outs[i]
+                place[0, rows] = high
+                place[1, rows] = low
 
     count = len(pair) * PIVOTS
+    shapes = [
+        pltpu.HBM((width // step, 2, count, step), jnp.bfloat16) if step else pltpu.VMEM((2, count, width), jnp.bfloat16)
+        for _, width, step in spans
+    ]
     return pl.pallas_call(
         body,
-        in_specs=[FAR] * len(pair) + [FAR],
+        in_specs=[FAR] * (len(pair) + 1),
         out_specs=[WHOLE] * len(spans),
-        out_shape=[space((2, count, width), jnp.bfloat16) for _, width in spans],
-        scratch_shapes=[pltpu.VMEM((count, width), jnp.float32) for _, width in spans]
+        out_shape=shapes,
+        scratch_shapes=[pltpu.VMEM((count, width), jnp.float32) for _, width, _ in spans]
         + [pltpu.SemaphoreType.DMA((len(spans), len(pair)))],
-        compiler_params=pltpu.CompilerParams(vmem_limit_bytes=24 * 1024 * 1024),
-    )(*map(far, pair), after)
+        compiler_params=pltpu.CompilerParams(vmem_limit_bytes=28 * 1024 * 1024),
+    )(*map(far, pair), far(after))
 
 
 def pivot_apply(solved, own, swapped):
@@ -174,10 +178,8 @@
         self.started.append(move)
         return move
 
-    def columns(self, source, target, step):
-        width = source.shape[2]
-        spans = [pl.ds(at, step) for at in range(0, width, step)]
-        return [self.start(source.at[:, :, span], target.at[:, :, span]) for span in spans]
+    def chunks(self, source, target):
+        return [self.start(source.at[k], target.at[k]) for k in range(source.shape[0])]
 
 
 def finish(moves):
@@ -258,9 +260,9 @@
 
         tables_refs = take(4)
         received_ref, factors_ref, beside_ref = take(3)
+        updates_ref = take(n_updates)
         sides_refs = take(n_sides)
         (weights_far,) = take(1)
-        updates_far = take(n_updates)
         outs = take(n_outs)
         semaphores, b_ref, own_ref, weights_ref = take(4)
         moves = Moves(semaphores)
@@ -284,13 +286,15 @@
                 for flip in range(2):
                     for x in range(4):
                         bring(sides_refs[high].at[flip, x], x * 4 + (y1 ^ high) * 2 + (y0 ^ flip))
-        columns = moves.columns(weights_far, weights_ref, 512)
+        columns = moves.chunks(weights_far, weights_ref)
         if level < 3:
-            updates_ref, part_ref = refs
-            update_columns = moves.columns(updates_far[0], updates_ref, 256)
+            part_ref = refs[0]
         if level == 1:
-            for flip in range(2):
-                leaving.append(moves.start(sides_refs[1 + flip].at[:, :, pl.ds(PIVOTS, PIVOTS)], outs[2].at[flip]))
+            passing_ref = refs[1]
+            passing = [
+                moves.start(sides_refs[1 + flip].at[:, :, pl.ds(PIVOTS, PIVOTS)], passing_ref.at[flip])
+                for flip in range(2)
+            ]
         totals = [None, None]
         for child in range(2):
             if level == 1:
@@ -310,15 +314,17 @@
         for k in range(chunks):
             columns[k].wait()
             at = slice(k * 512, (k + 1) * 512)
-            solved += product(b_ref[:, at], weights_ref[0, :, at], weights_ref[1, :, at], 1)
+            solved += product(b_ref[:, at], weights_ref[k, 0], weights_ref[k, 1], 1)
         weighted = pivot_apply(solved, *both_factors(level, factors_ref, beside_ref))
         if level < 3:
             own_ref[...] = weighted
             leaving.append(moves.start(own_ref, outs[1]))
+            if level == 1:
+                finish(passing)
+                leaving.append(moves.start(passing_ref, outs[2]))
             for k in range(update_len // 256):
-                update_columns[k].wait()
                 at = slice(k * 256, (k + 1) * 256)
-                part_ref[:, at] = product(solved, updates_ref[0, :, at], updates_ref[1, :, at], 0)
+                part_ref[:, at] = product(solved, updates_ref[0][0, :, at], updates_ref[0][1, :, at], 0)
             for i in range(8):
                 source = part_ref if level == 1 else part_ref.at[:, pl.ds(i * BLOCK, BLOCK)]
                 leaving.append(moves.start(source, outs[0].at[i]))
@@ -326,7 +332,7 @@
             sent_ref, keep_ref, beyond_ref = outs
             for k in range(chunks):
                 at = slice(k * 512, (k + 1) * 512)
-                b_ref[:, at] = product(weighted, weights_ref[0, :, at], weights_ref[1, :, at], 0)
+                b_ref[:, at] = product(weighted, weights_ref[k, 0], weights_ref[k, 1], 0)
             for child in range(2):
                 for k in range(8):
                     where = block_at(child_block(3, tables_refs, child, k))
@@ -346,16 +352,20 @@
         3: [(16, HALF, BLOCK), (4, 2, HALF, 256), (4, 2, HALF, 256)],
     }[level]
     operands = [*map(far, tables), received, close(factors), close(partner_factors)]
-    operands += map(far, [*sides, weights] + ([updates] if level < 3 else []))
-    specs = [SCALARS] * 4 + [WHOLE] * 3 + [FAR] * (len(operands) - 7)
+    operands += [close(updates)] if level < 3 else []
+    n_close = len(operands) - 4
+    operands += map(far, [*sides, weights])
+    specs = [SCALARS] * 4 + [WHOLE] * n_close + [FAR] * (n_sides + 1)
     scratch = [
         pltpu.SemaphoreType.DMA((80,)),
         pltpu.VMEM((HALF, span), jnp.float32),
         pltpu.VMEM((HALF, 256), jnp.float32),
-        pltpu.VMEM((2, 256, span), jnp.bfloat16),
+        pltpu.VMEM((chunks, 2, 256, 512), jnp.bfloat16),
     ]
     if level < 3:
-        scratch += [pltpu.VMEM((2, 256, update_len), jnp.bfloat16), pltpu.VMEM((HALF, update_len), jnp.float32)]
+        scratch.append(pltpu.VMEM((HALF, update_len), jnp.float32))
+    if level == 1:
+        scratch.append(pltpu.VMEM((2, 4, SIDES, PIVOTS), jnp.float32))
     return call(body, outs, operands, specs, scratch, spaces="H" * n_outs)
 
 
@@ -376,15 +386,14 @@
             return taken
 
         tables_refs = take(4)
-        (received_ref,) = take(1)
-        weighted_far, weights_far, updates_far = take(3)
+        received_ref, updates_ref = take(2)
+        weighted_far, weights_far = take(2)
         answers_far = take(n_answers)
         outs = take(n_outs)
-        semaphores, x_ref, weighted_ref, weights_ref, updates_ref, pieces_ref = take(6)
+        semaphores, x_ref, weighted_ref, weights_ref, pieces_ref = take(5)
         moves = Moves(semaphores)
         arriving = moves.start(weighted_far, weighted_ref)
-        update_columns = moves.columns(updates_far, updates_ref, 256)
-        columns = moves.columns(weights_far, weights_ref, 512)
+        columns = moves.chunks(weights_far, weights_ref)
         leaving = []
         if level == 2:
             own_ref, other_ref, sums_ref = refs
@@ -399,12 +408,11 @@
                 chosen = total[:, at]
             else:
                 chosen = jnp.concatenate([received_ref[2 * k], received_ref[2 * k + 1]], 1)
-            update_columns[k].wait()
             target -= product(chosen, updates_ref[0, :, at], updates_ref[1, :, at], 1)
         for k in range(chunks):
             columns[k].wait()
             at = slice(k * 512, (k + 1) * 512)
-            x_ref[:, at] = product(target, weights_ref[0, :, at], weights_ref[1, :, at], 0)
+            x_ref[:, at] = product(target, weights_ref[k, 0], weights_ref[k, 1], 0)
         for child in range(2):
             for k in range(blocks):
                 where = block_at(child_block(level, tables_refs, child, k))
@@ -430,14 +438,13 @@
 
     outs = [(8, HALF, blocks * BLOCK)]
     outs += [(4, HALF, 256)] if level == 1 else [(2, 4, HALF, 256), (2, 4, HALF, 256)]
-    operands = [*map(far, tables), received, *map(far, [weighted, weights, updates, *answers])]
-    specs = [SCALARS] * 4 + [WHOLE] + [FAR] * (len(operands) - 5)
+    operands = [*map(far, tables), received, close(updates), *map(far, [weighted, weights, *answers])]
+    specs = [SCALARS] * 4 + [WHOLE] * 2 + [FAR] * (len(operands) - 6)
     scratch = [
         pltpu.SemaphoreType.DMA((64,)),
         pltpu.VMEM((HALF, span), jnp.float32),
         pltpu.VMEM((HALF, 256), jnp.float32),
-        pltpu.VMEM((2, 256, span), jnp.bfloat16),
-        pltpu.VMEM((2, 256, update_len), jnp.bfloat16),
+        pltpu.VMEM((chunks, 2, 256, 512), jnp.bfloat16),
         pltpu.VMEM((2, HALF, blocks * BLOCK), jnp.float32),
     ]
     if level == 2:
@@ -519,20 +526,20 @@
     inverse_after, update_after, _ = lax.optimization_barrier((inverse, update, packed))
     partner_inverse = with_partner(inverse_after)
     partner_update = with_partner(update_after)
-    (weights0,) = prepared([inverse], [(0, 512)], far(packed), pltpu.VMEM)
-    (updates0,) = prepared([update], [(0, 256)], far(packed), pltpu.VMEM)
+    (weights0,) = prepared([inverse], [(0, 512, None)], packed)
+    (updates0,) = prepared([update], [(0, 256, None)], packed)
     tables = sibling_tables(update_targets)
 
     sent, weighted0, sides1, near = level_zero_forward(first, weights0, updates0, factors)
     beyond = across(near, "y0")
     received = exchange(sent, ("c", "x"))
-    weights1, weights2, weights3 = prepared(
-        [inverse, partner_inverse], [(512, 1024), (1536, 2048), (3584, 4096)], far(sent)
-    )
-    updates1, updates2 = prepared([update, partner_update], [(256, 512), (768, 1024)], far(sent))
+    (weights1,) = prepared([inverse, partner_inverse], [(512, 1024, 512)], sent)
+    (updates1,) = prepared([update, partner_update], [(256, 512, None)], sent)
     sent, weighted1, near3 = forward(
         1, received, [sides1, near, beyond], tables, weights1, updates1, factors, partner_factors
     )
+    weights2, weights3 = prepared([inverse, partner_inverse], [(1536, 2048, 512), (3584, 4096, 512)], sent)
+    (updates2,) = prepared([update, partner_update], [(768, 1024, None)], sent)
     beyond3 = across(near3, "y1")
     received = exchange(sent, pair)
     sent, weighted2 = forward(2, received, [near, beyond], tables, weights2, updates2, factors, partner_factors)

time: 198 us -> 181 us (0.914)
  blocking collectives: 29.8 us -> 14.6 us
  Pallas kernels: 58 us -> 47.9 us
  starting transfers between devices: 56 us -> 60.4 us
  waiting for transfers between devices: 49.6 us -> 54 us
    all_to_all x2 -> x1, blocking collectives: 29.8 us -> 14.6 us  [exchange(): return lax.all_to_all(value, axes, 0, 0, tiled=True)]
    pallas_call x11, Pallas kernels: 47.2 us -> 35.7 us  [call(): pl.pallas_call(body, in_specs=specs, out_specs=[FAR if k == 'H' else WHOL...]
    all_to_all x8 -> x9, waiting for transfers between devices: 40.3 us -> 44.4 us  [exchange(): return lax.all_to_all(value, axes, 0, 0, tiled=True)]
    all_to_all x8 -> x9, starting transfers between devices: 39.5 us -> 43.3 us  [exchange(): return lax.all_to_all(value, axes, 0, 0, tiled=True)]
    pallas_call x4 -> x6, Pallas kernels: 10.8 us -> 12.2 us  [prepared(): pl.pallas_call(body, in_specs=[FAR] * (len(pair) + 1), out_specs=[WHOLE]...]
  transfers between devices with their start and end apart: 20 -> 21, of which waited for: 12 -> 13; matrix products, arithmetic and copies ran while one was open for 1% -> 1% of each run, Pallas kernels for 9% -> 10%
where the time goes in v6:
time: 181 us; the launch traced here: 180 us
  starting transfers between devices  60.4 us (33%)
  waiting for transfers between devices  54 us (30%)
  Pallas kernels  47.9 us (26%)
  blocking collectives  14.6 us (8%)
  local copies, waits for them, and re-layouts  2.66 us (1%)
    all_to_all x9, waiting for transfers between devices, exchange(): return lax.all_to_all(value, axes, 0, 0, tiled=True)  44.4 us
    all_to_all x9, starting transfers between devices, exchange(): return lax.all_to_all(value, axes, 0, 0, tiled=True)  43.3 us
    pallas_call x11, Pallas kernels, call(): pl.pallas_call(body, in_specs=specs, out_specs=[FAR if k == 'H' else WHOL...  35.7 us
    all_to_all x1, blocking collectives, exchange(): return lax.all_to_all(value, axes, 0, 0, tiled=True)  14.6 us
    pallas_call x6, Pallas kernels, prepared(): pl.pallas_call(body, in_specs=[FAR] * (len(pair) + 1), out_specs=[WHOLE]...  12.2 us
    ppermute x4, starting transfers between devices, across(): return lax.ppermute(value, axis, [(0, 1), (1, 0)])  9.48 us
    ppermute x7, starting transfers between devices, with_partner(): return lax.ppermute(value, 'c', [(0, 1), (1, 0)])  4.99 us
    ppermute x4, waiting for transfers between devices, across(): return lax.ppermute(value, axis, [(0, 1), (1, 0)])  4.24 us
  transfers between devices with their start and end apart: 21, of which 13 were waited for; matrix products, arithmetic and copies ran while one was open for 1% of the time, Pallas kernels for 10%

profile of v6, /device:TPU:1, one launch (start us, length us, event | category | flops | bytes accessed | tf_op | source)
XLA Modules:
  0.0 180.0 jit_solution(6045438350143199562)
XLA Ops:
  0.0 1.4 collective-permute-start.3
  1.4 1.3 collective-permute-done.3.beside_ref
  2.7 1.9 %shard_map.73.refs_1_ = f32[4,96,512]{2,1,0:T(8,128)} custom-call(f32[96,512]{1,0:T(8,128)} %bitcast.16, f32[96,512]{1,0:T(8,128)S(1)} %collective-permute-done.3.beside_ref), custom_call_target="tpu_custom_call" | custom-call | tf_op jit(solution)/shard_map/pallas_call | solution.py:70
  4.9 4.1 %all-to-all-start = ((f32[4,96,512]{2,1,0:T(8,128)}), f32[4,96,512]{2,1,0:T(8,128)S(1)}, u32[]{:S(2)}, u32[]{:S(2)}) async-start(f32[4,96,512]{2,1,0:T(8,128)} %shard_map.73.refs_1_), calls=%async_computation | async-start | bytes 1572864 | tf_op jit(solution)/shard_map/all_to_all | solution.py:41
  9.5 1.1 shard_map.76.factors_ref.refs_5_
  10.6 1.0 shard_map.74.weights_ref
  11.6 0.9 shard_map.75.updates_ref
  12.5 8.5 %all-to-all-done.first_ref = f32[4,96,512]{2,1,0:T(8,128)S(1)} async-done(((f32[4,96,512]{2,1,0:T(8,128)}), f32[4,96,512]{2,1,0:T(8,128)S(1)}, u32[]{:S(2)}, u32[]{:S(2)}) %all-to-all-start) | async-done | bytes 786464 | tf_op jit(solution)/shard_map/all_to_all | solution.py:41
  21.0 1.4 shard_map.77
  22.4 1.4 collective-permute-start.6
  23.8 4.9 %all-to-all-start.1 = ((f32[8,48,256]{2,1,0:T(8,128)}), f32[8,48,256]{2,1,0:T(8,128)S(1)}, u32[]{:S(2)}, u32[]{:S(2)}) async-start(f32[8,48,256]{2,1,0:T(8,128)} %get-tuple-element.26.refs_2_), calls=%async_computation.1 | async-start | bytes 786432 | tf_op jit(solution)/shard_map/all_to_all | solution.py:41
  28.9 2.6 %collective-permute-start = (s32[1,14]{1,0:T(1,128)S(1)}, s32[1,14]{1,0:T(1,128)S(1)}, u32[]{:S(2)}, u32[]{:S(2)}) collective-permute-start(s32[1,14]{1,0:T(1,128)S(1)} %copy-done.5), channel_id=1, source_target_pairs={{0,8},{4,20},{8,0},{12,28},{16,24},{20,4},{24,16},{28,12},{1,9},{5... | collective-permute-start | bytes 176 | tf_op jit(solution)/shard_map/ppermute | solution.py:511
  31.5 3.1 %collective-permute-done.refs_1_ = s32[1,14]{1,0:T(1,128)S(1)} collective-permute-done((s32[1,14]{1,0:T(1,128)S(1)}, s32[1,14]{1,0:T(1,128)S(1)}, u32[]{:S(2)}, u32[]{:S(2)}) %collective-permute-start) | collective-permute-done | bytes 88 | tf_op jit(solution)/shard_map/ppermute | solution.py:511
  35.5 1.1 shard_map.78.refs_7_.refs_5_
  36.6 2.3 %shard_map.79.refs_11_.refs_7_ = bf16[2,2,256,512]{3,2,1,0:T(8,128)(2,1)} custom-call(f32[128,7680]{1,0:T(8,128)} %bitcast.9, f32[128,7680]{1,0:T(8,128)} %collective-permute-done.7.refs_1_, f32[8,48,256]{2,1,0:T(8,128)} %get-tuple-element.26.refs_2_), custom_call_target="tpu_custom_call" | custom-call | tf_op jit(solution)/shard_map/pallas_call | solution.py:114
  39.7 4.9 %shard_map.80 = (f32[8,48,512]{2,1,0:T(8,128)}, f32[48,256]{1,0:T(8,128)}, f32[2,4,96,128]{3,2,1,0:T(8,128)}) custom-call(s32[1,14]{1,0:T(1,128)} %refs_0_.9, s32[1,14]{1,0:T(1,128)} %copy-done.6, s32[1,14]{1,0:T(1,128)} %copy-done.7, s32[1,14]{1,0:T(1,128)} %copy-done.8, f32[8,48,256]{2,1,0:T(8,128)S(1)} %all-to-all-done.1.refs_4_, ...), custom_call_target="tpu_custom_call" | custom-call | tf_op jit(solution)/shard_map/pallas_call | solution.py:70
  44.6 3.6 %all-to-all-start.2 = ((f32[8,48,512]{2,1,0:T(8,128)}), f32[8,48,512]{2,1,0:T(8,128)S(1)}, u32[]{:S(2)}, u32[]{:S(2)}) async-start(f32[8,48,512]{2,1,0:T(8,128)} %get-tuple-element.31.refs_2_), calls=%async_computation.2 | async-start | bytes 1572864 | tf_op jit(solution)/shard_map/all_to_all | solution.py:41
  48.1 5.5 %shard_map.82 = (bf16[4,2,256,512]{3,2,1,0:T(8,128)(2,1)}, bf16[8,2,256,512]{3,2,1,0:T(8,128)(2,1)}) custom-call(f32[128,7680]{1,0:T(8,128)} %bitcast.10, f32[128,7680]{1,0:T(8,128)} %collective-permute-done.7.refs_1_, f32[8,48,512]{2,1,0:T(8,128)} %get-tuple-element.31.refs_2_), custom_call_target="tpu_custom_call" | custom-call | tf_op jit(solution)/shard_map/pallas_call | solution.py:114
  53.7 1.4 shard_map.81.refs_7_.refs_5_
  55.1 5.1 %all-to-all-done.2.refs_4_ = f32[8,48,512]{2,1,0:T(8,128)S(1)} async-done(((f32[8,48,512]{2,1,0:T(8,128)}), f32[8,48,512]{2,1,0:T(8,128)S(1)}, u32[]{:S(2)}, u32[]{:S(2)}) %all-to-all-start.2) | async-done | bytes 786464 | tf_op jit(solution)/shard_map/all_to_all | solution.py:41
  60.2 5.5 %shard_map.83 = (f32[8,48,128]{2,1,0:T(8,128)}, f32[48,256]{1,0:T(8,128)}) custom-call(s32[1,14]{1,0:T(1,128)} %refs_0_.9, s32[1,14]{1,0:T(1,128)} %copy-done.6, s32[1,14]{1,0:T(1,128)} %copy-done.7, s32[1,14]{1,0:T(1,128)} %copy-done.8, f32[8,48,512]{2,1,0:T(8,128)S(1)} %all-to-all-done.2.refs_4_, f32[2,512]{1,0:T(2,128)S(1)} %shard_map.76.factors_ref.refs_5_, ...), custom_call_target="tpu_custom_call" | custom-call | tf_op jit(solution)/shard_map/pallas_call | solution.py:70
  65.7 3.4 %all-to-all-start.3 = ((f32[8,48,128]{2,1,0:T(8,128)}), f32[8,48,128]{2,1,0:T(8,128)S(1)}, u32[]{:S(2)}, u32[]{:S(2)}) async-start(f32[8,48,128]{2,1,0:T(8,128)} %get-tuple-element.33), calls=%async_computation.3 | async-start | bytes 393216 | tf_op jit(solution)/shard_map/all_to_all | solution.py:41
  69.1 3.9 %collective-permute-start.8 = (f32[2,4,96,128]{3,2,1,0:T(8,128)S(1)}, f32[2,4,96,128]{3,2,1,0:T(8,128)S(1)}, u32[]{:S(2)}, u32[]{:S(2)}) collective-permute-start(f32[2,4,96,128]{3,2,1,0:T(8,128)S(1)} %copy-done.2), channel_id=1, source_target_pairs={{0,16},{16,0},{1,17},{17,1},{2,18},{18,2},{3,19},{19,3},{4,20},{20... | collective-permute-start | bytes 1179656 | tf_op jit(solution)/shard_map/ppermute | solution.py:49
  73.0 1.6 all-to-all-done.3
  74.6 0.8 broadcast_in_dim.6
  75.4 6.4 %all-to-all-start.4 = ((f32[16,48,128]{2,1,0:T(8,128)}), f32[16,48,128]{2,1,0:T(8,128)S(1)}, u32[]{:S(2)}, u32[]{:S(2)}) async-start(f32[16,48,128]{2,1,0:T(8,128)} %broadcast_in_dim.6), calls=%async_computation.4 | async-start | bytes 786432 | tf_op jit(solution)/shard_map/all_to_all | solution.py:41
  81.7 2.0 %collective-permute-done.8.refs_8_ = f32[2,4,96,128]{3,2,1,0:T(8,128)S(1)} collective-permute-done((f32[2,4,96,128]{3,2,1,0:T(8,128)S(1)}, f32[2,4,96,128]{3,2,1,0:T(8,128)S(1)}, u32[]{:S(2)}, u32[]{:S(2)}) %collective-permute-start.8) | collective-permute-done | bytes 393248 | tf_op jit(solution)/shard_map/ppermute | solution.py:49
  83.8 5.9 %all-to-all-done.4.refs_4_ = f32[16,48,128]{2,1,0:T(8,128)S(1)} async-done(((f32[16,48,128]{2,1,0:T(8,128)}), f32[16,48,128]{2,1,0:T(8,128)S(1)}, u32[]{:S(2)}, u32[]{:S(2)}) %all-to-all-start.4) | async-done | bytes 393248 | tf_op jit(solution)/shard_map/all_to_all | solution.py:41
  89.7 9.2 %shard_map.84 = (f32[16,48,128]{2,1,0:T(8,128)}, f32[4,2,48,256]{3,2,1,0:T(8,128)}, f32[4,2,48,256]{3,2,1,0:T(8,128)}) custom-call(s32[1,14]{1,0:T(1,128)} %refs_0_.9, s32[1,14]{1,0:T(1,128)} %copy-done.6, s32[1,14]{1,0:T(1,128)} %copy-done.7, s32[1,14]{1,0:T(1,128)} %copy-done.8, f32[16,48,128]{2,1,0:T(8,128)S(1)} %all-to-all-done.4.refs_4_, ...), custom_call_target="tpu_custom_call" | custom-call | tf_op jit(solution)/shard_map/pallas_call | solution.py:70
  99.0 3.7 %all-to-all-start.5 = ((f32[16,48,128]{2,1,0:T(8,128)}), f32[16,48,128]{2,1,0:T(8,128)S(1)}, u32[]{:S(2)}, u32[]{:S(2)}) async-start(f32[16,48,128]{2,1,0:T(8,128)} %get-tuple-element.36), calls=%async_computation.5 | async-start | bytes 786432 | tf_op jit(solution)/shard_map/all_to_all | solution.py:41
  102.7 2.9 %collective-permute-start.9 = (f32[4,2,48,256]{3,2,1,0:T(8,128)}, f32[4,2,48,256]{3,2,1,0:T(8,128)S(1)}, u32[]{:S(2)}, u32[]{:S(2)}) collective-permute-start(f32[4,2,48,256]{3,2,1,0:T(8,128)} %get-tuple-element.39), channel_id=1, source_target_pairs={{0,16},{16,0},{1,17},{17,1},{2,18},{18,2},{3,19},{19,3},{4,20},{20... | collective-permute-start | bytes 1179656 | tf_op jit(solution)/shard_map/ppermute | solution.py:49
  105.6 5.3 %all-to-all-done.5 = f32[16,48,128]{2,1,0:T(8,128)S(1)} async-done(((f32[16,48,128]{2,1,0:T(8,128)}), f32[16,48,128]{2,1,0:T(8,128)S(1)}, u32[]{:S(2)}, u32[]{:S(2)}) %all-to-all-start.5) | async-done | bytes 393248 | tf_op jit(solution)/shard_map/all_to_all | solution.py:41
  110.9 0.7 broadcast_in_dim.7
  111.6 3.4 %all-to-all-start.6 = ((f32[8,48,128]{2,1,0:T(8,128)}), f32[8,48,128]{2,1,0:T(8,128)S(1)}, u32[]{:S(2)}, u32[]{:S(2)}) async-start(f32[8,48,128]{2,1,0:T(8,128)} %broadcast_in_dim.7), calls=%async_computation.6 | async-start | bytes 393216 | tf_op jit(solution)/shard_map/all_to_all | solution.py:41
  115.0 2.2 %collective-permute-done.9.refs_9_ = f32[4,2,48,256]{3,2,1,0:T(8,128)S(1)} collective-permute-done((f32[4,2,48,256]{3,2,1,0:T(8,128)}, f32[4,2,48,256]{3,2,1,0:T(8,128)S(1)}, u32[]{:S(2)}, u32[]{:S(2)}) %collective-permute-start.9) | collective-permute-done | bytes 393248 | tf_op jit(solution)/shard_map/ppermute | solution.py:49
  117.2 3.3 %all-to-all-done.6.refs_4_ = f32[8,48,128]{2,1,0:T(8,128)S(1)} async-done(((f32[8,48,128]{2,1,0:T(8,128)}), f32[8,48,128]{2,1,0:T(8,128)S(1)}, u32[]{:S(2)}, u32[]{:S(2)}) %all-to-all-start.6) | async-done | bytes 196640 | tf_op jit(solution)/shard_map/all_to_all | solution.py:41
  120.5 4.8 %shard_map.85 = (f32[8,48,512]{2,1,0:T(8,128)}, f32[2,4,48,256]{3,2,1,0:T(8,128)}, f32[2,4,48,256]{3,2,1,0:T(8,128)}) custom-call(s32[1,14]{1,0:T(1,128)} %refs_0_.9, s32[1,14]{1,0:T(1,128)} %copy-done.6, s32[1,14]{1,0:T(1,128)} %copy-done.7, s32[1,14]{1,0:T(1,128)} %copy-done.8, f32[8,48,128]{2,1,0:T(8,128)S(1)} %all-to-all-done.6.refs_4_, ...), custom_call_target="tpu_custom_call" | custom-call | tf_op jit(solution)/shard_map/pallas_call | solution.py:70
  125.3 3.6 %all-to-all-start.7 = ((f32[8,48,512]{2,1,0:T(8,128)}), f32[8,48,512]{2,1,0:T(8,128)S(1)}, u32[]{:S(2)}, u32[]{:S(2)}) async-start(f32[8,48,512]{2,1,0:T(8,128)} %get-tuple-element.40), calls=%async_computation.7 | async-start | bytes 1572864 | tf_op jit(solution)/shard_map/all_to_all | solution.py:41
  128.9 1.4 collective-permute-start.10
  130.3 7.0 %all-to-all-done.7.refs_4_ = f32[8,48,512]{2,1,0:T(8,128)S(1)} async-done(((f32[8,48,512]{2,1,0:T(8,128)}), f32[8,48,512]{2,1,0:T(8,128)S(1)}, u32[]{:S(2)}, u32[]{:S(2)}) %all-to-all-start.7) | async-done | bytes 786464 | tf_op jit(solution)/shard_map/all_to_all | solution.py:41
  137.2 3.7 %shard_map.86 = (f32[8,48,256]{2,1,0:T(8,128)}, f32[4,48,256]{2,1,0:T(8,128)}) custom-call(s32[1,14]{1,0:T(1,128)} %refs_0_.9, s32[1,14]{1,0:T(1,128)} %copy-done.6, s32[1,14]{1,0:T(1,128)} %copy-done.7, s32[1,14]{1,0:T(1,128)} %copy-done.8, f32[8,48,512]{2,1,0:T(8,128)S(1)} %all-to-all-done.7.refs_4_, bf16[2,256,512]{2,1,0:T(8,128)(2,1)S(1)} %shard_map.78.refs_7_.refs_5_, ...), custom_call_target="tpu_custom_call" | custom-call | tf_op jit(solution)/shard_map/pallas_call | solution.py:70
  140.9 10.2 %all-to-all-start.8 = ((f32[8,48,256]{2,1,0:T(8,128)}), f32[8,48,256]{2,1,0:T(8,128)S(1)}, u32[]{:S(2)}, u32[]{:S(2)}) async-start(f32[8,48,256]{2,1,0:T(8,128)} %get-tuple-element.42), calls=%async_computation.8 | async-start | bytes 786432 | tf_op jit(solution)/shard_map/all_to_all | solution.py:41
  151.2 7.7 %all-to-all-done.8.received_ref = f32[8,48,256]{2,1,0:T(8,128)S(1)} async-done(((f32[8,48,256]{2,1,0:T(8,128)}), f32[8,48,256]{2,1,0:T(8,128)S(1)}, u32[]{:S(2)}, u32[]{:S(2)}) %all-to-all-start.8) | async-done | bytes 393248 | tf_op jit(solution)/shard_map/all_to_all | solution.py:41
  158.9 2.5 %shard_map.87 = f32[4,96,512]{2,1,0:T(8,128)} custom-call(f32[8,48,256]{2,1,0:T(8,128)S(1)} %all-to-all-done.8.received_ref, f32[96,128]{1,0:T(8,128)} %get-tuple-element.43.weighted_ref, f32[4,48,256]{2,1,0:T(8,128)} %get-tuple-element.44.nearest_ref, f32[2,4,48,256]{3,2,1,0:T(8,128)} %get-tuple-element.45.kept_ref, ...), custom_call_target="tpu_custom_call" | custom-call | tf_op jit(solution)/shard_map/pallas_call | solution.py:70
  161.4 14.6 %all_to_all.50.received_ref = f32[4,96,512]{2,1,0:T(8,128)S(1)} all-to-all(f32[4,96,512]{2,1,0:T(8,128)} %shard_map.87), channel_id=1, replica_groups=mesh['z'=4,'y1'=2,'y0'=2,'c'=2,'x'=4] {'x'}, dimensions={0} | all-to-all | bytes 1572864 | tf_op jit(solution)/shard_map/all_to_all | solution.py:41
  176.1 2.2 %collective-permute-start.11 = (f32[96,512]{1,0:T(8,128)S(1)}, f32[96,512]{1,0:T(8,128)S(1)}, u32[]{:S(2)}, u32[]{:S(2)}) collective-permute-start(f32[96,512]{1,0:T(8,128)S(1)} %shard_map.88.total_ref), channel_id=1, source_target_pairs={{0,4},{4,0},{1,5},{5,1},{2,6},{6,2},{3,7},{7,3},{8,12},{12,8},{9,1... | collective-permute-start | bytes 589832 | tf_op jit(solution)/shard_map/ppermute | solution.py:45
  178.2 1.1 collective-permute-done.11.beside_ref
  179.3 0.7 shard_map.89
  (34 shorter events, 2.7 us)
Async XLA Ops:
  0.0 2.7 %collective-permute-start.3 = (f32[96,512]{1,0:T(8,128)}, f32[96,512]{1,0:T(8,128)S(1)}, u32[]{:S(2)}, u32[]{:S(2)}) collective-permute-start(f32[96,512]{1,0:T(8,128)} %bitcast.15), channel_id=1, source_target_pairs={{0,4},{4,0},{1,5},{5,1},{2,6},{6,2},{3,7},{7,3},{8,12},{12,8},{9,1... | collective-permute-start | bytes 589832 | tf_op jit(solution)/shard_map/ppermute | solution.py:45
  4.6 32.0 %collective-permute-start.7 = (f32[128,7680]{1,0:T(8,128)}, f32[128,7680]{1,0:T(8,128)}, u32[]{:S(2)}, u32[]{:S(2)}) collective-permute-start(f32[128,7680]{1,0:T(8,128)} %bitcast.7), channel_id=1, source_target_pairs={{0,4},{4,0},{1,5},{5,1},{2,6},{6,2},{3,7},{7,3},{8,12},{12,8},{9,1... | collective-permute-start | bytes 11796488 | tf_op jit(solution)/shard_map/ppermute | solution.py:45
  4.9 16.1 %all-to-all-start = ((f32[4,96,512]{2,1,0:T(8,128)}), f32[4,96,512]{2,1,0:T(8,128)S(1)}, u32[]{:S(2)}, u32[]{:S(2)}) async-start(f32[4,96,512]{2,1,0:T(8,128)} %shard_map.73.refs_1_), calls=%async_computation | async-start | bytes 1572864 | tf_op jit(solution)/shard_map/all_to_all | solution.py:41
  9.1 25.5 %collective-permute-start.5 = (f32[128,1792]{1,0:T(8,128)}, f32[128,1792]{1,0:T(8,128)S(1)}, u32[]{:S(2)}, u32[]{:S(2)}) collective-permute-start(f32[128,1792]{1,0:T(8,128)} %bitcast.11), channel_id=1, source_target_pairs={{0,4},{4,0},{1,5},{5,1},{2,6},{6,2},{3,7},{7,3},{8,12},{12,8},{9,1... | collective-permute-start | bytes 2752520 | tf_op jit(solution)/shard_map/ppermute | solution.py:45
  10.5 18.3 %copy-start.5 = (s32[1,14]{1,0:T(1,128)S(1)}, s32[1,14]{1,0:T(1,128)}, u32[]{:S(2)}) copy-start(s32[1,14]{1,0:T(1,128)} %refs_0_.9) | copy-start | bytes 172
  22.4 16.6 %collective-permute-start.6 = (f32[4,96,256]{2,1,0:T(8,128)}, f32[4,96,256]{2,1,0:T(8,128)S(1)}, u32[]{:S(2)}, u32[]{:S(2)}) collective-permute-start(f32[4,96,256]{2,1,0:T(8,128)} %get-tuple-element.29.refs_9_.refs_8_), channel_id=1, source_target_pairs={{0,8},{8,0},{1,9},{9,1},{2,10},{10,2},{3,11},{11,3},{4,12},{12,4},... | collective-permute-start | bytes 1179656 | tf_op jit(solution)/shard_map/ppermute | solution.py:49
  23.8 15.2 %all-to-all-start.1 = ((f32[8,48,256]{2,1,0:T(8,128)}), f32[8,48,256]{2,1,0:T(8,128)S(1)}, u32[]{:S(2)}, u32[]{:S(2)}) async-start(f32[8,48,256]{2,1,0:T(8,128)} %get-tuple-element.26.refs_2_), calls=%async_computation.1 | async-start | bytes 786432 | tf_op jit(solution)/shard_map/all_to_all | solution.py:41
  28.7 10.2 %collective-permute-start.4 = (f32[2,512]{1,0:T(2,128)S(1)}, f32[2,512]{1,0:T(2,128)S(1)}, u32[]{:S(2)}, u32[]{:S(2)}) collective-permute-start(f32[2,512]{1,0:T(2,128)S(1)} %shard_map.76.factors_ref.refs_5_), channel_id=1, source_target_pairs={{0,4},{4,0},{1,5},{5,1},{2,6},{6,2},{3,7},{7,3},{8,12},{12,8},{9,1... | collective-permute-start | bytes 12296 | tf_op jit(solution)/shard_map/ppermute | solution.py:45
  28.9 5.7 %collective-permute-start = (s32[1,14]{1,0:T(1,128)S(1)}, s32[1,14]{1,0:T(1,128)S(1)}, u32[]{:S(2)}, u32[]{:S(2)}) collective-permute-start(s32[1,14]{1,0:T(1,128)S(1)} %copy-done.5), channel_id=1, source_target_pairs={{0,8},{4,20},{8,0},{12,28},{16,24},{20,4},{24,16},{28,12},{1,9},{5... | collective-permute-start | bytes 176 | tf_op jit(solution)/shard_map/ppermute | solution.py:511
  34.5 4.4 %copy-start.6 = (s32[1,14]{1,0:T(1,128)}, s32[1,14]{1,0:T(1,128)S(1)}, u32[]{:S(2)}) copy-start(s32[1,14]{1,0:T(1,128)S(1)} %collective-permute-done.refs_1_) | copy-start | bytes 172
  34.5 4.3 %collective-permute-start.1 = (s32[1,14]{1,0:T(1,128)S(1)}, s32[1,14]{1,0:T(1,128)S(1)}, u32[]{:S(2)}, u32[]{:S(2)}) collective-permute-start(s32[1,14]{1,0:T(1,128)S(1)} %copy-done.5), channel_id=1, source_target_pairs={{0,4},{4,0},{1,5},{5,1},{2,6},{6,2},{3,7},{7,3},{8,12},{12,8},{9,1... | collective-permute-start | bytes 176 | tf_op jit(solution)/shard_map/ppermute | solution.py:45
  34.5 1.0 copy-start
  34.6 4.3 %collective-permute-start.2 = (s32[1,14]{1,0:T(1,128)S(1)}, s32[1,14]{1,0:T(1,128)S(1)}, u32[]{:S(2)}, u32[]{:S(2)}) collective-permute-start(s32[1,14]{1,0:T(1,128)S(1)} %collective-permute-done.refs_1_), channel_id=1, source_target_pairs={{0,4},{4,0},{1,5},{5,1},{2,6},{6,2},{3,7},{7,3},{8,12},{12,8},{9,1... | collective-permute-start | bytes 176 | tf_op jit(solution)/shard_map/ppermute | solution.py:45
  38.9 0.6 copy-start.7
  38.9 0.6 copy-start.8
  39.0 0.7 copy-start.1
  44.6 15.6 %all-to-all-start.2 = ((f32[8,48,512]{2,1,0:T(8,128)}), f32[8,48,512]{2,1,0:T(8,128)S(1)}, u32[]{:S(2)}, u32[]{:S(2)}) async-start(f32[8,48,512]{2,1,0:T(8,128)} %get-tuple-element.31.refs_2_), calls=%async_computation.2 | async-start | bytes 1572864 | tf_op jit(solution)/shard_map/all_to_all | solution.py:41
  53.7 15.4 %copy-start.2 = (f32[2,4,96,128]{3,2,1,0:T(8,128)S(1)}, f32[2,4,96,128]{3,2,1,0:T(8,128)}, u32[]{:S(2)}) copy-start(f32[2,4,96,128]{3,2,1,0:T(8,128)} %get-tuple-element.34.refs_7_) | copy-start | bytes 1179652
  65.7 8.9 %all-to-all-start.3 = ((f32[8,48,128]{2,1,0:T(8,128)}), f32[8,48,128]{2,1,0:T(8,128)S(1)}, u32[]{:S(2)}, u32[]{:S(2)}) async-start(f32[8,48,128]{2,1,0:T(8,128)} %get-tuple-element.33), calls=%async_computation.3 | async-start | bytes 393216 | tf_op jit(solution)/shard_map/all_to_all | solution.py:41
  69.1 14.7 %collective-permute-start.8 = (f32[2,4,96,128]{3,2,1,0:T(8,128)S(1)}, f32[2,4,96,128]{3,2,1,0:T(8,128)S(1)}, u32[]{:S(2)}, u32[]{:S(2)}) collective-permute-start(f32[2,4,96,128]{3,2,1,0:T(8,128)S(1)} %copy-done.2), channel_id=1, source_target_pairs={{0,16},{16,0},{1,17},{17,1},{2,18},{18,2},{3,19},{19,3},{4,20},{20... | collective-permute-start | bytes 1179656 | tf_op jit(solution)/shard_map/ppermute | solution.py:49
  75.4 14.4 %all-to-all-start.4 = ((f32[16,48,128]{2,1,0:T(8,128)}), f32[16,48,128]{2,1,0:T(8,128)S(1)}, u32[]{:S(2)}, u32[]{:S(2)}) async-start(f32[16,48,128]{2,1,0:T(8,128)} %broadcast_in_dim.6), calls=%async_computation.4 | async-start | bytes 786432 | tf_op jit(solution)/shard_map/all_to_all | solution.py:41
  83.8 5.9 %copy-start.3 = (f32[2,4,96,128]{3,2,1,0:T(8,128)}, f32[2,4,96,128]{3,2,1,0:T(8,128)S(1)}, u32[]{:S(2)}) copy-start(f32[2,4,96,128]{3,2,1,0:T(8,128)S(1)} %collective-permute-done.8.refs_8_) | copy-start | bytes 1179652
  99.0 11.9 %all-to-all-start.5 = ((f32[16,48,128]{2,1,0:T(8,128)}), f32[16,48,128]{2,1,0:T(8,128)S(1)}, u32[]{:S(2)}, u32[]{:S(2)}) async-start(f32[16,48,128]{2,1,0:T(8,128)} %get-tuple-element.36), calls=%async_computation.5 | async-start | bytes 786432 | tf_op jit(solution)/shard_map/all_to_all | solution.py:41
  102.7 14.5 %collective-permute-start.9 = (f32[4,2,48,256]{3,2,1,0:T(8,128)}, f32[4,2,48,256]{3,2,1,0:T(8,128)S(1)}, u32[]{:S(2)}, u32[]{:S(2)}) collective-permute-start(f32[4,2,48,256]{3,2,1,0:T(8,128)} %get-tuple-element.39), channel_id=1, source_target_pairs={{0,16},{16,0},{1,17},{17,1},{2,18},{18,2},{3,19},{19,3},{4,20},{20... | collective-permute-start | bytes 1179656 | tf_op jit(solution)/shard_map/ppermute | solution.py:49
  111.6 8.9 %all-to-all-start.6 = ((f32[8,48,128]{2,1,0:T(8,128)}), f32[8,48,128]{2,1,0:T(8,128)S(1)}, u32[]{:S(2)}, u32[]{:S(2)}) async-start(f32[8,48,128]{2,1,0:T(8,128)} %broadcast_in_dim.7), calls=%async_computation.6 | async-start | bytes 393216 | tf_op jit(solution)/shard_map/all_to_all | solution.py:41
  117.2 3.3 %copy-start.4 = (f32[4,2,48,256]{3,2,1,0:T(8,128)}, f32[4,2,48,256]{3,2,1,0:T(8,128)S(1)}, u32[]{:S(2)}) copy-start(f32[4,2,48,256]{3,2,1,0:T(8,128)S(1)} %collective-permute-done.9.refs_9_) | copy-start | bytes 1179652
  125.3 11.9 %all-to-all-start.7 = ((f32[8,48,512]{2,1,0:T(8,128)}), f32[8,48,512]{2,1,0:T(8,128)S(1)}, u32[]{:S(2)}, u32[]{:S(2)}) async-start(f32[8,48,512]{2,1,0:T(8,128)} %get-tuple-element.40), calls=%async_computation.7 | async-start | bytes 1572864 | tf_op jit(solution)/shard_map/all_to_all | solution.py:41
  128.9 22.3 %collective-permute-start.10 = (f32[2,4,48,256]{3,2,1,0:T(8,128)}, f32[2,4,48,256]{3,2,1,0:T(8,128)S(1)}, u32[]{:S(2)}, u32[]{:S(2)}) collective-permute-start(f32[2,4,48,256]{3,2,1,0:T(8,128)} %get-tuple-element.46), channel_id=1, source_target_pairs={{0,8},{8,0},{1,9},{9,1},{2,10},{10,2},{3,11},{11,3},{4,12},{12,4},... | collective-permute-start | bytes 1179656 | tf_op jit(solution)/shard_map/ppermute | solution.py:49
  140.9 17.9 %all-to-all-start.8 = ((f32[8,48,256]{2,1,0:T(8,128)}), f32[8,48,256]{2,1,0:T(8,128)S(1)}, u32[]{:S(2)}, u32[]{:S(2)}) async-start(f32[8,48,256]{2,1,0:T(8,128)} %get-tuple-element.42), calls=%async_computation.8 | async-start | bytes 786432 | tf_op jit(solution)/shard_map/all_to_all | solution.py:41
  176.1 3.2 %collective-permute-start.11 = (f32[96,512]{1,0:T(8,128)S(1)}, f32[96,512]{1,0:T(8,128)S(1)}, u32[]{:S(2)}, u32[]{:S(2)}) collective-permute-start(f32[96,512]{1,0:T(8,128)S(1)} %shard_map.88.total_ref), channel_id=1, source_target_pairs={{0,4},{4,0},{1,5},{5,1},{2,6},{6,2},{3,7},{7,3},{8,12},{12,8},{9,1... | collective-permute-start | bytes 589832 | tf_op jit(solution)/shard_map/ppermute | solution.py:45

commit v7 on v6

--- a/solution.py
+++ b/solution.py
@@ -28,7 +28,9 @@
     def dot(a, b):
         return lax.dot_general(a, b, dims, preferred_element_type=jnp.float32)
 
-    return dot(left_high, high) + (dot(left_high, low) + dot(left_low, high))
+    both = dot(jnp.concatenate([left_high, left_low], 0), high)
+    rows = left.shape[0]
+    return both[:rows] + (dot(left_high, low) + both[rows:])
 
 
 def dot_full(left, right):
@@ -416,9 +418,15 @@
         for child in range(2):
             for k in range(blocks):
                 where = block_at(child_block(level, tables_refs, child, k))
-                pieces_ref[child, :, k * BLOCK : (k + 1) * BLOCK] = x_ref[:, where]
-            for x in range(4):
-                leaving.append(moves.start(pieces_ref.at[child], outs[0].at[x * 2 + child]))
+                at = slice(k * BLOCK, (k + 1) * BLOCK)
+                if level == 1:
+                    for x in range(4):
+                        outs[0][x * 2 + child, :, at] = x_ref[:, where]
+                else:
+                    pieces_ref[child, :, at] = x_ref[:, where]
+            if level == 2:
+                for x in range(4):
+                    leaving.append(moves.start(pieces_ref.at[child], outs[0].at[x * 2 + child]))
         if level == 1:
             for x in range(4):
                 leaving.append(moves.start(x_ref.at[:, pl.ds(x * 256, 256)], outs[1].at[x]))
@@ -449,7 +457,7 @@
     ]
     if level == 2:
         scratch += [pltpu.VMEM((4, 2, HALF, 256), jnp.float32)] * 2 + [pltpu.VMEM((2, 4, HALF, 256), jnp.float32)]
-    return call(body, outs, operands, specs, scratch, spaces="H" * n_outs)
+    return call(body, outs, operands, specs, scratch, spaces="vH" if level == 1 else "HHH")
 
 
 def level_zero_backward(received, weighted, weights, updates, nearest, kept, other):
@@ -473,7 +481,7 @@
         [(4, SIDES, 512)],
         [received, *map(far, [weighted, nearest, kept]), other, close(weights), close(updates)],
         [WHOLE] * 7,
-        spaces="h",
+        spaces="v",
     )[0]
 
 
@@ -528,7 +536,9 @@
     partner_update = with_partner(update_after)
     (weights0,) = prepared([inverse], [(0, 512, None)], packed)
     (updates0,) = prepared([update], [(0, 256, None)], packed)
-    tables = sibling_tables(update_targets)
+    first, partner_factors, *tables = lax.optimization_barrier(
+        (first, partner_factors, *sibling_tables(update_targets))
+    )
 
     sent, weighted0, sides1, near = level_zero_forward(first, weights0, updates0, factors)
     beyond = across(near, "y0")
@@ -551,6 +561,7 @@
     other = across(other, "y0")
     received = exchange(sent, pair)
     sent, nearest = backward(1, received, weighted1, tables, weights1, updates1, [])
+    sent, other = lax.optimization_barrier((sent, other))
     received = exchange(sent, ("x", "c"))
     sent = level_zero_backward(received, weighted0, weights0, updates0, nearest, kept, other)
     total = summed(exchange(sent, ("x",)))

time: 181 us -> 176 us (0.972)
  blocking collectives: 14.6 us -> 29.2 us
  starting transfers between devices: 60.4 us -> 47.4 us
  Pallas kernels: 47.9 us -> 44 us
  waiting for transfers between devices: 54 us -> 50.4 us
    all_to_all x1 -> x2, blocking collectives: 14.6 us -> 29.2 us  [exchange(): return lax.all_to_all(value, axes, 0, 0, tiled=True)]
    all_to_all x9 -> x8, starting transfers between devices: 43.3 us -> 31.8 us  [exchange(): return lax.all_to_all(value, axes, 0, 0, tiled=True)]
    all_to_all x9 -> x8, waiting for transfers between devices: 44.4 us -> 37.9 us  [exchange(): return lax.all_to_all(value, axes, 0, 0, tiled=True)]
    ppermute x4, waiting for transfers between devices: 4.24 us -> 9 us  [across(): return lax.ppermute(value, axis, [(0, 1), (1, 0)])]
    pallas_call x11, Pallas kernels: 35.7 us -> 31.8 us  [call(): pl.pallas_call(body, in_specs=specs, out_specs=[FAR if k == 'H' else WHOL...]
    ppermute x1, waiting for transfers between devices: 3.05 us -> 1.14 us  [sibling_tables(): side = lax.ppermute(targets, ('y1', 'y0', 'c'), pairs)]
  transfers between devices with their start and end apart: 21 -> 20, of which waited for: 13 -> 14; matrix products, arithmetic and copies ran while one was open for 1% -> 1% of each run, Pallas kernels for 10% -> 10%
where the time goes in v7:
time: 176 us; the launch traced here: 174 us
  waiting for transfers between devices  50.4 us (29%)
  starting transfers between devices  47.4 us (27%)
  Pallas kernels  44 us (25%)
  blocking collectives  29.2 us (17%)
  local copies, waits for them, and re-layouts  3.21 us (2%)
    all_to_all x8, waiting for transfers between devices, exchange(): return lax.all_to_all(value, axes, 0, 0, tiled=True)  37.9 us
    pallas_call x11, Pallas kernels, call(): pl.pallas_call(body, in_specs=specs, out_specs=[FAR if k == 'H' else WHOL...  31.8 us
    all_to_all x8, starting transfers between devices, exchange(): return lax.all_to_all(value, axes, 0, 0, tiled=True)  31.8 us
    all_to_all x2, blocking collectives, exchange(): return lax.all_to_all(value, axes, 0, 0, tiled=True)  29.2 us
    pallas_call x6, Pallas kernels, prepared(): pl.pallas_call(body, in_specs=[FAR] * (len(pair) + 1), out_specs=[WHOLE]...  12.2 us
    ppermute x4, waiting for transfers between devices, across(): return lax.ppermute(value, axis, [(0, 1), (1, 0)])  9 us
    ppermute x4, starting transfers between devices, across(): return lax.ppermute(value, axis, [(0, 1), (1, 0)])  8.31 us
    ppermute x7, starting transfers between devices, with_partner(): return lax.ppermute(value, 'c', [(0, 1), (1, 0)])  4.37 us
  transfers between devices with their start and end apart: 20, of which 14 were waited for; matrix products, arithmetic and copies ran while one was open for 1% of the time, Pallas kernels for 10%

profile of v7, /device:TPU:1, one launch (start us, length us, event | category | flops | bytes accessed | tf_op | source)
XLA Modules:
  0.0 174.5 jit_solution(17396358364053136902)
XLA Ops:
  0.0 1.4 collective-permute-start
  1.4 1.3 collective-permute-done.beside_ref
  2.7 1.9 %shard_map.73.refs_1_ = f32[4,96,512]{2,1,0:T(8,128)} custom-call(f32[96,512]{1,0:T(8,128)} %bitcast.16, f32[96,512]{1,0:T(8,128)S(1)} %collective-permute-done.beside_ref), custom_call_target="tpu_custom_call" | custom-call | tf_op jit(solution)/shard_map/pallas_call | solution.py:72
  4.9 4.1 %all-to-all-start = ((f32[4,96,512]{2,1,0:T(8,128)}), f32[4,96,512]{2,1,0:T(8,128)S(1)}, u32[]{:S(2)}, u32[]{:S(2)}) async-start(f32[4,96,512]{2,1,0:T(8,128)} %shard_map.73.refs_1_), calls=%async_computation | async-start | bytes 1572864 | tf_op jit(solution)/shard_map/all_to_all | solution.py:43
  9.5 1.1 shard_map.74.factors_ref.refs_5_
  10.7 2.9 %collective-permute-start.2 = (s32[1,14]{1,0:T(1,128)}, s32[1,14]{1,0:T(1,128)S(1)}, u32[]{:S(2)}, u32[]{:S(2)}) collective-permute-start(s32[1,14]{1,0:T(1,128)} %refs_0_.4), channel_id=1, source_target_pairs={{0,8},{4,20},{8,0},{12,28},{16,24},{20,4},{24,16},{28,12},{1,9},{5... | collective-permute-start | bytes 176 | tf_op jit(solution)/shard_map/ppermute | solution.py:519
  13.6 1.1 collective-permute-done.2.refs_1_
  14.8 1.0 shard_map.75.weights_ref
  15.8 0.9 shard_map.76.updates_ref
  16.8 4.2 %all-to-all-done.first_ref = f32[4,96,512]{2,1,0:T(8,128)S(1)} async-done(((f32[4,96,512]{2,1,0:T(8,128)}), f32[4,96,512]{2,1,0:T(8,128)S(1)}, u32[]{:S(2)}, u32[]{:S(2)}) %all-to-all-start) | async-done | bytes 786464 | tf_op jit(solution)/shard_map/all_to_all | solution.py:43
  21.0 1.3 shard_map.77
  22.4 1.4 collective-permute-start.6
  23.7 4.9 %all-to-all-start.1 = ((f32[8,48,256]{2,1,0:T(8,128)}), f32[8,48,256]{2,1,0:T(8,128)S(1)}, u32[]{:S(2)}, u32[]{:S(2)}) async-start(f32[8,48,256]{2,1,0:T(8,128)} %get-tuple-element.39.refs_2_), calls=%async_computation.1 | async-start | bytes 786432 | tf_op jit(solution)/shard_map/all_to_all | solution.py:43
  28.7 1.0 copy-done
  29.6 1.1 shard_map.78.refs_7_.refs_5_
  30.7 2.3 %shard_map.79.refs_11_.refs_7_ = bf16[2,2,256,512]{3,2,1,0:T(8,128)(2,1)} custom-call(f32[128,7680]{1,0:T(8,128)} %bitcast.9, f32[128,7680]{1,0:T(8,128)} %collective-permute-done.7.refs_1_, f32[8,48,256]{2,1,0:T(8,128)} %get-tuple-element.39.refs_2_), custom_call_target="tpu_custom_call" | custom-call | tf_op jit(solution)/shard_map/pallas_call | solution.py:116
  33.0 3.6 %all-to-all-done.1.refs_4_ = f32[8,48,256]{2,1,0:T(8,128)S(1)} async-done(((f32[8,48,256]{2,1,0:T(8,128)}), f32[8,48,256]{2,1,0:T(8,128)S(1)}, u32[]{:S(2)}, u32[]{:S(2)}) %all-to-all-start.1) | async-done | bytes 393248 | tf_op jit(solution)/shard_map/all_to_all | solution.py:43
  37.4 4.6 %shard_map.80 = (f32[8,48,512]{2,1,0:T(8,128)}, f32[48,256]{1,0:T(8,128)}, f32[2,4,96,128]{3,2,1,0:T(8,128)}) custom-call(s32[1,14]{1,0:T(1,128)} %refs_0_.4, s32[1,14]{1,0:T(1,128)} %copy-done.5, s32[1,14]{1,0:T(1,128)} %copy-done.6, s32[1,14]{1,0:T(1,128)} %copy-done.7, f32[8,48,256]{2,1,0:T(8,128)S(1)} %all-to-all-done.1.refs_4_, ...), custom_call_target="tpu_custom_call" | custom-call | tf_op jit(solution)/shard_map/pallas_call | solution.py:72
  42.0 3.6 %all-to-all-start.2 = ((f32[8,48,512]{2,1,0:T(8,128)}), f32[8,48,512]{2,1,0:T(8,128)S(1)}, u32[]{:S(2)}, u32[]{:S(2)}) async-start(f32[8,48,512]{2,1,0:T(8,128)} %get-tuple-element.45.refs_2_), calls=%async_computation.2 | async-start | bytes 1572864 | tf_op jit(solution)/shard_map/all_to_all | solution.py:43
  45.6 5.5 %shard_map.82 = (bf16[4,2,256,512]{3,2,1,0:T(8,128)(2,1)}, bf16[8,2,256,512]{3,2,1,0:T(8,128)(2,1)}) custom-call(f32[128,7680]{1,0:T(8,128)} %bitcast.10, f32[128,7680]{1,0:T(8,128)} %collective-permute-done.7.refs_1_, f32[8,48,512]{2,1,0:T(8,128)} %get-tuple-element.45.refs_2_), custom_call_target="tpu_custom_call" | custom-call | tf_op jit(solution)/shard_map/pallas_call | solution.py:116
  51.1 1.4 shard_map.81.refs_7_.refs_5_
  52.5 5.6 %all-to-all-done.2.refs_4_ = f32[8,48,512]{2,1,0:T(8,128)S(1)} async-done(((f32[8,48,512]{2,1,0:T(8,128)}), f32[8,48,512]{2,1,0:T(8,128)S(1)}, u32[]{:S(2)}, u32[]{:S(2)}) %all-to-all-start.2) | async-done | bytes 786464 | tf_op jit(solution)/shard_map/all_to_all | solution.py:43
  58.1 4.9 %shard_map.83 = (f32[8,48,128]{2,1,0:T(8,128)}, f32[48,256]{1,0:T(8,128)}) custom-call(s32[1,14]{1,0:T(1,128)} %refs_0_.4, s32[1,14]{1,0:T(1,128)} %copy-done.5, s32[1,14]{1,0:T(1,128)} %copy-done.6, s32[1,14]{1,0:T(1,128)} %copy-done.7, f32[8,48,512]{2,1,0:T(8,128)S(1)} %all-to-all-done.2.refs_4_, f32[2,512]{1,0:T(2,128)S(1)} %shard_map.74.factors_ref.refs_5_, ...), custom_call_target="tpu_custom_call" | custom-call | tf_op jit(solution)/shard_map/pallas_call | solution.py:72
  63.0 3.4 %all-to-all-start.3 = ((f32[8,48,128]{2,1,0:T(8,128)}), f32[8,48,128]{2,1,0:T(8,128)S(1)}, u32[]{:S(2)}, u32[]{:S(2)}) async-start(f32[8,48,128]{2,1,0:T(8,128)} %get-tuple-element.47), calls=%async_computation.3 | async-start | bytes 393216 | tf_op jit(solution)/shard_map/all_to_all | solution.py:43
  66.5 2.7 %collective-permute-start.8 = (f32[2,4,96,128]{3,2,1,0:T(8,128)S(1)}, f32[2,4,96,128]{3,2,1,0:T(8,128)S(1)}, u32[]{:S(2)}, u32[]{:S(2)}) collective-permute-start(f32[2,4,96,128]{3,2,1,0:T(8,128)S(1)} %copy-done.2), channel_id=1, source_target_pairs={{0,16},{16,0},{1,17},{17,1},{2,18},{18,2},{3,19},{19,3},{4,20},{20... | collective-permute-start | bytes 1179656 | tf_op jit(solution)/shard_map/ppermute | solution.py:51
  69.2 2.8 %all-to-all-done.3 = f32[8,48,128]{2,1,0:T(8,128)S(1)} async-done(((f32[8,48,128]{2,1,0:T(8,128)}), f32[8,48,128]{2,1,0:T(8,128)S(1)}, u32[]{:S(2)}, u32[]{:S(2)}) %all-to-all-start.3) | async-done | bytes 196640 | tf_op jit(solution)/shard_map/all_to_all | solution.py:43
  72.0 0.8 broadcast_in_dim.6
  72.8 5.1 %all-to-all-start.4 = ((f32[16,48,128]{2,1,0:T(8,128)}), f32[16,48,128]{2,1,0:T(8,128)S(1)}, u32[]{:S(2)}, u32[]{:S(2)}) async-start(f32[16,48,128]{2,1,0:T(8,128)} %broadcast_in_dim.6), calls=%async_computation.4 | async-start | bytes 786432 | tf_op jit(solution)/shard_map/all_to_all | solution.py:43
  77.9 1.9 %collective-permute-done.8.refs_8_ = f32[2,4,96,128]{3,2,1,0:T(8,128)S(1)} collective-permute-done((f32[2,4,96,128]{3,2,1,0:T(8,128)S(1)}, f32[2,4,96,128]{3,2,1,0:T(8,128)S(1)}, u32[]{:S(2)}, u32[]{:S(2)}) %collective-permute-start.8) | collective-permute-done | bytes 393248 | tf_op jit(solution)/shard_map/ppermute | solution.py:51
  79.8 6.1 %all-to-all-done.4.refs_4_ = f32[16,48,128]{2,1,0:T(8,128)S(1)} async-done(((f32[16,48,128]{2,1,0:T(8,128)}), f32[16,48,128]{2,1,0:T(8,128)S(1)}, u32[]{:S(2)}, u32[]{:S(2)}) %all-to-all-start.4) | async-done | bytes 393248 | tf_op jit(solution)/shard_map/all_to_all | solution.py:43
  85.9 7.7 %shard_map.84 = (f32[16,48,128]{2,1,0:T(8,128)}, f32[4,2,48,256]{3,2,1,0:T(8,128)}, f32[4,2,48,256]{3,2,1,0:T(8,128)}) custom-call(s32[1,14]{1,0:T(1,128)} %refs_0_.4, s32[1,14]{1,0:T(1,128)} %copy-done.5, s32[1,14]{1,0:T(1,128)} %copy-done.6, s32[1,14]{1,0:T(1,128)} %copy-done.7, f32[16,48,128]{2,1,0:T(8,128)S(1)} %all-to-all-done.4.refs_4_, ...), custom_call_target="tpu_custom_call" | custom-call | tf_op jit(solution)/shard_map/pallas_call | solution.py:72
  93.6 3.7 %all-to-all-start.5 = ((f32[16,48,128]{2,1,0:T(8,128)}), f32[16,48,128]{2,1,0:T(8,128)S(1)}, u32[]{:S(2)}, u32[]{:S(2)}) async-start(f32[16,48,128]{2,1,0:T(8,128)} %get-tuple-element.50), calls=%async_computation.5 | async-start | bytes 786432 | tf_op jit(solution)/shard_map/all_to_all | solution.py:43
  97.3 2.9 %collective-permute-start.9 = (f32[4,2,48,256]{3,2,1,0:T(8,128)}, f32[4,2,48,256]{3,2,1,0:T(8,128)S(1)}, u32[]{:S(2)}, u32[]{:S(2)}) collective-permute-start(f32[4,2,48,256]{3,2,1,0:T(8,128)} %get-tuple-element.53), channel_id=1, source_target_pairs={{0,16},{16,0},{1,17},{17,1},{2,18},{18,2},{3,19},{19,3},{4,20},{20... | collective-permute-start | bytes 1179656 | tf_op jit(solution)/shard_map/ppermute | solution.py:51
  100.2 5.3 %all-to-all-done.5 = f32[16,48,128]{2,1,0:T(8,128)S(1)} async-done(((f32[16,48,128]{2,1,0:T(8,128)}), f32[16,48,128]{2,1,0:T(8,128)S(1)}, u32[]{:S(2)}, u32[]{:S(2)}) %all-to-all-start.5) | async-done | bytes 393248 | tf_op jit(solution)/shard_map/all_to_all | solution.py:43
  106.2 3.4 %all-to-all-start.6 = ((f32[8,48,128]{2,1,0:T(8,128)}), f32[8,48,128]{2,1,0:T(8,128)S(1)}, u32[]{:S(2)}, u32[]{:S(2)}) async-start(f32[8,48,128]{2,1,0:T(8,128)} %broadcast_in_dim.7), calls=%async_computation.6 | async-start | bytes 393216 | tf_op jit(solution)/shard_map/all_to_all | solution.py:43
  109.6 2.1 %collective-permute-done.9.refs_9_ = f32[4,2,48,256]{3,2,1,0:T(8,128)S(1)} collective-permute-done((f32[4,2,48,256]{3,2,1,0:T(8,128)}, f32[4,2,48,256]{3,2,1,0:T(8,128)S(1)}, u32[]{:S(2)}, u32[]{:S(2)}) %collective-permute-start.9) | collective-permute-done | bytes 393248 | tf_op jit(solution)/shard_map/ppermute | solution.py:51
  111.7 3.4 %all-to-all-done.6.refs_4_ = f32[8,48,128]{2,1,0:T(8,128)S(1)} async-done(((f32[8,48,128]{2,1,0:T(8,128)}), f32[8,48,128]{2,1,0:T(8,128)S(1)}, u32[]{:S(2)}, u32[]{:S(2)}) %all-to-all-start.6) | async-done | bytes 196640 | tf_op jit(solution)/shard_map/all_to_all | solution.py:43
  115.1 4.5 %shard_map.85 = (f32[8,48,512]{2,1,0:T(8,128)}, f32[2,4,48,256]{3,2,1,0:T(8,128)}, f32[2,4,48,256]{3,2,1,0:T(8,128)}) custom-call(s32[1,14]{1,0:T(1,128)} %refs_0_.4, s32[1,14]{1,0:T(1,128)} %copy-done.5, s32[1,14]{1,0:T(1,128)} %copy-done.6, s32[1,14]{1,0:T(1,128)} %copy-done.7, f32[8,48,128]{2,1,0:T(8,128)S(1)} %all-to-all-done.6.refs_4_, ...), custom_call_target="tpu_custom_call" | custom-call | tf_op jit(solution)/shard_map/pallas_call | solution.py:72
  119.6 3.6 %all-to-all-start.7 = ((f32[8,48,512]{2,1,0:T(8,128)}), f32[8,48,512]{2,1,0:T(8,128)S(1)}, u32[]{:S(2)}, u32[]{:S(2)}) async-start(f32[8,48,512]{2,1,0:T(8,128)} %get-tuple-element.54), calls=%async_computation.7 | async-start | bytes 1572864 | tf_op jit(solution)/shard_map/all_to_all | solution.py:43
  123.2 1.4 collective-permute-start.10
  124.5 7.0 %all-to-all-done.7.refs_4_ = f32[8,48,512]{2,1,0:T(8,128)S(1)} async-done(((f32[8,48,512]{2,1,0:T(8,128)}), f32[8,48,512]{2,1,0:T(8,128)S(1)}, u32[]{:S(2)}, u32[]{:S(2)}) %all-to-all-start.7) | async-done | bytes 786464 | tf_op jit(solution)/shard_map/all_to_all | solution.py:43
  131.5 3.4 %shard_map.86 = (f32[8,48,256]{2,1,0:T(8,128)S(1)}, f32[4,48,256]{2,1,0:T(8,128)}) custom-call(s32[1,14]{1,0:T(1,128)} %refs_0_.4, s32[1,14]{1,0:T(1,128)} %copy-done.5, s32[1,14]{1,0:T(1,128)} %copy-done.6, s32[1,14]{1,0:T(1,128)} %copy-done.7, f32[8,48,512]{2,1,0:T(8,128)S(1)} %all-to-all-done.7.refs_4_, ...), custom_call_target="tpu_custom_call" | custom-call | tf_op jit(solution)/shard_map/pallas_call | solution.py:72
  135.0 5.0 %collective-permute-done.10.other_ref = f32[2,4,48,256]{3,2,1,0:T(8,128)S(1)} collective-permute-done((f32[2,4,48,256]{3,2,1,0:T(8,128)}, f32[2,4,48,256]{3,2,1,0:T(8,128)S(1)}, u32[]{:S(2)}, u32[]{:S(2)}) %collective-permute-start.10) | collective-permute-done | bytes 393248 | tf_op jit(solution)/shard_map/ppermute | solution.py:51
  139.9 15.4 %all_to_all.50.received_ref = f32[8,48,256]{2,1,0:T(8,128)S(1)} all-to-all(f32[8,48,256]{2,1,0:T(8,128)S(1)} %get-tuple-element.58), channel_id=1, replica_groups=mesh['z'=4,'y1'=2,'y0'=2,'c'=2,'x'=4] {'x','c'}, dimensions={0} | all-to-all | bytes 786432 | tf_op jit(solution)/shard_map/all_to_all | solution.py:43
  155.3 1.6 shard_map.87
  157.0 13.8 %all_to_all.51.received_ref = f32[4,96,512]{2,1,0:T(8,128)S(1)} all-to-all(f32[4,96,512]{2,1,0:T(8,128)S(1)} %shard_map.87), channel_id=1, replica_groups=mesh['z'=4,'y1'=2,'y0'=2,'c'=2,'x'=4] {'x'}, dimensions={0} | all-to-all | bytes 1572864 | tf_op jit(solution)/shard_map/all_to_all | solution.py:43
  170.8 2.0 %collective-permute-start.11 = (f32[96,512]{1,0:T(8,128)S(1)}, f32[96,512]{1,0:T(8,128)S(1)}, u32[]{:S(2)}, u32[]{:S(2)}) collective-permute-start(f32[96,512]{1,0:T(8,128)S(1)} %shard_map.88.total_ref), channel_id=1, source_target_pairs={{0,4},{4,0},{1,5},{5,1},{2,6},{6,2},{3,7},{7,3},{8,12},{12,8},{9,1... | collective-permute-start | bytes 589832 | tf_op jit(solution)/shard_map/ppermute | solution.py:47
  172.7 1.1 collective-permute-done.11.beside_ref
  (31 shorter events, 3.3 us)
Async XLA Ops:
  0.0 2.7 %collective-permute-start = (f32[96,512]{1,0:T(8,128)}, f32[96,512]{1,0:T(8,128)S(1)}, u32[]{:S(2)}, u32[]{:S(2)}) collective-permute-start(f32[96,512]{1,0:T(8,128)} %bitcast.15), channel_id=1, source_target_pairs={{0,4},{4,0},{1,5},{5,1},{2,6},{6,2},{3,7},{7,3},{8,12},{12,8},{9,1... | collective-permute-start | bytes 589832 | tf_op jit(solution)/shard_map/ppermute | solution.py:47
  4.6 26.2 %collective-permute-start.7 = (f32[128,7680]{1,0:T(8,128)}, f32[128,7680]{1,0:T(8,128)}, u32[]{:S(2)}, u32[]{:S(2)}) collective-permute-start(f32[128,7680]{1,0:T(8,128)} %bitcast.7), channel_id=1, source_target_pairs={{0,4},{4,0},{1,5},{5,1},{2,6},{6,2},{3,7},{7,3},{8,12},{12,8},{9,1... | collective-permute-start | bytes 11796488 | tf_op jit(solution)/shard_map/ppermute | solution.py:47
  4.9 16.1 %all-to-all-start = ((f32[4,96,512]{2,1,0:T(8,128)}), f32[4,96,512]{2,1,0:T(8,128)S(1)}, u32[]{:S(2)}, u32[]{:S(2)}) async-start(f32[4,96,512]{2,1,0:T(8,128)} %shard_map.73.refs_1_), calls=%async_computation | async-start | bytes 1572864 | tf_op jit(solution)/shard_map/all_to_all | solution.py:43
  9.1 19.6 %collective-permute-start.5 = (f32[128,1792]{1,0:T(8,128)}, f32[128,1792]{1,0:T(8,128)S(1)}, u32[]{:S(2)}, u32[]{:S(2)}) collective-permute-start(f32[128,1792]{1,0:T(8,128)} %bitcast.11), channel_id=1, source_target_pairs={{0,4},{4,0},{1,5},{5,1},{2,6},{6,2},{3,7},{7,3},{8,12},{12,8},{9,1... | collective-permute-start | bytes 2752520 | tf_op jit(solution)/shard_map/ppermute | solution.py:47
  10.5 6.3 %collective-permute-start.1 = (f32[2,512]{1,0:T(2,128)S(1)}, f32[2,512]{1,0:T(2,128)S(1)}, u32[]{:S(2)}, u32[]{:S(2)}) collective-permute-start(f32[2,512]{1,0:T(2,128)S(1)} %shard_map.74.factors_ref.refs_5_), channel_id=1, source_target_pairs={{0,4},{4,0},{1,5},{5,1},{2,6},{6,2},{3,7},{7,3},{8,12},{12,8},{9,1... | collective-permute-start | bytes 12296 | tf_op jit(solution)/shard_map/ppermute | solution.py:47
  10.7 4.1 %collective-permute-start.2 = (s32[1,14]{1,0:T(1,128)}, s32[1,14]{1,0:T(1,128)S(1)}, u32[]{:S(2)}, u32[]{:S(2)}) collective-permute-start(s32[1,14]{1,0:T(1,128)} %refs_0_.4), channel_id=1, source_target_pairs={{0,8},{4,20},{8,0},{12,28},{16,24},{20,4},{24,16},{28,12},{1,9},{5... | collective-permute-start | bytes 176 | tf_op jit(solution)/shard_map/ppermute | solution.py:519
  13.6 3.2 %collective-permute-start.3 = (s32[1,14]{1,0:T(1,128)}, s32[1,14]{1,0:T(1,128)S(1)}, u32[]{:S(2)}, u32[]{:S(2)}) collective-permute-start(s32[1,14]{1,0:T(1,128)} %refs_0_.4), channel_id=1, source_target_pairs={{0,4},{4,0},{1,5},{5,1},{2,6},{6,2},{3,7},{7,3},{8,12},{12,8},{9,1... | collective-permute-start | bytes 176 | tf_op jit(solution)/shard_map/ppermute | solution.py:47
  14.8 7.6 %copy-start.5 = (s32[1,14]{1,0:T(1,128)}, s32[1,14]{1,0:T(1,128)S(1)}, u32[]{:S(2)}) copy-start(s32[1,14]{1,0:T(1,128)S(1)} %collective-permute-done.2.refs_1_) | copy-start | bytes 172
  14.8 2.0 %collective-permute-start.4 = (s32[1,14]{1,0:T(1,128)S(1)}, s32[1,14]{1,0:T(1,128)S(1)}, u32[]{:S(2)}, u32[]{:S(2)}) collective-permute-start(s32[1,14]{1,0:T(1,128)S(1)} %collective-permute-done.2.refs_1_), channel_id=1, source_target_pairs={{0,4},{4,0},{1,5},{5,1},{2,6},{6,2},{3,7},{7,3},{8,12},{12,8},{9,1... | collective-permute-start | bytes 176 | tf_op jit(solution)/shard_map/ppermute | solution.py:47
  16.8 16.2 %copy-start.6 = (s32[1,14]{1,0:T(1,128)}, s32[1,14]{1,0:T(1,128)S(1)}, u32[]{:S(2)}) copy-start(s32[1,14]{1,0:T(1,128)S(1)} %collective-permute-done.3.refs_2_) | copy-start | bytes 172
  16.8 16.2 %copy-start.7 = (s32[1,14]{1,0:T(1,128)}, s32[1,14]{1,0:T(1,128)S(1)}, u32[]{:S(2)}) copy-start(s32[1,14]{1,0:T(1,128)S(1)} %collective-permute-done.4.refs_3_) | copy-start | bytes 172
  22.4 14.3 %collective-permute-start.6 = (f32[4,96,256]{2,1,0:T(8,128)}, f32[4,96,256]{2,1,0:T(8,128)S(1)}, u32[]{:S(2)}, u32[]{:S(2)}) collective-permute-start(f32[4,96,256]{2,1,0:T(8,128)} %get-tuple-element.43.refs_9_.refs_8_), channel_id=1, source_target_pairs={{0,8},{8,0},{1,9},{9,1},{2,10},{10,2},{3,11},{11,3},{4,12},{12,4},... | collective-permute-start | bytes 1179656 | tf_op jit(solution)/shard_map/ppermute | solution.py:51
  23.7 12.9 %all-to-all-start.1 = ((f32[8,48,256]{2,1,0:T(8,128)}), f32[8,48,256]{2,1,0:T(8,128)S(1)}, u32[]{:S(2)}, u32[]{:S(2)}) async-start(f32[8,48,256]{2,1,0:T(8,128)} %get-tuple-element.39.refs_2_), calls=%async_computation.1 | async-start | bytes 786432 | tf_op jit(solution)/shard_map/all_to_all | solution.py:43
  28.7 1.0 copy-start
  36.6 0.7 copy-start.1
  42.0 16.1 %all-to-all-start.2 = ((f32[8,48,512]{2,1,0:T(8,128)}), f32[8,48,512]{2,1,0:T(8,128)S(1)}, u32[]{:S(2)}, u32[]{:S(2)}) async-start(f32[8,48,512]{2,1,0:T(8,128)} %get-tuple-element.45.refs_2_), calls=%async_computation.2 | async-start | bytes 1572864 | tf_op jit(solution)/shard_map/all_to_all | solution.py:43
  51.1 15.3 %copy-start.2 = (f32[2,4,96,128]{3,2,1,0:T(8,128)S(1)}, f32[2,4,96,128]{3,2,1,0:T(8,128)}, u32[]{:S(2)}) copy-start(f32[2,4,96,128]{3,2,1,0:T(8,128)} %get-tuple-element.48.refs_7_) | copy-start | bytes 1179652
  63.0 9.0 %all-to-all-start.3 = ((f32[8,48,128]{2,1,0:T(8,128)}), f32[8,48,128]{2,1,0:T(8,128)S(1)}, u32[]{:S(2)}, u32[]{:S(2)}) async-start(f32[8,48,128]{2,1,0:T(8,128)} %get-tuple-element.47), calls=%async_computation.3 | async-start | bytes 393216 | tf_op jit(solution)/shard_map/all_to_all | solution.py:43
  66.5 13.4 %collective-permute-start.8 = (f32[2,4,96,128]{3,2,1,0:T(8,128)S(1)}, f32[2,4,96,128]{3,2,1,0:T(8,128)S(1)}, u32[]{:S(2)}, u32[]{:S(2)}) collective-permute-start(f32[2,4,96,128]{3,2,1,0:T(8,128)S(1)} %copy-done.2), channel_id=1, source_target_pairs={{0,16},{16,0},{1,17},{17,1},{2,18},{18,2},{3,19},{19,3},{4,20},{20... | collective-permute-start | bytes 1179656 | tf_op jit(solution)/shard_map/ppermute | solution.py:51
  72.8 13.1 %all-to-all-start.4 = ((f32[16,48,128]{2,1,0:T(8,128)}), f32[16,48,128]{2,1,0:T(8,128)S(1)}, u32[]{:S(2)}, u32[]{:S(2)}) async-start(f32[16,48,128]{2,1,0:T(8,128)} %broadcast_in_dim.6), calls=%async_computation.4 | async-start | bytes 786432 | tf_op jit(solution)/shard_map/all_to_all | solution.py:43
  79.8 6.1 %copy-start.3 = (f32[2,4,96,128]{3,2,1,0:T(8,128)}, f32[2,4,96,128]{3,2,1,0:T(8,128)S(1)}, u32[]{:S(2)}) copy-start(f32[2,4,96,128]{3,2,1,0:T(8,128)S(1)} %collective-permute-done.8.refs_8_) | copy-start | bytes 1179652
  93.6 11.9 %all-to-all-start.5 = ((f32[16,48,128]{2,1,0:T(8,128)}), f32[16,48,128]{2,1,0:T(8,128)S(1)}, u32[]{:S(2)}, u32[]{:S(2)}) async-start(f32[16,48,128]{2,1,0:T(8,128)} %get-tuple-element.50), calls=%async_computation.5 | async-start | bytes 786432 | tf_op jit(solution)/shard_map/all_to_all | solution.py:43
  97.3 14.4 %collective-permute-start.9 = (f32[4,2,48,256]{3,2,1,0:T(8,128)}, f32[4,2,48,256]{3,2,1,0:T(8,128)S(1)}, u32[]{:S(2)}, u32[]{:S(2)}) collective-permute-start(f32[4,2,48,256]{3,2,1,0:T(8,128)} %get-tuple-element.53), channel_id=1, source_target_pairs={{0,16},{16,0},{1,17},{17,1},{2,18},{18,2},{3,19},{19,3},{4,20},{20... | collective-permute-start | bytes 1179656 | tf_op jit(solution)/shard_map/ppermute | solution.py:51
  106.2 8.9 %all-to-all-start.6 = ((f32[8,48,128]{2,1,0:T(8,128)}), f32[8,48,128]{2,1,0:T(8,128)S(1)}, u32[]{:S(2)}, u32[]{:S(2)}) async-start(f32[8,48,128]{2,1,0:T(8,128)} %broadcast_in_dim.7), calls=%async_computation.6 | async-start | bytes 393216 | tf_op jit(solution)/shard_map/all_to_all | solution.py:43
  111.7 3.4 %copy-start.4 = (f32[4,2,48,256]{3,2,1,0:T(8,128)}, f32[4,2,48,256]{3,2,1,0:T(8,128)S(1)}, u32[]{:S(2)}) copy-start(f32[4,2,48,256]{3,2,1,0:T(8,128)S(1)} %collective-permute-done.9.refs_9_) | copy-start | bytes 1179652
  119.6 11.9 %all-to-all-start.7 = ((f32[8,48,512]{2,1,0:T(8,128)}), f32[8,48,512]{2,1,0:T(8,128)S(1)}, u32[]{:S(2)}, u32[]{:S(2)}) async-start(f32[8,48,512]{2,1,0:T(8,128)} %get-tuple-element.54), calls=%async_computation.7 | async-start | bytes 1572864 | tf_op jit(solution)/shard_map/all_to_all | solution.py:43
  123.2 16.7 %collective-permute-start.10 = (f32[2,4,48,256]{3,2,1,0:T(8,128)}, f32[2,4,48,256]{3,2,1,0:T(8,128)S(1)}, u32[]{:S(2)}, u32[]{:S(2)}) collective-permute-start(f32[2,4,48,256]{3,2,1,0:T(8,128)} %get-tuple-element.57), channel_id=1, source_target_pairs={{0,8},{8,0},{1,9},{9,1},{2,10},{10,2},{3,11},{11,3},{4,12},{12,4},... | collective-permute-start | bytes 1179656 | tf_op jit(solution)/shard_map/ppermute | solution.py:51
  170.8 3.0 %collective-permute-start.11 = (f32[96,512]{1,0:T(8,128)S(1)}, f32[96,512]{1,0:T(8,128)S(1)}, u32[]{:S(2)}, u32[]{:S(2)}) collective-permute-start(f32[96,512]{1,0:T(8,128)S(1)} %shard_map.88.total_ref), channel_id=1, source_target_pairs={{0,4},{4,0},{1,5},{5,1},{2,6},{6,2},{3,7},{7,3},{8,12},{12,8},{9,1... | collective-permute-start | bytes 589832 | tf_op jit(solution)/shard_map/ppermute | solution.py:47

commit v8 on v6

--- a/solution.py
+++ b/solution.py
@@ -28,7 +28,9 @@
     def dot(a, b):
         return lax.dot_general(a, b, dims, preferred_element_type=jnp.float32)
 
-    return dot(left_high, high) + (dot(left_high, low) + dot(left_low, high))
+    both = dot(jnp.concatenate([left_high, left_low], 0), high)
+    rows = left.shape[0]
+    return both[:rows] + (dot(left_high, low) + both[rows:])
 
 
 def dot_full(left, right):
@@ -249,7 +251,7 @@
     blocks = (2, 4, 8)[level - 1]
     n_sides = len(sides)
     n_updates = 1 if level < 3 else 0
-    n_outs = (3, 2, 3)[level - 1]
+    n_outs = (2, 2, 3)[level - 1]
 
     def body(*refs):
         refs = list(refs)
@@ -289,12 +291,6 @@
         columns = moves.chunks(weights_far, weights_ref)
         if level < 3:
             part_ref = refs[0]
-        if level == 1:
-            passing_ref = refs[1]
-            passing = [
-                moves.start(sides_refs[1 + flip].at[:, :, pl.ds(PIVOTS, PIVOTS)], passing_ref.at[flip])
-                for flip in range(2)
-            ]
         totals = [None, None]
         for child in range(2):
             if level == 1:
@@ -319,9 +315,6 @@
         if level < 3:
             own_ref[...] = weighted
             leaving.append(moves.start(own_ref, outs[1]))
-            if level == 1:
-                finish(passing)
-                leaving.append(moves.start(passing_ref, outs[2]))
             for k in range(update_len // 256):
                 at = slice(k * 256, (k + 1) * 256)
                 part_ref[:, at] = product(solved, updates_ref[0][0, :, at], updates_ref[0][1, :, at], 0)
@@ -347,7 +340,7 @@
         finish(leaving)
 
     outs = {
-        1: [(8, HALF, 512), (HALF, 256), (2, 4, SIDES, PIVOTS)],
+        1: [(8, HALF, 512), (HALF, 256)],
         2: [(8, HALF, BLOCK), (HALF, 256)],
         3: [(16, HALF, BLOCK), (4, 2, HALF, 256), (4, 2, HALF, 256)],
     }[level]
@@ -364,8 +357,6 @@
     ]
     if level < 3:
         scratch.append(pltpu.VMEM((HALF, update_len), jnp.float32))
-    if level == 1:
-        scratch.append(pltpu.VMEM((2, 4, SIDES, PIVOTS), jnp.float32))
     return call(body, outs, operands, specs, scratch, spaces="H" * n_outs)
 
 
@@ -416,7 +407,8 @@
         for child in range(2):
             for k in range(blocks):
                 where = block_at(child_block(level, tables_refs, child, k))
-                pieces_ref[child, :, k * BLOCK : (k + 1) * BLOCK] = x_ref[:, where]
+                at = slice(k * BLOCK, (k + 1) * BLOCK)
+                pieces_ref[child, :, at] = x_ref[:, where]
             for x in range(4):
                 leaving.append(moves.start(pieces_ref.at[child], outs[0].at[x * 2 + child]))
         if level == 1:
@@ -473,7 +465,7 @@
         [(4, SIDES, 512)],
         [received, *map(far, [weighted, nearest, kept]), other, close(weights), close(updates)],
         [WHOLE] * 7,
-        spaces="h",
+        spaces="v",
     )[0]
 
 
@@ -528,20 +520,22 @@
     partner_update = with_partner(update_after)
     (weights0,) = prepared([inverse], [(0, 512, None)], packed)
     (updates0,) = prepared([update], [(0, 256, None)], packed)
-    tables = sibling_tables(update_targets)
+    first, partner_factors, *tables = lax.optimization_barrier(
+        (first, partner_factors, *sibling_tables(update_targets))
+    )
 
     sent, weighted0, sides1, near = level_zero_forward(first, weights0, updates0, factors)
     beyond = across(near, "y0")
     received = exchange(sent, ("c", "x"))
     (weights1,) = prepared([inverse, partner_inverse], [(512, 1024, 512)], sent)
     (updates1,) = prepared([update, partner_update], [(256, 512, None)], sent)
-    sent, weighted1, near3 = forward(
-        1, received, [sides1, near, beyond], tables, weights1, updates1, factors, partner_factors
-    )
+    sent, weighted1 = forward(1, received, [sides1], tables, weights1, updates1, factors, partner_factors)
+    sent, beyond = lax.optimization_barrier((sent, beyond))
     weights2, weights3 = prepared([inverse, partner_inverse], [(1536, 2048, 512), (3584, 4096, 512)], sent)
     (updates2,) = prepared([update, partner_update], [(768, 1024, None)], sent)
+    received = exchange(sent, pair)
+    near3, _ = lax.optimization_barrier((jnp.stack([near[:, :, PIVOTS:], beyond[:, :, PIVOTS:]]), sent))
     beyond3 = across(near3, "y1")
-    received = exchange(sent, pair)
     sent, weighted2 = forward(2, received, [near, beyond], tables, weights2, updates2, factors, partner_factors)
     received = exchange(summed_copies(exchange(sent, pair), 16), plane)
     sent, kept3, other3 = forward(3, received, [near3, beyond3], tables, weights3, None, factors, partner_factors)

time: 181 us -> 173 us (0.956)
  Pallas kernels: 47.9 us -> 43.9 us
  starting transfers between devices: 60.4 us -> 58 us
    pallas_call x11, Pallas kernels: 35.7 us -> 31.7 us  [call(): pl.pallas_call(body, in_specs=specs, out_specs=[FAR if k == 'H' else WHOL...]
    ppermute x1, waiting for transfers between devices: 3.05 us -> 1.14 us  [sibling_tables(): side = lax.ppermute(targets, ('y1', 'y0', 'c'), pairs)]
  transfers between devices with their start and end apart: 21 -> 21, of which waited for: 13 -> 14; matrix products, arithmetic and copies ran while one was open for 1% -> 1% of each run, Pallas kernels for 10% -> 13%
where the time goes in v8:
time: 173 us; the launch traced here: 171 us
  starting transfers between devices  58 us (34%)
  waiting for transfers between devices  53 us (31%)
  Pallas kernels  43.9 us (25%)
  blocking collectives  13.6 us (8%)
  local copies, waits for them, and re-layouts  2.49 us (1%)
    all_to_all x9, waiting for transfers between devices, exchange(): return lax.all_to_all(value, axes, 0, 0, tiled=True)  45.4 us
    all_to_all x9, starting transfers between devices, exchange(): return lax.all_to_all(value, axes, 0, 0, tiled=True)  42.3 us
    pallas_call x11, Pallas kernels, call(): pl.pallas_call(body, in_specs=specs, out_specs=[FAR if k == 'H' else WHOL...  31.7 us
    all_to_all x1, blocking collectives, exchange(): return lax.all_to_all(value, axes, 0, 0, tiled=True)  13.6 us
    pallas_call x6, Pallas kernels, prepared(): pl.pallas_call(body, in_specs=[FAR] * (len(pair) + 1), out_specs=[WHOLE]...  12.2 us
    ppermute x4, starting transfers between devices, across(): return lax.ppermute(value, axis, [(0, 1), (1, 0)])  8.31 us
    ppermute x7, starting transfers between devices, with_partner(): return lax.ppermute(value, 'c', [(0, 1), (1, 0)])  4.56 us
    ppermute x4, waiting for transfers between devices, across(): return lax.ppermute(value, axis, [(0, 1), (1, 0)])  4.16 us
  transfers between devices with their start and end apart: 21, of which 14 were waited for; matrix products, arithmetic and copies ran while one was open for 1% of the time, Pallas kernels for 13%

profile of v8, /device:TPU:1, one launch (start us, length us, event | category | flops | bytes accessed | tf_op | source)
XLA Modules:
  0.0 171.5 jit_solution(17823530144774927634)
XLA Ops:
  0.0 1.4 collective-permute-start
  1.4 1.3 collective-permute-done.beside_ref
  2.7 1.9 %shard_map.73.refs_1_ = f32[4,96,512]{2,1,0:T(8,128)} custom-call(f32[96,512]{1,0:T(8,128)} %bitcast.20, f32[96,512]{1,0:T(8,128)S(1)} %collective-permute-done.beside_ref), custom_call_target="tpu_custom_call" | custom-call | tf_op jit(solution)/shard_map/pallas_call | solution.py:72
  4.9 4.1 %all-to-all-start = ((f32[4,96,512]{2,1,0:T(8,128)}), f32[4,96,512]{2,1,0:T(8,128)S(1)}, u32[]{:S(2)}, u32[]{:S(2)}) async-start(f32[4,96,512]{2,1,0:T(8,128)} %shard_map.73.refs_1_), calls=%async_computation | async-start | bytes 1572864 | tf_op jit(solution)/shard_map/all_to_all | solution.py:43
  9.5 1.1 shard_map.74.factors_ref.refs_5_
  10.7 2.9 %collective-permute-start.2 = (s32[1,14]{1,0:T(1,128)}, s32[1,14]{1,0:T(1,128)S(1)}, u32[]{:S(2)}, u32[]{:S(2)}) collective-permute-start(s32[1,14]{1,0:T(1,128)} %refs_0_.4), channel_id=1, source_target_pairs={{0,8},{4,20},{8,0},{12,28},{16,24},{20,4},{24,16},{28,12},{1,9},{5... | collective-permute-start | bytes 176 | tf_op jit(solution)/shard_map/ppermute | solution.py:503
  13.6 1.1 collective-permute-done.2.refs_1_
  14.8 1.0 shard_map.75.weights_ref
  15.8 0.9 shard_map.76.updates_ref
  16.8 4.2 %all-to-all-done.first_ref = f32[4,96,512]{2,1,0:T(8,128)S(1)} async-done(((f32[4,96,512]{2,1,0:T(8,128)}), f32[4,96,512]{2,1,0:T(8,128)S(1)}, u32[]{:S(2)}, u32[]{:S(2)}) %all-to-all-start) | async-done | bytes 786464 | tf_op jit(solution)/shard_map/all_to_all | solution.py:43
  21.0 1.3 shard_map.77
  22.4 1.4 collective-permute-start.7
  23.7 4.9 %all-to-all-start.1 = ((f32[8,48,256]{2,1,0:T(8,128)}), f32[8,48,256]{2,1,0:T(8,128)S(1)}, u32[]{:S(2)}, u32[]{:S(2)}) async-start(f32[8,48,256]{2,1,0:T(8,128)} %get-tuple-element.39.refs_2_), calls=%async_computation.1 | async-start | bytes 786432 | tf_op jit(solution)/shard_map/all_to_all | solution.py:43
  28.7 0.9 copy-done
  29.6 1.1 shard_map.78.refs_7_.refs_5_
  30.7 2.3 %shard_map.79.refs_9_.refs_7_ = bf16[2,2,256,512]{3,2,1,0:T(8,128)(2,1)} custom-call(f32[128,7680]{1,0:T(8,128)} %bitcast.13, f32[128,7680]{1,0:T(8,128)} %collective-permute-done.6.refs_1_, f32[8,48,256]{2,1,0:T(8,128)} %get-tuple-element.39.refs_2_), custom_call_target="tpu_custom_call" | custom-call | tf_op jit(solution)/shard_map/pallas_call | solution.py:116
  33.1 3.5 %all-to-all-done.1.refs_4_ = f32[8,48,256]{2,1,0:T(8,128)S(1)} async-done(((f32[8,48,256]{2,1,0:T(8,128)}), f32[8,48,256]{2,1,0:T(8,128)S(1)}, u32[]{:S(2)}, u32[]{:S(2)}) %all-to-all-start.1) | async-done | bytes 393248 | tf_op jit(solution)/shard_map/all_to_all | solution.py:43
  36.6 4.5 %shard_map.80 = (f32[8,48,512]{2,1,0:T(8,128)}, f32[48,256]{1,0:T(8,128)}) custom-call(s32[1,14]{1,0:T(1,128)} %refs_0_.4, s32[1,14]{1,0:T(1,128)} %copy-done.7, s32[1,14]{1,0:T(1,128)} %copy-done.8, s32[1,14]{1,0:T(1,128)} %copy-done.9, f32[8,48,256]{2,1,0:T(8,128)S(1)} %all-to-all-done.1.refs_4_, f32[2,512]{1,0:T(2,128)S(1)} %shard_map.74.factors_ref.refs_5_, ...), custom_call_target="tpu_custom_call" | custom-call | tf_op jit(solution)/shard_map/pallas_call | solution.py:72
  41.1 3.6 %all-to-all-start.2 = ((f32[8,48,512]{2,1,0:T(8,128)}), f32[8,48,512]{2,1,0:T(8,128)S(1)}, u32[]{:S(2)}, u32[]{:S(2)}) async-start(f32[8,48,512]{2,1,0:T(8,128)} %get-tuple-element.46.refs_2_), calls=%async_computation.2 | async-start | bytes 1572864 | tf_op jit(solution)/shard_map/all_to_all | solution.py:43
  44.7 5.6 %shard_map.82 = (bf16[4,2,256,512]{3,2,1,0:T(8,128)(2,1)}, bf16[8,2,256,512]{3,2,1,0:T(8,128)(2,1)}) custom-call(f32[128,7680]{1,0:T(8,128)} %bitcast.14, f32[128,7680]{1,0:T(8,128)} %collective-permute-done.6.refs_1_, f32[8,48,512]{2,1,0:T(8,128)} %get-tuple-element.46.refs_2_), custom_call_target="tpu_custom_call" | custom-call | tf_op jit(solution)/shard_map/pallas_call | solution.py:116
  50.3 1.3 shard_map.81.refs_7_.refs_5_
  51.6 5.6 %all-to-all-done.2.refs_4_ = f32[8,48,512]{2,1,0:T(8,128)S(1)} async-done(((f32[8,48,512]{2,1,0:T(8,128)}), f32[8,48,512]{2,1,0:T(8,128)S(1)}, u32[]{:S(2)}, u32[]{:S(2)}) %all-to-all-start.2) | async-done | bytes 786464 | tf_op jit(solution)/shard_map/all_to_all | solution.py:43
  57.2 4.9 %shard_map.83 = (f32[8,48,128]{2,1,0:T(8,128)}, f32[48,256]{1,0:T(8,128)}) custom-call(s32[1,14]{1,0:T(1,128)} %refs_0_.4, s32[1,14]{1,0:T(1,128)} %copy-done.7, s32[1,14]{1,0:T(1,128)} %copy-done.8, s32[1,14]{1,0:T(1,128)} %copy-done.9, f32[8,48,512]{2,1,0:T(8,128)S(1)} %all-to-all-done.2.refs_4_, f32[2,512]{1,0:T(2,128)S(1)} %shard_map.74.factors_ref.refs_5_, ...), custom_call_target="tpu_custom_call" | custom-call | tf_op jit(solution)/shard_map/pallas_call | solution.py:72
  62.2 3.4 %all-to-all-start.3 = ((f32[8,48,128]{2,1,0:T(8,128)}), f32[8,48,128]{2,1,0:T(8,128)S(1)}, u32[]{:S(2)}, u32[]{:S(2)}) async-start(f32[8,48,128]{2,1,0:T(8,128)} %get-tuple-element.49), calls=%async_computation.3 | async-start | bytes 393216 | tf_op jit(solution)/shard_map/all_to_all | solution.py:43
  65.7 2.7 %collective-permute-start.8 = (f32[2,4,96,128]{3,2,1,0:T(8,128)S(1)}, f32[2,4,96,128]{3,2,1,0:T(8,128)S(1)}, u32[]{:S(2)}, u32[]{:S(2)}) collective-permute-start(f32[2,4,96,128]{3,2,1,0:T(8,128)S(1)} %pad_maximum_fusion.refs_7_), channel_id=1, source_target_pairs={{0,16},{16,0},{1,17},{17,1},{2,18},{18,2},{3,19},{19,3},{4,20},{20... | collective-permute-start | bytes 1179656 | tf_op jit(solution)/shard_map/ppermute | solution.py:51
  68.4 2.8 %all-to-all-done.3 = f32[8,48,128]{2,1,0:T(8,128)S(1)} async-done(((f32[8,48,128]{2,1,0:T(8,128)}), f32[8,48,128]{2,1,0:T(8,128)S(1)}, u32[]{:S(2)}, u32[]{:S(2)}) %all-to-all-start.3) | async-done | bytes 196640 | tf_op jit(solution)/shard_map/all_to_all | solution.py:43
  71.2 0.8 broadcast_in_dim.6
  72.0 5.1 %all-to-all-start.4 = ((f32[16,48,128]{2,1,0:T(8,128)}), f32[16,48,128]{2,1,0:T(8,128)S(1)}, u32[]{:S(2)}, u32[]{:S(2)}) async-start(f32[16,48,128]{2,1,0:T(8,128)} %broadcast_in_dim.6), calls=%async_computation.4 | async-start | bytes 786432 | tf_op jit(solution)/shard_map/all_to_all | solution.py:43
  77.1 2.0 %collective-permute-done.8.refs_8_ = f32[2,4,96,128]{3,2,1,0:T(8,128)S(1)} collective-permute-done((f32[2,4,96,128]{3,2,1,0:T(8,128)S(1)}, f32[2,4,96,128]{3,2,1,0:T(8,128)S(1)}, u32[]{:S(2)}, u32[]{:S(2)}) %collective-permute-start.8) | collective-permute-done | bytes 393248 | tf_op jit(solution)/shard_map/ppermute | solution.py:51
  79.1 6.0 %all-to-all-done.4.refs_4_ = f32[16,48,128]{2,1,0:T(8,128)S(1)} async-done(((f32[16,48,128]{2,1,0:T(8,128)}), f32[16,48,128]{2,1,0:T(8,128)S(1)}, u32[]{:S(2)}, u32[]{:S(2)}) %all-to-all-start.4) | async-done | bytes 393248 | tf_op jit(solution)/shard_map/all_to_all | solution.py:43
  85.1 7.6 %shard_map.84 = (f32[16,48,128]{2,1,0:T(8,128)}, f32[4,2,48,256]{3,2,1,0:T(8,128)}, f32[4,2,48,256]{3,2,1,0:T(8,128)}) custom-call(s32[1,14]{1,0:T(1,128)} %refs_0_.4, s32[1,14]{1,0:T(1,128)} %copy-done.7, s32[1,14]{1,0:T(1,128)} %copy-done.8, s32[1,14]{1,0:T(1,128)} %copy-done.9, f32[16,48,128]{2,1,0:T(8,128)S(1)} %all-to-all-done.4.refs_4_, ...), custom_call_target="tpu_custom_call" | custom-call | tf_op jit(solution)/shard_map/pallas_call | solution.py:72
  92.7 3.7 %all-to-all-start.5 = ((f32[16,48,128]{2,1,0:T(8,128)}), f32[16,48,128]{2,1,0:T(8,128)S(1)}, u32[]{:S(2)}, u32[]{:S(2)}) async-start(f32[16,48,128]{2,1,0:T(8,128)} %get-tuple-element.52), calls=%async_computation.5 | async-start | bytes 786432 | tf_op jit(solution)/shard_map/all_to_all | solution.py:43
  96.4 2.9 %collective-permute-start.9 = (f32[4,2,48,256]{3,2,1,0:T(8,128)}, f32[4,2,48,256]{3,2,1,0:T(8,128)S(1)}, u32[]{:S(2)}, u32[]{:S(2)}) collective-permute-start(f32[4,2,48,256]{3,2,1,0:T(8,128)} %get-tuple-element.55), channel_id=1, source_target_pairs={{0,16},{16,0},{1,17},{17,1},{2,18},{18,2},{3,19},{19,3},{4,20},{20... | collective-permute-start | bytes 1179656 | tf_op jit(solution)/shard_map/ppermute | solution.py:51
  99.3 5.3 %all-to-all-done.5 = f32[16,48,128]{2,1,0:T(8,128)S(1)} async-done(((f32[16,48,128]{2,1,0:T(8,128)}), f32[16,48,128]{2,1,0:T(8,128)S(1)}, u32[]{:S(2)}, u32[]{:S(2)}) %all-to-all-start.5) | async-done | bytes 393248 | tf_op jit(solution)/shard_map/all_to_all | solution.py:43
  105.2 3.4 %all-to-all-start.6 = ((f32[8,48,128]{2,1,0:T(8,128)}), f32[8,48,128]{2,1,0:T(8,128)S(1)}, u32[]{:S(2)}, u32[]{:S(2)}) async-start(f32[8,48,128]{2,1,0:T(8,128)} %broadcast_in_dim.7), calls=%async_computation.6 | async-start | bytes 393216 | tf_op jit(solution)/shard_map/all_to_all | solution.py:43
  108.6 2.1 %collective-permute-done.9.refs_9_ = f32[4,2,48,256]{3,2,1,0:T(8,128)S(1)} collective-permute-done((f32[4,2,48,256]{3,2,1,0:T(8,128)}, f32[4,2,48,256]{3,2,1,0:T(8,128)S(1)}, u32[]{:S(2)}, u32[]{:S(2)}) %collective-permute-start.9) | collective-permute-done | bytes 393248 | tf_op jit(solution)/shard_map/ppermute | solution.py:51
  110.8 3.4 %all-to-all-done.6.refs_4_ = f32[8,48,128]{2,1,0:T(8,128)S(1)} async-done(((f32[8,48,128]{2,1,0:T(8,128)}), f32[8,48,128]{2,1,0:T(8,128)S(1)}, u32[]{:S(2)}, u32[]{:S(2)}) %all-to-all-start.6) | async-done | bytes 196640 | tf_op jit(solution)/shard_map/all_to_all | solution.py:43
  114.1 4.5 %shard_map.85 = (f32[8,48,512]{2,1,0:T(8,128)}, f32[2,4,48,256]{3,2,1,0:T(8,128)}, f32[2,4,48,256]{3,2,1,0:T(8,128)}) custom-call(s32[1,14]{1,0:T(1,128)} %refs_0_.4, s32[1,14]{1,0:T(1,128)} %copy-done.7, s32[1,14]{1,0:T(1,128)} %copy-done.8, s32[1,14]{1,0:T(1,128)} %copy-done.9, f32[8,48,128]{2,1,0:T(8,128)S(1)} %all-to-all-done.6.refs_4_, ...), custom_call_target="tpu_custom_call" | custom-call | tf_op jit(solution)/shard_map/pallas_call | solution.py:72
  118.6 3.6 %all-to-all-start.7 = ((f32[8,48,512]{2,1,0:T(8,128)}), f32[8,48,512]{2,1,0:T(8,128)S(1)}, u32[]{:S(2)}, u32[]{:S(2)}) async-start(f32[8,48,512]{2,1,0:T(8,128)} %get-tuple-element.56), calls=%async_computation.7 | async-start | bytes 1572864 | tf_op jit(solution)/shard_map/all_to_all | solution.py:43
  122.2 1.4 collective-permute-start.10
  123.6 7.0 %all-to-all-done.7.refs_4_ = f32[8,48,512]{2,1,0:T(8,128)S(1)} async-done(((f32[8,48,512]{2,1,0:T(8,128)}), f32[8,48,512]{2,1,0:T(8,128)S(1)}, u32[]{:S(2)}, u32[]{:S(2)}) %all-to-all-start.7) | async-done | bytes 786464 | tf_op jit(solution)/shard_map/all_to_all | solution.py:43
  130.5 3.5 %shard_map.86 = (f32[8,48,256]{2,1,0:T(8,128)}, f32[4,48,256]{2,1,0:T(8,128)}) custom-call(s32[1,14]{1,0:T(1,128)} %refs_0_.4, s32[1,14]{1,0:T(1,128)} %copy-done.7, s32[1,14]{1,0:T(1,128)} %copy-done.8, s32[1,14]{1,0:T(1,128)} %copy-done.9, f32[8,48,512]{2,1,0:T(8,128)S(1)} %all-to-all-done.7.refs_4_, bf16[2,256,512]{2,1,0:T(8,128)(2,1)S(1)} %shard_map.78.refs_7_.refs_5_, ...), custom_call_target="tpu_custom_call" | custom-call | tf_op jit(solution)/shard_map/pallas_call | solution.py:72
  134.1 10.5 %all-to-all-start.8 = ((f32[8,48,256]{2,1,0:T(8,128)}), f32[8,48,256]{2,1,0:T(8,128)S(1)}, u32[]{:S(2)}, u32[]{:S(2)}) async-start(f32[8,48,256]{2,1,0:T(8,128)} %get-tuple-element.58), calls=%async_computation.8 | async-start | bytes 786432 | tf_op jit(solution)/shard_map/all_to_all | solution.py:43
  144.6 7.7 %all-to-all-done.8.received_ref = f32[8,48,256]{2,1,0:T(8,128)S(1)} async-done(((f32[8,48,256]{2,1,0:T(8,128)}), f32[8,48,256]{2,1,0:T(8,128)S(1)}, u32[]{:S(2)}, u32[]{:S(2)}) %all-to-all-start.8) | async-done | bytes 393248 | tf_op jit(solution)/shard_map/all_to_all | solution.py:43
  152.3 1.6 shard_map.87
  153.9 13.6 %all_to_all.50.received_ref = f32[4,96,512]{2,1,0:T(8,128)S(1)} all-to-all(f32[4,96,512]{2,1,0:T(8,128)S(1)} %shard_map.87), channel_id=1, replica_groups=mesh['z'=4,'y1'=2,'y0'=2,'c'=2,'x'=4] {'x'}, dimensions={0} | all-to-all | bytes 1572864 | tf_op jit(solution)/shard_map/all_to_all | solution.py:43
  167.6 2.2 %collective-permute-start.11 = (f32[96,512]{1,0:T(8,128)S(1)}, f32[96,512]{1,0:T(8,128)S(1)}, u32[]{:S(2)}, u32[]{:S(2)}) collective-permute-start(f32[96,512]{1,0:T(8,128)S(1)} %shard_map.88.total_ref), channel_id=1, source_target_pairs={{0,4},{4,0},{1,5},{5,1},{2,6},{6,2},{3,7},{7,3},{8,12},{12,8},{9,1... | collective-permute-start | bytes 589832 | tf_op jit(solution)/shard_map/ppermute | solution.py:47
  169.7 1.1 collective-permute-done.11.beside_ref
  (39 shorter events, 2.6 us)
Async XLA Ops:
  0.0 2.7 %collective-permute-start = (f32[96,512]{1,0:T(8,128)}, f32[96,512]{1,0:T(8,128)S(1)}, u32[]{:S(2)}, u32[]{:S(2)}) collective-permute-start(f32[96,512]{1,0:T(8,128)} %bitcast.19), channel_id=1, source_target_pairs={{0,4},{4,0},{1,5},{5,1},{2,6},{6,2},{3,7},{7,3},{8,12},{12,8},{9,1... | collective-permute-start | bytes 589832 | tf_op jit(solution)/shard_map/ppermute | solution.py:47
  4.6 26.2 %collective-permute-start.6 = (f32[128,7680]{1,0:T(8,128)}, f32[128,7680]{1,0:T(8,128)}, u32[]{:S(2)}, u32[]{:S(2)}) collective-permute-start(f32[128,7680]{1,0:T(8,128)} %bitcast.11), channel_id=1, source_target_pairs={{0,4},{4,0},{1,5},{5,1},{2,6},{6,2},{3,7},{7,3},{8,12},{12,8},{9,1... | collective-permute-start | bytes 11796488 | tf_op jit(solution)/shard_map/ppermute | solution.py:47
  4.9 16.1 %all-to-all-start = ((f32[4,96,512]{2,1,0:T(8,128)}), f32[4,96,512]{2,1,0:T(8,128)S(1)}, u32[]{:S(2)}, u32[]{:S(2)}) async-start(f32[4,96,512]{2,1,0:T(8,128)} %shard_map.73.refs_1_), calls=%async_computation | async-start | bytes 1572864 | tf_op jit(solution)/shard_map/all_to_all | solution.py:43
  9.1 19.6 %collective-permute-start.5 = (f32[128,1792]{1,0:T(8,128)}, f32[128,1792]{1,0:T(8,128)S(1)}, u32[]{:S(2)}, u32[]{:S(2)}) collective-permute-start(f32[128,1792]{1,0:T(8,128)} %bitcast.15), channel_id=1, source_target_pairs={{0,4},{4,0},{1,5},{5,1},{2,6},{6,2},{3,7},{7,3},{8,12},{12,8},{9,1... | collective-permute-start | bytes 2752520 | tf_op jit(solution)/shard_map/ppermute | solution.py:47
  10.5 6.3 %collective-permute-start.1 = (f32[2,512]{1,0:T(2,128)S(1)}, f32[2,512]{1,0:T(2,128)S(1)}, u32[]{:S(2)}, u32[]{:S(2)}) collective-permute-start(f32[2,512]{1,0:T(2,128)S(1)} %shard_map.74.factors_ref.refs_5_), channel_id=1, source_target_pairs={{0,4},{4,0},{1,5},{5,1},{2,6},{6,2},{3,7},{7,3},{8,12},{12,8},{9,1... | collective-permute-start | bytes 12296 | tf_op jit(solution)/shard_map/ppermute | solution.py:47
  10.7 4.1 %collective-permute-start.2 = (s32[1,14]{1,0:T(1,128)}, s32[1,14]{1,0:T(1,128)S(1)}, u32[]{:S(2)}, u32[]{:S(2)}) collective-permute-start(s32[1,14]{1,0:T(1,128)} %refs_0_.4), channel_id=1, source_target_pairs={{0,8},{4,20},{8,0},{12,28},{16,24},{20,4},{24,16},{28,12},{1,9},{5... | collective-permute-start | bytes 176 | tf_op jit(solution)/shard_map/ppermute | solution.py:503
  13.6 3.2 %collective-permute-start.3 = (s32[1,14]{1,0:T(1,128)}, s32[1,14]{1,0:T(1,128)S(1)}, u32[]{:S(2)}, u32[]{:S(2)}) collective-permute-start(s32[1,14]{1,0:T(1,128)} %refs_0_.4), channel_id=1, source_target_pairs={{0,4},{4,0},{1,5},{5,1},{2,6},{6,2},{3,7},{7,3},{8,12},{12,8},{9,1... | collective-permute-start | bytes 176 | tf_op jit(solution)/shard_map/ppermute | solution.py:47
  14.8 7.6 %copy-start.7 = (s32[1,14]{1,0:T(1,128)}, s32[1,14]{1,0:T(1,128)S(1)}, u32[]{:S(2)}) copy-start(s32[1,14]{1,0:T(1,128)S(1)} %collective-permute-done.2.refs_1_) | copy-start | bytes 172
  14.8 2.0 %collective-permute-start.4 = (s32[1,14]{1,0:T(1,128)S(1)}, s32[1,14]{1,0:T(1,128)S(1)}, u32[]{:S(2)}, u32[]{:S(2)}) collective-permute-start(s32[1,14]{1,0:T(1,128)S(1)} %collective-permute-done.2.refs_1_), channel_id=1, source_target_pairs={{0,4},{4,0},{1,5},{5,1},{2,6},{6,2},{3,7},{7,3},{8,12},{12,8},{9,1... | collective-permute-start | bytes 176 | tf_op jit(solution)/shard_map/ppermute | solution.py:47
  16.8 16.3 %copy-start.8 = (s32[1,14]{1,0:T(1,128)}, s32[1,14]{1,0:T(1,128)S(1)}, u32[]{:S(2)}) copy-start(s32[1,14]{1,0:T(1,128)S(1)} %collective-permute-done.3.refs_2_) | copy-start | bytes 172
  16.8 16.3 %copy-start.9 = (s32[1,14]{1,0:T(1,128)}, s32[1,14]{1,0:T(1,128)S(1)}, u32[]{:S(2)}) copy-start(s32[1,14]{1,0:T(1,128)S(1)} %collective-permute-done.4.refs_3_) | copy-start | bytes 172
  22.4 18.8 %collective-permute-start.7 = (f32[4,96,256]{2,1,0:T(8,128)}, f32[4,96,256]{2,1,0:T(8,128)S(1)}, u32[]{:S(2)}, u32[]{:S(2)}) collective-permute-start(f32[4,96,256]{2,1,0:T(8,128)} %get-tuple-element.45.refs_8_), channel_id=1, source_target_pairs={{0,8},{8,0},{1,9},{9,1},{2,10},{10,2},{3,11},{11,3},{4,12},{12,4},... | collective-permute-start | bytes 1179656 | tf_op jit(solution)/shard_map/ppermute | solution.py:51
  23.7 12.9 %all-to-all-start.1 = ((f32[8,48,256]{2,1,0:T(8,128)}), f32[8,48,256]{2,1,0:T(8,128)S(1)}, u32[]{:S(2)}, u32[]{:S(2)}) async-start(f32[8,48,256]{2,1,0:T(8,128)} %get-tuple-element.39.refs_2_), calls=%async_computation.1 | async-start | bytes 786432 | tf_op jit(solution)/shard_map/all_to_all | solution.py:43
  28.7 0.9 copy-start
  30.7 14.0 %copy-start.4 = (f32[4,96,256]{2,1,0:T(8,128)S(1)}, f32[4,96,256]{2,1,0:T(8,128)}, u32[]{:S(2)}) copy-start(f32[4,96,256]{2,1,0:T(8,128)} %get-tuple-element.45.refs_8_) | copy-start | bytes 1179652
  41.1 9.2 %copy-start.2 = (f32[4,96,256]{2,1,0:T(8,128)}, f32[4,96,256]{2,1,0:T(8,128)S(1)}, u32[]{:S(2)}) copy-start(f32[4,96,256]{2,1,0:T(8,128)S(1)} %collective-permute-done.7.refs_9_) | copy-start | bytes 1179652
  41.1 16.1 %all-to-all-start.2 = ((f32[8,48,512]{2,1,0:T(8,128)}), f32[8,48,512]{2,1,0:T(8,128)S(1)}, u32[]{:S(2)}, u32[]{:S(2)}) async-start(f32[8,48,512]{2,1,0:T(8,128)} %get-tuple-element.46.refs_2_), calls=%async_computation.2 | async-start | bytes 1572864 | tf_op jit(solution)/shard_map/all_to_all | solution.py:43
  51.6 14.0 %copy-start.3 = (f32[4,96,256]{2,1,0:T(8,128)S(1)}, f32[4,96,256]{2,1,0:T(8,128)}, u32[]{:S(2)}) copy-start(f32[4,96,256]{2,1,0:T(8,128)} %copy-done.2) | copy-start | bytes 1179652
  62.2 9.0 %all-to-all-start.3 = ((f32[8,48,128]{2,1,0:T(8,128)}), f32[8,48,128]{2,1,0:T(8,128)S(1)}, u32[]{:S(2)}, u32[]{:S(2)}) async-start(f32[8,48,128]{2,1,0:T(8,128)} %get-tuple-element.49), calls=%async_computation.3 | async-start | bytes 393216 | tf_op jit(solution)/shard_map/all_to_all | solution.py:43
  65.7 19.4 %copy-start.1 = (f32[2,4,96,128]{3,2,1,0:T(8,128)}, f32[2,4,96,128]{3,2,1,0:T(8,128)S(1)}, u32[]{:S(2)}) copy-start(f32[2,4,96,128]{3,2,1,0:T(8,128)S(1)} %pad_maximum_fusion.refs_7_) | copy-start | bytes 1179652
  65.7 13.4 %collective-permute-start.8 = (f32[2,4,96,128]{3,2,1,0:T(8,128)S(1)}, f32[2,4,96,128]{3,2,1,0:T(8,128)S(1)}, u32[]{:S(2)}, u32[]{:S(2)}) collective-permute-start(f32[2,4,96,128]{3,2,1,0:T(8,128)S(1)} %pad_maximum_fusion.refs_7_), channel_id=1, source_target_pairs={{0,16},{16,0},{1,17},{17,1},{2,18},{18,2},{3,19},{19,3},{4,20},{20... | collective-permute-start | bytes 1179656 | tf_op jit(solution)/shard_map/ppermute | solution.py:51
  72.0 13.1 %all-to-all-start.4 = ((f32[16,48,128]{2,1,0:T(8,128)}), f32[16,48,128]{2,1,0:T(8,128)S(1)}, u32[]{:S(2)}, u32[]{:S(2)}) async-start(f32[16,48,128]{2,1,0:T(8,128)} %broadcast_in_dim.6), calls=%async_computation.4 | async-start | bytes 786432 | tf_op jit(solution)/shard_map/all_to_all | solution.py:43
  79.1 6.0 %copy-start.5 = (f32[2,4,96,128]{3,2,1,0:T(8,128)}, f32[2,4,96,128]{3,2,1,0:T(8,128)S(1)}, u32[]{:S(2)}) copy-start(f32[2,4,96,128]{3,2,1,0:T(8,128)S(1)} %collective-permute-done.8.refs_8_) | copy-start | bytes 1179652
  92.7 11.8 %all-to-all-start.5 = ((f32[16,48,128]{2,1,0:T(8,128)}), f32[16,48,128]{2,1,0:T(8,128)S(1)}, u32[]{:S(2)}, u32[]{:S(2)}) async-start(f32[16,48,128]{2,1,0:T(8,128)} %get-tuple-element.52), calls=%async_computation.5 | async-start | bytes 786432 | tf_op jit(solution)/shard_map/all_to_all | solution.py:43
  96.4 14.4 %collective-permute-start.9 = (f32[4,2,48,256]{3,2,1,0:T(8,128)}, f32[4,2,48,256]{3,2,1,0:T(8,128)S(1)}, u32[]{:S(2)}, u32[]{:S(2)}) collective-permute-start(f32[4,2,48,256]{3,2,1,0:T(8,128)} %get-tuple-element.55), channel_id=1, source_target_pairs={{0,16},{16,0},{1,17},{17,1},{2,18},{18,2},{3,19},{19,3},{4,20},{20... | collective-permute-start | bytes 1179656 | tf_op jit(solution)/shard_map/ppermute | solution.py:51
  105.2 8.9 %all-to-all-start.6 = ((f32[8,48,128]{2,1,0:T(8,128)}), f32[8,48,128]{2,1,0:T(8,128)S(1)}, u32[]{:S(2)}, u32[]{:S(2)}) async-start(f32[8,48,128]{2,1,0:T(8,128)} %broadcast_in_dim.7), calls=%async_computation.6 | async-start | bytes 393216 | tf_op jit(solution)/shard_map/all_to_all | solution.py:43
  110.8 3.4 %copy-start.6 = (f32[4,2,48,256]{3,2,1,0:T(8,128)}, f32[4,2,48,256]{3,2,1,0:T(8,128)S(1)}, u32[]{:S(2)}) copy-start(f32[4,2,48,256]{3,2,1,0:T(8,128)S(1)} %collective-permute-done.9.refs_9_) | copy-start | bytes 1179652
  118.6 11.9 %all-to-all-start.7 = ((f32[8,48,512]{2,1,0:T(8,128)}), f32[8,48,512]{2,1,0:T(8,128)S(1)}, u32[]{:S(2)}, u32[]{:S(2)}) async-start(f32[8,48,512]{2,1,0:T(8,128)} %get-tuple-element.56), calls=%async_computation.7 | async-start | bytes 1572864 | tf_op jit(solution)/shard_map/all_to_all | solution.py:43
  122.2 22.4 %collective-permute-start.10 = (f32[2,4,48,256]{3,2,1,0:T(8,128)}, f32[2,4,48,256]{3,2,1,0:T(8,128)S(1)}, u32[]{:S(2)}, u32[]{:S(2)}) collective-permute-start(f32[2,4,48,256]{3,2,1,0:T(8,128)} %get-tuple-element.62), channel_id=1, source_target_pairs={{0,8},{8,0},{1,9},{9,1},{2,10},{10,2},{3,11},{11,3},{4,12},{12,4},... | collective-permute-start | bytes 1179656 | tf_op jit(solution)/shard_map/ppermute | solution.py:51
  134.1 18.2 %all-to-all-start.8 = ((f32[8,48,256]{2,1,0:T(8,128)}), f32[8,48,256]{2,1,0:T(8,128)S(1)}, u32[]{:S(2)}, u32[]{:S(2)}) async-start(f32[8,48,256]{2,1,0:T(8,128)} %get-tuple-element.58), calls=%async_computation.8 | async-start | bytes 786432 | tf_op jit(solution)/shard_map/all_to_all | solution.py:43
  167.6 3.2 %collective-permute-start.11 = (f32[96,512]{1,0:T(8,128)S(1)}, f32[96,512]{1,0:T(8,128)S(1)}, u32[]{:S(2)}, u32[]{:S(2)}) collective-permute-start(f32[96,512]{1,0:T(8,128)S(1)} %shard_map.88.total_ref), channel_id=1, source_target_pairs={{0,4},{4,0},{1,5},{5,1},{2,6},{6,2},{3,7},{7,3},{8,12},{12,8},{9,1... | collective-permute-start | bytes 589832 | tf_op jit(solution)/shard_map/ppermute | solution.py:47

commit v9 on v8

--- a/solution.py
+++ b/solution.py
@@ -6,7 +6,7 @@
 from jax.experimental.pallas import tpu as pltpu
 from jax.sharding import Mesh, PartitionSpec as P
 
-LEVELS = 4
+
 BLOCK = 128
 PIVOTS = 128
 SIDES = 96
@@ -155,19 +155,30 @@
     return call(body, [(2, diagonal.shape[1])], operands, [WHOLE] * 3, spaces="v")[0]
 
 
-def packed_sides(sides, beside):
-    def body(sides_ref, beside_ref, out_ref):
+def gathered_sides(own, other):
+    def body(own_ref, other_ref, one_ref, near_ref):
         c = lax.axis_index("c")
-        mine = pl.ds(pl.multiple_of(c * HALF, 8), HALF)
-        theirs = pl.ds(pl.multiple_of((1 - c) * HALF, 8), HALF)
-        own = sides_ref[mine, PIVOTS:]
-        other = beside_ref[mine, PIVOTS:]
-        for i in range(4):
-            out_ref[i, :, :PIVOTS] = sides_ref[:, :PIVOTS]
-            out_ref[i, mine, PIVOTS:] = own
-            out_ref[i, theirs, PIVOTS:] = other
-
-    return call(body, [(4, SIDES, 512)], [far(sides), beside], [WHOLE] * 2, spaces="h")[0]
+        for rows, source in ((c, own_ref), (1 - c, other_ref)):
+            place = pl.ds(pl.multiple_of(rows * HALF, 8), HALF)
+            for x in range(4):
+                one_ref[x, place] = source[x, :, :PIVOTS]
+                near_ref[x, place] = source[x, :, PIVOTS:]
+
+    return call(body, [(4, SIDES, PIVOTS), (4, SIDES, 256)], [far(own), other], [WHOLE] * 2, spaces="hh")
+
+
+def upper_answers(nearest, kept, other):
+    def body(nearest_ref, kept_ref, other_ref, own_ref, give_ref):
+        c = lax.axis_index("c")
+        for core, out in ((c, own_ref), (1 - c, give_ref)):
+            at = block_at(core)
+            for x in range(4):
+                out[x, :, :PIVOTS] = nearest_ref[x, :, at]
+                for i in range(2):
+                    piece = kept_ref[i, x, :, at] + other_ref[i, x, :, at]
+                    out[x, :, (1 + i) * PIVOTS : (2 + i) * PIVOTS] = piece
+
+    return call(body, [(4, HALF, 384)] * 2, [far(nearest), far(kept), other], [WHOLE] * 3, spaces="hh")
 
 
 class Moves:
@@ -191,12 +202,13 @@
 
 def level_zero_forward(first, weights, updates, factors):
     def body(first_ref, weights_ref, updates_ref, factors_ref, *refs):
-        sent_ref, weighted_ref, one_ref, upper_ref, part_ref, own_ref, semaphores = refs
+        sent_ref, weighted_ref, keep_ref, give_ref, part_ref, own_ref, semaphores = refs
         moves = Moves(semaphores)
-        leaving = [
-            moves.start(first_ref.at[:, :, pl.ds(PIVOTS, PIVOTS)], one_ref),
-            moves.start(first_ref.at[:, :, pl.ds(2 * PIVOTS, 2 * PIVOTS)], upper_ref),
-        ]
+        core = lax.axis_index("c")
+        leaving = []
+        for half, out in ((core, keep_ref), (1 - core, give_ref)):
+            rows = pl.ds(pl.multiple_of(half * HALF, 8), HALF)
+            leaving.append(moves.start(first_ref.at[:, rows, pl.ds(PIVOTS, 3 * PIVOTS)], out))
         gathered = jnp.concatenate([first_ref[q, :, :PIVOTS] for q in range(4)], 1)
         solved = product(gathered, weights_ref[0], weights_ref[1], 1)
         part_ref[...] = product(solved, updates_ref[0], updates_ref[1], 0)
@@ -209,7 +221,7 @@
 
     return call(
         body,
-        [(8, HALF, 256), (SIDES, PIVOTS), (4, SIDES, PIVOTS), (4, SIDES, 256)],
+        [(8, HALF, 256), (SIDES, PIVOTS), (4, HALF, 384), (4, HALF, 384)],
         [close(first), close(weights), close(updates), close(factors)],
         [WHOLE] * 4,
         [
@@ -234,13 +246,8 @@
 
 
 def both_factors(level, factors, beside):
-    c = lax.axis_index("c")
     at = slice(level * PIVOTS, (level + 1) * PIVOTS)
     return [jnp.concatenate([factors[i : i + 1, at], beside[i : i + 1, at]], 1) for i in range(2)]
-
-
-def halves(rows):
-    return jnp.concatenate([rows[:HALF], rows[HALF:]], 1)
 
 
 def forward(level, received, sides, tables, weights, updates, factors, partner_factors):
@@ -268,7 +275,7 @@
         outs = take(n_outs)
         semaphores, b_ref, own_ref, weights_ref = take(4)
         moves = Moves(semaphores)
-        x0, y0, y1 = lax.axis_index("x"), lax.axis_index("y0"), lax.axis_index("y1")
+        y0, y1 = lax.axis_index("y0"), lax.axis_index("y1")
 
         arriving, leaving = [], []
 
@@ -444,16 +451,13 @@
     return call(body, outs, operands, specs, scratch, spaces="H" * n_outs)
 
 
-def level_zero_backward(received, weighted, weights, updates, nearest, kept, other):
-    def body(received_ref, weighted_ref, nearest_ref, kept_ref, other_ref, weights_ref, updates_ref, sent_ref):
-        for x in range(4):
-            for c in range(2):
-                half = slice(c * HALF, (c + 1) * HALF)
-                at = slice(c * PIVOTS, (c + 1) * PIVOTS)
-                sent_ref[x, half, PIVOTS : 2 * PIVOTS] = nearest_ref[x, :, at]
-                for i in range(2):
-                    piece = kept_ref[i, x, :, at] + other_ref[i, x, :, at]
-                    sent_ref[x, half, (2 + i) * PIVOTS : (3 + i) * PIVOTS] = piece
+def level_zero_backward(received, weighted, weights, updates, own, other):
+    def body(received_ref, weighted_ref, own_ref, other_ref, weights_ref, updates_ref, sent_ref):
+        core = lax.axis_index("c")
+        for half, source in ((core, own_ref), (1 - core, other_ref)):
+            place = pl.ds(pl.multiple_of(half * HALF, 8), HALF)
+            for x in range(4):
+                sent_ref[x, place, PIVOTS:] = source[x]
         chosen = jnp.concatenate([sum(received_ref[x * 2 + c] for x in range(4)) for c in range(2)], 0)
         target = weighted_ref[...] - product(chosen, updates_ref[0], updates_ref[1], 1)
         part = product(target, weights_ref[0], weights_ref[1], 0)
@@ -463,8 +467,8 @@
     return call(
         body,
         [(4, SIDES, 512)],
-        [received, *map(far, [weighted, nearest, kept]), other, close(weights), close(updates)],
-        [WHOLE] * 7,
+        [received, far(weighted), far(own), other, close(weights), close(updates)],
+        [WHOLE] * 6,
         spaces="v",
     )[0]
 
@@ -474,18 +478,6 @@
         out_ref[...] = (received_ref[0] + received_ref[1]) + (received_ref[2] + received_ref[3])
 
     return call(body, [(SIDES, 512)], [received], [WHOLE])[0]
-
-
-def unpacked(total, beside):
-    def body(total_ref, beside_ref, out_ref):
-        c = lax.axis_index("c")
-        mine = pl.ds(pl.multiple_of(c * HALF, 8), HALF)
-        theirs = pl.ds(pl.multiple_of((1 - c) * HALF, 8), HALF)
-        out_ref[:, :PIVOTS] = total_ref[:, :PIVOTS]
-        out_ref[mine, PIVOTS:] = total_ref[mine, PIVOTS:]
-        out_ref[theirs, PIVOTS:] = beside_ref[mine, PIVOTS:]
-
-    return call(body, [(SIDES, 512)], [total, beside], [WHOLE] * 2)[0]
 
 
 def summed_copies(received, count):
@@ -511,7 +503,7 @@
     plane = ("x", "y1", "y0")
     pair = ("x", "y0")
 
-    packed = packed_sides(sides, with_partner(sides))
+    packed = jnp.broadcast_to(sides[None], (4, *sides.shape))
     first = exchange(packed, ("x",))
     factors = pivot_factors(pivot_pairs[0], pivot_diagonal[0], pivot_coupling[0])
     partner_factors = with_partner(factors)
@@ -524,9 +516,11 @@
         (first, partner_factors, *sibling_tables(update_targets))
     )
 
-    sent, weighted0, sides1, near = level_zero_forward(first, weights0, updates0, factors)
+    sent, weighted0, keep, give = level_zero_forward(first, weights0, updates0, factors)
+    received = exchange(sent, ("c", "x"))
+    give = with_partner(give)
+    sides1, near = gathered_sides(keep, give)
     beyond = across(near, "y0")
-    received = exchange(sent, ("c", "x"))
     (weights1,) = prepared([inverse, partner_inverse], [(512, 1024, 512)], sent)
     (updates1,) = prepared([update, partner_update], [(256, 512, None)], sent)
     sent, weighted1 = forward(1, received, [sides1], tables, weights1, updates1, factors, partner_factors)
@@ -546,9 +540,9 @@
     received = exchange(sent, pair)
     sent, nearest = backward(1, received, weighted1, tables, weights1, updates1, [])
     received = exchange(sent, ("x", "c"))
-    sent = level_zero_backward(received, weighted0, weights0, updates0, nearest, kept, other)
-    total = summed(exchange(sent, ("x",)))
-    return unpacked(total, with_partner(total))[None, None]
+    keep, give = upper_answers(nearest, kept, other)
+    sent = level_zero_backward(received, weighted0, weights0, updates0, keep, with_partner(give))
+    return summed(exchange(sent, ("x",)))[None, None]
 
 
 def solution(mesh):
@@ -565,4 +559,5 @@
         P(leaf, "x", None),
     )
     out_specs = P(leaf, "x", None, None)
+
     return jax.shard_map(per_device, mesh=fine, in_specs=in_specs, out_specs=out_specs, check_vma=False)

time: 173 us -> 172 us (level)
  waiting for transfers between devices: 53 us -> 49.7 us
  local copies, waits for them, and re-layouts: 2.49 us -> 4.42 us
  Pallas kernels: 43.9 us -> 45.7 us
    all_to_all x9, waiting for transfers between devices: 45.4 us -> 41.5 us  [exchange(): return lax.all_to_all(value, axes, 0, 0, tiled=True)]
    broadcast_in_dim x0 -> x1, local copies, waits for them, and re-layouts: none -> 1.92 us  [per_device(): packed = jnp.broadcast_to(sides[None], (4, *sides.shape))]
    pallas_call x11, Pallas kernels: 31.7 us -> 33.5 us  [call(): pl.pallas_call(body, in_specs=specs, out_specs=[FAR if k == 'H' else WHOL...]
  transfers between devices with their start and end apart: 21 -> 21, of which waited for: 14 -> 14; matrix products, arithmetic and copies ran while one was open for 1% -> 1% of each run, Pallas kernels for 13% -> 16%
where the time goes in v9:
time: 172 us; the launch traced here: 170 us
  starting transfers between devices  56.3 us (33%)
  waiting for transfers between devices  49.7 us (29%)
  Pallas kernels  45.7 us (27%)
  blocking collectives  13.6 us (8%)
  local copies, waits for them, and re-layouts  4.42 us (3%)
    all_to_all x9, waiting for transfers between devices, exchange(): return lax.all_to_all(value, axes, 0, 0, tiled=True)  41.5 us
    all_to_all x9, starting transfers between devices, exchange(): return lax.all_to_all(value, axes, 0, 0, tiled=True)  41.4 us
    pallas_call x11, Pallas kernels, call(): pl.pallas_call(body, in_specs=specs, out_specs=[FAR if k == 'H' else WHOL...  33.5 us
    all_to_all x1, blocking collectives, exchange(): return lax.all_to_all(value, axes, 0, 0, tiled=True)  13.6 us
    pallas_call x6, Pallas kernels, prepared(): pl.pallas_call(body, in_specs=[FAR] * (len(pair) + 1), out_specs=[WHOLE]...  12.2 us
    ppermute x4, starting transfers between devices, across(): return lax.ppermute(value, axis, [(0, 1), (1, 0)])  8.22 us
    ppermute x4, waiting for transfers between devices, across(): return lax.ppermute(value, axis, [(0, 1), (1, 0)])  4.17 us
    ppermute x7, waiting for transfers between devices, with_partner(): return lax.ppermute(value, 'c', [(0, 1), (1, 0)])  4.03 us
  transfers between devices with their start and end apart: 21, of which 14 were waited for; matrix products, arithmetic and copies ran while one was open for 1% of the time, Pallas kernels for 16%

profile of v9, /device:TPU:1, one launch (start us, length us, event | category | flops | bytes accessed | tf_op | source)
XLA Modules:
  0.0 170.1 jit_solution(349440631613031389)
XLA Ops:
  0.0 1.9 %broadcast_in_dim.11.refs_1_ = f32[4,96,512]{2,1,0:T(8,128)} broadcast(f32[96,512]{1,0:T(8,128)} %bitcast.19), dimensions={1,2} | broadcast | bytes 983040 | tf_op jit(solution)/shard_map/broadcast_in_dim | solution.py:506
  1.9 1.4 collective-permute-start.6
  3.3 4.1 %all-to-all-start = ((f32[4,96,512]{2,1,0:T(8,128)}), f32[4,96,512]{2,1,0:T(8,128)S(1)}, u32[]{:S(2)}, u32[]{:S(2)}) async-start(f32[4,96,512]{2,1,0:T(8,128)} %broadcast_in_dim.11.refs_1_), calls=%async_computation | async-start | bytes 1572864 | tf_op jit(solution)/shard_map/all_to_all | solution.py:43
  7.7 1.1 shard_map.73.factors_ref.refs_5_
  9.1 2.9 %collective-permute-start.1 = (s32[1,14]{1,0:T(1,128)}, s32[1,14]{1,0:T(1,128)S(1)}, u32[]{:S(2)}, u32[]{:S(2)}) collective-permute-start(s32[1,14]{1,0:T(1,128)} %refs_0_.4), channel_id=1, source_target_pairs={{0,8},{4,20},{8,0},{12,28},{16,24},{20,4},{24,16},{28,12},{1,9},{5... | collective-permute-start | bytes 176 | tf_op jit(solution)/shard_map/ppermute | solution.py:495
  12.0 1.0 shard_map.74.weights_ref
  13.0 0.9 shard_map.75.updates_ref
  15.4 4.2 %all-to-all-done.first_ref = f32[4,96,512]{2,1,0:T(8,128)S(1)} async-done(((f32[4,96,512]{2,1,0:T(8,128)}), f32[4,96,512]{2,1,0:T(8,128)S(1)}, u32[]{:S(2)}, u32[]{:S(2)}) %all-to-all-start) | async-done | bytes 786464 | tf_op jit(solution)/shard_map/all_to_all | solution.py:43
  19.5 1.4 shard_map.76
  20.9 1.2 collective-permute-start.5
  22.1 1.4 collective-permute-done.5.other_ref
  23.6 1.8 %shard_map.78 = (f32[4,96,128]{2,1,0:T(8,128)}, f32[4,96,256]{2,1,0:T(8,128)}) custom-call(f32[4,48,384]{2,1,0:T(8,128)} %get-tuple-element.46.own_ref, f32[4,48,384]{2,1,0:T(8,128)S(1)} %collective-permute-done.5.other_ref), custom_call_target="tpu_custom_call" | custom-call | tf_op jit(solution)/shard_map/pallas_call | solution.py:72
  25.4 1.3 collective-permute-start.7
  26.7 4.0 %all-to-all-start.1 = ((f32[8,48,256]{2,1,0:T(8,128)}), f32[8,48,256]{2,1,0:T(8,128)S(1)}, u32[]{:S(2)}, u32[]{:S(2)}) async-start(f32[8,48,256]{2,1,0:T(8,128)} %get-tuple-element.43.refs_2_), calls=%async_computation.1 | async-start | bytes 786432 | tf_op jit(solution)/shard_map/all_to_all | solution.py:43
  30.7 1.0 copy-done
  31.7 1.1 shard_map.77.refs_7_.refs_5_
  32.8 2.3 %shard_map.79.refs_9_.refs_7_ = bf16[2,2,256,512]{3,2,1,0:T(8,128)(2,1)} custom-call(f32[128,7680]{1,0:T(8,128)} %bitcast.13, f32[128,7680]{1,0:T(8,128)} %collective-permute-done.6.refs_1_, f32[8,48,256]{2,1,0:T(8,128)} %get-tuple-element.43.refs_2_), custom_call_target="tpu_custom_call" | custom-call | tf_op jit(solution)/shard_map/pallas_call | solution.py:116
  35.1 3.5 %all-to-all-done.1.refs_4_ = f32[8,48,256]{2,1,0:T(8,128)S(1)} async-done(((f32[8,48,256]{2,1,0:T(8,128)}), f32[8,48,256]{2,1,0:T(8,128)S(1)}, u32[]{:S(2)}, u32[]{:S(2)}) %all-to-all-start.1) | async-done | bytes 393248 | tf_op jit(solution)/shard_map/all_to_all | solution.py:43
  38.7 4.5 %shard_map.80 = (f32[8,48,512]{2,1,0:T(8,128)}, f32[48,256]{1,0:T(8,128)}) custom-call(s32[1,14]{1,0:T(1,128)} %refs_0_.4, s32[1,14]{1,0:T(1,128)} %copy-done.7, s32[1,14]{1,0:T(1,128)} %copy-done.8, s32[1,14]{1,0:T(1,128)} %copy-done.9, f32[8,48,256]{2,1,0:T(8,128)S(1)} %all-to-all-done.1.refs_4_, f32[2,512]{1,0:T(2,128)S(1)} %shard_map.73.factors_ref.refs_5_, ...), custom_call_target="tpu_custom_call" | custom-call | tf_op jit(solution)/shard_map/pallas_call | solution.py:72
  43.2 3.6 %all-to-all-start.2 = ((f32[8,48,512]{2,1,0:T(8,128)}), f32[8,48,512]{2,1,0:T(8,128)S(1)}, u32[]{:S(2)}, u32[]{:S(2)}) async-start(f32[8,48,512]{2,1,0:T(8,128)} %get-tuple-element.52.refs_2_), calls=%async_computation.2 | async-start | bytes 1572864 | tf_op jit(solution)/shard_map/all_to_all | solution.py:43
  46.8 5.6 %shard_map.82 = (bf16[4,2,256,512]{3,2,1,0:T(8,128)(2,1)}, bf16[8,2,256,512]{3,2,1,0:T(8,128)(2,1)}) custom-call(f32[128,7680]{1,0:T(8,128)} %bitcast.14, f32[128,7680]{1,0:T(8,128)} %collective-permute-done.6.refs_1_, f32[8,48,512]{2,1,0:T(8,128)} %get-tuple-element.52.refs_2_), custom_call_target="tpu_custom_call" | custom-call | tf_op jit(solution)/shard_map/pallas_call | solution.py:116
  52.4 1.3 shard_map.81.refs_7_.refs_5_
  53.7 5.6 %all-to-all-done.2.refs_4_ = f32[8,48,512]{2,1,0:T(8,128)S(1)} async-done(((f32[8,48,512]{2,1,0:T(8,128)}), f32[8,48,512]{2,1,0:T(8,128)S(1)}, u32[]{:S(2)}, u32[]{:S(2)}) %all-to-all-start.2) | async-done | bytes 786464 | tf_op jit(solution)/shard_map/all_to_all | solution.py:43
  59.3 5.0 %shard_map.83 = (f32[8,48,128]{2,1,0:T(8,128)}, f32[48,256]{1,0:T(8,128)}) custom-call(s32[1,14]{1,0:T(1,128)} %refs_0_.4, s32[1,14]{1,0:T(1,128)} %copy-done.7, s32[1,14]{1,0:T(1,128)} %copy-done.8, s32[1,14]{1,0:T(1,128)} %copy-done.9, f32[8,48,512]{2,1,0:T(8,128)S(1)} %all-to-all-done.2.refs_4_, f32[2,512]{1,0:T(2,128)S(1)} %shard_map.73.factors_ref.refs_5_, ...), custom_call_target="tpu_custom_call" | custom-call | tf_op jit(solution)/shard_map/pallas_call | solution.py:72
  64.2 3.4 %all-to-all-start.3 = ((f32[8,48,128]{2,1,0:T(8,128)}), f32[8,48,128]{2,1,0:T(8,128)S(1)}, u32[]{:S(2)}, u32[]{:S(2)}) async-start(f32[8,48,128]{2,1,0:T(8,128)} %get-tuple-element.55), calls=%async_computation.3 | async-start | bytes 393216 | tf_op jit(solution)/shard_map/all_to_all | solution.py:43
  67.7 2.7 %collective-permute-start.8 = (f32[2,4,96,128]{3,2,1,0:T(8,128)S(1)}, f32[2,4,96,128]{3,2,1,0:T(8,128)S(1)}, u32[]{:S(2)}, u32[]{:S(2)}) collective-permute-start(f32[2,4,96,128]{3,2,1,0:T(8,128)S(1)} %pad_maximum_fusion.refs_7_), channel_id=1, source_target_pairs={{0,16},{16,0},{1,17},{17,1},{2,18},{18,2},{3,19},{19,3},{4,20},{20... | collective-permute-start | bytes 1179656 | tf_op jit(solution)/shard_map/ppermute | solution.py:51
  70.4 2.8 %all-to-all-done.3 = f32[8,48,128]{2,1,0:T(8,128)S(1)} async-done(((f32[8,48,128]{2,1,0:T(8,128)}), f32[8,48,128]{2,1,0:T(8,128)S(1)}, u32[]{:S(2)}, u32[]{:S(2)}) %all-to-all-start.3) | async-done | bytes 196640 | tf_op jit(solution)/shard_map/all_to_all | solution.py:43
  74.0 5.1 %all-to-all-start.4 = ((f32[16,48,128]{2,1,0:T(8,128)}), f32[16,48,128]{2,1,0:T(8,128)S(1)}, u32[]{:S(2)}, u32[]{:S(2)}) async-start(f32[16,48,128]{2,1,0:T(8,128)} %broadcast_in_dim.24), calls=%async_computation.4 | async-start | bytes 786432 | tf_op jit(solution)/shard_map/all_to_all | solution.py:43
  79.1 2.0 %collective-permute-done.8.refs_8_ = f32[2,4,96,128]{3,2,1,0:T(8,128)S(1)} collective-permute-done((f32[2,4,96,128]{3,2,1,0:T(8,128)S(1)}, f32[2,4,96,128]{3,2,1,0:T(8,128)S(1)}, u32[]{:S(2)}, u32[]{:S(2)}) %collective-permute-start.8) | collective-permute-done | bytes 393248 | tf_op jit(solution)/shard_map/ppermute | solution.py:51
  81.1 6.0 %all-to-all-done.4.refs_4_ = f32[16,48,128]{2,1,0:T(8,128)S(1)} async-done(((f32[16,48,128]{2,1,0:T(8,128)}), f32[16,48,128]{2,1,0:T(8,128)S(1)}, u32[]{:S(2)}, u32[]{:S(2)}) %all-to-all-start.4) | async-done | bytes 393248 | tf_op jit(solution)/shard_map/all_to_all | solution.py:43
  87.1 7.6 %shard_map.84 = (f32[16,48,128]{2,1,0:T(8,128)}, f32[4,2,48,256]{3,2,1,0:T(8,128)}, f32[4,2,48,256]{3,2,1,0:T(8,128)}) custom-call(s32[1,14]{1,0:T(1,128)} %refs_0_.4, s32[1,14]{1,0:T(1,128)} %copy-done.7, s32[1,14]{1,0:T(1,128)} %copy-done.8, s32[1,14]{1,0:T(1,128)} %copy-done.9, f32[16,48,128]{2,1,0:T(8,128)S(1)} %all-to-all-done.4.refs_4_, ...), custom_call_target="tpu_custom_call" | custom-call | tf_op jit(solution)/shard_map/pallas_call | solution.py:72
  94.7 3.7 %all-to-all-start.5 = ((f32[16,48,128]{2,1,0:T(8,128)}), f32[16,48,128]{2,1,0:T(8,128)S(1)}, u32[]{:S(2)}, u32[]{:S(2)}) async-start(f32[16,48,128]{2,1,0:T(8,128)} %get-tuple-element.58), calls=%async_computation.5 | async-start | bytes 786432 | tf_op jit(solution)/shard_map/all_to_all | solution.py:43
  98.4 2.9 %collective-permute-start.9 = (f32[4,2,48,256]{3,2,1,0:T(8,128)}, f32[4,2,48,256]{3,2,1,0:T(8,128)S(1)}, u32[]{:S(2)}, u32[]{:S(2)}) collective-permute-start(f32[4,2,48,256]{3,2,1,0:T(8,128)} %get-tuple-element.61), channel_id=1, source_target_pairs={{0,16},{16,0},{1,17},{17,1},{2,18},{18,2},{3,19},{19,3},{4,20},{20... | collective-permute-start | bytes 1179656 | tf_op jit(solution)/shard_map/ppermute | solution.py:51
  101.3 5.3 %all-to-all-done.5 = f32[16,48,128]{2,1,0:T(8,128)S(1)} async-done(((f32[16,48,128]{2,1,0:T(8,128)}), f32[16,48,128]{2,1,0:T(8,128)S(1)}, u32[]{:S(2)}, u32[]{:S(2)}) %all-to-all-start.5) | async-done | bytes 393248 | tf_op jit(solution)/shard_map/all_to_all | solution.py:43
  107.3 3.4 %all-to-all-start.6 = ((f32[8,48,128]{2,1,0:T(8,128)}), f32[8,48,128]{2,1,0:T(8,128)S(1)}, u32[]{:S(2)}, u32[]{:S(2)}) async-start(f32[8,48,128]{2,1,0:T(8,128)} %broadcast_in_dim.25), calls=%async_computation.6 | async-start | bytes 393216 | tf_op jit(solution)/shard_map/all_to_all | solution.py:43
  110.7 2.1 %collective-permute-done.9.refs_9_ = f32[4,2,48,256]{3,2,1,0:T(8,128)S(1)} collective-permute-done((f32[4,2,48,256]{3,2,1,0:T(8,128)}, f32[4,2,48,256]{3,2,1,0:T(8,128)S(1)}, u32[]{:S(2)}, u32[]{:S(2)}) %collective-permute-start.9) | collective-permute-done | bytes 393248 | tf_op jit(solution)/shard_map/ppermute | solution.py:51
  112.8 3.4 %all-to-all-done.6.refs_4_ = f32[8,48,128]{2,1,0:T(8,128)S(1)} async-done(((f32[8,48,128]{2,1,0:T(8,128)}), f32[8,48,128]{2,1,0:T(8,128)S(1)}, u32[]{:S(2)}, u32[]{:S(2)}) %all-to-all-start.6) | async-done | bytes 196640 | tf_op jit(solution)/shard_map/all_to_all | solution.py:43
  116.2 4.5 %shard_map.85 = (f32[8,48,512]{2,1,0:T(8,128)}, f32[2,4,48,256]{3,2,1,0:T(8,128)}, f32[2,4,48,256]{3,2,1,0:T(8,128)}) custom-call(s32[1,14]{1,0:T(1,128)} %refs_0_.4, s32[1,14]{1,0:T(1,128)} %copy-done.7, s32[1,14]{1,0:T(1,128)} %copy-done.8, s32[1,14]{1,0:T(1,128)} %copy-done.9, f32[8,48,128]{2,1,0:T(8,128)S(1)} %all-to-all-done.6.refs_4_, ...), custom_call_target="tpu_custom_call" | custom-call | tf_op jit(solution)/shard_map/pallas_call | solution.py:72
  120.7 3.6 %all-to-all-start.7 = ((f32[8,48,512]{2,1,0:T(8,128)}), f32[8,48,512]{2,1,0:T(8,128)S(1)}, u32[]{:S(2)}, u32[]{:S(2)}) async-start(f32[8,48,512]{2,1,0:T(8,128)} %get-tuple-element.62), calls=%async_computation.7 | async-start | bytes 1572864 | tf_op jit(solution)/shard_map/all_to_all | solution.py:43
  124.2 1.4 collective-permute-start.10
  125.6 7.0 %all-to-all-done.7.refs_4_ = f32[8,48,512]{2,1,0:T(8,128)S(1)} async-done(((f32[8,48,512]{2,1,0:T(8,128)}), f32[8,48,512]{2,1,0:T(8,128)S(1)}, u32[]{:S(2)}, u32[]{:S(2)}) %all-to-all-start.7) | async-done | bytes 786464 | tf_op jit(solution)/shard_map/all_to_all | solution.py:43
  132.6 3.5 %shard_map.86 = (f32[8,48,256]{2,1,0:T(8,128)}, f32[4,48,256]{2,1,0:T(8,128)}) custom-call(s32[1,14]{1,0:T(1,128)} %refs_0_.4, s32[1,14]{1,0:T(1,128)} %copy-done.7, s32[1,14]{1,0:T(1,128)} %copy-done.8, s32[1,14]{1,0:T(1,128)} %copy-done.9, f32[8,48,512]{2,1,0:T(8,128)S(1)} %all-to-all-done.7.refs_4_, bf16[2,256,512]{2,1,0:T(8,128)(2,1)S(1)} %shard_map.77.refs_7_.refs_5_, ...), custom_call_target="tpu_custom_call" | custom-call | tf_op jit(solution)/shard_map/pallas_call | solution.py:72
  136.1 10.5 %all-to-all-start.8 = ((f32[8,48,256]{2,1,0:T(8,128)}), f32[8,48,256]{2,1,0:T(8,128)S(1)}, u32[]{:S(2)}, u32[]{:S(2)}) async-start(f32[8,48,256]{2,1,0:T(8,128)} %get-tuple-element.64), calls=%async_computation.8 | async-start | bytes 786432 | tf_op jit(solution)/shard_map/all_to_all | solution.py:43
  146.6 2.0 %shard_map.87 = (f32[4,48,384]{2,1,0:T(8,128)}, f32[4,48,384]{2,1,0:T(8,128)}) custom-call(f32[4,48,256]{2,1,0:T(8,128)} %get-tuple-element.66.nearest_ref, f32[2,4,48,256]{3,2,1,0:T(8,128)} %get-tuple-element.67.kept_ref, f32[2,4,48,256]{3,2,1,0:T(8,128)S(1)} %collective-permute-done.10.other_ref), custom_call_target="tpu_custom_call" | custom-call | tf_op jit(solution)/shard_map/pallas_call | solution.py:72
  148.6 1.8 %collective-permute-done.11.other_ref = f32[4,48,384]{2,1,0:T(8,128)S(1)} collective-permute-done((f32[4,48,384]{2,1,0:T(8,128)}, f32[4,48,384]{2,1,0:T(8,128)S(1)}, u32[]{:S(2)}, u32[]{:S(2)}) %collective-permute-start.11) | collective-permute-done | bytes 294944 | tf_op jit(solution)/shard_map/ppermute | solution.py:47
  150.4 3.9 %all-to-all-done.8.received_ref = f32[8,48,256]{2,1,0:T(8,128)S(1)} async-done(((f32[8,48,256]{2,1,0:T(8,128)}), f32[8,48,256]{2,1,0:T(8,128)S(1)}, u32[]{:S(2)}, u32[]{:S(2)}) %all-to-all-start.8) | async-done | bytes 393248 | tf_op jit(solution)/shard_map/all_to_all | solution.py:43
  154.3 1.5 shard_map.88
  155.8 13.6 %all_to_all.50.received_ref = f32[4,96,512]{2,1,0:T(8,128)S(1)} all-to-all(f32[4,96,512]{2,1,0:T(8,128)S(1)} %shard_map.88), channel_id=1, replica_groups=mesh['z'=4,'y1'=2,'y0'=2,'c'=2,'x'=4] {'x'}, dimensions={0} | all-to-all | bytes 1572864 | tf_op jit(solution)/shard_map/all_to_all | solution.py:43
  (40 shorter events, 4.4 us)
Async XLA Ops:
  1.9 30.8 %collective-permute-start.6 = (f32[128,7680]{1,0:T(8,128)}, f32[128,7680]{1,0:T(8,128)}, u32[]{:S(2)}, u32[]{:S(2)}) collective-permute-start(f32[128,7680]{1,0:T(8,128)} %bitcast.11), channel_id=1, source_target_pairs={{0,4},{4,0},{1,5},{5,1},{2,6},{6,2},{3,7},{7,3},{8,12},{12,8},{9,1... | collective-permute-start | bytes 11796488 | tf_op jit(solution)/shard_map/ppermute | solution.py:47
  3.3 16.2 %all-to-all-start = ((f32[4,96,512]{2,1,0:T(8,128)}), f32[4,96,512]{2,1,0:T(8,128)S(1)}, u32[]{:S(2)}, u32[]{:S(2)}) async-start(f32[4,96,512]{2,1,0:T(8,128)} %broadcast_in_dim.11.refs_1_), calls=%async_computation | async-start | bytes 1572864 | tf_op jit(solution)/shard_map/all_to_all | solution.py:43
  7.4 23.3 %collective-permute-start.4 = (f32[128,1792]{1,0:T(8,128)}, f32[128,1792]{1,0:T(8,128)S(1)}, u32[]{:S(2)}, u32[]{:S(2)}) collective-permute-start(f32[128,1792]{1,0:T(8,128)} %bitcast.15), channel_id=1, source_target_pairs={{0,4},{4,0},{1,5},{5,1},{2,6},{6,2},{3,7},{7,3},{8,12},{12,8},{9,1... | collective-permute-start | bytes 2752520 | tf_op jit(solution)/shard_map/ppermute | solution.py:47
  8.8 6.6 %collective-permute-start = (f32[2,512]{1,0:T(2,128)S(1)}, f32[2,512]{1,0:T(2,128)S(1)}, u32[]{:S(2)}, u32[]{:S(2)}) collective-permute-start(f32[2,512]{1,0:T(2,128)S(1)} %shard_map.73.factors_ref.refs_5_), channel_id=1, source_target_pairs={{0,4},{4,0},{1,5},{5,1},{2,6},{6,2},{3,7},{7,3},{8,12},{12,8},{9,1... | collective-permute-start | bytes 12296 | tf_op jit(solution)/shard_map/ppermute | solution.py:47
  9.1 4.9 %collective-permute-start.1 = (s32[1,14]{1,0:T(1,128)}, s32[1,14]{1,0:T(1,128)S(1)}, u32[]{:S(2)}, u32[]{:S(2)}) collective-permute-start(s32[1,14]{1,0:T(1,128)} %refs_0_.4), channel_id=1, source_target_pairs={{0,8},{4,20},{8,0},{12,28},{16,24},{20,4},{24,16},{28,12},{1,9},{5... | collective-permute-start | bytes 176 | tf_op jit(solution)/shard_map/ppermute | solution.py:495
  12.0 2.6 %collective-permute-start.2 = (s32[1,14]{1,0:T(1,128)}, s32[1,14]{1,0:T(1,128)S(1)}, u32[]{:S(2)}, u32[]{:S(2)}) collective-permute-start(s32[1,14]{1,0:T(1,128)} %refs_0_.4), channel_id=1, source_target_pairs={{0,4},{4,0},{1,5},{5,1},{2,6},{6,2},{3,7},{7,3},{8,12},{12,8},{9,1... | collective-permute-start | bytes 176 | tf_op jit(solution)/shard_map/ppermute | solution.py:47
  14.0 21.1 %copy-start.7 = (s32[1,14]{1,0:T(1,128)}, s32[1,14]{1,0:T(1,128)S(1)}, u32[]{:S(2)}) copy-start(s32[1,14]{1,0:T(1,128)S(1)} %collective-permute-done.1.refs_1_) | copy-start | bytes 172
  14.0 1.4 collective-permute-start.3
  14.6 20.5 %copy-start.8 = (s32[1,14]{1,0:T(1,128)}, s32[1,14]{1,0:T(1,128)S(1)}, u32[]{:S(2)}) copy-start(s32[1,14]{1,0:T(1,128)S(1)} %collective-permute-done.2.refs_2_) | copy-start | bytes 172
  15.4 19.7 %copy-start.9 = (s32[1,14]{1,0:T(1,128)}, s32[1,14]{1,0:T(1,128)S(1)}, u32[]{:S(2)}) copy-start(s32[1,14]{1,0:T(1,128)S(1)} %collective-permute-done.3.refs_3_) | copy-start | bytes 172
  20.9 2.6 %collective-permute-start.5 = (f32[4,48,384]{2,1,0:T(8,128)}, f32[4,48,384]{2,1,0:T(8,128)S(1)}, u32[]{:S(2)}, u32[]{:S(2)}) collective-permute-start(f32[4,48,384]{2,1,0:T(8,128)} %get-tuple-element.47), channel_id=1, source_target_pairs={{0,4},{4,0},{1,5},{5,1},{2,6},{6,2},{3,7},{7,3},{8,12},{12,8},{9,1... | collective-permute-start | bytes 884744 | tf_op jit(solution)/shard_map/ppermute | solution.py:47
  25.4 17.8 %collective-permute-start.7 = (f32[4,96,256]{2,1,0:T(8,128)}, f32[4,96,256]{2,1,0:T(8,128)S(1)}, u32[]{:S(2)}, u32[]{:S(2)}) collective-permute-start(f32[4,96,256]{2,1,0:T(8,128)} %get-tuple-element.51.refs_8_), channel_id=1, source_target_pairs={{0,8},{8,0},{1,9},{9,1},{2,10},{10,2},{3,11},{11,3},{4,12},{12,4},... | collective-permute-start | bytes 1179656 | tf_op jit(solution)/shard_map/ppermute | solution.py:51
  26.7 12.0 %all-to-all-start.1 = ((f32[8,48,256]{2,1,0:T(8,128)}), f32[8,48,256]{2,1,0:T(8,128)S(1)}, u32[]{:S(2)}, u32[]{:S(2)}) async-start(f32[8,48,256]{2,1,0:T(8,128)} %get-tuple-element.43.refs_2_), calls=%async_computation.1 | async-start | bytes 786432 | tf_op jit(solution)/shard_map/all_to_all | solution.py:43
  30.7 1.0 copy-start
  32.8 14.0 %copy-start.4 = (f32[4,96,256]{2,1,0:T(8,128)S(1)}, f32[4,96,256]{2,1,0:T(8,128)}, u32[]{:S(2)}) copy-start(f32[4,96,256]{2,1,0:T(8,128)} %get-tuple-element.51.refs_8_) | copy-start | bytes 1179652
  43.2 9.2 %copy-start.2 = (f32[4,96,256]{2,1,0:T(8,128)}, f32[4,96,256]{2,1,0:T(8,128)S(1)}, u32[]{:S(2)}) copy-start(f32[4,96,256]{2,1,0:T(8,128)S(1)} %collective-permute-done.7.refs_9_) | copy-start | bytes 1179652
  43.2 16.1 %all-to-all-start.2 = ((f32[8,48,512]{2,1,0:T(8,128)}), f32[8,48,512]{2,1,0:T(8,128)S(1)}, u32[]{:S(2)}, u32[]{:S(2)}) async-start(f32[8,48,512]{2,1,0:T(8,128)} %get-tuple-element.52.refs_2_), calls=%async_computation.2 | async-start | bytes 1572864 | tf_op jit(solution)/shard_map/all_to_all | solution.py:43
  53.7 14.0 %copy-start.3 = (f32[4,96,256]{2,1,0:T(8,128)S(1)}, f32[4,96,256]{2,1,0:T(8,128)}, u32[]{:S(2)}) copy-start(f32[4,96,256]{2,1,0:T(8,128)} %copy-done.2) | copy-start | bytes 1179652
  64.2 9.0 %all-to-all-start.3 = ((f32[8,48,128]{2,1,0:T(8,128)}), f32[8,48,128]{2,1,0:T(8,128)S(1)}, u32[]{:S(2)}, u32[]{:S(2)}) async-start(f32[8,48,128]{2,1,0:T(8,128)} %get-tuple-element.55), calls=%async_computation.3 | async-start | bytes 393216 | tf_op jit(solution)/shard_map/all_to_all | solution.py:43
  67.7 19.4 %copy-start.1 = (f32[2,4,96,128]{3,2,1,0:T(8,128)}, f32[2,4,96,128]{3,2,1,0:T(8,128)S(1)}, u32[]{:S(2)}) copy-start(f32[2,4,96,128]{3,2,1,0:T(8,128)S(1)} %pad_maximum_fusion.refs_7_) | copy-start | bytes 1179652
  67.7 13.4 %collective-permute-start.8 = (f32[2,4,96,128]{3,2,1,0:T(8,128)S(1)}, f32[2,4,96,128]{3,2,1,0:T(8,128)S(1)}, u32[]{:S(2)}, u32[]{:S(2)}) collective-permute-start(f32[2,4,96,128]{3,2,1,0:T(8,128)S(1)} %pad_maximum_fusion.refs_7_), channel_id=1, source_target_pairs={{0,16},{16,0},{1,17},{17,1},{2,18},{18,2},{3,19},{19,3},{4,20},{20... | collective-permute-start | bytes 1179656 | tf_op jit(solution)/shard_map/ppermute | solution.py:51
  74.0 13.1 %all-to-all-start.4 = ((f32[16,48,128]{2,1,0:T(8,128)}), f32[16,48,128]{2,1,0:T(8,128)S(1)}, u32[]{:S(2)}, u32[]{:S(2)}) async-start(f32[16,48,128]{2,1,0:T(8,128)} %broadcast_in_dim.24), calls=%async_computation.4 | async-start | bytes 786432 | tf_op jit(solution)/shard_map/all_to_all | solution.py:43
  81.1 6.0 %copy-start.5 = (f32[2,4,96,128]{3,2,1,0:T(8,128)}, f32[2,4,96,128]{3,2,1,0:T(8,128)S(1)}, u32[]{:S(2)}) copy-start(f32[2,4,96,128]{3,2,1,0:T(8,128)S(1)} %collective-permute-done.8.refs_8_) | copy-start | bytes 1179652
  94.7 11.8 %all-to-all-start.5 = ((f32[16,48,128]{2,1,0:T(8,128)}), f32[16,48,128]{2,1,0:T(8,128)S(1)}, u32[]{:S(2)}, u32[]{:S(2)}) async-start(f32[16,48,128]{2,1,0:T(8,128)} %get-tuple-element.58), calls=%async_computation.5 | async-start | bytes 786432 | tf_op jit(solution)/shard_map/all_to_all | solution.py:43
  98.4 14.4 %collective-permute-start.9 = (f32[4,2,48,256]{3,2,1,0:T(8,128)}, f32[4,2,48,256]{3,2,1,0:T(8,128)S(1)}, u32[]{:S(2)}, u32[]{:S(2)}) collective-permute-start(f32[4,2,48,256]{3,2,1,0:T(8,128)} %get-tuple-element.61), channel_id=1, source_target_pairs={{0,16},{16,0},{1,17},{17,1},{2,18},{18,2},{3,19},{19,3},{4,20},{20... | collective-permute-start | bytes 1179656 | tf_op jit(solution)/shard_map/ppermute | solution.py:51
  107.3 8.9 %all-to-all-start.6 = ((f32[8,48,128]{2,1,0:T(8,128)}), f32[8,48,128]{2,1,0:T(8,128)S(1)}, u32[]{:S(2)}, u32[]{:S(2)}) async-start(f32[8,48,128]{2,1,0:T(8,128)} %broadcast_in_dim.25), calls=%async_computation.6 | async-start | bytes 393216 | tf_op jit(solution)/shard_map/all_to_all | solution.py:43
  112.8 3.4 %copy-start.6 = (f32[4,2,48,256]{3,2,1,0:T(8,128)}, f32[4,2,48,256]{3,2,1,0:T(8,128)S(1)}, u32[]{:S(2)}) copy-start(f32[4,2,48,256]{3,2,1,0:T(8,128)S(1)} %collective-permute-done.9.refs_9_) | copy-start | bytes 1179652
  120.7 11.9 %all-to-all-start.7 = ((f32[8,48,512]{2,1,0:T(8,128)}), f32[8,48,512]{2,1,0:T(8,128)S(1)}, u32[]{:S(2)}, u32[]{:S(2)}) async-start(f32[8,48,512]{2,1,0:T(8,128)} %get-tuple-element.62), calls=%async_computation.7 | async-start | bytes 1572864 | tf_op jit(solution)/shard_map/all_to_all | solution.py:43
  124.2 22.4 %collective-permute-start.10 = (f32[2,4,48,256]{3,2,1,0:T(8,128)}, f32[2,4,48,256]{3,2,1,0:T(8,128)S(1)}, u32[]{:S(2)}, u32[]{:S(2)}) collective-permute-start(f32[2,4,48,256]{3,2,1,0:T(8,128)} %get-tuple-element.68), channel_id=1, source_target_pairs={{0,8},{8,0},{1,9},{9,1},{2,10},{10,2},{3,11},{11,3},{4,12},{12,4},... | collective-permute-start | bytes 1179656 | tf_op jit(solution)/shard_map/ppermute | solution.py:51
  136.1 18.2 %all-to-all-start.8 = ((f32[8,48,256]{2,1,0:T(8,128)}), f32[8,48,256]{2,1,0:T(8,128)S(1)}, u32[]{:S(2)}, u32[]{:S(2)}) async-start(f32[8,48,256]{2,1,0:T(8,128)} %get-tuple-element.64), calls=%async_computation.8 | async-start | bytes 786432 | tf_op jit(solution)/shard_map/all_to_all | solution.py:43
  148.6 1.8 %collective-permute-start.11 = (f32[4,48,384]{2,1,0:T(8,128)}, f32[4,48,384]{2,1,0:T(8,128)S(1)}, u32[]{:S(2)}, u32[]{:S(2)}) collective-permute-start(f32[4,48,384]{2,1,0:T(8,128)} %get-tuple-element.70), channel_id=1, source_target_pairs={{0,4},{4,0},{1,5},{5,1},{2,6},{6,2},{3,7},{7,3},{8,12},{12,8},{9,1... | collective-permute-start | bytes 884744 | tf_op jit(solution)/shard_map/ppermute | solution.py:47

commit v10 on v9

--- a/solution.py
+++ b/solution.py
@@ -191,8 +191,8 @@
         self.started.append(move)
         return move
 
-    def chunks(self, source, target):
-        return [self.start(source.at[k], target.at[k]) for k in range(source.shape[0])]
+    def chunks(self, source, target, which):
+        return [self.start(source.at[k], target.at[k]) for k in which]
 
 
 def finish(moves):
@@ -295,7 +295,7 @@
                 for flip in range(2):
                     for x in range(4):
                         bring(sides_refs[high].at[flip, x], x * 4 + (y1 ^ high) * 2 + (y0 ^ flip))
-        columns = moves.chunks(weights_far, weights_ref)
+        columns = moves.chunks(weights_far, weights_ref, range(min(2, chunks)))
         if level < 3:
             part_ref = refs[0]
         totals = [None, None]
@@ -305,6 +305,7 @@
             elif level == 2:
                 totals[child] = sum(received_ref[x * 2 + child] for x in range(4))
         finish(arriving)
+        columns += moves.chunks(weights_far, weights_ref, range(2, chunks))
         for child in range(2):
             for k in range(blocks):
                 if level < 3:
@@ -391,14 +392,15 @@
         semaphores, x_ref, weighted_ref, weights_ref, pieces_ref = take(5)
         moves = Moves(semaphores)
         arriving = moves.start(weighted_far, weighted_ref)
-        columns = moves.chunks(weights_far, weights_ref)
+        columns = moves.chunks(weights_far, weights_ref, range(min(2, chunks)))
         leaving = []
+        if level == 1:
+            total = sum(received_ref[i] for i in range(8))
+        arriving.wait()
+        columns += moves.chunks(weights_far, weights_ref, range(2, chunks))
         if level == 2:
             own_ref, other_ref, sums_ref = refs
             both = [moves.start(answers_far[0], own_ref), moves.start(answers_far[1], other_ref)]
-        if level == 1:
-            total = sum(received_ref[i] for i in range(8))
-        arriving.wait()
         target = weighted_ref[...]
         for k in range(update_len // 256):
             at = slice(k * 256, (k + 1) * 256)

time: 172 us -> 173 us (level)
  transfers between devices with their start and end apart: 21 -> 21, of which waited for: 14 -> 14; matrix products, arithmetic and copies ran while one was open for 1% -> 1% of each run, Pallas kernels for 16% -> 15%
where the time goes in v10:
time: 173 us; the launch traced here: 171 us
  starting transfers between devices  56.3 us (33%)
  waiting for transfers between devices  49.7 us (29%)
  Pallas kernels  46.6 us (27%)
  blocking collectives  13.6 us (8%)
  local copies, waits for them, and re-layouts  4.42 us (3%)
    all_to_all x9, waiting for transfers between devices, exchange(): return lax.all_to_all(value, axes, 0, 0, tiled=True)  41.5 us
    all_to_all x9, starting transfers between devices, exchange(): return lax.all_to_all(value, axes, 0, 0, tiled=True)  41.4 us
    pallas_call x11, Pallas kernels, call(): pl.pallas_call(body, in_specs=specs, out_specs=[FAR if k == 'H' else WHOL...  34.4 us
    all_to_all x1, blocking collectives, exchange(): return lax.all_to_all(value, axes, 0, 0, tiled=True)  13.6 us
    pallas_call x6, Pallas kernels, prepared(): pl.pallas_call(body, in_specs=[FAR] * (len(pair) + 1), out_specs=[WHOLE]...  12.2 us
    ppermute x4, starting transfers between devices, across(): return lax.ppermute(value, axis, [(0, 1), (1, 0)])  8.22 us
    ppermute x4, waiting for transfers between devices, across(): return lax.ppermute(value, axis, [(0, 1), (1, 0)])  4.17 us
    ppermute x7, waiting for transfers between devices, with_partner(): return lax.ppermute(value, 'c', [(0, 1), (1, 0)])  4.03 us
  transfers between devices with their start and end apart: 21, of which 14 were waited for; matrix products, arithmetic and copies ran while one was open for 1% of the time, Pallas kernels for 15%

profile of v10, /device:TPU:1, one launch (start us, length us, event | category | flops | bytes accessed | tf_op | source)
XLA Modules:
  0.0 171.0 jit_solution(2666715638577246583)
XLA Ops:
  0.0 1.9 %broadcast_in_dim.11.refs_1_ = f32[4,96,512]{2,1,0:T(8,128)} broadcast(f32[96,512]{1,0:T(8,128)} %bitcast.19), dimensions={1,2} | broadcast | bytes 983040 | tf_op jit(solution)/shard_map/broadcast_in_dim | solution.py:508
  1.9 1.4 collective-permute-start.6
  3.3 4.1 %all-to-all-start = ((f32[4,96,512]{2,1,0:T(8,128)}), f32[4,96,512]{2,1,0:T(8,128)S(1)}, u32[]{:S(2)}, u32[]{:S(2)}) async-start(f32[4,96,512]{2,1,0:T(8,128)} %broadcast_in_dim.11.refs_1_), calls=%async_computation | async-start | bytes 1572864 | tf_op jit(solution)/shard_map/all_to_all | solution.py:43
  7.7 1.1 shard_map.73.factors_ref.refs_5_
  9.1 2.9 %collective-permute-start.1 = (s32[1,14]{1,0:T(1,128)}, s32[1,14]{1,0:T(1,128)S(1)}, u32[]{:S(2)}, u32[]{:S(2)}) collective-permute-start(s32[1,14]{1,0:T(1,128)} %refs_0_.4), channel_id=1, source_target_pairs={{0,8},{4,20},{8,0},{12,28},{16,24},{20,4},{24,16},{28,12},{1,9},{5... | collective-permute-start | bytes 176 | tf_op jit(solution)/shard_map/ppermute | solution.py:497
  12.0 1.0 shard_map.74.weights_ref
  13.0 0.9 shard_map.75.updates_ref
  15.4 4.2 %all-to-all-done.first_ref = f32[4,96,512]{2,1,0:T(8,128)S(1)} async-done(((f32[4,96,512]{2,1,0:T(8,128)}), f32[4,96,512]{2,1,0:T(8,128)S(1)}, u32[]{:S(2)}, u32[]{:S(2)}) %all-to-all-start) | async-done | bytes 786464 | tf_op jit(solution)/shard_map/all_to_all | solution.py:43
  19.5 1.4 shard_map.76
  20.9 1.2 collective-permute-start.5
  22.1 1.4 collective-permute-done.5.other_ref
  23.6 1.8 %shard_map.78 = (f32[4,96,128]{2,1,0:T(8,128)}, f32[4,96,256]{2,1,0:T(8,128)}) custom-call(f32[4,48,384]{2,1,0:T(8,128)} %get-tuple-element.46.own_ref, f32[4,48,384]{2,1,0:T(8,128)S(1)} %collective-permute-done.5.other_ref), custom_call_target="tpu_custom_call" | custom-call | tf_op jit(solution)/shard_map/pallas_call | solution.py:72
  25.4 1.3 collective-permute-start.7
  26.7 4.0 %all-to-all-start.1 = ((f32[8,48,256]{2,1,0:T(8,128)}), f32[8,48,256]{2,1,0:T(8,128)S(1)}, u32[]{:S(2)}, u32[]{:S(2)}) async-start(f32[8,48,256]{2,1,0:T(8,128)} %get-tuple-element.43.refs_2_), calls=%async_computation.1 | async-start | bytes 786432 | tf_op jit(solution)/shard_map/all_to_all | solution.py:43
  30.7 1.0 copy-done
  31.7 1.1 shard_map.77.refs_7_.refs_5_
  32.8 2.3 %shard_map.79.refs_9_.refs_7_ = bf16[2,2,256,512]{3,2,1,0:T(8,128)(2,1)} custom-call(f32[128,7680]{1,0:T(8,128)} %bitcast.13, f32[128,7680]{1,0:T(8,128)} %collective-permute-done.6.refs_1_, f32[8,48,256]{2,1,0:T(8,128)} %get-tuple-element.43.refs_2_), custom_call_target="tpu_custom_call" | custom-call | tf_op jit(solution)/shard_map/pallas_call | solution.py:116
  35.1 3.5 %all-to-all-done.1.refs_4_ = f32[8,48,256]{2,1,0:T(8,128)S(1)} async-done(((f32[8,48,256]{2,1,0:T(8,128)}), f32[8,48,256]{2,1,0:T(8,128)S(1)}, u32[]{:S(2)}, u32[]{:S(2)}) %all-to-all-start.1) | async-done | bytes 393248 | tf_op jit(solution)/shard_map/all_to_all | solution.py:43
  38.7 4.5 %shard_map.80 = (f32[8,48,512]{2,1,0:T(8,128)}, f32[48,256]{1,0:T(8,128)}) custom-call(s32[1,14]{1,0:T(1,128)} %refs_0_.4, s32[1,14]{1,0:T(1,128)} %copy-done.7, s32[1,14]{1,0:T(1,128)} %copy-done.8, s32[1,14]{1,0:T(1,128)} %copy-done.9, f32[8,48,256]{2,1,0:T(8,128)S(1)} %all-to-all-done.1.refs_4_, f32[2,512]{1,0:T(2,128)S(1)} %shard_map.73.factors_ref.refs_5_, ...), custom_call_target="tpu_custom_call" | custom-call | tf_op jit(solution)/shard_map/pallas_call | solution.py:72
  43.2 3.6 %all-to-all-start.2 = ((f32[8,48,512]{2,1,0:T(8,128)}), f32[8,48,512]{2,1,0:T(8,128)S(1)}, u32[]{:S(2)}, u32[]{:S(2)}) async-start(f32[8,48,512]{2,1,0:T(8,128)} %get-tuple-element.52.refs_2_), calls=%async_computation.2 | async-start | bytes 1572864 | tf_op jit(solution)/shard_map/all_to_all | solution.py:43
  46.8 5.6 %shard_map.82 = (bf16[4,2,256,512]{3,2,1,0:T(8,128)(2,1)}, bf16[8,2,256,512]{3,2,1,0:T(8,128)(2,1)}) custom-call(f32[128,7680]{1,0:T(8,128)} %bitcast.14, f32[128,7680]{1,0:T(8,128)} %collective-permute-done.6.refs_1_, f32[8,48,512]{2,1,0:T(8,128)} %get-tuple-element.52.refs_2_), custom_call_target="tpu_custom_call" | custom-call | tf_op jit(solution)/shard_map/pallas_call | solution.py:116
  52.4 1.3 shard_map.81.refs_7_.refs_5_
  53.7 5.6 %all-to-all-done.2.refs_4_ = f32[8,48,512]{2,1,0:T(8,128)S(1)} async-done(((f32[8,48,512]{2,1,0:T(8,128)}), f32[8,48,512]{2,1,0:T(8,128)S(1)}, u32[]{:S(2)}, u32[]{:S(2)}) %all-to-all-start.2) | async-done | bytes 786464 | tf_op jit(solution)/shard_map/all_to_all | solution.py:43
  59.3 5.2 %shard_map.83 = (f32[8,48,128]{2,1,0:T(8,128)}, f32[48,256]{1,0:T(8,128)}) custom-call(s32[1,14]{1,0:T(1,128)} %refs_0_.4, s32[1,14]{1,0:T(1,128)} %copy-done.7, s32[1,14]{1,0:T(1,128)} %copy-done.8, s32[1,14]{1,0:T(1,128)} %copy-done.9, f32[8,48,512]{2,1,0:T(8,128)S(1)} %all-to-all-done.2.refs_4_, f32[2,512]{1,0:T(2,128)S(1)} %shard_map.73.factors_ref.refs_5_, ...), custom_call_target="tpu_custom_call" | custom-call | tf_op jit(solution)/shard_map/pallas_call | solution.py:72
  64.5 3.4 %all-to-all-start.3 = ((f32[8,48,128]{2,1,0:T(8,128)}), f32[8,48,128]{2,1,0:T(8,128)S(1)}, u32[]{:S(2)}, u32[]{:S(2)}) async-start(f32[8,48,128]{2,1,0:T(8,128)} %get-tuple-element.55), calls=%async_computation.3 | async-start | bytes 393216 | tf_op jit(solution)/shard_map/all_to_all | solution.py:43
  67.9 2.7 %collective-permute-start.8 = (f32[2,4,96,128]{3,2,1,0:T(8,128)S(1)}, f32[2,4,96,128]{3,2,1,0:T(8,128)S(1)}, u32[]{:S(2)}, u32[]{:S(2)}) collective-permute-start(f32[2,4,96,128]{3,2,1,0:T(8,128)S(1)} %pad_maximum_fusion.refs_7_), channel_id=1, source_target_pairs={{0,16},{16,0},{1,17},{17,1},{2,18},{18,2},{3,19},{19,3},{4,20},{20... | collective-permute-start | bytes 1179656 | tf_op jit(solution)/shard_map/ppermute | solution.py:51
  70.6 2.8 %all-to-all-done.3 = f32[8,48,128]{2,1,0:T(8,128)S(1)} async-done(((f32[8,48,128]{2,1,0:T(8,128)}), f32[8,48,128]{2,1,0:T(8,128)S(1)}, u32[]{:S(2)}, u32[]{:S(2)}) %all-to-all-start.3) | async-done | bytes 196640 | tf_op jit(solution)/shard_map/all_to_all | solution.py:43
  74.2 5.1 %all-to-all-start.4 = ((f32[16,48,128]{2,1,0:T(8,128)}), f32[16,48,128]{2,1,0:T(8,128)S(1)}, u32[]{:S(2)}, u32[]{:S(2)}) async-start(f32[16,48,128]{2,1,0:T(8,128)} %broadcast_in_dim.24), calls=%async_computation.4 | async-start | bytes 786432 | tf_op jit(solution)/shard_map/all_to_all | solution.py:43
  79.3 2.0 %collective-permute-done.8.refs_8_ = f32[2,4,96,128]{3,2,1,0:T(8,128)S(1)} collective-permute-done((f32[2,4,96,128]{3,2,1,0:T(8,128)S(1)}, f32[2,4,96,128]{3,2,1,0:T(8,128)S(1)}, u32[]{:S(2)}, u32[]{:S(2)}) %collective-permute-start.8) | collective-permute-done | bytes 393248 | tf_op jit(solution)/shard_map/ppermute | solution.py:51
  81.4 6.0 %all-to-all-done.4.refs_4_ = f32[16,48,128]{2,1,0:T(8,128)S(1)} async-done(((f32[16,48,128]{2,1,0:T(8,128)}), f32[16,48,128]{2,1,0:T(8,128)S(1)}, u32[]{:S(2)}, u32[]{:S(2)}) %all-to-all-start.4) | async-done | bytes 393248 | tf_op jit(solution)/shard_map/all_to_all | solution.py:43
  87.3 7.7 %shard_map.84 = (f32[16,48,128]{2,1,0:T(8,128)}, f32[4,2,48,256]{3,2,1,0:T(8,128)}, f32[4,2,48,256]{3,2,1,0:T(8,128)}) custom-call(s32[1,14]{1,0:T(1,128)} %refs_0_.4, s32[1,14]{1,0:T(1,128)} %copy-done.7, s32[1,14]{1,0:T(1,128)} %copy-done.8, s32[1,14]{1,0:T(1,128)} %copy-done.9, f32[16,48,128]{2,1,0:T(8,128)S(1)} %all-to-all-done.4.refs_4_, ...), custom_call_target="tpu_custom_call" | custom-call | tf_op jit(solution)/shard_map/pallas_call | solution.py:72
  95.1 3.7 %all-to-all-start.5 = ((f32[16,48,128]{2,1,0:T(8,128)}), f32[16,48,128]{2,1,0:T(8,128)S(1)}, u32[]{:S(2)}, u32[]{:S(2)}) async-start(f32[16,48,128]{2,1,0:T(8,128)} %get-tuple-element.58), calls=%async_computation.5 | async-start | bytes 786432 | tf_op jit(solution)/shard_map/all_to_all | solution.py:43
  98.8 2.9 %collective-permute-start.9 = (f32[4,2,48,256]{3,2,1,0:T(8,128)}, f32[4,2,48,256]{3,2,1,0:T(8,128)S(1)}, u32[]{:S(2)}, u32[]{:S(2)}) collective-permute-start(f32[4,2,48,256]{3,2,1,0:T(8,128)} %get-tuple-element.61), channel_id=1, source_target_pairs={{0,16},{16,0},{1,17},{17,1},{2,18},{18,2},{3,19},{19,3},{4,20},{20... | collective-permute-start | bytes 1179656 | tf_op jit(solution)/shard_map/ppermute | solution.py:51
  101.7 5.3 %all-to-all-done.5 = f32[16,48,128]{2,1,0:T(8,128)S(1)} async-done(((f32[16,48,128]{2,1,0:T(8,128)}), f32[16,48,128]{2,1,0:T(8,128)S(1)}, u32[]{:S(2)}, u32[]{:S(2)}) %all-to-all-start.5) | async-done | bytes 393248 | tf_op jit(solution)/shard_map/all_to_all | solution.py:43
  107.7 3.4 %all-to-all-start.6 = ((f32[8,48,128]{2,1,0:T(8,128)}), f32[8,48,128]{2,1,0:T(8,128)S(1)}, u32[]{:S(2)}, u32[]{:S(2)}) async-start(f32[8,48,128]{2,1,0:T(8,128)} %broadcast_in_dim.25), calls=%async_computation.6 | async-start | bytes 393216 | tf_op jit(solution)/shard_map/all_to_all | solution.py:43
  111.1 2.1 %collective-permute-done.9.refs_9_ = f32[4,2,48,256]{3,2,1,0:T(8,128)S(1)} collective-permute-done((f32[4,2,48,256]{3,2,1,0:T(8,128)}, f32[4,2,48,256]{3,2,1,0:T(8,128)S(1)}, u32[]{:S(2)}, u32[]{:S(2)}) %collective-permute-start.9) | collective-permute-done | bytes 393248 | tf_op jit(solution)/shard_map/ppermute | solution.py:51
  113.2 3.4 %all-to-all-done.6.refs_4_ = f32[8,48,128]{2,1,0:T(8,128)S(1)} async-done(((f32[8,48,128]{2,1,0:T(8,128)}), f32[8,48,128]{2,1,0:T(8,128)S(1)}, u32[]{:S(2)}, u32[]{:S(2)}) %all-to-all-start.6) | async-done | bytes 196640 | tf_op jit(solution)/shard_map/all_to_all | solution.py:43
  116.5 5.0 %shard_map.85 = (f32[8,48,512]{2,1,0:T(8,128)}, f32[2,4,48,256]{3,2,1,0:T(8,128)}, f32[2,4,48,256]{3,2,1,0:T(8,128)}) custom-call(s32[1,14]{1,0:T(1,128)} %refs_0_.4, s32[1,14]{1,0:T(1,128)} %copy-done.7, s32[1,14]{1,0:T(1,128)} %copy-done.8, s32[1,14]{1,0:T(1,128)} %copy-done.9, f32[8,48,128]{2,1,0:T(8,128)S(1)} %all-to-all-done.6.refs_4_, ...), custom_call_target="tpu_custom_call" | custom-call | tf_op jit(solution)/shard_map/pallas_call | solution.py:72
  121.6 3.6 %all-to-all-start.7 = ((f32[8,48,512]{2,1,0:T(8,128)}), f32[8,48,512]{2,1,0:T(8,128)S(1)}, u32[]{:S(2)}, u32[]{:S(2)}) async-start(f32[8,48,512]{2,1,0:T(8,128)} %get-tuple-element.62), calls=%async_computation.7 | async-start | bytes 1572864 | tf_op jit(solution)/shard_map/all_to_all | solution.py:43
  125.1 1.4 collective-permute-start.10
  126.5 7.0 %all-to-all-done.7.refs_4_ = f32[8,48,512]{2,1,0:T(8,128)S(1)} async-done(((f32[8,48,512]{2,1,0:T(8,128)}), f32[8,48,512]{2,1,0:T(8,128)S(1)}, u32[]{:S(2)}, u32[]{:S(2)}) %all-to-all-start.7) | async-done | bytes 786464 | tf_op jit(solution)/shard_map/all_to_all | solution.py:43
  133.5 3.5 %shard_map.86 = (f32[8,48,256]{2,1,0:T(8,128)}, f32[4,48,256]{2,1,0:T(8,128)}) custom-call(s32[1,14]{1,0:T(1,128)} %refs_0_.4, s32[1,14]{1,0:T(1,128)} %copy-done.7, s32[1,14]{1,0:T(1,128)} %copy-done.8, s32[1,14]{1,0:T(1,128)} %copy-done.9, f32[8,48,512]{2,1,0:T(8,128)S(1)} %all-to-all-done.7.refs_4_, bf16[2,256,512]{2,1,0:T(8,128)(2,1)S(1)} %shard_map.77.refs_7_.refs_5_, ...), custom_call_target="tpu_custom_call" | custom-call | tf_op jit(solution)/shard_map/pallas_call | solution.py:72
  137.0 10.5 %all-to-all-start.8 = ((f32[8,48,256]{2,1,0:T(8,128)}), f32[8,48,256]{2,1,0:T(8,128)S(1)}, u32[]{:S(2)}, u32[]{:S(2)}) async-start(f32[8,48,256]{2,1,0:T(8,128)} %get-tuple-element.64), calls=%async_computation.8 | async-start | bytes 786432 | tf_op jit(solution)/shard_map/all_to_all | solution.py:43
  147.5 2.0 %shard_map.87 = (f32[4,48,384]{2,1,0:T(8,128)}, f32[4,48,384]{2,1,0:T(8,128)}) custom-call(f32[4,48,256]{2,1,0:T(8,128)} %get-tuple-element.66.nearest_ref, f32[2,4,48,256]{3,2,1,0:T(8,128)} %get-tuple-element.67.kept_ref, f32[2,4,48,256]{3,2,1,0:T(8,128)S(1)} %collective-permute-done.10.other_ref), custom_call_target="tpu_custom_call" | custom-call | tf_op jit(solution)/shard_map/pallas_call | solution.py:72
  149.5 1.8 %collective-permute-done.11.other_ref = f32[4,48,384]{2,1,0:T(8,128)S(1)} collective-permute-done((f32[4,48,384]{2,1,0:T(8,128)}, f32[4,48,384]{2,1,0:T(8,128)S(1)}, u32[]{:S(2)}, u32[]{:S(2)}) %collective-permute-start.11) | collective-permute-done | bytes 294944 | tf_op jit(solution)/shard_map/ppermute | solution.py:47
  151.3 3.9 %all-to-all-done.8.received_ref = f32[8,48,256]{2,1,0:T(8,128)S(1)} async-done(((f32[8,48,256]{2,1,0:T(8,128)}), f32[8,48,256]{2,1,0:T(8,128)S(1)}, u32[]{:S(2)}, u32[]{:S(2)}) %all-to-all-start.8) | async-done | bytes 393248 | tf_op jit(solution)/shard_map/all_to_all | solution.py:43
  155.2 1.5 shard_map.88
  156.7 13.6 %all_to_all.50.received_ref = f32[4,96,512]{2,1,0:T(8,128)S(1)} all-to-all(f32[4,96,512]{2,1,0:T(8,128)S(1)} %shard_map.88), channel_id=1, replica_groups=mesh['z'=4,'y1'=2,'y0'=2,'c'=2,'x'=4] {'x'}, dimensions={0} | all-to-all | bytes 1572864 | tf_op jit(solution)/shard_map/all_to_all | solution.py:43
  (40 shorter events, 4.4 us)
Async XLA Ops:
  1.9 30.8 %collective-permute-start.6 = (f32[128,7680]{1,0:T(8,128)}, f32[128,7680]{1,0:T(8,128)}, u32[]{:S(2)}, u32[]{:S(2)}) collective-permute-start(f32[128,7680]{1,0:T(8,128)} %bitcast.11), channel_id=1, source_target_pairs={{0,4},{4,0},{1,5},{5,1},{2,6},{6,2},{3,7},{7,3},{8,12},{12,8},{9,1... | collective-permute-start | bytes 11796488 | tf_op jit(solution)/shard_map/ppermute | solution.py:47
  3.3 16.2 %all-to-all-start = ((f32[4,96,512]{2,1,0:T(8,128)}), f32[4,96,512]{2,1,0:T(8,128)S(1)}, u32[]{:S(2)}, u32[]{:S(2)}) async-start(f32[4,96,512]{2,1,0:T(8,128)} %broadcast_in_dim.11.refs_1_), calls=%async_computation | async-start | bytes 1572864 | tf_op jit(solution)/shard_map/all_to_all | solution.py:43
  7.4 23.3 %collective-permute-start.4 = (f32[128,1792]{1,0:T(8,128)}, f32[128,1792]{1,0:T(8,128)S(1)}, u32[]{:S(2)}, u32[]{:S(2)}) collective-permute-start(f32[128,1792]{1,0:T(8,128)} %bitcast.15), channel_id=1, source_target_pairs={{0,4},{4,0},{1,5},{5,1},{2,6},{6,2},{3,7},{7,3},{8,12},{12,8},{9,1... | collective-permute-start | bytes 2752520 | tf_op jit(solution)/shard_map/ppermute | solution.py:47
  8.8 6.6 %collective-permute-start = (f32[2,512]{1,0:T(2,128)S(1)}, f32[2,512]{1,0:T(2,128)S(1)}, u32[]{:S(2)}, u32[]{:S(2)}) collective-permute-start(f32[2,512]{1,0:T(2,128)S(1)} %shard_map.73.factors_ref.refs_5_), channel_id=1, source_target_pairs={{0,4},{4,0},{1,5},{5,1},{2,6},{6,2},{3,7},{7,3},{8,12},{12,8},{9,1... | collective-permute-start | bytes 12296 | tf_op jit(solution)/shard_map/ppermute | solution.py:47
  9.1 4.9 %collective-permute-start.1 = (s32[1,14]{1,0:T(1,128)}, s32[1,14]{1,0:T(1,128)S(1)}, u32[]{:S(2)}, u32[]{:S(2)}) collective-permute-start(s32[1,14]{1,0:T(1,128)} %refs_0_.4), channel_id=1, source_target_pairs={{0,8},{4,20},{8,0},{12,28},{16,24},{20,4},{24,16},{28,12},{1,9},{5... | collective-permute-start | bytes 176 | tf_op jit(solution)/shard_map/ppermute | solution.py:497
  12.0 2.6 %collective-permute-start.2 = (s32[1,14]{1,0:T(1,128)}, s32[1,14]{1,0:T(1,128)S(1)}, u32[]{:S(2)}, u32[]{:S(2)}) collective-permute-start(s32[1,14]{1,0:T(1,128)} %refs_0_.4), channel_id=1, source_target_pairs={{0,4},{4,0},{1,5},{5,1},{2,6},{6,2},{3,7},{7,3},{8,12},{12,8},{9,1... | collective-permute-start | bytes 176 | tf_op jit(solution)/shard_map/ppermute | solution.py:47
  14.0 21.1 %copy-start.7 = (s32[1,14]{1,0:T(1,128)}, s32[1,14]{1,0:T(1,128)S(1)}, u32[]{:S(2)}) copy-start(s32[1,14]{1,0:T(1,128)S(1)} %collective-permute-done.1.refs_1_) | copy-start | bytes 172
  14.0 1.4 collective-permute-start.3
  14.6 20.5 %copy-start.8 = (s32[1,14]{1,0:T(1,128)}, s32[1,14]{1,0:T(1,128)S(1)}, u32[]{:S(2)}) copy-start(s32[1,14]{1,0:T(1,128)S(1)} %collective-permute-done.2.refs_2_) | copy-start | bytes 172
  15.4 19.7 %copy-start.9 = (s32[1,14]{1,0:T(1,128)}, s32[1,14]{1,0:T(1,128)S(1)}, u32[]{:S(2)}) copy-start(s32[1,14]{1,0:T(1,128)S(1)} %collective-permute-done.3.refs_3_) | copy-start | bytes 172
  20.9 2.6 %collective-permute-start.5 = (f32[4,48,384]{2,1,0:T(8,128)}, f32[4,48,384]{2,1,0:T(8,128)S(1)}, u32[]{:S(2)}, u32[]{:S(2)}) collective-permute-start(f32[4,48,384]{2,1,0:T(8,128)} %get-tuple-element.47), channel_id=1, source_target_pairs={{0,4},{4,0},{1,5},{5,1},{2,6},{6,2},{3,7},{7,3},{8,12},{12,8},{9,1... | collective-permute-start | bytes 884744 | tf_op jit(solution)/shard_map/ppermute | solution.py:47
  25.4 17.8 %collective-permute-start.7 = (f32[4,96,256]{2,1,0:T(8,128)}, f32[4,96,256]{2,1,0:T(8,128)S(1)}, u32[]{:S(2)}, u32[]{:S(2)}) collective-permute-start(f32[4,96,256]{2,1,0:T(8,128)} %get-tuple-element.51.refs_8_), channel_id=1, source_target_pairs={{0,8},{8,0},{1,9},{9,1},{2,10},{10,2},{3,11},{11,3},{4,12},{12,4},... | collective-permute-start | bytes 1179656 | tf_op jit(solution)/shard_map/ppermute | solution.py:51
  26.7 12.0 %all-to-all-start.1 = ((f32[8,48,256]{2,1,0:T(8,128)}), f32[8,48,256]{2,1,0:T(8,128)S(1)}, u32[]{:S(2)}, u32[]{:S(2)}) async-start(f32[8,48,256]{2,1,0:T(8,128)} %get-tuple-element.43.refs_2_), calls=%async_computation.1 | async-start | bytes 786432 | tf_op jit(solution)/shard_map/all_to_all | solution.py:43
  30.7 1.0 copy-start
  32.8 14.0 %copy-start.4 = (f32[4,96,256]{2,1,0:T(8,128)S(1)}, f32[4,96,256]{2,1,0:T(8,128)}, u32[]{:S(2)}) copy-start(f32[4,96,256]{2,1,0:T(8,128)} %get-tuple-element.51.refs_8_) | copy-start | bytes 1179652
  43.2 9.2 %copy-start.2 = (f32[4,96,256]{2,1,0:T(8,128)}, f32[4,96,256]{2,1,0:T(8,128)S(1)}, u32[]{:S(2)}) copy-start(f32[4,96,256]{2,1,0:T(8,128)S(1)} %collective-permute-done.7.refs_9_) | copy-start | bytes 1179652
  43.2 16.1 %all-to-all-start.2 = ((f32[8,48,512]{2,1,0:T(8,128)}), f32[8,48,512]{2,1,0:T(8,128)S(1)}, u32[]{:S(2)}, u32[]{:S(2)}) async-start(f32[8,48,512]{2,1,0:T(8,128)} %get-tuple-element.52.refs_2_), calls=%async_computation.2 | async-start | bytes 1572864 | tf_op jit(solution)/shard_map/all_to_all | solution.py:43
  53.7 14.2 %copy-start.3 = (f32[4,96,256]{2,1,0:T(8,128)S(1)}, f32[4,96,256]{2,1,0:T(8,128)}, u32[]{:S(2)}) copy-start(f32[4,96,256]{2,1,0:T(8,128)} %copy-done.2) | copy-start | bytes 1179652
  64.5 9.0 %all-to-all-start.3 = ((f32[8,48,128]{2,1,0:T(8,128)}), f32[8,48,128]{2,1,0:T(8,128)S(1)}, u32[]{:S(2)}, u32[]{:S(2)}) async-start(f32[8,48,128]{2,1,0:T(8,128)} %get-tuple-element.55), calls=%async_computation.3 | async-start | bytes 393216 | tf_op jit(solution)/shard_map/all_to_all | solution.py:43
  67.9 19.4 %copy-start.1 = (f32[2,4,96,128]{3,2,1,0:T(8,128)}, f32[2,4,96,128]{3,2,1,0:T(8,128)S(1)}, u32[]{:S(2)}) copy-start(f32[2,4,96,128]{3,2,1,0:T(8,128)S(1)} %pad_maximum_fusion.refs_7_) | copy-start | bytes 1179652
  67.9 13.4 %collective-permute-start.8 = (f32[2,4,96,128]{3,2,1,0:T(8,128)S(1)}, f32[2,4,96,128]{3,2,1,0:T(8,128)S(1)}, u32[]{:S(2)}, u32[]{:S(2)}) collective-permute-start(f32[2,4,96,128]{3,2,1,0:T(8,128)S(1)} %pad_maximum_fusion.refs_7_), channel_id=1, source_target_pairs={{0,16},{16,0},{1,17},{17,1},{2,18},{18,2},{3,19},{19,3},{4,20},{20... | collective-permute-start | bytes 1179656 | tf_op jit(solution)/shard_map/ppermute | solution.py:51
  74.2 13.1 %all-to-all-start.4 = ((f32[16,48,128]{2,1,0:T(8,128)}), f32[16,48,128]{2,1,0:T(8,128)S(1)}, u32[]{:S(2)}, u32[]{:S(2)}) async-start(f32[16,48,128]{2,1,0:T(8,128)} %broadcast_in_dim.24), calls=%async_computation.4 | async-start | bytes 786432 | tf_op jit(solution)/shard_map/all_to_all | solution.py:43
  81.4 6.0 %copy-start.5 = (f32[2,4,96,128]{3,2,1,0:T(8,128)}, f32[2,4,96,128]{3,2,1,0:T(8,128)S(1)}, u32[]{:S(2)}) copy-start(f32[2,4,96,128]{3,2,1,0:T(8,128)S(1)} %collective-permute-done.8.refs_8_) | copy-start | bytes 1179652
  95.1 11.8 %all-to-all-start.5 = ((f32[16,48,128]{2,1,0:T(8,128)}), f32[16,48,128]{2,1,0:T(8,128)S(1)}, u32[]{:S(2)}, u32[]{:S(2)}) async-start(f32[16,48,128]{2,1,0:T(8,128)} %get-tuple-element.58), calls=%async_computation.5 | async-start | bytes 786432 | tf_op jit(solution)/shard_map/all_to_all | solution.py:43
  98.8 14.4 %collective-permute-start.9 = (f32[4,2,48,256]{3,2,1,0:T(8,128)}, f32[4,2,48,256]{3,2,1,0:T(8,128)S(1)}, u32[]{:S(2)}, u32[]{:S(2)}) collective-permute-start(f32[4,2,48,256]{3,2,1,0:T(8,128)} %get-tuple-element.61), channel_id=1, source_target_pairs={{0,16},{16,0},{1,17},{17,1},{2,18},{18,2},{3,19},{19,3},{4,20},{20... | collective-permute-start | bytes 1179656 | tf_op jit(solution)/shard_map/ppermute | solution.py:51
  107.7 8.9 %all-to-all-start.6 = ((f32[8,48,128]{2,1,0:T(8,128)}), f32[8,48,128]{2,1,0:T(8,128)S(1)}, u32[]{:S(2)}, u32[]{:S(2)}) async-start(f32[8,48,128]{2,1,0:T(8,128)} %broadcast_in_dim.25), calls=%async_computation.6 | async-start | bytes 393216 | tf_op jit(solution)/shard_map/all_to_all | solution.py:43
  113.2 3.4 %copy-start.6 = (f32[4,2,48,256]{3,2,1,0:T(8,128)}, f32[4,2,48,256]{3,2,1,0:T(8,128)S(1)}, u32[]{:S(2)}) copy-start(f32[4,2,48,256]{3,2,1,0:T(8,128)S(1)} %collective-permute-done.9.refs_9_) | copy-start | bytes 1179652
  121.6 11.9 %all-to-all-start.7 = ((f32[8,48,512]{2,1,0:T(8,128)}), f32[8,48,512]{2,1,0:T(8,128)S(1)}, u32[]{:S(2)}, u32[]{:S(2)}) async-start(f32[8,48,512]{2,1,0:T(8,128)} %get-tuple-element.62), calls=%async_computation.7 | async-start | bytes 1572864 | tf_op jit(solution)/shard_map/all_to_all | solution.py:43
  125.1 22.4 %collective-permute-start.10 = (f32[2,4,48,256]{3,2,1,0:T(8,128)}, f32[2,4,48,256]{3,2,1,0:T(8,128)S(1)}, u32[]{:S(2)}, u32[]{:S(2)}) collective-permute-start(f32[2,4,48,256]{3,2,1,0:T(8,128)} %get-tuple-element.68), channel_id=1, source_target_pairs={{0,8},{8,0},{1,9},{9,1},{2,10},{10,2},{3,11},{11,3},{4,12},{12,4},... | collective-permute-start | bytes 1179656 | tf_op jit(solution)/shard_map/ppermute | solution.py:51
  137.0 18.2 %all-to-all-start.8 = ((f32[8,48,256]{2,1,0:T(8,128)}), f32[8,48,256]{2,1,0:T(8,128)S(1)}, u32[]{:S(2)}, u32[]{:S(2)}) async-start(f32[8,48,256]{2,1,0:T(8,128)} %get-tuple-element.64), calls=%async_computation.8 | async-start | bytes 786432 | tf_op jit(solution)/shard_map/all_to_all | solution.py:43
  149.5 1.8 %collective-permute-start.11 = (f32[4,48,384]{2,1,0:T(8,128)}, f32[4,48,384]{2,1,0:T(8,128)S(1)}, u32[]{:S(2)}, u32[]{:S(2)}) collective-permute-start(f32[4,48,384]{2,1,0:T(8,128)} %get-tuple-element.70), channel_id=1, source_target_pairs={{0,4},{4,0},{1,5},{5,1},{2,6},{6,2},{3,7},{7,3},{8,12},{12,8},{9,1... | collective-permute-start | bytes 884744 | tf_op jit(solution)/shard_map/ppermute | solution.py:47
